TPU v7x, 128 devices: a whole 4x4x4 slice. The times are simulated.
128 devices in a mesh: lat: 8 (over z, y_hi), lon: 16 (over x, y_lo, core).
Axes of the slice: x: 4, y: 4 (y_hi: 2, y_lo: 2; y = y_hi * 2 + y_lo), z: 4, core: 2. Of those that a mesh axis runs over, the one named last changes fastest.
Arguments:
- tokens: bfloat16 [96, 384, 512], P('lat', 'lon'), may hold values from -100 to 100
- fine_gain: float32 [512], replicated, may hold values from 0.5 to 1.5
- fine_qkv: bfloat16 [512, 768], replicated, may hold values from -20 to 20
- fine_proj: bfloat16 [256, 512], replicated, may hold values from -0.375 to 0.375
- merge_gain: float32 [2048], replicated, may hold values from 0.5 to 1.5
- merge_weight: bfloat16 [2048, 512], replicated, may hold values from -0.125 to 0.125
- coarse_gain: float32 [512], replicated, may hold values from 0.5 to 1.5
- coarse_qkv: bfloat16 [512, 1536], replicated, may hold values from -20 to 20
- coarse_proj: bfloat16 [512, 512], replicated, may hold values from -0.25 to 0.25
- cotangent: bfloat16 [48, 192, 512], P('lat', 'lon'), may hold values from -6 to 6
Outputs:
- output: bfloat16 [48, 192, 512], P('lat', 'lon')
- grad_tokens: bfloat16 [96, 384, 512], P('lat', 'lon')
- grad_fine_gain: float32 [512], P(('lat', 'lon'))
- grad_fine_qkv: float32 [512, 768], P(('lat', 'lon'))
- grad_fine_proj: float32 [256, 512], P(('lat', 'lon'))
- grad_merge_gain: float32 [2048], P(('lat', 'lon'))
- grad_merge_weight: float32 [2048, 512], P(('lat', 'lon'))
- grad_coarse_gain: float32 [512], P(('lat', 'lon'))
- grad_coarse_qkv: float32 [512, 1536], P(('lat', 'lon'))
- grad_coarse_proj: float32 [512, 512], P(('lat', 'lon'))
All inputs are finite; a program needn't handle non-finite values.
Results may differ from a plain program's by a relative error of at most 0.028.
Values may be sent and summed in bfloat16 or wider, within the bound.
No kernel may reach another device: no remote copies, remote signals or barrier semaphores. Data moves between devices by JAX's collectives and lax.ppermute only.
A program may use at most 128 MiB of HBM per device.

v0:
```python
import jax
import jax.numpy as jnp
from jax import lax
from jax.sharding import PartitionSpec as P

HF = 4
HC = 8
WLAT = 6
WLON = 12
SLAT = 3
SLON = 6


EPSILON = 1e-05


def from_behind(value, axis, steps):
    count = lax.axis_size(axis)
    pairs = [(source, (source + steps) % count) for source in range(count)]
    return lax.ppermute(value, axis, pairs)


def in_blocks(shard, dim, peers):
    dims = shard.shape
    tiles = shard.reshape(*dims[:dim], peers, dims[dim] // peers, *dims[dim + 1 :])
    return jnp.moveaxis(tiles, dim, 0)


def sum_together(arrays, axis, dims):
    peers = lax.axis_size(axis)
    tiles = [in_blocks(a, dim, peers) for a, dim in zip(arrays, dims)]
    lines = jnp.concatenate([b.reshape(peers, -1) for b in tiles], axis=1)
    span = max(16, -(-lines.shape[1] // 1024) * 8)
    lines = jnp.pad(lines, ((0, 0), (0, span * 128 - lines.shape[1]))).reshape(-1, 128)
    flat, at, finished = (lax.psum_scatter(lines, axis, tiled=True).reshape(-1), 0, [])
    for b in tiles:
        part = b[0]
        finished.append(flat[at : at + part.size].reshape(part.shape))
        at += part.size
    return tuple(finished)


def layer_norm(values, gains):
    center = jnp.mean(values, axis=-1, keepdims=True)
    shifted = values - center
    spread = jnp.mean(shifted * shifted, axis=-1, keepdims=True)
    return shifted * lax.rsqrt(spread + EPSILON) * gains


def window_attention(packed, row_offset, total_rows, head_count):
    row_count, col_count = (packed.shape[0], packed.shape[1])
    head_size = packed.shape[2] // (3 * head_count)
    lat_windows = row_count // WLAT
    lon_windows = col_count // WLON
    grouped = packed.reshape(lat_windows, WLAT, lon_windows, WLON, 3, head_count, head_size)
    grouped = grouped.transpose(4, 0, 2, 5, 1, 3, 6).reshape(
        3, lat_windows, lon_windows, head_count, WLAT * WLON, head_size
    )
    queries = grouped[0].astype(jnp.float32)
    keys_all = grouped[1].astype(jnp.float32)
    values_all = grouped[2].astype(jnp.float32)
    scores = jnp.einsum("abhqd,abhkd->abhqk", queries, keys_all) * head_size ** (-0.5)
    row_index = row_offset + jnp.arange(row_count, dtype=jnp.int32)
    region = (row_index >= total_rows - SLAT).reshape(lat_windows, WLAT)
    region = jnp.broadcast_to(region[:, :, None], (lat_windows, WLAT, WLON)).reshape(
        lat_windows, WLAT * WLON
    )
    allowed = region[:, None, None, :, None] == region[:, None, None, None, :]
    scores = jnp.where(allowed, scores, -1000000000.0)
    largest = jnp.max(scores, axis=-1, keepdims=True)
    exponent = jnp.exp(scores - largest)
    attn_weights = (exponent / jnp.sum(exponent, axis=-1, keepdims=True)).astype(jnp.bfloat16)
    mixed_out = jnp.einsum(
        "abhqk,abhkd->abhqd", attn_weights.astype(jnp.float32), values_all
    ).astype(jnp.bfloat16)
    mixed_out = mixed_out.reshape(lat_windows, lon_windows, head_count, WLAT, WLON, head_size)
    return mixed_out.transpose(0, 3, 1, 4, 2, 5).reshape(
        row_count, col_count, head_count * head_size
    )


def block_forward(rolled, gains, weight_qkv, weight_proj, row_offset, total_rows, head_count):
    normed = layer_norm(rolled.astype(jnp.float32), gains).astype(jnp.bfloat16)
    packed = jnp.dot(normed, weight_qkv, preferred_element_type=jnp.float32).astype(jnp.bfloat16)
    mixed_out = window_attention(packed, row_offset, total_rows, head_count)
    added = jnp.dot(mixed_out, weight_proj, preferred_element_type=jnp.float32)
    result = (rolled.astype(jnp.float32) + added).astype(jnp.bfloat16)
    return (result, (normed, packed, mixed_out))


def block_backward(
    grad_out, rolled, gains, weight_qkv, weight_proj, saved, row_offset, total_rows, head_count
):
    normed, packed, mixed_out = saved
    grad_mixed = lax.dot_general(
        grad_out, weight_proj, (((2,), (1,)), ((), ())), preferred_element_type=jnp.float32
    ).astype(jnp.bfloat16)
    grad_proj = lax.dot_general(
        mixed_out, grad_out, (((0, 1), (0, 1)), ((), ())), preferred_element_type=jnp.float32
    )

    def attend_only(packed_in):
        return window_attention(packed_in, row_offset, total_rows, head_count)

    _, attend_back = jax.vjp(attend_only, packed)
    grad_packed = attend_back(grad_mixed)[0]
    grad_normed = lax.dot_general(
        grad_packed, weight_qkv, (((2,), (1,)), ((), ())), preferred_element_type=jnp.float32
    ).astype(jnp.bfloat16)
    grad_qkv = lax.dot_general(
        normed, grad_packed, (((0, 1), (0, 1)), ((), ())), preferred_element_type=jnp.float32
    )
    _, norm_back = jax.vjp(layer_norm, rolled.astype(jnp.float32), gains)
    grad_input, grad_gain = norm_back(grad_normed.astype(jnp.float32))
    grad_rolled = (grad_out.astype(jnp.float32) + grad_input).astype(jnp.bfloat16)
    return (grad_rolled, grad_gain, grad_qkv, grad_proj)


def merge_tokens(patch_grid):
    row_count, col_count, breadth = patch_grid.shape
    reshaped = patch_grid.reshape(row_count // 2, 2, col_count // 2, 2, breadth)
    return reshaped.transpose(0, 2, 3, 1, 4).reshape(row_count // 2, col_count // 2, 4 * breadth)


def split_tokens(merged_grid):
    row_count, col_count, breadth = merged_grid.shape
    narrow = breadth // 4
    reshaped = merged_grid.reshape(row_count, col_count, 2, 2, narrow)
    return reshaped.transpose(0, 3, 1, 2, 4).reshape(2 * row_count, 2 * col_count, narrow)


def merge_forward(fine_grid, gains, weight):
    packed_grid = merge_tokens(fine_grid)
    normed = layer_norm(packed_grid.astype(jnp.float32), gains).astype(jnp.bfloat16)
    merged = jnp.dot(normed, weight, preferred_element_type=jnp.float32).astype(jnp.bfloat16)
    return (merged, (packed_grid, normed))


def merge_backward(grad_merged, saved, gains, weight):
    packed_grid, normed = saved
    grad_normed = lax.dot_general(
        grad_merged, weight, (((2,), (1,)), ((), ())), preferred_element_type=jnp.float32
    ).astype(jnp.bfloat16)
    grad_weight = lax.dot_general(
        normed, grad_merged, (((0, 1), (0, 1)), ((), ())), preferred_element_type=jnp.float32
    )
    _, norm_back = jax.vjp(layer_norm, packed_grid.astype(jnp.float32), gains)
    grad_packed, grad_gain = norm_back(grad_normed.astype(jnp.float32))
    return (split_tokens(grad_packed.astype(jnp.bfloat16)), grad_gain, grad_weight)


def rotate_ahead(patch_grid):
    arrived = from_behind(patch_grid[:SLAT], "lat", -1)
    patch_grid = jnp.concatenate([patch_grid[SLAT:], arrived], axis=0)
    arrived = from_behind(patch_grid[:, :SLON], "lon", -1)
    return jnp.concatenate([patch_grid[:, SLON:], arrived], axis=1)


def rotate_back(patch_grid):
    arrived = from_behind(patch_grid[-SLAT:], "lat", 1)
    patch_grid = jnp.concatenate([arrived, patch_grid[:-SLAT]], axis=0)
    arrived = from_behind(patch_grid[:, -SLON:], "lon", 1)
    return jnp.concatenate([arrived, patch_grid[:, :-SLON]], axis=1)


def local(
    tokens,
    fine_gain,
    fine_qkv,
    fine_proj,
    merge_gain,
    merge_weight,
    coarse_gain,
    coarse_qkv,
    coarse_proj,
    cotangent,
):
    fine_rows = tokens.shape[0]
    coarse_rows = fine_rows // 2
    lat_count = lax.axis_size("lat")
    lat_place = lax.axis_index("lat")
    fine_total = fine_rows * lat_count
    coarse_total = coarse_rows * lat_count
    fine_offset = lat_place * fine_rows
    coarse_offset = lat_place * coarse_rows
    grad_scale = (fine_total * tokens.shape[1] * lax.axis_size("lon") // 4) ** (-0.5)
    rolled_fine = rotate_ahead(tokens)
    fine_result, fine_saved = block_forward(
        rolled_fine, fine_gain, fine_qkv, fine_proj, fine_offset, fine_total, HF
    )
    fine_grid = rotate_back(fine_result)
    merged, merge_saved = merge_forward(fine_grid, merge_gain, merge_weight)
    rolled_coarse = rotate_ahead(merged)
    coarse_result, coarse_saved = block_forward(
        rolled_coarse, coarse_gain, coarse_qkv, coarse_proj, coarse_offset, coarse_total, HC
    )
    output = rotate_back(coarse_result)
    grad_coarse_out = rotate_ahead(cotangent)
    grad_rolled_coarse, coarse_gain_sum, coarse_qkv_sum, coarse_proj_sum = block_backward(
        grad_coarse_out,
        rolled_coarse,
        coarse_gain,
        coarse_qkv,
        coarse_proj,
        coarse_saved,
        coarse_offset,
        coarse_total,
        HC,
    )
    grad_merged = rotate_back(grad_rolled_coarse)
    grad_fine_grid, merge_gain_sum, merge_weight_sum = merge_backward(
        grad_merged, merge_saved, merge_gain, merge_weight
    )
    grad_fine_out = rotate_ahead(grad_fine_grid)
    grad_rolled_fine, fine_gain_sum, fine_qkv_sum, fine_proj_sum = block_backward(
        grad_fine_out,
        rolled_fine,
        fine_gain,
        fine_qkv,
        fine_proj,
        fine_saved,
        fine_offset,
        fine_total,
        HF,
    )
    grad_tokens = rotate_back(grad_rolled_fine)
    summed = sum_together(
        (
            fine_gain_sum,
            fine_qkv_sum,
            fine_proj_sum,
            merge_gain_sum,
            merge_weight_sum,
            coarse_gain_sum,
            coarse_qkv_sum,
            coarse_proj_sum,
        ),
        ("lat", "lon"),
        (0, 0, 0, 0, 0, 0, 0, 0),
    )
    fine_gain_sum, fine_qkv_sum, fine_proj_sum = (summed[0], summed[1], summed[2])
    merge_gain_sum, merge_weight_sum = (summed[3], summed[4])
    coarse_gain_sum, coarse_qkv_sum, coarse_proj_sum = (summed[5], summed[6], summed[7])
    return (
        output,
        grad_tokens,
        fine_gain_sum * grad_scale,
        fine_qkv_sum * grad_scale,
        fine_proj_sum * grad_scale,
        merge_gain_sum * grad_scale,
        merge_weight_sum * grad_scale,
        coarse_gain_sum * grad_scale,
        coarse_qkv_sum * grad_scale,
        coarse_proj_sum * grad_scale,
    )


def solution(mesh):
    return jax.shard_map(
        local,
        mesh=mesh,
        in_specs=(
            P("lat", "lon", None),
            P(),
            P(),
            P(),
            P(),
            P(),
            P(),
            P(),
            P(),
            P("lat", "lon", None),
        ),
        out_specs=(
            P("lat", "lon", None),
            P("lat", "lon", None),
            P(("lat", "lon")),
            P(("lat", "lon"), None),
            P(("lat", "lon"), None),
            P(("lat", "lon")),
            P(("lat", "lon"), None),
            P(("lat", "lon")),
            P(("lat", "lon"), None),
            P(("lat", "lon"), None),
        ),
        check_vma=False,
    )
```

profile of v0, /device:TPU:0, one launch (start us, length us, event | category | flops | bytes accessed | tf_op | source)
XLA Modules:
  0.0 853.0 jit_solution(14642206828945929549)
XLA Ops:
  8.3 6.8 collective-permute-start
  15.1 1.4 fusion.111
  18.3 2.7 collective-permute-start.1
  21.1 2.1 collective-permute-done.1
  23.7 1.6 convolution_convert_fusion.2
  25.3 1.4 reshape.409
  26.7 1.5 copy.158
  29.8 1.4 fusion.114
  35.8 3.0 collective-permute-start.2
  39.5 4.4 collective-permute-done.2
  44.6 3.8 collective-permute-start.9
  48.4 1.7 collective-permute-done.3
  51.0 1.4 reshape.435
  55.1 1.6 reshape.433
  57.9 1.8 collective-permute-start.4
  60.9 2.9 collective-permute-done.4
  68.2 1.9 convolution_convert_fusion.1
  72.9 1.7 copy.121
  76.2 1.3 fusion.115
  80.5 2.0 copy.133
  82.5 1.9 copy.134
  84.4 2.0 reshape.421
  86.5 2.2 fusion.67
  90.3 1.7 collective-permute-start.10
  92.0 2.3 convolution_bitcast_fusion
  96.4 2.0 collective-permute-done.10
  99.3 2.1 convolution_bitcast_fusion.3
  102.1 2.7 reshape_reshape.19
  104.8 4.8 reshape_reshape.18
  109.6 1.7 multiply_reduce_fusion.1
  112.7 2.1 collective-permute-start.12
  114.8 3.6 convolution_bitcast_fusion.1
  119.1 5.0 reshape_reshape.17
  124.1 3.6 collective-permute-start.13
  127.8 2.1 collective-permute-done.13
  134.6 1.7 fusion.40
  136.3 1.9 convolution_bitcast_fusion.2
  139.4 1.7 reshape_reshape.15
  141.1 13.8 %concatenate.67 = f32[128,20504]{1,0:T(8,128)} concatenate(f32[128,4]{1,0:T(8,128)S(1)} %reshape.428, f32[128,3072]{1,0:T(8,128)S(1)} %reshape_reshape.15, f32[128,1024]{1,0:T(8,128)S(1)} %reshape_reshape.16, f32[128,16]{1,0:T(8,128)S(1)} %copy-done.25, f32[128,8192]{1,0:T(8,128)} %reshape_reshape.17, f32[128,4]{1,0:T(8,128)S(1)} %copy-done.24, f32[128,6144]{1,0:T(8,128)} %reshape_reshape.18, ...), dimensions={1} | concatenate | bytes 20996096 | tf_op jit(solution)/shard_map/concatenate | solution.py:32
  154.9 9.2 %pad.28 = f32[128,21504]{1,0:T(8,128)} pad(f32[128,20504]{1,0:T(8,128)} %concatenate.67, f32[]{:T(128)} %constant.25.clone.1), padding=0_0x0_1000 | pad | bytes 21508100 | tf_op jit(solution)/shard_map/jit(_pad)/pad | solution.py:34
  164.1 10.9 %reshape.431 = f32[21504,128]{1,0:T(8,128)} reshape(f32[128,21504]{1,0:T(8,128)} %pad.28) | data formatting | bytes 22020096 | tf_op jit(solution)/shard_map/reshape | solution.py:34
  176.0 1.4 fusion.16
  177.4 2.4 collective-permute-start.6
  181.1 4.4 collective-permute-done.6
  185.7 3.5 collective-permute-done.14
  189.4 1.9 collective-permute-done.7
  192.0 3.5 collective-permute-done.15
  196.3 640.2 %reduce-scatter.5.cloned.1.call-done = f32[168,128]{1,0:T(8,128)} async-done(((f32[21504,128]{1,0:T(8,128)}), f32[168,128]{1,0:T(8,128)}) %reduce-scatter.5.cloned.1.call-update) | async-done | bytes 86032
  (262 shorter events, 55.1 us)
Async XLA Ops:
  7.2 49.5 %copy-start = (bf16[2048,512]{1,0:T(8,128)(2,1)S(1)}, bf16[2048,512]{1,0:T(8,128)(2,1)}, u32[]{:S(2)}) copy-start(bf16[2048,512]{1,0:T(8,128)(2,1)} %param.15) | copy-start | bytes 6291460
  7.2 16.4 %copy-start.55 = (f32[512]{0:T(512)S(1)}, f32[512]{0:T(512)}, u32[]{:S(2)}) copy-start(f32[512]{0:T(512)} %param.11) | copy-start | bytes 6148
  7.2 829.3 %reduce-scatter.5.cloned.1.call-start = ((), (), s32[]{:S(2)}) async-start(), calls=%async_computation.1 | async-start | bytes 11096064
  8.3 10.0 %collective-permute-start = (bf16[3,24,512]{2,1,0:T(8,128)(2,1)S(1)}, bf16[3,24,512]{2,1,0:T(8,128)(2,1)S(1)}, u32[]{:S(2)}, u32[]{:S(2)}) collective-permute-start(bf16[3,24,512]{2,1,0:T(8,128)(2,1)S(1)} %slice.151), channel_id=1, source_target_pairs={{0,112},{16,0},{32,16},{48,32},{64,48},{80,64},{96,80},{112,96},{1... | collective-permute-start | bytes 221192 | tf_op jit(solution)/shard_map/ppermute | solution.py:20
  16.5 27.5 %collective-permute-start.8 = (bf16[3,12,512]{2,1,0:T(8,128)(2,1)}, bf16[3,12,512]{2,1,0:T(8,128)(2,1)S(1)}, u32[]{:S(2)}, u32[]{:S(2)}) collective-permute-start(bf16[3,12,512]{2,1,0:T(8,128)(2,1)} %get-tuple-element.39), channel_id=1, source_target_pairs={{0,112},{16,0},{32,16},{48,32},{64,48},{80,64},{96,80},{112,96},{1... | collective-permute-start | bytes 110600 | tf_op jit(solution)/shard_map/ppermute | solution.py:20
  18.1 11.7 %copy-start.39 = (pred[2,72,72]{1,2,0:T(8,128)(4,1)}, pred[2,72,72]{1,2,0:T(8,128)(4,1)S(1)}, u32[]{:S(2)}) copy-start(pred[2,72,72]{1,2,0:T(8,128)(4,1)S(1)} %broadcast_compare_fusion.2) | copy-start | bytes 31108
  18.3 4.9 collective-permute-start.1
  23.6 4.5 copy-start.37
  23.6 4.5 copy-start.33
  29.6 3.5 copy-start.21
  29.8 3.2 copy-start.10
  32.1 3.7 copy-start.35
  34.5 17.9 %copy-start.12 = (bf16[12,24,256]{2,1,0:T(8,128)(2,1)}, bf16[12,24,256]{2,1,0:T(8,128)(2,1)S(1)}, u32[]{:S(2)}) copy-start(bf16[12,24,256]{2,1,0:T(8,128)(2,1)S(1)} %reshape.411) | copy-start | bytes 442372
  35.8 8.0 collective-permute-start.2
  43.9 6.2 collective-permute-start.3
  44.6 15.1 %copy-start.17 = (bf16[6,6,512]{2,1,0:T(8,128)(2,1)}, bf16[6,6,512]{2,1,0:T(8,128)(2,1)S(1)}, u32[]{:S(2)}) copy-start(bf16[6,6,512]{2,1,0:T(8,128)(2,1)S(1)} %get-tuple-element.36) | copy-start | bytes 110596
  44.6 15.0 %collective-permute-start.9 = (bf16[6,6,512]{2,1,0:T(8,128)(2,1)}, bf16[6,6,512]{2,1,0:T(8,128)(2,1)S(1)}, u32[]{:S(2)}, u32[]{:S(2)}) collective-permute-start(bf16[6,6,512]{2,1,0:T(8,128)(2,1)} %get-tuple-element.37), channel_id=1, source_target_pairs={{0,15},{1,0},{2,1},{3,2},{4,3},{5,4},{6,5},{7,6},{8,7},{9,8},{10,9... | collective-permute-start | bytes 110600 | tf_op jit(solution)/shard_map/ppermute | solution.py:20
  52.5 4.3 copy-start.28
  53.3 4.0 copy-start.41
  56.7 2.9 copy-start.7
  57.9 5.9 collective-permute-start.4
  59.7 7.3 copy-start.26
  64.6 2.0 collective-permute-start.5
  76.1 3.0 copy-start.14
  76.1 3.0 copy-start.53
  86.4 3.0 copy-start.18
  86.4 3.0 copy-start.27
  86.5 5.6 copy-start.8
  90.3 4.1 copy-start.30
  90.3 4.1 copy-start.46
  90.3 4.1 copy-start.48
  90.3 8.1 collective-permute-start.10
  94.3 7.1 copy-start.59
  96.4 8.4 copy-start.19
  99.2 10.4 %collective-permute-start.11 = (bf16[6,6,512]{2,1,0:T(8,128)(2,1)S(1)}, bf16[6,6,512]{2,1,0:T(8,128)(2,1)S(1)}, u32[]{:S(2)}, u32[]{:S(2)}) collective-permute-start(bf16[6,6,512]{2,1,0:T(8,128)(2,1)S(1)} %fusion.85), channel_id=1, source_target_pairs={{0,1},{1,2},{2,3},{3,4},{4,5},{5,6},{6,7},{7,8},{8,9},{9,10},{10,1... | collective-permute-start | bytes 110600 | tf_op jit(solution)/shard_map/ppermute | solution.py:20
  104.8 4.8 copy-start.16
  112.7 11.4 %collective-permute-start.12 = (bf16[3,24,512]{2,1,0:T(8,128)(2,1)S(1)}, bf16[3,24,512]{2,1,0:T(8,128)(2,1)S(1)}, u32[]{:S(2)}, u32[]{:S(2)}) collective-permute-start(bf16[3,24,512]{2,1,0:T(8,128)(2,1)S(1)} %slice.221), channel_id=1, source_target_pairs={{0,112},{16,0},{32,16},{48,32},{64,48},{80,64},{96,80},{112,96},{1... | collective-permute-start | bytes 221192 | tf_op jit(solution)/shard_map/ppermute | solution.py:20
  119.1 10.8 %copy-start.23 = (bf16[256,512]{1,0:T(8,128)(2,1)S(1)}, bf16[256,512]{1,0:T(8,128)(2,1)}, u32[]{:S(2)}) copy-start(bf16[256,512]{1,0:T(8,128)(2,1)} %param.13) | copy-start | bytes 786436
  124.0 6.7 copy-start.3
  124.0 6.7 copy-start.36
  124.1 5.8 collective-permute-start.13
  129.9 8.3 copy-start.32
  175.1 4.8 copy-start.58
  176.0 670.1 %copy-start.1 = (bf16[2048,512]{1,0:T(8,128)(2,1)S(1)}, bf16[2048,512]{1,0:T(8,128)(2,1)}, u32[]{:S(2)}) copy-start(bf16[2048,512]{1,0:T(8,128)(2,1)} %param.15) | copy-start | bytes 6291460
  177.4 8.1 collective-permute-start.6
  181.0 8.2 collective-permute-start.14
  185.6 5.7 collective-permute-start.7
  189.3 6.2 collective-permute-start.15
  (30 other events, 45.4 us)
Sparse Core Ops, SparseCore 0:
  175.2 661.2 reduce-scatter.4
where the time goes:
time: 855 us; the launch traced here: 853 us
  waiting for transfers between devices  669 us (78%)
  local copies, waits for them, and re-layouts  89.1 us (10%)
  matrix products  30.6 us (4%)
  starting transfers between devices  29 us (3%)
  other arithmetic  20 us (2%)
  between operations  15.2 us (2%)
    unnamed x2, waiting for transfers between devices  640 us
    ppermute x16, waiting for transfers between devices, from_behind(): return lax.ppermute(value, axis, pairs)  29 us
    ppermute x16, starting transfers between devices, from_behind(): return lax.ppermute(value, axis, pairs)  28.9 us
  transfers between devices with their start and end apart: 17, of which 12 were waited for; matrix products, arithmetic and copies ran while one was open for 6% of the time, Pallas kernels for 0%

commit v1 on v0

--- a/solution.py
+++ b/solution.py
@@ -26,13 +26,15 @@
     return jnp.moveaxis(tiles, dim, 0)
 
 
-def sum_together(arrays, axis, dims):
-    peers = lax.axis_size(axis)
+def sum_together(arrays, axes, dims):
+    peers = lax.axis_size(axes)
     tiles = [in_blocks(a, dim, peers) for a, dim in zip(arrays, dims)]
-    lines = jnp.concatenate([b.reshape(peers, -1) for b in tiles], axis=1)
-    span = max(16, -(-lines.shape[1] // 1024) * 8)
-    lines = jnp.pad(lines, ((0, 0), (0, span * 128 - lines.shape[1]))).reshape(-1, 128)
-    flat, at, finished = (lax.psum_scatter(lines, axis, tiled=True).reshape(-1), 0, [])
+    lines = jnp.concatenate([b.reshape(peers, -1).astype(jnp.bfloat16) for b in tiles], axis=1)
+    span = -(-lines.shape[1] // 2048) * 16
+    lines = jnp.pad(lines, ((0, 0), (0, span * 128 - lines.shape[1]))).reshape(peers, span, 128)
+    arrived = lax.all_to_all(lines, axes, 0, 0)
+    flat = jnp.sum(arrived.astype(jnp.float32), axis=0).reshape(-1)
+    at, finished = 0, []
     for b in tiles:
         part = b[0]
         finished.append(flat[at : at + part.size].reshape(part.shape))

time: 855 us -> 262 us (0.31)
  waiting for transfers between devices: 669 us -> 88.6 us
  between operations: 15.2 us -> 1.69 us
  local copies, waits for them, and re-layouts: 89.1 us -> 80.2 us
    unnamed x2 -> x0, waiting for transfers between devices: 640 us -> none
    ppermute x16, waiting for transfers between devices: 29 us -> 88.6 us  [from_behind(): return lax.ppermute(value, axis, pairs)]
    convert_element_type x0 -> x8, local copies, waits for them, and re-layouts: none -> 14.4 us  [sum_together(): b.reshape(peers, -1).astype(jnp.bfloat16)]
    another operation x9 -> x4, local copies, waits for them, and re-layouts: 18.4 us -> 4.95 us  [the longest x5 14.3 us: sum_together(): lines = jnp.concatenate([b.reshape(peers, -1) for b in tiles], axis=1)]
    reshape x4 -> x0, local copies, waits for them, and re-layouts: 12.5 us -> none  [the longest x1 10.9 us: sum_together(): jnp.pad(lines, ((0, 0), (0, span * 128 - lines.shape[1]))).reshape(-1, 128)]
    pad x1 -> x0, local copies, waits for them, and re-layouts: 9.22 us -> none  [sum_together(): jnp.pad(lines, ((0, 0), (0, span * 128 - lines.shape[1]))).reshape(-1, 128)]
  transfers between devices with their start and end apart: 17 -> 17, of which waited for: 12 -> 11; matrix products, arithmetic and copies ran while one was open for 6% -> 18% of each run, Pallas kernels for 0% -> 0%
where the time goes in v1:
time: 262 us; the launch traced here: 259 us
  waiting for transfers between devices  88.6 us (34%)
  local copies, waits for them, and re-layouts  80.2 us (31%)
  starting transfers between devices  36.6 us (14%)
  matrix products  31 us (12%)
  other arithmetic  21.2 us (8%)
    ppermute x16, waiting for transfers between devices, from_behind(): return lax.ppermute(value, axis, pairs)  88.6 us
    ppermute x16, starting transfers between devices, from_behind(): return lax.ppermute(value, axis, pairs)  29.5 us
    convert_element_type x8, local copies, waits for them, and re-layouts, sum_together(): b.reshape(peers, -1).astype(jnp.bfloat16)  14.4 us
    concatenate x1, local copies, waits for them, and re-layouts, sum_together(): jnp.concatenate([b.reshape(peers, -1).astype(jnp.bfloat16) for b in tiles...  12.1 us
    unnamed x126, local copies, waits for them, and re-layouts  11.4 us
    reshape x6, local copies, waits for them, and re-layouts, window_attention(): packed.reshape(lat_windows, WLAT, lon_windows, WLON, 3, head_count, head_...  9.98 us
    all_to_all x1, starting transfers between devices, sum_together(): arrived = lax.all_to_all(lines, axes, 0, 0)  7.09 us
  transfers between devices with their start and end apart: 17, of which 11 were waited for; matrix products, arithmetic and copies ran while one was open for 18% of the time, Pallas kernels for 0%

profile of v1, /device:TPU:0, one launch (start us, length us, event | category | flops | bytes accessed | tf_op | source)
XLA Modules:
  0.0 259.3 jit_solution(1060268671051543129)
XLA Ops:
  1.7 6.8 %collective-permute-start = (bf16[3,24,512]{2,1,0:T(8,128)(2,1)S(1)}, bf16[3,24,512]{2,1,0:T(8,128)(2,1)S(1)}, u32[]{:S(2)}, u32[]{:S(2)}) collective-permute-start(bf16[3,24,512]{2,1,0:T(8,128)(2,1)S(1)} %slice.151), channel_id=1, source_target_pairs={{0,112},{16,0},{32,16},{48,32},{64,48},{80,64},{96,80},{112,96},{1... | collective-permute-start | bytes 221192 | tf_op jit(solution)/shard_map/ppermute | solution.py:20
  8.5 1.5 fusion.114
  12.8 2.7 %collective-permute-start.1 = (bf16[12,6,512]{2,1,0:T(8,128)(2,1)S(1)}, bf16[12,6,512]{2,1,0:T(8,128)(2,1)S(1)}, u32[]{:S(2)}, u32[]{:S(2)}) collective-permute-start(bf16[12,6,512]{2,1,0:T(8,128)(2,1)S(1)} %pad_maximum_fusion.9), channel_id=1, source_target_pairs={{0,15},{1,0},{2,1},{3,2},{4,3},{5,4},{6,5},{7,6},{8,7},{9,8},{10,9... | collective-permute-start | bytes 221192 | tf_op jit(solution)/shard_map/ppermute | solution.py:20
  15.6 2.1 collective-permute-done.1
  20.6 1.9 reshape.411
  29.5 3.0 %collective-permute-start.2 = (bf16[3,24,512]{2,1,0:T(8,128)(2,1)S(1)}, bf16[3,24,512]{2,1,0:T(8,128)(2,1)S(1)}, u32[]{:S(2)}, u32[]{:S(2)}) collective-permute-start(bf16[3,24,512]{2,1,0:T(8,128)(2,1)S(1)} %slice.201), channel_id=1, source_target_pairs={{0,16},{16,32},{32,48},{48,64},{64,80},{80,96},{96,112},{112,0},{1... | collective-permute-start | bytes 221192 | tf_op jit(solution)/shard_map/ppermute | solution.py:20
  33.2 4.4 %collective-permute-done.2 = bf16[3,24,512]{2,1,0:T(8,128)(2,1)S(1)} collective-permute-done((bf16[3,24,512]{2,1,0:T(8,128)(2,1)S(1)}, bf16[3,24,512]{2,1,0:T(8,128)(2,1)S(1)}, u32[]{:S(2)}, u32[]{:S(2)}) %collective-permute-start.2) | collective-permute-done | bytes 73760 | tf_op jit(solution)/shard_map/ppermute | solution.py:20
  38.5 3.9 %collective-permute-start.9 = (bf16[6,6,512]{2,1,0:T(8,128)(2,1)S(1)}, bf16[6,6,512]{2,1,0:T(8,128)(2,1)S(1)}, u32[]{:S(2)}, u32[]{:S(2)}) collective-permute-start(bf16[6,6,512]{2,1,0:T(8,128)(2,1)S(1)} %get-tuple-element.37), channel_id=1, source_target_pairs={{0,15},{1,0},{2,1},{3,2},{4,3},{5,4},{6,5},{7,6},{8,7},{9,8},{10,9... | collective-permute-start | bytes 110600 | tf_op jit(solution)/shard_map/ppermute | solution.py:20
  44.7 1.4 reshape.434
  48.3 1.6 reshape.432
  52.9 4.0 %collective-permute-done.4 = bf16[3,12,512]{2,1,0:T(8,128)(2,1)} collective-permute-done((bf16[3,12,512]{2,1,0:T(8,128)(2,1)}, bf16[3,12,512]{2,1,0:T(8,128)(2,1)}, u32[]{:S(2)}, u32[]{:S(2)}) %collective-permute-start.4) | collective-permute-done | bytes 36896 | tf_op jit(solution)/shard_map/ppermute | solution.py:20
  60.1 2.6 convolution_convert_fusion.1
  62.7 2.0 reshape.414
  66.6 1.7 copy.85
  68.3 1.7 copy.87
  75.1 2.0 copy.97
  77.2 1.9 copy.98
  79.0 2.0 reshape.423
  81.1 2.2 fusion.70
  84.0 1.5 fusion.68
  87.0 1.7 collective-permute-start.10
  88.7 1.8 fusion
  93.2 1.8 collective-permute-done.10
  95.9 2.0 fusion.8
  98.6 2.2 convert_element_type.287
  100.8 3.7 %convert_element_type.285 = bf16[128,6144]{1,0:T(8,128)(2,1)} reshape(bf16[512,1536]{1,0:T(8,128)(2,1)} %fusion) | data formatting | bytes 3145728 | tf_op jit(solution)/shard_map/convert_element_type | solution.py:32
  104.6 1.7 multiply_reduce_fusion.1
  107.6 2.2 collective-permute-start.12
  109.8 3.0 %bitcast_convert_fusion = bf16[2048,512]{1,0:T(8,128)(2,1)} fusion(f32[6,12,2048]{2,1,0:T(8,128)S(1)} %reshape.432, f32[2048]{0:T(1024)S(1)} %copy-done.30, f32[6,12]{1,0:T(8,128)S(1)} %copy-done.46, f32[6,12]{1,0:T(8,128)S(1)} %broadcast_multiply_fusion.2, bf16[3,12,512]{2,1,0:T(8,128)(2,1)S(1)} %get-tuple-element.35, ...), kind=kOutput, calls=%fused_computation.2 | convolution fusion | flops 152854528 | bytes 2806336 | tf_op jit(solution)/shard_map/dot_general | solution.py:146
  113.5 2.9 %convert_element_type.281 = bf16[128,8192]{1,0:T(8,128)(2,1)S(1)} reshape(bf16[2048,512]{1,0:T(8,128)(2,1)} %bitcast_convert_fusion) | data formatting | bytes 4194304 | tf_op jit(solution)/shard_map/convert_element_type | solution.py:32
  116.5 3.6 %collective-permute-start.13 = (bf16[12,6,512]{2,1,0:T(8,128)(2,1)S(1)}, bf16[12,6,512]{2,1,0:T(8,128)(2,1)S(1)}, u32[]{:S(2)}, u32[]{:S(2)}) collective-permute-start(bf16[12,6,512]{2,1,0:T(8,128)(2,1)S(1)} %pad_maximum_fusion.5), channel_id=1, source_target_pairs={{0,15},{1,0},{2,1},{3,2},{4,3},{5,4},{6,5},{7,6},{8,7},{9,8},{10,9... | collective-permute-start | bytes 221192 | tf_op jit(solution)/shard_map/ppermute | solution.py:20
  120.2 2.1 collective-permute-done.13
  128.0 1.5 convert_reduce_fusion.2
  131.8 1.6 copy.109
  134.6 2.6 reshape.429
  137.2 1.8 fusion.43
  139.1 1.6 bitcast_convert_fusion.1
  141.8 1.8 convert_element_type.277
  144.1 2.3 convert_element_type.275
  146.4 12.1 %concatenate.67 = bf16[128,20504]{1,0:T(8,128)(2,1)} concatenate(bf16[128,4]{1,0:T(8,128)(2,1)S(1)} %convert_element_type.273, bf16[128,3072]{1,0:T(8,128)(2,1)} %convert_element_type.275, bf16[128,1024]{1,0:T(8,128)(2,1)} %convert_element_type.277, bf16[128,16]{1,0:T(8,128)(2,1)S(1)} %copy-done.34, bf16[128,8192]{1,0:T(8,128)(2,1)S(1)} %convert_element_type.281, ...), dimensions={1} | concatenate | bytes 10498048 | tf_op jit(solution)/shard_map/concatenate | solution.py:32
  158.4 3.1 %pad_bitcast_fusion = bf16[16,8,176,128]{3,1,2,0:T(8,128)(2,1)S(1)} fusion(bf16[128,20504]{1,0:T(8,128)(2,1)} %concatenate.67), kind=kLoop, calls=%fused_computation.1 | loop fusion | bytes 11016192
  161.6 3.8 %copy.119 = bf16[16,8,176,128]{3,2,1,0:T(8,128)(2,1)} copy(bf16[16,8,176,128]{3,1,2,0:T(8,128)(2,1)S(1)} %pad_bitcast_fusion) | data formatting | bytes 11534336
  165.4 7.1 %all-to-all-start = ((bf16[128,176,128]{2,1,0:T(8,128)(2,1)}), bf16[128,176,128]{2,1,0:T(8,128)(2,1)}, u32[]{:S(2)}, u32[]{:S(2)}) async-start(bf16[128,176,128]{2,1,0:T(8,128)(2,1)} %bitcast.144), calls=%async_computation | async-start | bytes 11534336 | tf_op jit(solution)/shard_map/all_to_all | solution.py:35
  172.8 2.5 collective-permute-start.6
  175.6 1.6 collective-permute-start.14
  177.2 65.7 %collective-permute-done.6 = bf16[3,12,512]{2,1,0:T(8,128)(2,1)S(1)} collective-permute-done((bf16[3,12,512]{2,1,0:T(8,128)(2,1)S(1)}, bf16[3,12,512]{2,1,0:T(8,128)(2,1)S(1)}, u32[]{:S(2)}, u32[]{:S(2)}) %collective-permute-start.6) | collective-permute-done | bytes 36896 | tf_op jit(solution)/shard_map/ppermute | solution.py:20
  244.3 4.4 %collective-permute-done.7 = bf16[6,6,512]{2,1,0:T(8,128)(2,1)S(1)} collective-permute-done((bf16[6,6,512]{2,1,0:T(8,128)(2,1)S(1)}, bf16[6,6,512]{2,1,0:T(8,128)(2,1)S(1)}, u32[]{:S(2)}, u32[]{:S(2)}) %collective-permute-start.7) | collective-permute-done | bytes 36896 | tf_op jit(solution)/shard_map/ppermute | solution.py:20
  251.2 3.5 %convert_reduce_fusion = f32[176,128]{1,0:T(8,128)S(1)} fusion(bf16[128,176,128]{2,1,0:T(8,128)(2,1)} %all-to-all-done), kind=kLoop, calls=%fused_computation | loop fusion | flops 5744640 | bytes 5857280 | tf_op jit(solution)/shard_map/reduce_sum | solution.py:36
  (264 shorter events, 61.1 us)
Async XLA Ops:
  0.6 49.2 %copy-start = (bf16[2048,512]{1,0:T(8,128)(2,1)S(1)}, bf16[2048,512]{1,0:T(8,128)(2,1)}, u32[]{:S(2)}) copy-start(bf16[2048,512]{1,0:T(8,128)(2,1)} %param.15) | copy-start | bytes 6291460
  0.7 18.7 %copy-start.57 = (f32[512]{0:T(512)S(1)}, f32[512]{0:T(512)}, u32[]{:S(2)}) copy-start(f32[512]{0:T(512)} %param.11) | copy-start | bytes 6148
  0.7 18.7 %copy-start.16 = (bf16[512,768]{1,0:T(8,128)(2,1)S(1)}, bf16[512,768]{1,0:T(8,128)(2,1)}, u32[]{:S(2)}) copy-start(bf16[512,768]{1,0:T(8,128)(2,1)} %param.12) | copy-start | bytes 2359300
  1.7 11.1 %collective-permute-start = (bf16[3,24,512]{2,1,0:T(8,128)(2,1)S(1)}, bf16[3,24,512]{2,1,0:T(8,128)(2,1)S(1)}, u32[]{:S(2)}, u32[]{:S(2)}) collective-permute-start(bf16[3,24,512]{2,1,0:T(8,128)(2,1)S(1)} %slice.151), channel_id=1, source_target_pairs={{0,112},{16,0},{32,16},{48,32},{64,48},{80,64},{96,80},{112,96},{1... | collective-permute-start | bytes 221192 | tf_op jit(solution)/shard_map/ppermute | solution.py:20
  10.0 27.7 %collective-permute-start.8 = (bf16[3,12,512]{2,1,0:T(8,128)(2,1)}, bf16[3,12,512]{2,1,0:T(8,128)(2,1)}, u32[]{:S(2)}, u32[]{:S(2)}) collective-permute-start(bf16[3,12,512]{2,1,0:T(8,128)(2,1)} %get-tuple-element.39), channel_id=1, source_target_pairs={{0,112},{16,0},{32,16},{48,32},{64,48},{80,64},{96,80},{112,96},{1... | collective-permute-start | bytes 110600 | tf_op jit(solution)/shard_map/ppermute | solution.py:20
  12.8 4.9 %collective-permute-start.1 = (bf16[12,6,512]{2,1,0:T(8,128)(2,1)S(1)}, bf16[12,6,512]{2,1,0:T(8,128)(2,1)S(1)}, u32[]{:S(2)}, u32[]{:S(2)}) collective-permute-start(bf16[12,6,512]{2,1,0:T(8,128)(2,1)S(1)} %pad_maximum_fusion.9), channel_id=1, source_target_pairs={{0,15},{1,0},{2,1},{3,2},{4,3},{5,4},{6,5},{7,6},{8,7},{9,8},{10,9... | collective-permute-start | bytes 221192 | tf_op jit(solution)/shard_map/ppermute | solution.py:20
  25.7 6.7 %copy-start.61 = (pred[72]{0:T(512)(128)(4,1)S(1)}, pred[72]{0:T(512)(128)(4,1)}, u32[]{:S(2)}) copy-start(pred[72]{0:T(512)(128)(4,1)} %eq.35) | copy-start | bytes 220
  27.9 9.8 %copy-start.27 = (bf16[3,12,512]{2,1,0:T(8,128)(2,1)S(1)}, bf16[3,12,512]{2,1,0:T(8,128)(2,1)}, u32[]{:S(2)}) copy-start(bf16[3,12,512]{2,1,0:T(8,128)(2,1)} %get-tuple-element.38) | copy-start | bytes 110596
  28.2 15.6 %copy-start.17 = (bf16[12,24,256]{2,1,0:T(8,128)(2,1)}, bf16[12,24,256]{2,1,0:T(8,128)(2,1)S(1)}, u32[]{:S(2)}) copy-start(bf16[12,24,256]{2,1,0:T(8,128)(2,1)S(1)} %reshape.413) | copy-start | bytes 442372
  29.5 8.0 %collective-permute-start.2 = (bf16[3,24,512]{2,1,0:T(8,128)(2,1)S(1)}, bf16[3,24,512]{2,1,0:T(8,128)(2,1)S(1)}, u32[]{:S(2)}, u32[]{:S(2)}) collective-permute-start(bf16[3,24,512]{2,1,0:T(8,128)(2,1)S(1)} %slice.201), channel_id=1, source_target_pairs={{0,16},{16,32},{32,48},{48,64},{64,80},{80,96},{96,112},{112,0},{1... | collective-permute-start | bytes 221192 | tf_op jit(solution)/shard_map/ppermute | solution.py:20
  37.6 6.2 %collective-permute-start.3 = (bf16[12,6,512]{2,1,0:T(8,128)(2,1)S(1)}, bf16[12,6,512]{2,1,0:T(8,128)(2,1)S(1)}, u32[]{:S(2)}, u32[]{:S(2)}) collective-permute-start(bf16[12,6,512]{2,1,0:T(8,128)(2,1)S(1)} %pad_maximum_fusion.8), channel_id=1, source_target_pairs={{0,1},{1,2},{2,3},{3,4},{4,5},{5,6},{6,7},{7,8},{8,9},{9,10},{10,1... | collective-permute-start | bytes 221192 | tf_op jit(solution)/shard_map/ppermute | solution.py:20
  38.5 13.2 %copy-start.21 = (bf16[6,6,512]{2,1,0:T(8,128)(2,1)}, bf16[6,6,512]{2,1,0:T(8,128)(2,1)S(1)}, u32[]{:S(2)}) copy-start(bf16[6,6,512]{2,1,0:T(8,128)(2,1)S(1)} %get-tuple-element.36) | copy-start | bytes 110596
  38.5 13.2 %collective-permute-start.9 = (bf16[6,6,512]{2,1,0:T(8,128)(2,1)S(1)}, bf16[6,6,512]{2,1,0:T(8,128)(2,1)S(1)}, u32[]{:S(2)}, u32[]{:S(2)}) collective-permute-start(bf16[6,6,512]{2,1,0:T(8,128)(2,1)S(1)} %get-tuple-element.37), channel_id=1, source_target_pairs={{0,15},{1,0},{2,1},{3,2},{4,3},{5,4},{6,5},{7,6},{8,7},{9,8},{10,9... | collective-permute-start | bytes 110600 | tf_op jit(solution)/shard_map/ppermute | solution.py:20
  46.1 3.7 %copy-start.30 = (f32[2048]{0:T(1024)S(1)}, f32[2048]{0:T(1024)}, u32[]{:S(2)}) copy-start(f32[2048]{0:T(1024)} %param.14) | copy-start | bytes 24580
  46.9 3.4 %copy-start.51 = (f32[6,12]{1,0:T(8,128)}, f32[6,12]{1,0:T(8,128)S(1)}, u32[]{:S(2)}) copy-start(f32[6,12]{1,0:T(8,128)S(1)} %multiply_reduce_fusion.3) | copy-start | bytes 868
  51.0 5.9 %collective-permute-start.4 = (bf16[3,12,512]{2,1,0:T(8,128)(2,1)}, bf16[3,12,512]{2,1,0:T(8,128)(2,1)}, u32[]{:S(2)}, u32[]{:S(2)}) collective-permute-start(bf16[3,12,512]{2,1,0:T(8,128)(2,1)} %get-tuple-element.45), channel_id=1, source_target_pairs={{0,112},{16,0},{32,16},{48,32},{64,48},{80,64},{96,80},{112,96},{1... | collective-permute-start | bytes 110600 | tf_op jit(solution)/shard_map/ppermute | solution.py:20
  51.7 13.1 %copy-start.28 = (bf16[6,6,512]{2,1,0:T(8,128)(2,1)}, bf16[6,6,512]{2,1,0:T(8,128)(2,1)S(1)}, u32[]{:S(2)}) copy-start(bf16[6,6,512]{2,1,0:T(8,128)(2,1)S(1)} %collective-permute-done.9) | copy-start | bytes 110596
  57.8 2.0 collective-permute-start.5
  60.1 6.5 %copy-start.53 = (f32[6,12]{1,0:T(8,128)}, f32[6,12]{1,0:T(8,128)S(1)}, u32[]{:S(2)}) copy-start(f32[6,12]{1,0:T(8,128)S(1)} %fusion.69) | copy-start | bytes 868
  60.1 6.5 %copy-start.47 = (f32[6,12]{1,0:T(8,128)}, f32[6,12]{1,0:T(8,128)S(1)}, u32[]{:S(2)}) copy-start(f32[6,12]{1,0:T(8,128)S(1)} %fusion.96) | copy-start | bytes 868
  62.7 8.0 %copy-start.54 = (pred[72,72]{0,1:T(8,128)(4,1)S(1)}, pred[72,72]{0,1:T(8,128)(4,1)}, u32[]{:S(2)}) copy-start(pred[72,72]{0,1:T(8,128)(4,1)} %broadcast_compare_fusion.3) | copy-start | bytes 15556
  74.1 7.0 %copy-start.55 = (f32[512]{0:T(512)S(1)}, f32[512]{0:T(512)}, u32[]{:S(2)}) copy-start(f32[512]{0:T(512)} %param.16) | copy-start | bytes 6148
  77.2 6.9 %copy-start.48 = (f32[6,12]{1,0:T(8,128)S(1)}, f32[6,12]{1,0:T(8,128)}, u32[]{:S(2)}) copy-start(f32[6,12]{1,0:T(8,128)} %copy-done.47) | copy-start | bytes 868
  77.2 8.4 %copy-start.22 = (bf16[6,6,512]{2,1,0:T(8,128)(2,1)S(1)}, bf16[6,6,512]{2,1,0:T(8,128)(2,1)}, u32[]{:S(2)}) copy-start(bf16[6,6,512]{2,1,0:T(8,128)(2,1)} %copy-done.21) | copy-start | bytes 110596
  77.2 8.4 %copy-start.29 = (bf16[6,6,512]{2,1,0:T(8,128)(2,1)S(1)}, bf16[6,6,512]{2,1,0:T(8,128)(2,1)}, u32[]{:S(2)}) copy-start(bf16[6,6,512]{2,1,0:T(8,128)(2,1)} %copy-done.28) | copy-start | bytes 110596
  81.1 7.6 %copy-start.9 = (bf16[6,12,1536]{2,1,0:T(8,128)(2,1)S(1)}, bf16[6,12,1536]{2,1,0:T(8,128)(2,1)}, u32[]{:S(2)}) copy-start(bf16[6,12,1536]{2,1,0:T(8,128)(2,1)} %reshape.423) | copy-start | bytes 663556
  81.1 7.6 %copy-start.56 = (f32[512]{0:T(512)S(1)}, f32[512]{0:T(512)}, u32[]{:S(2)}) copy-start(f32[512]{0:T(512)} %param.16) | copy-start | bytes 6148
  87.0 3.5 %copy-start.5 = (f32[8,72,72]{1,2,0:T(8,128)S(1)}, f32[8,72,72]{1,2,0:T(8,128)}, u32[]{:S(2)}) copy-start(f32[8,72,72]{1,2,0:T(8,128)} %copy-done.4) | copy-start | bytes 497668
  87.0 8.0 %collective-permute-start.10 = (bf16[3,12,512]{2,1,0:T(8,128)(2,1)}, bf16[3,12,512]{2,1,0:T(8,128)(2,1)}, u32[]{:S(2)}, u32[]{:S(2)}) collective-permute-start(bf16[3,12,512]{2,1,0:T(8,128)(2,1)} %get-tuple-element.34), channel_id=1, source_target_pairs={{0,16},{16,32},{32,48},{48,64},{64,80},{80,96},{96,112},{112,0},{1... | collective-permute-start | bytes 110600 | tf_op jit(solution)/shard_map/ppermute | solution.py:20
  90.5 7.4 %copy-start.60 = (bf16[512]{0:T(512)(128)(2,1)S(1)}, bf16[512]{0:T(512)(128)(2,1)}, u32[]{:S(2)}) copy-start(bf16[512]{0:T(512)(128)(2,1)} %get-tuple-element.14) | copy-start | bytes 3076
  95.8 8.8 %collective-permute-start.11 = (bf16[6,6,512]{2,1,0:T(8,128)(2,1)S(1)}, bf16[6,6,512]{2,1,0:T(8,128)(2,1)S(1)}, u32[]{:S(2)}, u32[]{:S(2)}) collective-permute-start(bf16[6,6,512]{2,1,0:T(8,128)(2,1)S(1)} %fusion.88), channel_id=1, source_target_pairs={{0,1},{1,2},{2,3},{3,4},{4,5},{5,6},{6,7},{7,8},{8,9},{9,10},{10,1... | collective-permute-start | bytes 110600 | tf_op jit(solution)/shard_map/ppermute | solution.py:20
  107.6 8.8 %collective-permute-start.12 = (bf16[3,24,512]{2,1,0:T(8,128)(2,1)S(1)}, bf16[3,24,512]{2,1,0:T(8,128)(2,1)S(1)}, u32[]{:S(2)}, u32[]{:S(2)}) collective-permute-start(bf16[3,24,512]{2,1,0:T(8,128)(2,1)S(1)} %slice.221), channel_id=1, source_target_pairs={{0,112},{16,0},{32,16},{48,32},{64,48},{80,64},{96,80},{112,96},{1... | collective-permute-start | bytes 221192 | tf_op jit(solution)/shard_map/ppermute | solution.py:20
  116.4 10.6 %copy-start.3 = (f32[2,2,4,72,72]{3,4,2,1,0:T(8,128)S(1)}, f32[2,2,4,72,72]{3,4,2,1,0:T(8,128)}, u32[]{:S(2)}) copy-start(f32[2,2,4,72,72]{3,4,2,1,0:T(8,128)} %copy-done.2) | copy-start | bytes 995332
  116.4 10.6 %copy-start.41 = (f32[2,2,4,72]{3,2,1,0:T(4,128)S(1)}, f32[2,2,4,72]{3,2,1,0:T(4,128)}, u32[]{:S(2)}) copy-start(f32[2,2,4,72]{3,2,1,0:T(4,128)} %copy-done.40) | copy-start | bytes 13828
  116.5 5.8 %collective-permute-start.13 = (bf16[12,6,512]{2,1,0:T(8,128)(2,1)S(1)}, bf16[12,6,512]{2,1,0:T(8,128)(2,1)S(1)}, u32[]{:S(2)}, u32[]{:S(2)}) collective-permute-start(bf16[12,6,512]{2,1,0:T(8,128)(2,1)S(1)} %pad_maximum_fusion.5), channel_id=1, source_target_pairs={{0,15},{1,0},{2,1},{3,2},{4,3},{5,4},{6,5},{7,6},{8,7},{9,8},{10,9... | collective-permute-start | bytes 221192 | tf_op jit(solution)/shard_map/ppermute | solution.py:20
  131.8 5.4 %copy-start.58 = (f32[512]{0:T(512)S(1)}, f32[512]{0:T(512)}, u32[]{:S(2)}) copy-start(f32[512]{0:T(512)} %param.11) | copy-start | bytes 6148
  134.6 4.5 %copy-start.39 = (f32[12,24]{1,0:T(8,128)S(1)}, f32[12,24]{1,0:T(8,128)}, u32[]{:S(2)}) copy-start(f32[12,24]{1,0:T(8,128)} %copy-done.38) | copy-start | bytes 3460
  141.8 4.6 %copy-start.33 = (bf16[128,4]{1,0:T(8,128)(2,1)S(1)}, bf16[128,4]{1,0:T(8,128)(2,1)}, u32[]{:S(2)}) copy-start(bf16[128,4]{1,0:T(8,128)(2,1)} %convert_element_type.283) | copy-start | bytes 3076
  141.8 4.6 %copy-start.34 = (bf16[128,16]{1,0:T(8,128)(2,1)S(1)}, bf16[128,16]{1,0:T(8,128)(2,1)}, u32[]{:S(2)}) copy-start(bf16[128,16]{1,0:T(8,128)(2,1)} %convert_element_type.279) | copy-start | bytes 12292
  165.4 7.1 %copy-start.7 = (bf16[512,512]{1,0:T(8,128)(2,1)S(1)}, bf16[512,512]{1,0:T(8,128)(2,1)}, u32[]{:S(2)}) copy-start(bf16[512,512]{1,0:T(8,128)(2,1)} %param.18) | copy-start | bytes 1572868
  165.4 7.1 %copy-start.23 = (bf16[6,12,512]{2,1,0:T(8,128)(2,1)S(1)}, bf16[6,12,512]{2,1,0:T(8,128)(2,1)}, u32[]{:S(2)}) copy-start(bf16[6,12,512]{2,1,0:T(8,128)(2,1)} %reshape.419) | copy-start | bytes 221188
  165.4 9.8 %copy-start.37 = (bf16[12,6,512]{2,1,0:T(8,128)(2,1)S(1)}, bf16[12,6,512]{2,1,0:T(8,128)(2,1)}, u32[]{:S(2)}) copy-start(bf16[12,6,512]{2,1,0:T(8,128)(2,1)} %copy-done.35) | copy-start | bytes 221188
  165.4 85.9 %all-to-all-start = ((bf16[128,176,128]{2,1,0:T(8,128)(2,1)}), bf16[128,176,128]{2,1,0:T(8,128)(2,1)}, u32[]{:S(2)}, u32[]{:S(2)}) async-start(bf16[128,176,128]{2,1,0:T(8,128)(2,1)} %bitcast.144), calls=%async_computation | async-start | bytes 11534336 | tf_op jit(solution)/shard_map/all_to_all | solution.py:35
  172.8 70.2 %collective-permute-start.6 = (bf16[3,12,512]{2,1,0:T(8,128)(2,1)S(1)}, bf16[3,12,512]{2,1,0:T(8,128)(2,1)S(1)}, u32[]{:S(2)}, u32[]{:S(2)}) collective-permute-start(bf16[3,12,512]{2,1,0:T(8,128)(2,1)S(1)} %get-tuple-element.40), channel_id=1, source_target_pairs={{0,16},{16,32},{32,48},{48,64},{64,80},{80,96},{96,112},{112,0},{1... | collective-permute-start | bytes 110600 | tf_op jit(solution)/shard_map/ppermute | solution.py:20
  175.6 68.6 %collective-permute-start.14 = (bf16[3,24,512]{2,1,0:T(8,128)(2,1)S(1)}, bf16[3,24,512]{2,1,0:T(8,128)(2,1)S(1)}, u32[]{:S(2)}, u32[]{:S(2)}) collective-permute-start(bf16[3,24,512]{2,1,0:T(8,128)(2,1)S(1)} %slice.224), channel_id=1, source_target_pairs={{0,16},{16,32},{32,48},{48,64},{64,80},{80,96},{96,112},{112,0},{1... | collective-permute-start | bytes 221192 | tf_op jit(solution)/shard_map/ppermute | solution.py:20
  243.0 5.7 %collective-permute-start.7 = (bf16[6,6,512]{2,1,0:T(8,128)(2,1)S(1)}, bf16[6,6,512]{2,1,0:T(8,128)(2,1)S(1)}, u32[]{:S(2)}, u32[]{:S(2)}) collective-permute-start(bf16[6,6,512]{2,1,0:T(8,128)(2,1)S(1)} %fusion.90), channel_id=1, source_target_pairs={{0,1},{1,2},{2,3},{3,4},{4,5},{5,6},{6,7},{7,8},{8,9},{9,10},{10,1... | collective-permute-start | bytes 110600 | tf_op jit(solution)/shard_map/ppermute | solution.py:20
  244.2 6.2 %collective-permute-start.15 = (bf16[12,6,512]{2,1,0:T(8,128)(2,1)S(1)}, bf16[12,6,512]{2,1,0:T(8,128)(2,1)S(1)}, u32[]{:S(2)}, u32[]{:S(2)}) collective-permute-start(bf16[12,6,512]{2,1,0:T(8,128)(2,1)S(1)} %pad_maximum_fusion.4), channel_id=1, source_target_pairs={{0,1},{1,2},{2,3},{3,4},{4,5},{5,6},{6,7},{7,8},{8,9},{9,10},{10,1... | collective-permute-start | bytes 221192 | tf_op jit(solution)/shard_map/ppermute | solution.py:20
  250.4 8.9 %copy-start.1 = (bf16[2048,512]{1,0:T(8,128)(2,1)S(1)}, bf16[2048,512]{1,0:T(8,128)(2,1)}, u32[]{:S(2)}) copy-start(bf16[2048,512]{1,0:T(8,128)(2,1)} %param.15) | copy-start | bytes 6291460
  (31 other events, 61.5 us)

commit v2 on v0

v2 whole, which is shorter than its diff:
```python
import jax
import jax.numpy as jnp
import numpy as np
from jax import lax
from jax.experimental import pallas as pl
from jax.experimental.pallas import tpu as pltpu
from jax.sharding import Mesh, PartitionSpec as P

D = 512
HF = 4
HC = 8
CELLS = 72
WINDOWS = 4
ROWS = 12
COLS = 24
EPSILON = 1e-05
NEGATIVE = -1000000000.0
LOWEST = -3.0e38
INTERPRET = False

F32 = jnp.float32
BF16 = jnp.bfloat16


def window_order():
    return [
        (6 * a + r, 12 * b + c) for a in range(2) for b in range(2) for r in range(6) for c in range(12)
    ]


def patch_order():
    return [
        (2 * r + dr, 2 * c + dc) for dc in range(2) for dr in range(2) for r in range(6) for c in range(12)
    ]


def plain_order(rows, cols):
    return [(r, c) for r in range(rows) for c in range(cols)]


def leading(rows, cols):
    half_r, half_c = (3, 6)
    side = [(r, c) for r in range(half_r, rows) for c in range(half_c)]
    edge = [(r, c) for r in range(half_r) for c in range(half_c, cols)]
    corner = [(r, c) for r in range(half_r) for c in range(half_c)]
    return (side, edge, corner)


def trailing(rows, cols):
    half_r, half_c = (3, 6)
    side = [(r, c) for r in range(rows - half_r) for c in range(cols - half_c, cols)]
    edge = [(r, c) for r in range(rows - half_r, rows) for c in range(cols - half_c)]
    corner = [(r, c) for r in range(rows - half_r, rows) for c in range(cols - half_c, cols)]
    return (side, edge, corner)


SLOTS = (80, 80, 48)
COARSE_AT = (56, 56, 24)
STACK = sum(SLOTS)


def pick(order, cells, places, total):
    where = {cell: i for i, cell in enumerate(order)}
    matrix = np.zeros((total, len(order)), np.float32)
    for place, cell in zip(places, cells):
        matrix[place, where[cell]] = 1.0
    return matrix


def send_matrix(order, pieces, starts):
    cells, places, at = [], [], 0
    for piece, start, slot in zip(pieces, starts, SLOTS):
        cells += piece
        places += [at + start + i for i in range(len(piece))]
        at += slot
    return pick(order, cells, places, STACK)


def take_matrices(own_order, out_cells, pieces, starts, shift, rows, cols):
    own = {cell: i for i, cell in enumerate(own_order)}
    stack, at = {}, 0
    for piece, start, slot in zip(pieces, starts, SLOTS):
        for i, cell in enumerate(piece):
            stack[cell] = at + start + i
        at += slot
    main = np.zeros((len(out_cells), len(own_order)), np.float32)
    halo = np.zeros((len(out_cells), STACK), np.float32)
    for i, cell in enumerate(out_cells):
        if cell is None:
            continue
        r, c = (cell[0] + shift[0], cell[1] + shift[1])
        if 0 <= r < rows and 0 <= c < cols:
            main[i, own[r, c]] = 1.0
        else:
            halo[i, stack[r % rows, c % cols]] = 1.0
    return main, halo


def padded_rows(rows, cols, height):
    return [(r, c) if c < cols else None for r in range(rows) for c in range(height)]


ZERO3 = (0, 0, 0)
PLAIN_F = plain_order(ROWS, COLS)
PLAIN_C = plain_order(6, 12)
TABLES = dict(
    tok_send=send_matrix(PLAIN_F, leading(ROWS, COLS), ZERO3),
    cot_send=send_matrix(PLAIN_C, leading(6, 12), COARSE_AT),
)
TABLES["tok_main"], TABLES["tok_halo"] = take_matrices(
    PLAIN_F, window_order(), leading(ROWS, COLS), ZERO3, (3, 6), ROWS, COLS
)
TABLES["cot_main"], TABLES["cot_halo"] = take_matrices(
    PLAIN_C, PLAIN_C, leading(6, 12), COARSE_AT, (3, 6), 6, 12
)
TABLES["y_send"] = send_matrix(window_order(), leading(ROWS, COLS), ZERO3)
TABLES["y_main"], TABLES["y_halo"] = take_matrices(
    window_order(), patch_order(), leading(ROWS, COLS), ZERO3, (3, 6), ROWS, COLS
)
TABLES["df_send"] = send_matrix(patch_order(), trailing(ROWS, COLS), ZERO3)
TABLES["df_main"], TABLES["df_halo"] = take_matrices(
    patch_order(), window_order(), trailing(ROWS, COLS), ZERO3, (-3, -6), ROWS, COLS
)
TABLES["out_send"] = send_matrix(PLAIN_C, trailing(6, 12), COARSE_AT)
TABLES["out_main"], TABLES["out_halo"] = take_matrices(
    PLAIN_C, padded_rows(6, 12, 16), trailing(6, 12), COARSE_AT, (-3, -6), 6, 12
)
TABLES["dx_send"] = send_matrix(window_order(), trailing(ROWS, COLS), ZERO3)
TABLES["dx_main"], TABLES["dx_halo"] = take_matrices(
    window_order(), PLAIN_F, trailing(ROWS, COLS), ZERO3, (-3, -6), ROWS, COLS
)


def table(name):
    return jnp.asarray(TABLES[name], BF16)


def mm(a, b):
    return lax.dot_general(a, b, (((1,), (0,)), ((), ())), preferred_element_type=F32)


def mm_nt(a, b):
    return lax.dot_general(a, b, (((1,), (1,)), ((), ())), preferred_element_type=F32)


def mm_tn(a, b):
    return lax.dot_general(a, b, (((0,), (0,)), ((), ())), preferred_element_type=F32)


def rounded(x):
    return x.astype(BF16).astype(F32)


def call(kernel, outs, *args, scratch=()):
    return pl.pallas_call(
        kernel,
        out_shape=[jax.ShapeDtypeStruct(s, d) for s, d in outs],
        scratch_shapes=list(scratch),
        interpret=INTERPRET,
    )(*args)


def normalize(x):
    shifted = x - jnp.mean(x, axis=-1, keepdims=True)
    inverse = lax.rsqrt(jnp.mean(shifted * shifted, axis=-1, keepdims=True) + EPSILON)
    return shifted * inverse, inverse


def normalize_back(d, xhat, inverse):
    return inverse * (
        d - jnp.mean(d, axis=-1, keepdims=True) - xhat * jnp.mean(d * xhat, axis=-1, keepdims=True)
    )


def lane_half():
    lane = lax.broadcasted_iota(jnp.int32, (1, 128), 1)
    low = (lane < 64).astype(F32)
    return low, 1.0 - low


def stacked(x):
    low, high = lane_half()
    pad = jnp.zeros((128 - CELLS, 128), F32)
    return jnp.concatenate([x * low, pad, x * high, pad], axis=0).astype(BF16)


def unstacked(x):
    low, high = lane_half()
    return x[:CELLS] * low + x[128 : 128 + CELLS] * high


def key_lanes():
    lane = lax.broadcasted_iota(jnp.int32, (CELLS, 256), 1)
    return jnp.where(lane >= 128, lane - 128, lane)


def apart(split):
    row = lax.broadcasted_iota(jnp.int32, (CELLS, 256), 0)
    key = key_lanes()
    differ = (row >= CELLS // 2) != (key >= CELLS // 2)
    return jnp.logical_and(differ, split)


def halves(fn, x):
    return jnp.concatenate(
        [jnp.broadcast_to(fn(x[:, :128]), (CELLS, 128)), jnp.broadcast_to(fn(x[:, 128:]), (CELLS, 128))],
        axis=1,
    )


def attend(q, k2, v2, differ):
    scores = mm_nt(q.astype(BF16), k2) * 0.125
    scores = jnp.where(differ, NEGATIVE, scores)
    scores = jnp.where(key_lanes() < CELLS, scores, LOWEST)
    exponent = jnp.exp(scores - halves(lambda s: jnp.max(s, axis=1, keepdims=True), scores))
    weights = exponent / halves(lambda s: jnp.sum(s, axis=1, keepdims=True), exponent)
    return weights, mm(weights.astype(BF16), v2)


def attend_back(q, k2, v2, weights, differ, d):
    d = d.astype(BF16)
    dv = unstacked(mm_tn(weights.astype(BF16), d))
    dw = rounded(mm_nt(d, v2))
    ds = weights * (dw - halves(lambda s: jnp.sum(s, axis=1, keepdims=True), dw * weights))
    ds = jnp.where(differ, 0.0, ds * 0.125).astype(BF16)
    dq = mm(ds, k2)
    dk = unstacked(mm_tn(ds, q.astype(BF16)))
    return dq, dk, dv


def first_kernel(tok, cot, tok_send, cot_send, tok2d, side, edge, corner, cot2d):
    x = tok[...].astype(F32).reshape(ROWS * COLS, D).astype(BF16)
    tok2d[...] = x
    for r in range(6):
        cot2d[pl.ds(12 * r, 12), :] = cot[r].astype(F32)
    y = cot2d[...].astype(BF16)
    stack = (mm(tok_send[...], x) + mm(cot_send[...], y)).astype(BF16)
    side[...] = stack[:80]
    edge[...] = stack[80:160]
    corner[...] = stack[160:]


def fine_forward_kernel(
    seam, x_in, side, edge, corner, gain, wqkv, wproj, t_main, t_halo, y_send,
    x_out, n_out, p_out, w_out, m_out, y_out, side_out, edge_out, corner_out, mixed,
):
    halo = jnp.concatenate([side[...], edge[...], corner[...]], axis=0)
    x = mm(t_main[...], x_in[...]) + mm(t_halo[...], halo)
    x_out[...] = x.astype(BF16)
    xhat, _ = normalize(x)
    n = (xhat * gain[...]).astype(BF16)
    n_out[...] = n
    p_out[...] = rounded(mm(n, wqkv[...]))
    for w in range(WINDOWS):
        differ = apart((seam[0] == 1) if w >= 2 else False)
        for p in range(HF // 2):
            rows = pl.ds(CELLS * w, CELLS)
            q, k, v = (p_out[rows, pl.ds(256 * part + 128 * p, 128)] for part in range(3))
            weights, out = attend(q, stacked(k), stacked(v), differ)
            w_out[2 * w + p] = weights
            mixed[rows, pl.ds(128 * p, 128)] = out
    m = mixed[...].astype(BF16)
    m_out[...] = m
    y = (x + mm(m, wproj[...])).astype(BF16)
    y_out[...] = y
    stack = mm(y_send[...], y).astype(BF16)
    side_out[...] = stack[:80]
    edge_out[...] = stack[80:160]
    corner_out[...] = stack[160:]


def coarse_kernel(
    seam, y_in, side, edge, corner, cot_in, cside, cedge, ccorner,
    mgain, mweight, gain, wqkv, wproj, y_main, y_halo, c_main, c_halo, df_send, out_send,
    y2_out, df_out, side_out, edge_out, corner_out, fac_out, gains_out, packed, mixed, dpacked, wsave,
):
    halo = jnp.concatenate([side[...], edge[...], corner[...]], axis=0)
    patches = mm(y_main[...], y_in[...]) + mm(y_halo[...], halo)
    g = jnp.concatenate([patches[CELLS * i : CELLS * (i + 1)] for i in range(4)], axis=1)
    ghat, ginv = normalize(g)
    mn = (ghat * mgain[...]).astype(BF16)
    z = rounded(mm(mn, mweight[...]))
    zhat, zinv = normalize(z)
    n = (zhat * gain[...]).astype(BF16)
    packed[...] = rounded(mm(n, wqkv[...]))
    differ = apart(seam[0] == 1)
    for p in range(HC // 2):
        lanes = pl.ds(128 * p, 128)
        q, k, v = (packed[:, pl.ds(512 * part + 128 * p, 128)] for part in range(3))
        weights, out = attend(q, stacked(k), stacked(v), differ)
        wsave[p] = weights
        mixed[:, lanes] = out
    m = mixed[...].astype(BF16)
    y2 = (z + mm(m, wproj[...])).astype(BF16)
    y2_out[...] = y2

    chalo = jnp.concatenate([cside[...], cedge[...], ccorner[...]], axis=0)
    dy = mm(c_main[...], cot_in[...].astype(BF16)) + mm(c_halo[...], chalo)
    mixed[...] = rounded(mm_nt(dy.astype(BF16), wproj[...]))
    for p in range(HC // 2):
        q, k, v = (packed[:, pl.ds(512 * part + 128 * p, 128)] for part in range(3))
        grads = attend_back(q, stacked(k), stacked(v), wsave[p], differ, mixed[:, pl.ds(128 * p, 128)])
        for part in range(3):
            dpacked[:, pl.ds(512 * part + 128 * p, 128)] = grads[part]
    dp = dpacked[...].astype(BF16)
    dn = rounded(mm_nt(dp, wqkv[...]))
    gain_sum = jnp.sum(dn * zhat, axis=0, keepdims=True)
    dz = (dy + normalize_back(dn * gain[...], zhat, zinv)).astype(BF16)
    dmn = rounded(mm_nt(dz, mweight[...]))
    mgain_sum = jnp.sum(dmn * ghat, axis=0, keepdims=True)
    dg = normalize_back(dmn * mgain[...], ghat, ginv)
    df = jnp.concatenate([dg[:, D * i : D * (i + 1)] for i in range(4)], axis=0).astype(BF16)
    df_out[...] = df
    stack = (mm(df_send[...], df) + mm(out_send[...], y2)).astype(BF16)
    side_out[...] = stack[:80]
    edge_out[...] = stack[80:160]
    corner_out[...] = stack[160:]
    at = 0
    for piece in (mn, n, m, dz, dp, dy.astype(BF16)):
        fac_out[:, pl.ds(at, piece.shape[1])] = piece
        at += piece.shape[1]
    for i in range(4):
        gains_out[pl.ds(1 + i, 1), :] = mgain_sum[:, D * i : D * (i + 1)]
    gains_out[pl.ds(0, 1), :] = gain_sum
    gains_out[pl.ds(5, 3), :] = jnp.zeros((3, D), F32)


def fine_backward_kernel(
    seam, df_in, side, edge, corner, x_in, p_in, w_in, gain, wqkv, wproj, d_main, d_halo, dx_send, gains_in,
    dx_out, side_out, edge_out, corner_out, fac_out, gains_out, dmixed, dpacked,
):
    halo = jnp.concatenate([side[...], edge[...], corner[...]], axis=0)
    dy = mm(d_main[...], df_in[...]) + mm(d_halo[...], halo)
    dmixed[...] = rounded(mm_nt(dy.astype(BF16), wproj[...]))
    for w in range(WINDOWS):
        differ = apart((seam[0] == 1) if w >= 2 else False)
        for p in range(HF // 2):
            rows = pl.ds(CELLS * w, CELLS)
            q, k, v = (p_in[rows, pl.ds(256 * part + 128 * p, 128)] for part in range(3))
            d = dmixed[rows, pl.ds(128 * p, 128)]
            grads = attend_back(q, stacked(k), stacked(v), w_in[2 * w + p], differ, d)
            for part in range(3):
                dpacked[rows, pl.ds(256 * part + 128 * p, 128)] = grads[part]
    dp = dpacked[...].astype(BF16)
    dn = rounded(mm_nt(dp, wqkv[...]))
    xhat, inverse = normalize(x_in[...].astype(F32))
    gains_out[...] = gains_in[...]
    gains_out[pl.ds(5, 1), :] = jnp.sum(dn * xhat, axis=0, keepdims=True)
    dx = (dy + normalize_back(dn * gain[...], xhat, inverse)).astype(BF16)
    dx_out[...] = dx
    stack = mm(dx_send[...], dx).astype(BF16)
    side_out[...] = stack[:80]
    edge_out[...] = stack[80:160]
    corner_out[...] = stack[160:]
    fac_out[:, pl.ds(0, 768)] = dp
    fac_out[:, pl.ds(768, D)] = dy.astype(BF16)


def spread(width, place, block, wide, stride, offset, core):
    source = lax.broadcasted_iota(jnp.int32, (width, wide), 0)
    target = lax.broadcasted_iota(jnp.int32, (width, wide), 1)
    group = target // stride
    i = target - group * stride - offset
    inside = jnp.logical_and(i >= 0, i < block)
    match = source == (2 * group + core) * block + i
    return jnp.where(jnp.logical_and(inside, match), 1.0, 0.0).astype(BF16)


def both(own, other, lanes):
    return jnp.concatenate([own[:, lanes].astype(F32), other[:, lanes].astype(F32)], axis=0).astype(BF16)


def coarse_weights_kernel(place, own, other, out):
    core = place[0]
    groups = out.shape[0]
    rows = out.shape[1] // 2
    share = D // (2 * groups)
    at = lambda start, size: both(own, other, pl.ds(start, size))
    dz = at(2048 + 1024, D)
    block = spread(D, core, rows, D // 2, rows, 0, core)
    for b in range(4):
        left = mm(at(D * b, D), block).astype(BF16)
        g = D // 2 // rows
        out[pl.ds(g * b, g), pl.ds(0, rows), :] = mm_tn(left, dz).reshape(g, rows, D).astype(BF16)
    n = at(2048, D)
    m = at(2048 + D, D)
    total = None
    for j in range(4):
        right = at(2048 + 1536 + D * j, D)
        sel = spread(D, core, share, groups * rows, rows, share * j, core)
        left = mm(n if j < 3 else m, sel).astype(BF16)
        term = mm_tn(left, right)
        total = term if total is None else total + term
    out[:, pl.ds(rows, rows), :] = total.reshape(groups, rows, D).astype(BF16)


def fine_weights_kernel(place, n_own, n_other, m_own, m_other, own, other, gains, gains_other, out, chunks):
    core = place[0]
    groups = out.shape[0]
    rows = out.shape[1]
    share = D // (2 * groups)
    n = both(n_own, n_other, pl.ds(0, D))
    m = both(m_own, m_other, pl.ds(0, 256))
    total = None
    for j in range(3):
        right = both(own, other, pl.ds(256 * j, 256))
        left = mm(n, spread(D, core, share, groups * rows, rows, share * j, core)).astype(BF16)
        term = mm_tn(left, right)
        total = term if total is None else total + term
    for h in range(2):
        right = both(own, other, pl.ds(768 + 256 * h, 256))
        offset = 3 * share + (share // 2) * h
        left = mm(m, spread(256, core, share // 2, groups * rows, rows, offset, core)).astype(BF16)
        total = total + mm_tn(left, right)
    out[:, :, pl.ds(0, 256)] = total.reshape(groups, rows, 256).astype(BF16)
    both_gains = gains[...] + gains_other[...]
    for r in range(6):
        for q in range(4):
            chunks[pl.ds(4 * r + q, 1), :] = both_gains[r : r + 1, 128 * q : 128 * (q + 1)]
    chunks[pl.ds(24, 8), :] = jnp.zeros((8, 128), F32)
    target = lax.broadcasted_iota(jnp.int32, (groups * rows, 32), 0)
    source = lax.broadcasted_iota(jnp.int32, (groups * rows, 32), 1)
    g = target // rows
    r = target - g * rows
    device = 2 * g + core
    want = jnp.where(
        r == 0,
        device * share // 128,
        jnp.where(r == 1, 4 + device * 4 * share // 128, jnp.where(r == 2, 20 + device * share // 128, -1)),
    )
    choose = jnp.where(source == want, 1.0, 0.0).astype(BF16)
    out[:, :, pl.ds(256, 128)] = (
        mm(choose, chunks[...].astype(BF16)).reshape(groups, rows, 128).astype(BF16)
    )


def total_of(ref):
    def step(i, acc):
        return acc + ref[i].astype(F32)

    return lax.fori_loop(1, ref.shape[0], step, ref[0].astype(F32))


def last_kernel(
    scale, coarse, fine, y2, side, edge, corner, dx, dside, dedge, dcorner, out_main, out_halo, dx_main, dx_halo,
    out, grad, fqkv, fproj, merge, cqkv, cproj, gains,
):
    factor = scale[0]
    rows = coarse.shape[1] // 2
    share = rows // 4
    total = total_of(coarse) * factor
    merge[...] = total[:rows]
    for j in range(3):
        cqkv[:, pl.ds(D * j, D)] = total[rows + share * j : rows + share * (j + 1)]
    cproj[...] = total[rows + 3 * share :]
    total = total_of(fine) * factor
    for j in range(3):
        fqkv[:, pl.ds(256 * j, 256)] = total[share * j : share * (j + 1), :256]
    for h in range(2):
        start = 3 * share + share // 2 * h
        fproj[:, pl.ds(256 * h, 256)] = total[start : start + share // 2, :256]
    gains[...] = total[:8, 256:]
    halo = jnp.concatenate([side[...], edge[...], corner[...]], axis=0)
    y = mm(out_main[...], y2[...]) + mm(out_halo[...], halo)
    for r in range(6):
        out[r] = y[16 * r : 16 * r + 12].astype(BF16)
    halo = jnp.concatenate([dside[...], dedge[...], dcorner[...]], axis=0)
    d = mm(dx_main[...], dx[...]) + mm(dx_halo[...], halo)
    grad[...] = d.reshape(ROWS, COLS, D).astype(BF16)


SEAM = pl.BlockSpec(memory_space=pltpu.SMEM)


def scalar_call(kernel, outs, scalar, *args, scratch=()):
    vmem = pl.BlockSpec(memory_space=pltpu.VMEM)
    return pl.pallas_call(
        kernel,
        out_shape=[jax.ShapeDtypeStruct(s, d) for s, d in outs],
        in_specs=[SEAM] + [vmem] * len(args),
        out_specs=[vmem] * len(outs),
        scratch_shapes=list(scratch),
        interpret=INTERPRET,
    )(scalar, *args)


PIECES = [((s, D), BF16) for s in SLOTS]


def exchange(pieces, step):
    lat = lax.axis_size("lat")
    pair = lax.axis_size("pair")
    lon = 2 * pair
    arrived = []
    for piece, (dr, dc) in zip(pieces, ((0, 1), (1, 0), (1, 1))):
        pairs = []
        for r in range(lat):
            for c in range(lon):
                to = ((r + step * dr) % lat) * lon + (c + step * dc) % lon
                pairs.append((r * lon + c, to))
        arrived.append(lax.ppermute(piece, ("lat", "pair", "core"), pairs))
    return arrived


def partner(value):
    return lax.ppermute(value, "core", [(0, 1), (1, 0)])


def local(
    tokens, fine_gain, fine_qkv, fine_proj, merge_gain, merge_weight, coarse_gain, coarse_qkv, coarse_proj, cotangent
):
    lat_count = lax.axis_size("lat")
    groups = lat_count * lax.axis_size("pair")
    share = D // (2 * groups)
    rows = 4 * share
    seam = (lax.axis_index("lat") == lat_count - 1).astype(jnp.int32).reshape(1)
    core = lax.axis_index("core").astype(jnp.int32).reshape(1)
    grad_scale = (ROWS * COLS * 2 * groups // 4) ** (-0.5)
    fgain, mgain, cgain = (v.reshape(1, -1) for v in (fine_gain, merge_gain, coarse_gain))
    cells = WINDOWS * CELLS

    tok, *pieces, cot = call(
        first_kernel,
        [((cells, D), BF16)] + PIECES + [((CELLS, D), F32)],
        tokens, cotangent, table("tok_send"), table("cot_send"),
    )
    ahead = exchange(pieces, -1)
    x, n, p, w, m, y, *pieces = scalar_call(
        fine_forward_kernel,
        [
            ((cells, D), BF16), ((cells, D), BF16), ((cells, 768), F32), ((8, CELLS, 256), F32),
            ((cells, 256), BF16), ((cells, D), BF16),
        ]
        + PIECES,
        seam, tok, *ahead, fgain, fine_qkv, fine_proj, table("tok_main"), table("tok_halo"), table("y_send"),
        scratch=[pltpu.VMEM((cells, 256), F32)],
    )
    merged = exchange(pieces, -1)
    n_other, m_other = (partner(n), partner(m))
    y2, df, *rest = scalar_call(
        coarse_kernel,
        [((CELLS, D), BF16), ((cells, D), BF16)] + PIECES + [((CELLS, 5632), BF16), ((8, D), F32)],
        seam, y, *merged, cot, *ahead, mgain, merge_weight, cgain, coarse_qkv, coarse_proj,
        table("y_main"), table("y_halo"), table("cot_main"), table("cot_halo"), table("df_send"), table("out_send"),
        scratch=[
            pltpu.VMEM((CELLS, 1536), F32), pltpu.VMEM((CELLS, D), F32), pltpu.VMEM((CELLS, 1536), F32),
            pltpu.VMEM((4, CELLS, 256), F32),
        ],
    )
    pieces, fac, gains = (rest[:3], rest[3], rest[4])
    back = exchange(pieces, 1)
    fac_other = partner(fac)
    (coarse_part,) = scalar_call(
        coarse_weights_kernel, [((groups, 2 * rows, D), BF16)], core, fac, fac_other
    )
    dx, *rest = scalar_call(
        fine_backward_kernel,
        [((cells, D), BF16)] + PIECES + [((cells, 1280), BF16), ((8, D), F32)],
        seam, df, *back, x, p, w, fgain, fine_qkv, fine_proj, table("df_main"), table("df_halo"), table("dx_send"),
        gains,
        scratch=[pltpu.VMEM((cells, 256), F32), pltpu.VMEM((cells, 768), F32)],
    )
    pieces, fac, gains = (rest[:3], rest[3], rest[4])
    ended = exchange(pieces, 1)
    fac_other, gains_other = (partner(fac), partner(gains))
    (fine_part,) = scalar_call(
        fine_weights_kernel, [((groups, rows, 384), BF16)],
        core, n, n_other, m, m_other, fac, fac_other, gains, gains_other,
        scratch=[pltpu.VMEM((32, 128), F32)],
    )
    coarse_sum = lax.all_to_all(coarse_part, ("lat", "pair"), 0, 0)
    fine_sum = lax.all_to_all(fine_part, ("lat", "pair"), 0, 0)
    output, grad, fqkv, fproj, merge, cqkv, cproj, gain_sums = scalar_call(
        last_kernel,
        [
            ((6, 12, D), BF16), ((ROWS, COLS, D), BF16), ((share, 768), F32), ((share // 2, D), F32),
            ((rows, D), F32), ((share, 1536), F32), ((share, D), F32), ((8, 128), F32),
        ],
        jnp.full((1,), grad_scale, F32), coarse_sum, fine_sum, y2, *back, dx, *ended,
        table("out_main"), table("out_halo"), table("dx_main"), table("dx_halo"),
    )
    device = (lax.axis_index("lat") * lax.axis_size("pair") + lax.axis_index("pair")) * 2 + lax.axis_index("core")
    cg = lax.dynamic_slice(gain_sums[0], (device * share % 128,), (share,))
    mg = lax.dynamic_slice(gain_sums[1], (device * rows % 128,), (rows,))
    fg = lax.dynamic_slice(gain_sums[2], (device * share % 128,), (share,))
    return (output, grad, fg, fqkv, fproj, mg, merge, cg, cqkv, cproj)


def solution(mesh):
    lat, lon = (mesh.shape["lat"], mesh.shape["lon"])
    split = Mesh(mesh.devices.reshape(lat, lon // 2, 2), ("lat", "pair", "core"))
    lon = ("pair", "core")
    grid = P("lat", lon, None)
    whole = ("lat", "pair", "core")
    return jax.shard_map(
        local,
        mesh=split,
        in_specs=(grid, P(), P(), P(), P(), P(), P(), P(), P(), grid),
        out_specs=(
            grid, grid, P(whole), P(whole, None), P(whole, None), P(whole), P(whole, None), P(whole),
            P(whole, None), P(whole, None),
        ),
        check_vma=False,
    )
```

time: 855 us -> 145 us (0.17)
  waiting for transfers between devices: 669 us -> 58.2 us
  local copies, waits for them, and re-layouts: 89.1 us -> 7.16 us
  Pallas kernels: 0 us -> 44.6 us
  matrix products: 30.6 us -> 0 us
  other arithmetic: 20 us -> 0 us
  between operations: 15.2 us -> 0.86 us
    unnamed x2 -> x0, waiting for transfers between devices: 640 us -> none
    pallas_call x0 -> x7, Pallas kernels: none -> 44.6 us  [the longest x6 42.5 us: scalar_call(): pl.pallas_call(kernel, out_shape=[jax.ShapeDtypeStruct(s, d) for s, d in...]
    dot_general x27 -> x0, matrix products: 30.6 us -> none  [the longest x2 4.19 us: block_backward(): lax.dot_general(normed, grad_packed, (((0, 1), (0, 1)), ((), ())), prefer...]
    reshape x19 -> x0, local copies, waits for them, and re-layouts: 21.5 us -> none  [the longest x1 10.9 us: sum_together(): jnp.pad(lines, ((0, 0), (0, span * 128 - lines.shape[1]))).reshape(-1, 128)]
    ppermute x16 -> x17, waiting for transfers between devices: 29 us -> 48.4 us  [the longest x12 45.4 us: exchange(): arrived.append(lax.ppermute(piece, ('lat', 'pair', 'core'), pairs))]
    another operation x9 -> x0, local copies, waits for them, and re-layouts: 18.4 us -> none  [the longest x5 14.3 us: sum_together(): lines = jnp.concatenate([b.reshape(peers, -1) for b in tiles], axis=1)]
    concatenate x1 -> x0, local copies, waits for them, and re-layouts: 13.8 us -> none  [sum_together(): lines = jnp.concatenate([b.reshape(peers, -1) for b in tiles], axis=1)]
    all_to_all x0 -> x2, starting transfers between devices: none -> 10.3 us  [the longest x1 5.56 us: local(): fine_sum = lax.all_to_all(fine_part, ('lat', 'pair'), 0, 0)]
  transfers between devices with their start and end apart: 17 -> 19, of which waited for: 12 -> 9; matrix products, arithmetic and copies ran while one was open for 6% -> 0% of each run, Pallas kernels for 0% -> 11%
where the time goes in v2:
time: 145 us; the launch traced here: 144 us
  waiting for transfers between devices  58.2 us (40%)
  Pallas kernels  44.6 us (31%)
  starting transfers between devices  32.8 us (23%)
  local copies, waits for them, and re-layouts  7.16 us (5%)
    ppermute x12, waiting for transfers between devices, exchange(): arrived.append(lax.ppermute(piece, ('lat', 'pair', 'core'), pairs))  45.4 us
    pallas_call x6, Pallas kernels, scalar_call(): pl.pallas_call(kernel, out_shape=[jax.ShapeDtypeStruct(s, d) for s, d in...  42.5 us
    ppermute x12, starting transfers between devices, exchange(): arrived.append(lax.ppermute(piece, ('lat', 'pair', 'core'), pairs))  21.2 us
    all_to_all x1, waiting for transfers between devices, local(): fine_sum = lax.all_to_all(fine_part, ('lat', 'pair'), 0, 0)  9.05 us
    all_to_all x1, starting transfers between devices, local(): fine_sum = lax.all_to_all(fine_part, ('lat', 'pair'), 0, 0)  5.56 us
    unnamed x50, local copies, waits for them, and re-layouts  5.2 us
    all_to_all x1, starting transfers between devices, local(): coarse_sum = lax.all_to_all(coarse_part, ('lat', 'pair'), 0, 0)  4.78 us
    ppermute x5, waiting for transfers between devices, partner(): return lax.ppermute(value, 'core', [(0, 1), (1, 0)])  2.95 us
  transfers between devices with their start and end apart: 19, of which 9 were waited for; matrix products, arithmetic and copies ran while one was open for 0% of the time, Pallas kernels for 11%

profile of v2, /device:TPU:0, one launch (start us, length us, event | category | flops | bytes accessed | tf_op | source)
XLA Modules:
  0.0 143.6 jit_solution(4989151943312651353)
XLA Ops:
  0.6 2.1 %shard_map.339 = (bf16[288,512]{1,0:T(8,128)(2,1)}, bf16[80,512]{1,0:T(8,128)(2,1)}, bf16[80,512]{1,0:T(8,128)(2,1)}, bf16[48,512]{1,0:T(8,128)(2,1)}, f32[72,512]{1,0:T(8,128)}) custom-call(bf16[12,24,512]{2,1,0:T(8,128)(2,1)} %tok.1, bf16[6,12,512]{2,1,0:T(8,128)(2,1)} %cot.1, bf16[208,288]{1,0:T(8,128)(2,1)} %constant.83.clone.tok_send, ...), custom_call_target="tpu_custom_call" | custom-call | tf_op jit(solution)/shard_map/pallas_call | solution.py:155
  2.7 3.3 %collective-permute-start = (bf16[80,512]{1,0:T(8,128)(2,1)}, bf16[80,512]{1,0:T(8,128)(2,1)S(1)}, u32[]{:S(2)}, u32[]{:S(2)}) collective-permute-start(bf16[80,512]{1,0:T(8,128)(2,1)} %get-tuple-element.46), channel_id=1, source_target_pairs={{0,15},{1,0},{2,1},{3,2},{4,3},{5,4},{6,5},{7,6},{8,7},{9,8},{10,9... | collective-permute-start | bytes 245768 | tf_op jit(solution)/shard_map/ppermute | solution.py:501
  6.1 6.4 %collective-permute-start.1 = (bf16[80,512]{1,0:T(8,128)(2,1)}, bf16[80,512]{1,0:T(8,128)(2,1)S(1)}, u32[]{:S(2)}, u32[]{:S(2)}) collective-permute-start(bf16[80,512]{1,0:T(8,128)(2,1)} %get-tuple-element.47), channel_id=1, source_target_pairs={{0,112},{1,113},{2,114},{3,115},{4,116},{5,117},{6,118},{7,119},{8... | collective-permute-start | bytes 245768 | tf_op jit(solution)/shard_map/ppermute | solution.py:501
  12.4 0.2 collective-permute-start.2
  12.6 5.1 %collective-permute-done.2.corner.ccorner = bf16[48,512]{1,0:T(8,128)(2,1)S(1)} collective-permute-done((bf16[48,512]{1,0:T(8,128)(2,1)}, bf16[48,512]{1,0:T(8,128)(2,1)S(1)}, u32[]{:S(2)}, u32[]{:S(2)}) %collective-permute-start.2) | collective-permute-done | bytes 49184 | tf_op jit(solution)/shard_map/ppermute | solution.py:501
  17.7 0.6 copy-done.12
  18.3 0.0 copy-done.5
  18.3 6.4 %shard_map.340 = (bf16[288,512]{1,0:T(8,128)(2,1)}, bf16[288,512]{1,0:T(8,128)(2,1)}, f32[288,768]{1,0:T(8,128)}, f32[8,72,256]{2,1,0:T(8,128)}, bf16[288,256]{1...) custom-call(s32[1]{0:T(128)} %bitcast.1.seam, ...), custom_call_target="tpu_custom_call" | custom-call | tf_op jit(solution)/shard_map/pallas_call | solution.py:477
  24.7 0.4 collective-permute-start.3
  25.1 5.2 %collective-permute-start.4 = (bf16[80,512]{1,0:T(8,128)(2,1)}, bf16[80,512]{1,0:T(8,128)(2,1)S(1)}, u32[]{:S(2)}, u32[]{:S(2)}) collective-permute-start(bf16[80,512]{1,0:T(8,128)(2,1)} %get-tuple-element.51), channel_id=1, source_target_pairs={{0,112},{1,113},{2,114},{3,115},{4,116},{5,117},{6,118},{7,119},{8... | collective-permute-start | bytes 245768 | tf_op jit(solution)/shard_map/ppermute | solution.py:501
  30.3 5.2 %collective-permute-done.5.corner = bf16[48,512]{1,0:T(8,128)(2,1)S(1)} collective-permute-done((bf16[48,512]{1,0:T(8,128)(2,1)}, bf16[48,512]{1,0:T(8,128)(2,1)S(1)}, u32[]{:S(2)}, u32[]{:S(2)}) %collective-permute-start.5) | collective-permute-done | bytes 49184 | tf_op jit(solution)/shard_map/ppermute | solution.py:501
  35.5 0.6 copy-done.20
  36.2 0.0 copy-done.18
  36.2 9.7 %shard_map.341 = (bf16[72,512]{1,0:T(8,128)(2,1)}, bf16[288,512]{1,0:T(8,128)(2,1)}, bf16[80,512]{1,0:T(8,128)(2,1)}, bf16[80,512]{1,0:T(8,128)(2,1)}, bf16[48,5...) custom-call(s32[1]{0:T(128)} %bitcast.1.seam, bf16[288,512]{1,0:T(8,128)(2,1)} %get-tuple-element.49.y_in, ...), custom_call_target="tpu_custom_call" | custom-call | tf_op jit(solution)/shard_map/pallas_call | solution.py:477
  46.0 0.1 collective-permute-start.9
  46.0 0.1 collective-permute-start.10
  46.1 0.1 collective-permute-start.11
  46.2 10.2 %collective-permute-done.11.corner = bf16[48,512]{1,0:T(8,128)(2,1)S(1)} collective-permute-done((bf16[48,512]{1,0:T(8,128)(2,1)}, bf16[48,512]{1,0:T(8,128)(2,1)S(1)}, u32[]{:S(2)}, u32[]{:S(2)}) %collective-permute-start.11) | collective-permute-done | bytes 49184 | tf_op jit(solution)/shard_map/ppermute | solution.py:501
  56.4 0.6 copy-done.11
  57.0 0.0 copy-done.7
  57.0 0.0 copy-done.8
  57.1 6.6 %shard_map.343 = (bf16[288,512]{1,0:T(8,128)(2,1)}, bf16[80,512]{1,0:T(8,128)(2,1)}, bf16[80,512]{1,0:T(8,128)(2,1)}, bf16[48,512]{1,0:T(8,128)(2,1)}, bf16[288,1280]{1,0:T(8,128)(2,1)}, /*index=5*/f32[8,512]{1,0:T(8,128)}) custom-call(s32[1]{0:T(128)} %bitcast.1.seam, bf16[288,512]{1,0:T(8,128)(2,1)} %get-tuple-element.57.df_in, bf16[80,512]{1,0:T(8,128)(2,1)} %copy-done.7, ...), custom_call_target="tpu_custom_call" | custom-call | tf_op jit(solution)/shard_map/pallas_call | solution.py:477
  63.6 0.5 collective-permute-start.7
  64.1 0.3 collective-permute-start.8
  64.4 0.2 collective-permute-start.6
  64.7 0.3 collective-permute-start.13
  64.9 1.8 %collective-permute-done.8.m_other = bf16[288,256]{1,0:T(8,128)(2,1)S(1)} collective-permute-done((bf16[288,256]{1,0:T(8,128)(2,1)S(1)}, bf16[288,256]{1,0:T(8,128)(2,1)S(1)}, u32[]{:S(2)}, u32[]{:S(2)}) %collective-permute-start.8) | collective-permute-done | bytes 147488 | tf_op jit(solution)/shard_map/ppermute | solution.py:506
  66.7 1.2 collective-permute-done.13.gains_other
  67.9 0.6 copy-done.21
  68.5 0.1 copy-done.10
  68.6 0.3 copy-done.4
  68.8 9.0 %shard_map.344 = bf16[64,16,384]{2,1,0:T(8,128)(2,1)} custom-call(s32[1]{0:T(128)} %bitcast.place, bf16[288,512]{1,0:T(8,128)(2,1)} %get-tuple-element.55.n_own, bf16[288,512]{1,0:T(8,128)(2,1)} %copy-done.10, bf16[288,256]{1,0:T(8,128)(2,1)} %get-tuple-element.56.m_own, bf16[288,256]{1,0:T(8,128)(2,1)} %copy-done.14, ...), custom_call_target="tpu_custom_call" | custom-call | tf_op jit(solution)/shard_map/pallas_call | solution.py:477
  77.9 5.6 %all-to-all-start.1 = ((bf16[64,16,384]{2,1,0:T(8,128)(2,1)}), bf16[64,16,384]{2,1,0:T(8,128)(2,1)S(1)}, u32[]{:S(2)}, u32[]{:S(2)}) async-start(bf16[64,16,384]{2,1,0:T(8,128)(2,1)} %shard_map.344), calls=%async_computation.1 | async-start | bytes 1572864 | tf_op jit(solution)/shard_map/all_to_all | solution.py:572
  83.5 0.9 copy-done.3
  84.4 6.6 %shard_map.342 = bf16[64,32,512]{2,1,0:T(8,128)(2,1)} custom-call(s32[1]{0:T(128)} %bitcast.place, bf16[72,5632]{1,0:T(8,128)(2,1)} %get-tuple-element.54.own, bf16[72,5632]{1,0:T(8,128)(2,1)} %copy-done.3), custom_call_target="tpu_custom_call" | custom-call | tf_op jit(solution)/shard_map/pallas_call | solution.py:477
  91.0 9.0 %all-to-all-done.1.fine = bf16[64,16,384]{2,1,0:T(8,128)(2,1)S(1)} async-done(((bf16[64,16,384]{2,1,0:T(8,128)(2,1)}), bf16[64,16,384]{2,1,0:T(8,128)(2,1)S(1)}, u32[]{:S(2)}, u32[]{:S(2)}) %all-to-all-start.1) | async-done | bytes 786464 | tf_op jit(solution)/shard_map/all_to_all | solution.py:572
  100.0 4.8 %all-to-all-start = ((bf16[64,32,512]{2,1,0:T(8,128)(2,1)}), bf16[64,32,512]{2,1,0:T(8,128)(2,1)S(1)}, u32[]{:S(2)}, u32[]{:S(2)}) async-start(bf16[64,32,512]{2,1,0:T(8,128)(2,1)} %shard_map.342), calls=%async_computation | async-start | bytes 4194304 | tf_op jit(solution)/shard_map/all_to_all | solution.py:571
  104.8 0.1 collective-permute-start.14
  104.9 3.1 %collective-permute-start.15 = (bf16[80,512]{1,0:T(8,128)(2,1)S(1)}, bf16[80,512]{1,0:T(8,128)(2,1)S(1)}, u32[]{:S(2)}, u32[]{:S(2)}) collective-permute-start(bf16[80,512]{1,0:T(8,128)(2,1)S(1)} %copy-done.22), channel_id=1, source_target_pairs={{0,16},{1,17},{2,18},{3,19},{4,20},{5,21},{6,22},{7,23},{8,24},{9,... | collective-permute-start | bytes 245768 | tf_op jit(solution)/shard_map/ppermute | solution.py:501
  108.1 2.3 %collective-permute-start.16 = (bf16[48,512]{1,0:T(8,128)(2,1)S(1)}, bf16[48,512]{1,0:T(8,128)(2,1)S(1)}, u32[]{:S(2)}, u32[]{:S(2)}) collective-permute-start(bf16[48,512]{1,0:T(8,128)(2,1)S(1)} %copy-done.24), channel_id=1, source_target_pairs={{0,17},{1,18},{2,19},{3,20},{4,21},{5,22},{6,23},{7,24},{8,25},{9,... | collective-permute-start | bytes 147464 | tf_op jit(solution)/shard_map/ppermute | solution.py:501
  110.4 24.9 %collective-permute-done.16.dcorner = bf16[48,512]{1,0:T(8,128)(2,1)S(1)} collective-permute-done((bf16[48,512]{1,0:T(8,128)(2,1)S(1)}, bf16[48,512]{1,0:T(8,128)(2,1)S(1)}, u32[]{:S(2)}, u32[]{:S(2)}) %collective-permute-start.16) | collective-permute-done | bytes 49184 | tf_op jit(solution)/shard_map/ppermute | solution.py:501
  135.3 0.1 collective-permute-done.15.dedge
  135.3 0.8 all-to-all-done.coarse
  136.1 1.3 copy-done
  137.5 4.2 %shard_map.345 = (bf16[6,12,512]{2,1,0:T(8,128)(2,1)}, bf16[12,24,512]{2,1,0:T(8,128)(2,1)}, f32[4,768]{1,0:T(4,128)}, f32[2,512]{1,0:T(2,128)}, f32[16,512]{1,0...) custom-call(f32[1]{0:T(128)} %constant.71.clone.1.scale, bf16[64,32,512]{2,1,0:T(8,128)(2,1)} %copy-done, ...), custom_call_target="tpu_custom_call" | custom-call | tf_op jit(solution)/shard_map/pallas_call | solution.py:477
  141.6 0.8 fusion.3
  142.4 0.6 fusion.1
  143.0 0.6 fusion
  (50 shorter events, 0.1 us)
Async XLA Ops:
  2.7 14.9 %collective-permute-start = (bf16[80,512]{1,0:T(8,128)(2,1)}, bf16[80,512]{1,0:T(8,128)(2,1)S(1)}, u32[]{:S(2)}, u32[]{:S(2)}) collective-permute-start(bf16[80,512]{1,0:T(8,128)(2,1)} %get-tuple-element.46), channel_id=1, source_target_pairs={{0,15},{1,0},{2,1},{3,2},{4,3},{5,4},{6,5},{7,6},{8,7},{9,8},{10,9... | collective-permute-start | bytes 245768 | tf_op jit(solution)/shard_map/ppermute | solution.py:501
  6.1 11.6 %collective-permute-start.1 = (bf16[80,512]{1,0:T(8,128)(2,1)}, bf16[80,512]{1,0:T(8,128)(2,1)S(1)}, u32[]{:S(2)}, u32[]{:S(2)}) collective-permute-start(bf16[80,512]{1,0:T(8,128)(2,1)} %get-tuple-element.47), channel_id=1, source_target_pairs={{0,112},{1,113},{2,114},{3,115},{4,116},{5,117},{6,118},{7,119},{8... | collective-permute-start | bytes 245768 | tf_op jit(solution)/shard_map/ppermute | solution.py:501
  12.4 5.2 %collective-permute-start.2 = (bf16[48,512]{1,0:T(8,128)(2,1)}, bf16[48,512]{1,0:T(8,128)(2,1)S(1)}, u32[]{:S(2)}, u32[]{:S(2)}) collective-permute-start(bf16[48,512]{1,0:T(8,128)(2,1)} %get-tuple-element.48), channel_id=1, source_target_pairs={{0,127},{1,112},{2,113},{3,114},{4,115},{5,116},{6,117},{7,118},{8... | collective-permute-start | bytes 147464 | tf_op jit(solution)/shard_map/ppermute | solution.py:501
  17.7 0.6 copy-start.12
  17.7 0.6 copy-start.5
  17.7 0.7 copy-start.6
  24.7 10.8 %collective-permute-start.3 = (bf16[80,512]{1,0:T(8,128)(2,1)}, bf16[80,512]{1,0:T(8,128)(2,1)S(1)}, u32[]{:S(2)}, u32[]{:S(2)}) collective-permute-start(bf16[80,512]{1,0:T(8,128)(2,1)} %get-tuple-element.50), channel_id=1, source_target_pairs={{0,15},{1,0},{2,1},{3,2},{4,3},{5,4},{6,5},{7,6},{8,7},{9,8},{10,9... | collective-permute-start | bytes 245768 | tf_op jit(solution)/shard_map/ppermute | solution.py:501
  25.1 10.4 %collective-permute-start.4 = (bf16[80,512]{1,0:T(8,128)(2,1)}, bf16[80,512]{1,0:T(8,128)(2,1)S(1)}, u32[]{:S(2)}, u32[]{:S(2)}) collective-permute-start(bf16[80,512]{1,0:T(8,128)(2,1)} %get-tuple-element.51), channel_id=1, source_target_pairs={{0,112},{1,113},{2,114},{3,115},{4,116},{5,117},{6,118},{7,119},{8... | collective-permute-start | bytes 245768 | tf_op jit(solution)/shard_map/ppermute | solution.py:501
  30.3 5.2 %collective-permute-start.5 = (bf16[48,512]{1,0:T(8,128)(2,1)}, bf16[48,512]{1,0:T(8,128)(2,1)S(1)}, u32[]{:S(2)}, u32[]{:S(2)}) collective-permute-start(bf16[48,512]{1,0:T(8,128)(2,1)} %get-tuple-element.52), channel_id=1, source_target_pairs={{0,127},{1,112},{2,113},{3,114},{4,115},{5,116},{6,117},{7,118},{8... | collective-permute-start | bytes 147464 | tf_op jit(solution)/shard_map/ppermute | solution.py:501
  35.5 0.6 copy-start.20
  35.5 0.6 copy-start.17
  35.5 0.7 copy-start.18
  45.9 17.7 %copy-start.9 = (bf16[288,512]{1,0:T(8,128)(2,1)S(1)}, bf16[288,512]{1,0:T(8,128)(2,1)}, u32[]{:S(2)}) copy-start(bf16[288,512]{1,0:T(8,128)(2,1)} %get-tuple-element.55.n_own) | copy-start | bytes 884740
  45.9 18.2 %copy-start.13 = (bf16[288,256]{1,0:T(8,128)(2,1)S(1)}, bf16[288,256]{1,0:T(8,128)(2,1)}, u32[]{:S(2)}) copy-start(bf16[288,256]{1,0:T(8,128)(2,1)} %get-tuple-element.56.m_own) | copy-start | bytes 442372
  46.0 18.5 %copy-start.2 = (bf16[72,5632]{1,0:T(8,128)(2,1)S(1)}, bf16[72,5632]{1,0:T(8,128)(2,1)}, u32[]{:S(2)}) copy-start(bf16[72,5632]{1,0:T(8,128)(2,1)} %get-tuple-element.54.own) | copy-start | bytes 2433028
  46.0 10.4 %collective-permute-start.9 = (bf16[80,512]{1,0:T(8,128)(2,1)}, bf16[80,512]{1,0:T(8,128)(2,1)S(1)}, u32[]{:S(2)}, u32[]{:S(2)}) collective-permute-start(bf16[80,512]{1,0:T(8,128)(2,1)} %get-tuple-element.58), channel_id=1, source_target_pairs={{0,1},{1,2},{2,3},{3,4},{4,5},{5,6},{6,7},{7,8},{8,9},{9,10},{10,1... | collective-permute-start | bytes 245768 | tf_op jit(solution)/shard_map/ppermute | solution.py:501
  46.0 10.3 %collective-permute-start.10 = (bf16[80,512]{1,0:T(8,128)(2,1)}, bf16[80,512]{1,0:T(8,128)(2,1)S(1)}, u32[]{:S(2)}, u32[]{:S(2)}) collective-permute-start(bf16[80,512]{1,0:T(8,128)(2,1)} %get-tuple-element.59), channel_id=1, source_target_pairs={{0,16},{1,17},{2,18},{3,19},{4,20},{5,21},{6,22},{7,23},{8,24},{9,... | collective-permute-start | bytes 245768 | tf_op jit(solution)/shard_map/ppermute | solution.py:501
  46.1 10.2 %collective-permute-start.11 = (bf16[48,512]{1,0:T(8,128)(2,1)}, bf16[48,512]{1,0:T(8,128)(2,1)S(1)}, u32[]{:S(2)}, u32[]{:S(2)}) collective-permute-start(bf16[48,512]{1,0:T(8,128)(2,1)} %get-tuple-element.60), channel_id=1, source_target_pairs={{0,17},{1,18},{2,19},{3,20},{4,21},{5,22},{6,23},{7,24},{8,25},{9,... | collective-permute-start | bytes 147464 | tf_op jit(solution)/shard_map/ppermute | solution.py:501
  56.4 0.6 copy-start.11
  56.4 0.7 copy-start.7
  56.4 0.7 copy-start.8
  63.6 4.3 %collective-permute-start.12 = (bf16[288,1280]{1,0:T(8,128)(2,1)}, bf16[288,1280]{1,0:T(8,128)(2,1)S(1)}, u32[]{:S(2)}, u32[]{:S(2)}) collective-permute-start(bf16[288,1280]{1,0:T(8,128)(2,1)} %get-tuple-element.65.own), channel_id=1, source_target_pairs={{0,1},{1,0},{2,3},{3,2},{4,5},{5,4},{6,7},{7,6},{8,9},{9,8},{10,11... | collective-permute-start | bytes 2211848 | tf_op jit(solution)/shard_map/ppermute | solution.py:506
  63.6 4.2 %collective-permute-start.7 = (bf16[288,512]{1,0:T(8,128)(2,1)S(1)}, bf16[288,512]{1,0:T(8,128)(2,1)S(1)}, u32[]{:S(2)}, u32[]{:S(2)}) collective-permute-start(bf16[288,512]{1,0:T(8,128)(2,1)S(1)} %copy-done.9), channel_id=1, source_target_pairs={{0,1},{1,0},{2,3},{3,2},{4,5},{5,4},{6,7},{7,6},{8,9},{9,8},{10,11... | collective-permute-start | bytes 884744 | tf_op jit(solution)/shard_map/ppermute | solution.py:506
  64.1 2.5 %collective-permute-start.8 = (bf16[288,256]{1,0:T(8,128)(2,1)S(1)}, bf16[288,256]{1,0:T(8,128)(2,1)S(1)}, u32[]{:S(2)}, u32[]{:S(2)}) collective-permute-start(bf16[288,256]{1,0:T(8,128)(2,1)S(1)} %copy-done.13), channel_id=1, source_target_pairs={{0,1},{1,0},{2,3},{3,2},{4,5},{5,4},{6,7},{7,6},{8,9},{9,8},{10,11... | collective-permute-start | bytes 442376 | tf_op jit(solution)/shard_map/ppermute | solution.py:506
  64.4 19.1 %collective-permute-start.6 = (bf16[72,5632]{1,0:T(8,128)(2,1)S(1)}, bf16[72,5632]{1,0:T(8,128)(2,1)S(1)}, u32[]{:S(2)}, u32[]{:S(2)}) collective-permute-start(bf16[72,5632]{1,0:T(8,128)(2,1)S(1)} %copy-done.2), channel_id=1, source_target_pairs={{0,1},{1,0},{2,3},{3,2},{4,5},{5,4},{6,7},{7,6},{8,9},{9,8},{10,11... | collective-permute-start | bytes 2433032 | tf_op jit(solution)/shard_map/ppermute | solution.py:506
  64.7 3.2 %collective-permute-start.13 = (f32[8,512]{1,0:T(8,128)}, f32[8,512]{1,0:T(8,128)S(1)}, u32[]{:S(2)}, u32[]{:S(2)}) collective-permute-start(f32[8,512]{1,0:T(8,128)} %get-tuple-element.66.gains), channel_id=1, source_target_pairs={{0,1},{1,0},{2,3},{3,2},{4,5},{5,4},{6,7},{7,6},{8,9},{9,8},{10,11... | collective-permute-start | bytes 49160 | tf_op jit(solution)/shard_map/ppermute | solution.py:506
  66.7 1.2 copy-start.14
  67.9 0.6 copy-start.21
  67.9 0.7 copy-start.10
  67.9 1.0 copy-start.4
  77.9 22.1 %all-to-all-start.1 = ((bf16[64,16,384]{2,1,0:T(8,128)(2,1)}), bf16[64,16,384]{2,1,0:T(8,128)(2,1)S(1)}, u32[]{:S(2)}, u32[]{:S(2)}) async-start(bf16[64,16,384]{2,1,0:T(8,128)(2,1)} %shard_map.344), calls=%async_computation.1 | async-start | bytes 1572864 | tf_op jit(solution)/shard_map/all_to_all | solution.py:572
  83.5 0.9 copy-start.3
  91.0 13.9 %copy-start.23 = (bf16[80,512]{1,0:T(8,128)(2,1)S(1)}, bf16[80,512]{1,0:T(8,128)(2,1)}, u32[]{:S(2)}) copy-start(bf16[80,512]{1,0:T(8,128)(2,1)} %get-tuple-element.69) | copy-start | bytes 245764
  91.0 13.9 %copy-start.22 = (bf16[80,512]{1,0:T(8,128)(2,1)S(1)}, bf16[80,512]{1,0:T(8,128)(2,1)}, u32[]{:S(2)}) copy-start(bf16[80,512]{1,0:T(8,128)(2,1)} %get-tuple-element.70) | copy-start | bytes 245764
  91.0 17.1 %copy-start.24 = (bf16[48,512]{1,0:T(8,128)(2,1)S(1)}, bf16[48,512]{1,0:T(8,128)(2,1)}, u32[]{:S(2)}) copy-start(bf16[48,512]{1,0:T(8,128)(2,1)} %get-tuple-element.71) | copy-start | bytes 147460
  100.0 4.8 %copy-start.1 = (bf16[64,16,384]{2,1,0:T(8,128)(2,1)}, bf16[64,16,384]{2,1,0:T(8,128)(2,1)S(1)}, u32[]{:S(2)}) copy-start(bf16[64,16,384]{2,1,0:T(8,128)(2,1)S(1)} %all-to-all-done.1.fine) | copy-start | bytes 2359300
  100.0 36.1 %all-to-all-start = ((bf16[64,32,512]{2,1,0:T(8,128)(2,1)}), bf16[64,32,512]{2,1,0:T(8,128)(2,1)S(1)}, u32[]{:S(2)}, u32[]{:S(2)}) async-start(bf16[64,32,512]{2,1,0:T(8,128)(2,1)} %shard_map.342), calls=%async_computation | async-start | bytes 4194304 | tf_op jit(solution)/shard_map/all_to_all | solution.py:571
  104.8 30.4 %collective-permute-start.14 = (bf16[80,512]{1,0:T(8,128)(2,1)S(1)}, bf16[80,512]{1,0:T(8,128)(2,1)S(1)}, u32[]{:S(2)}, u32[]{:S(2)}) collective-permute-start(bf16[80,512]{1,0:T(8,128)(2,1)S(1)} %copy-done.23), channel_id=1, source_target_pairs={{0,1},{1,2},{2,3},{3,4},{4,5},{5,6},{6,7},{7,8},{8,9},{9,10},{10,1... | collective-permute-start | bytes 245768 | tf_op jit(solution)/shard_map/ppermute | solution.py:501
  104.9 30.4 %collective-permute-start.15 = (bf16[80,512]{1,0:T(8,128)(2,1)S(1)}, bf16[80,512]{1,0:T(8,128)(2,1)S(1)}, u32[]{:S(2)}, u32[]{:S(2)}) collective-permute-start(bf16[80,512]{1,0:T(8,128)(2,1)S(1)} %copy-done.22), channel_id=1, source_target_pairs={{0,16},{1,17},{2,18},{3,19},{4,20},{5,21},{6,22},{7,23},{8,24},{9,... | collective-permute-start | bytes 245768 | tf_op jit(solution)/shard_map/ppermute | solution.py:501
  108.1 27.2 %collective-permute-start.16 = (bf16[48,512]{1,0:T(8,128)(2,1)S(1)}, bf16[48,512]{1,0:T(8,128)(2,1)S(1)}, u32[]{:S(2)}, u32[]{:S(2)}) collective-permute-start(bf16[48,512]{1,0:T(8,128)(2,1)S(1)} %copy-done.24), channel_id=1, source_target_pairs={{0,17},{1,18},{2,19},{3,20},{4,21},{5,22},{6,23},{7,24},{8,25},{9,... | collective-permute-start | bytes 147464 | tf_op jit(solution)/shard_map/ppermute | solution.py:501
  135.3 0.9 copy-start.19
  135.3 0.9 copy-start.15
  135.3 0.8 copy-start.16
  136.1 1.3 copy-start

commit v3 on v2

--- a/solution.py
+++ b/solution.py
@@ -10,6 +10,7 @@
 HF = 4
 HC = 8
 CELLS = 72
+TALL = 80
 WINDOWS = 4
 ROWS = 12
 COLS = 24
@@ -17,6 +18,10 @@
 NEGATIVE = -1000000000.0
 LOWEST = -3.0e38
 INTERPRET = False
+VMEM_LIMIT = 12 * 1024 * 1024
+FLOPS = 5_000_000_000
+BYTES = 4_000_000
+
 
 F32 = jnp.float32
 BF16 = jnp.bfloat16
@@ -55,8 +60,8 @@
 
 
 SLOTS = (80, 80, 48)
+NARROW = (64, 64, 32)
 COARSE_AT = (56, 56, 24)
-STACK = sum(SLOTS)
 
 
 def pick(order, cells, places, total):
@@ -67,24 +72,24 @@
     return matrix
 
 
-def send_matrix(order, pieces, starts):
+def send_matrix(order, pieces, starts, slots=SLOTS):
     cells, places, at = [], [], 0
-    for piece, start, slot in zip(pieces, starts, SLOTS):
+    for piece, start, slot in zip(pieces, starts, slots):
         cells += piece
         places += [at + start + i for i in range(len(piece))]
         at += slot
-    return pick(order, cells, places, STACK)
-
-
-def take_matrices(own_order, out_cells, pieces, starts, shift, rows, cols):
+    return pick(order, cells, places, at)
+
+
+def take_matrices(own_order, out_cells, pieces, starts, shift, rows, cols, slots=SLOTS):
     own = {cell: i for i, cell in enumerate(own_order)}
     stack, at = {}, 0
-    for piece, start, slot in zip(pieces, starts, SLOTS):
+    for piece, start, slot in zip(pieces, starts, slots):
         for i, cell in enumerate(piece):
             stack[cell] = at + start + i
         at += slot
     main = np.zeros((len(out_cells), len(own_order)), np.float32)
-    halo = np.zeros((len(out_cells), STACK), np.float32)
+    halo = np.zeros((len(out_cells), at), np.float32)
     for i, cell in enumerate(out_cells):
         if cell is None:
             continue
@@ -113,9 +118,9 @@
 TABLES["cot_main"], TABLES["cot_halo"] = take_matrices(
     PLAIN_C, PLAIN_C, leading(6, 12), COARSE_AT, (3, 6), 6, 12
 )
-TABLES["y_send"] = send_matrix(window_order(), leading(ROWS, COLS), ZERO3)
+TABLES["y_send"] = send_matrix(window_order(), leading(ROWS, COLS), ZERO3, NARROW)
 TABLES["y_main"], TABLES["y_halo"] = take_matrices(
-    window_order(), patch_order(), leading(ROWS, COLS), ZERO3, (3, 6), ROWS, COLS
+    window_order(), patch_order(), leading(ROWS, COLS), ZERO3, (3, 6), ROWS, COLS, NARROW
 )
 TABLES["df_send"] = send_matrix(patch_order(), trailing(ROWS, COLS), ZERO3)
 TABLES["df_main"], TABLES["df_halo"] = take_matrices(
@@ -125,9 +130,9 @@
 TABLES["out_main"], TABLES["out_halo"] = take_matrices(
     PLAIN_C, padded_rows(6, 12, 16), trailing(6, 12), COARSE_AT, (-3, -6), 6, 12
 )
-TABLES["dx_send"] = send_matrix(window_order(), trailing(ROWS, COLS), ZERO3)
+TABLES["dx_send"] = send_matrix(window_order(), trailing(ROWS, COLS), ZERO3, NARROW)
 TABLES["dx_main"], TABLES["dx_halo"] = take_matrices(
-    window_order(), PLAIN_F, trailing(ROWS, COLS), ZERO3, (-3, -6), ROWS, COLS
+    window_order(), PLAIN_F, trailing(ROWS, COLS), ZERO3, (-3, -6), ROWS, COLS, NARROW
 )
 
 
@@ -156,8 +161,17 @@
         kernel,
         out_shape=[jax.ShapeDtypeStruct(s, d) for s, d in outs],
         scratch_shapes=list(scratch),
+        compiler_params=pltpu.CompilerParams(vmem_limit_bytes=VMEM_LIMIT),
+        cost_estimate=pl.CostEstimate(flops=FLOPS, bytes_accessed=BYTES, transcendentals=0),
         interpret=INTERPRET,
     )(*args)
+
+
+def cut(stack, *refs):
+    at = 0
+    for ref in refs:
+        ref[...] = stack[at : at + ref.shape[0]]
+        at += ref.shape[0]
 
 
 def normalize(x):
@@ -235,9 +249,7 @@
         cot2d[pl.ds(12 * r, 12), :] = cot[r].astype(F32)
     y = cot2d[...].astype(BF16)
     stack = (mm(tok_send[...], x) + mm(cot_send[...], y)).astype(BF16)
-    side[...] = stack[:80]
-    edge[...] = stack[80:160]
-    corner[...] = stack[160:]
+    cut(stack, side, edge, corner)
 
 
 def fine_forward_kernel(
@@ -264,9 +276,7 @@
     y = (x + mm(m, wproj[...])).astype(BF16)
     y_out[...] = y
     stack = mm(y_send[...], y).astype(BF16)
-    side_out[...] = stack[:80]
-    edge_out[...] = stack[80:160]
-    corner_out[...] = stack[160:]
+    cut(stack, side_out, edge_out, corner_out)
 
 
 def coarse_kernel(
@@ -312,13 +322,12 @@
     df = jnp.concatenate([dg[:, D * i : D * (i + 1)] for i in range(4)], axis=0).astype(BF16)
     df_out[...] = df
     stack = (mm(df_send[...], df) + mm(out_send[...], y2)).astype(BF16)
-    side_out[...] = stack[:80]
-    edge_out[...] = stack[80:160]
-    corner_out[...] = stack[160:]
+    cut(stack, side_out, edge_out, corner_out)
     at = 0
     for piece in (mn, n, m, dz, dp, dy.astype(BF16)):
-        fac_out[:, pl.ds(at, piece.shape[1])] = piece
+        fac_out[pl.ds(0, CELLS), pl.ds(at, piece.shape[1])] = piece
         at += piece.shape[1]
+    fac_out[pl.ds(CELLS, TALL - CELLS), :] = jnp.zeros((TALL - CELLS, at), BF16)
     for i in range(4):
         gains_out[pl.ds(1 + i, 1), :] = mgain_sum[:, D * i : D * (i + 1)]
     gains_out[pl.ds(0, 1), :] = gain_sum
@@ -349,88 +358,100 @@
     dx = (dy + normalize_back(dn * gain[...], xhat, inverse)).astype(BF16)
     dx_out[...] = dx
     stack = mm(dx_send[...], dx).astype(BF16)
-    side_out[...] = stack[:80]
-    edge_out[...] = stack[80:160]
-    corner_out[...] = stack[160:]
+    cut(stack, side_out, edge_out, corner_out)
     fac_out[:, pl.ds(0, 768)] = dp
     fac_out[:, pl.ds(768, D)] = dy.astype(BF16)
 
 
-def spread(width, place, block, wide, stride, offset, core):
-    source = lax.broadcasted_iota(jnp.int32, (width, wide), 0)
-    target = lax.broadcasted_iota(jnp.int32, (width, wide), 1)
-    group = target // stride
-    i = target - group * stride - offset
-    inside = jnp.logical_and(i >= 0, i < block)
-    match = source == (2 * group + core) * block + i
-    return jnp.where(jnp.logical_and(inside, match), 1.0, 0.0).astype(BF16)
-
-
-def both(own, other, lanes):
-    return jnp.concatenate([own[:, lanes].astype(F32), other[:, lanes].astype(F32)], axis=0).astype(BF16)
-
-
-def coarse_weights_kernel(place, own, other, out):
+def one_hot(want, width):
+    lane = lax.broadcasted_iota(jnp.int32, (want.shape[0], width), 1)
+    return jnp.where(lane == want, 1.0, 0.0).astype(BF16)
+
+
+def own_rows(share, width, core, by_group):
+    count = width // 2
+    groups = count // share
+    row = lax.broadcasted_iota(jnp.int32, (count, 1), 0)
+    low = share if by_group else groups
+    high_part = lax.shift_right_logical(row, low.bit_length() - 1)
+    low_part = lax.bitwise_and(row, low - 1)
+    group, i = (high_part, low_part) if by_group else (low_part, high_part)
+    return one_hot((2 * group + core) * share + i, width)
+
+
+def coarse_weights_kernel(place, own, other, merge_out, out, lines):
+    core = place[0]
+    groups, rows = out.shape[:2]
+    share = D // (2 * groups)
+
+    def at(start, size):
+        return jnp.concatenate([own[:, pl.ds(start, size)], other[:, pl.ds(start, size)]], axis=0)
+
+    dz = at(2048 + 1024, D)
+    select = own_rows(rows, D, core, True)
+    g = D // 2 // rows
+    for b in range(4):
+        left = mm_nt(select, at(D * b, D)).astype(BF16)
+        merge_out[pl.ds(g * b, g), :, :] = mm(left, dz).reshape(g, rows, D).astype(BF16)
+    select = own_rows(share, D, core, False)
+    n = mm_nt(select, at(2048, D)).astype(BF16)
+    m = mm_nt(select, at(2048 + D, D)).astype(BF16)
+    for j in range(4):
+        part = mm(n if j < 3 else m, at(2048 + 1536 + D * j, D))
+        for i in range(share):
+            for h in range(4):
+                lines[pl.ds(groups * rows * h + share * j + i, groups, rows), :] = part[groups * i : groups * (i + 1), 128 * h : 128 * h + 128]
+    for h in range(4):
+        out[:, :, pl.ds(128 * h, 128)] = lines[pl.ds(groups * rows * h, groups * rows), :].reshape(groups, rows, 128).astype(BF16)
+
+
+def fine_weights_kernel(
+    place, coarse, n_own, n_other, m_own, m_other, own, other, gains, gains_other, out, chunks, lines
+):
     core = place[0]
     groups = out.shape[0]
-    rows = out.shape[1] // 2
+    rows = 8
     share = D // (2 * groups)
-    at = lambda start, size: both(own, other, pl.ds(start, size))
-    dz = at(2048 + 1024, D)
-    block = spread(D, core, rows, D // 2, rows, 0, core)
-    for b in range(4):
-        left = mm(at(D * b, D), block).astype(BF16)
-        g = D // 2 // rows
-        out[pl.ds(g * b, g), pl.ds(0, rows), :] = mm_tn(left, dz).reshape(g, rows, D).astype(BF16)
-    n = at(2048, D)
-    m = at(2048 + D, D)
-    total = None
-    for j in range(4):
-        right = at(2048 + 1536 + D * j, D)
-        sel = spread(D, core, share, groups * rows, rows, share * j, core)
-        left = mm(n if j < 3 else m, sel).astype(BF16)
-        term = mm_tn(left, right)
-        total = term if total is None else total + term
-    out[:, pl.ds(rows, rows), :] = total.reshape(groups, rows, D).astype(BF16)
-
-
-def fine_weights_kernel(place, n_own, n_other, m_own, m_other, own, other, gains, gains_other, out, chunks):
-    core = place[0]
-    groups = out.shape[0]
-    rows = out.shape[1]
-    share = D // (2 * groups)
-    n = both(n_own, n_other, pl.ds(0, D))
-    m = both(m_own, m_other, pl.ds(0, 256))
-    total = None
-    for j in range(3):
-        right = both(own, other, pl.ds(256 * j, 256))
-        left = mm(n, spread(D, core, share, groups * rows, rows, share * j, core)).astype(BF16)
-        term = mm_tn(left, right)
-        total = term if total is None else total + term
-    for h in range(2):
-        right = both(own, other, pl.ds(768 + 256 * h, 256))
-        offset = 3 * share + (share // 2) * h
-        left = mm(m, spread(256, core, share // 2, groups * rows, rows, offset, core)).astype(BF16)
-        total = total + mm_tn(left, right)
-    out[:, :, pl.ds(0, 256)] = total.reshape(groups, rows, 256).astype(BF16)
+    top = coarse.shape[1]
+    out[:, pl.ds(0, top), pl.ds(0, D)] = coarse[...]
+    out[:, pl.ds(0, top), pl.ds(D, 128)] = jnp.zeros((groups, top, 128), BF16)
+    select = own_rows(share, D, core, False)
+    dp = lambda ref: ref[:, pl.ds(0, 768)]
+    dy = lambda ref: ref[:, pl.ds(768, D)]
+    n = [mm_nt(select, ref[...]).astype(BF16) for ref in (n_own, n_other)]
+    part = mm(n[0], dp(own)) + mm(n[1], dp(other))
+    half = share // 2
+    for i in range(share):
+        line = part[groups * i : groups * (i + 1)]
+        for h in range(4):
+            lines[pl.ds(groups * rows * h + i, groups, rows), :] = line[:, 128 * h : 128 * h + 128]
+        for h in range(2):
+            lines[pl.ds(groups * rows * (2 * (i // half) + h) + share + i % half, groups, rows), :] = line[:, 512 + 128 * h : 640 + 128 * h]
+    select = own_rows(half, 256, core, False)
+    m = [mm_nt(select, ref[...]).astype(BF16) for ref in (m_own, m_other)]
+    part = mm(m[0], dy(own)) + mm(m[1], dy(other))
+    for i in range(half):
+        line = part[groups * i : groups * (i + 1)]
+        for h in range(4):
+            lines[pl.ds(groups * rows * h + share + half + i, groups, rows), :] = line[:, 128 * h : 128 * h + 128]
+    for h in range(4):
+        out[:, pl.ds(top, rows), pl.ds(128 * h, 128)] = lines[pl.ds(groups * rows * h, groups * rows), :].reshape(groups, rows, 128).astype(BF16)
     both_gains = gains[...] + gains_other[...]
     for r in range(6):
         for q in range(4):
             chunks[pl.ds(4 * r + q, 1), :] = both_gains[r : r + 1, 128 * q : 128 * (q + 1)]
     chunks[pl.ds(24, 8), :] = jnp.zeros((8, 128), F32)
-    target = lax.broadcasted_iota(jnp.int32, (groups * rows, 32), 0)
-    source = lax.broadcasted_iota(jnp.int32, (groups * rows, 32), 1)
-    g = target // rows
-    r = target - g * rows
-    device = 2 * g + core
+    row = lax.broadcasted_iota(jnp.int32, (groups * rows, 1), 0)
+    device = 2 * lax.shift_right_logical(row, 3) + core
+    r = lax.bitwise_and(row, 7)
+    small = lax.shift_right_logical(device * share, 7)
     want = jnp.where(
         r == 0,
-        device * share // 128,
-        jnp.where(r == 1, 4 + device * 4 * share // 128, jnp.where(r == 2, 20 + device * share // 128, -1)),
-    )
-    choose = jnp.where(source == want, 1.0, 0.0).astype(BF16)
-    out[:, :, pl.ds(256, 128)] = (
-        mm(choose, chunks[...].astype(BF16)).reshape(groups, rows, 128).astype(BF16)
+        small,
+        jnp.where(r == 1, 4 + lax.shift_right_logical(device * share * 4, 7), jnp.where(r == 2, 20 + small, -1)),
+    )
+    out[:, pl.ds(top, rows), pl.ds(512, 128)] = (
+        mm(one_hot(want, 32), chunks[...].astype(BF16)).reshape(groups, rows, 128).astype(BF16)
     )
 
 
@@ -442,24 +463,27 @@
 
 
 def last_kernel(
-    scale, coarse, fine, y2, side, edge, corner, dx, dside, dedge, dcorner, out_main, out_halo, dx_main, dx_halo,
-    out, grad, fqkv, fproj, merge, cqkv, cproj, gains,
+    place, merge_in, rest, y2, side, edge, corner, dx, dside, dedge, dcorner, out_main, out_halo, dx_main, dx_halo,
+    out, grad, fgain, fqkv, fproj, mgain, merge, cgain, cqkv, cproj,
 ):
-    factor = scale[0]
-    rows = coarse.shape[1] // 2
+    rows = merge_in.shape[1]
     share = rows // 4
-    total = total_of(coarse) * factor
-    merge[...] = total[:rows]
+    half = share // 2
+    factor = (ROWS * COLS * D // share // 4) ** (-0.5)
+    merge[...] = total_of(merge_in) * factor
+    total = total_of(rest) * factor
     for j in range(3):
-        cqkv[:, pl.ds(D * j, D)] = total[rows + share * j : rows + share * (j + 1)]
-    cproj[...] = total[rows + 3 * share :]
-    total = total_of(fine) * factor
-    for j in range(3):
-        fqkv[:, pl.ds(256 * j, 256)] = total[share * j : share * (j + 1), :256]
+        cqkv[:, pl.ds(D * j, D)] = total[share * j : share * (j + 1), :D]
+    cproj[...] = total[3 * share : rows, :D]
+    total = total[rows:]
+    fqkv[:, pl.ds(0, D)] = total[:share, :D]
     for h in range(2):
-        start = 3 * share + share // 2 * h
-        fproj[:, pl.ds(256 * h, 256)] = total[start : start + share // 2, :256]
-    gains[...] = total[:8, 256:]
+        fqkv[pl.ds(half * h, half), pl.ds(D, 256)] = total[share : share + half, 256 * h : 256 * h + 256]
+    fproj[...] = total[share + half :, :D]
+    for r, (ref, size) in enumerate(((cgain, share), (mgain, rows), (fgain, share))):
+        first = lax.rem(place[0] * size, 128)
+        turned = pltpu.roll(total[:, D:], lax.rem(128 - first, 128), 1)
+        ref[...] = turned[r : r + 1, :size]
     halo = jnp.concatenate([side[...], edge[...], corner[...]], axis=0)
     y = mm(out_main[...], y2[...]) + mm(out_halo[...], halo)
     for r in range(6):
@@ -480,11 +504,10 @@
         in_specs=[SEAM] + [vmem] * len(args),
         out_specs=[vmem] * len(outs),
         scratch_shapes=list(scratch),
+        compiler_params=pltpu.CompilerParams(vmem_limit_bytes=VMEM_LIMIT),
+        cost_estimate=pl.CostEstimate(flops=FLOPS, bytes_accessed=BYTES, transcendentals=0),
         interpret=INTERPRET,
     )(scalar, *args)
-
-
-PIECES = [((s, D), BF16) for s in SLOTS]
 
 
 def exchange(pieces, step):
@@ -506,6 +529,10 @@
     return lax.ppermute(value, "core", [(0, 1), (1, 0)])
 
 
+def deal(value):
+    return lax.all_to_all(value, ("lat", "pair"), 0, 0)
+
+
 def local(
     tokens, fine_gain, fine_qkv, fine_proj, merge_gain, merge_weight, coarse_gain, coarse_qkv, coarse_proj, cotangent
 ):
@@ -515,31 +542,32 @@
     rows = 4 * share
     seam = (lax.axis_index("lat") == lat_count - 1).astype(jnp.int32).reshape(1)
     core = lax.axis_index("core").astype(jnp.int32).reshape(1)
-    grad_scale = (ROWS * COLS * 2 * groups // 4) ** (-0.5)
     fgain, mgain, cgain = (v.reshape(1, -1) for v in (fine_gain, merge_gain, coarse_gain))
     cells = WINDOWS * CELLS
 
-    tok, *pieces, cot = call(
+    pieces = [((size, D), BF16) for size in SLOTS]
+    narrow = [((size, D), BF16) for size in NARROW]
+    tok, *sent, cot = call(
         first_kernel,
-        [((cells, D), BF16)] + PIECES + [((CELLS, D), F32)],
+        [((cells, D), BF16)] + pieces + [((CELLS, D), F32)],
         tokens, cotangent, table("tok_send"), table("cot_send"),
     )
-    ahead = exchange(pieces, -1)
-    x, n, p, w, m, y, *pieces = scalar_call(
+    ahead = exchange(sent, -1)
+    x, n, p, w, m, y, *sent = scalar_call(
         fine_forward_kernel,
         [
             ((cells, D), BF16), ((cells, D), BF16), ((cells, 768), F32), ((8, CELLS, 256), F32),
             ((cells, 256), BF16), ((cells, D), BF16),
         ]
-        + PIECES,
+        + narrow,
         seam, tok, *ahead, fgain, fine_qkv, fine_proj, table("tok_main"), table("tok_halo"), table("y_send"),
         scratch=[pltpu.VMEM((cells, 256), F32)],
     )
-    merged = exchange(pieces, -1)
+    merged = exchange(sent, -1)
     n_other, m_other = (partner(n), partner(m))
-    y2, df, *rest = scalar_call(
+    y2, df, *sent, fac, gains = scalar_call(
         coarse_kernel,
-        [((CELLS, D), BF16), ((cells, D), BF16)] + PIECES + [((CELLS, 5632), BF16), ((8, D), F32)],
+        [((CELLS, D), BF16), ((cells, D), BF16)] + pieces + [((TALL, 5632), BF16), ((8, D), F32)],
         seam, y, *merged, cot, *ahead, mgain, merge_weight, cgain, coarse_qkv, coarse_proj,
         table("y_main"), table("y_halo"), table("cot_main"), table("cot_halo"), table("df_send"), table("out_send"),
         scratch=[
@@ -547,42 +575,41 @@
             pltpu.VMEM((4, CELLS, 256), F32),
         ],
     )
-    pieces, fac, gains = (rest[:3], rest[3], rest[4])
-    back = exchange(pieces, 1)
-    fac_other = partner(fac)
-    (coarse_part,) = scalar_call(
-        coarse_weights_kernel, [((groups, 2 * rows, D), BF16)], core, fac, fac_other
-    )
-    dx, *rest = scalar_call(
+    back = exchange(sent, 1)
+    merge_part, coarse_part = scalar_call(
+        coarse_weights_kernel,
+        [((groups, rows, D), BF16)] * 2,
+        core, fac, partner(fac),
+        scratch=[pltpu.VMEM((4 * groups * rows, 128), F32)],
+    )
+    merge_sum = deal(merge_part)
+    dx, *sent, fac, gains = scalar_call(
         fine_backward_kernel,
-        [((cells, D), BF16)] + PIECES + [((cells, 1280), BF16), ((8, D), F32)],
+        [((cells, D), BF16)] + narrow + [((cells, 1280), BF16), ((8, D), F32)],
         seam, df, *back, x, p, w, fgain, fine_qkv, fine_proj, table("df_main"), table("df_halo"), table("dx_send"),
         gains,
         scratch=[pltpu.VMEM((cells, 256), F32), pltpu.VMEM((cells, 768), F32)],
     )
-    pieces, fac, gains = (rest[:3], rest[3], rest[4])
-    ended = exchange(pieces, 1)
-    fac_other, gains_other = (partner(fac), partner(gains))
-    (fine_part,) = scalar_call(
-        fine_weights_kernel, [((groups, rows, 384), BF16)],
-        core, n, n_other, m, m_other, fac, fac_other, gains, gains_other,
-        scratch=[pltpu.VMEM((32, 128), F32)],
-    )
-    coarse_sum = lax.all_to_all(coarse_part, ("lat", "pair"), 0, 0)
-    fine_sum = lax.all_to_all(fine_part, ("lat", "pair"), 0, 0)
-    output, grad, fqkv, fproj, merge, cqkv, cproj, gain_sums = scalar_call(
+    ended = exchange(sent, 1)
+    (rest,) = scalar_call(
+        fine_weights_kernel,
+        [((groups, rows + 8, 640), BF16)],
+        core, coarse_part, n, n_other, m, m_other, fac, partner(fac), gains, partner(gains),
+        scratch=[pltpu.VMEM((32, 128), F32), pltpu.VMEM((4 * groups * 8, 128), F32)],
+    )
+    rest_sum = deal(rest)
+    device = (lax.axis_index("lat") * lax.axis_size("pair") + lax.axis_index("pair")) * 2 + lax.axis_index("core")
+    output, grad, fg, fqkv, fproj, mg, merge, cg, cqkv, cproj = scalar_call(
         last_kernel,
         [
-            ((6, 12, D), BF16), ((ROWS, COLS, D), BF16), ((share, 768), F32), ((share // 2, D), F32),
-            ((rows, D), F32), ((share, 1536), F32), ((share, D), F32), ((8, 128), F32),
+            ((6, 12, D), BF16), ((ROWS, COLS, D), BF16), ((1, share), F32), ((share, 768), F32),
+            ((share // 2, D), F32), ((1, rows), F32), ((rows, D), F32), ((1, share), F32), ((share, 1536), F32),
+            ((share, D), F32),
         ],
-        jnp.full((1,), grad_scale, F32), coarse_sum, fine_sum, y2, *back, dx, *ended,
+        device.astype(jnp.int32).reshape(1), merge_sum, rest_sum, y2, *back, dx, *ended,
         table("out_main"), table("out_halo"), table("dx_main"), table("dx_halo"),
     )
-    device = (lax.axis_index("lat") * lax.axis_size("pair") + lax.axis_index("pair")) * 2 + lax.axis_index("core")
-    cg = lax.dynamic_slice(gain_sums[0], (device * share % 128,), (share,))
-    mg = lax.dynamic_slice(gain_sums[1], (device * rows % 128,), (rows,))
-    fg = lax.dynamic_slice(gain_sums[2], (device * share % 128,), (share,))
+    fg, mg, cg = (v.reshape(-1) for v in (fg, mg, cg))
     return (output, grad, fg, fqkv, fproj, mg, merge, cg, cqkv, cproj)
 
 

time: 145 us -> 140 us (0.966)
  Pallas kernels: 44.6 us -> 23 us
  local copies, waits for them, and re-layouts: 7.16 us -> 23.7 us
    pallas_call x6, Pallas kernels: 42.5 us -> 22.7 us  [scalar_call(): pl.pallas_call(kernel, out_shape=[jax.ShapeDtypeStruct(s, d) for s, d in...]
    unnamed x50 -> x114, local copies, waits for them, and re-layouts: 5.2 us -> 23.7 us
    all_to_all x2, waiting for transfers between devices: 9.86 us -> 13.8 us  [deal(): return lax.all_to_all(value, ('lat', 'pair'), 0, 0)]
    ppermute x12, waiting for transfers between devices: 45.4 us -> 42.2 us  [exchange(): arrived.append(lax.ppermute(piece, ('lat', 'pair', 'core'), pairs))]
    pallas_call x1, Pallas kernels: 2.09 us -> 0.34 us  [call(): pl.pallas_call(kernel, out_shape=[jax.ShapeDtypeStruct(s, d) for s, d in...]
    ppermute x5, waiting for transfers between devices: 2.95 us -> 1.22 us  [partner(): return lax.ppermute(value, 'core', [(0, 1), (1, 0)])]
  transfers between devices with their start and end apart: 19 -> 19, of which waited for: 9 -> 8; matrix products, arithmetic and copies ran while one was open for 0% -> 0% of each run, Pallas kernels for 11% -> 6%
where the time goes in v3:
time: 140 us; the launch traced here: 138 us
  waiting for transfers between devices  57.2 us (41%)
  starting transfers between devices  33.3 us (24%)
  local copies, waits for them, and re-layouts  23.7 us (17%)
  Pallas kernels  23 us (16%)
    ppermute x12, waiting for transfers between devices, exchange(): arrived.append(lax.ppermute(piece, ('lat', 'pair', 'core'), pairs))  42.2 us
    unnamed x114, local copies, waits for them, and re-layouts  23.7 us
    pallas_call x6, Pallas kernels, scalar_call(): pl.pallas_call(kernel, out_shape=[jax.ShapeDtypeStruct(s, d) for s, d in...  22.7 us
    ppermute x12, starting transfers between devices, exchange(): arrived.append(lax.ppermute(piece, ('lat', 'pair', 'core'), pairs))  21.5 us
    all_to_all x2, waiting for transfers between devices, deal(): return lax.all_to_all(value, ('lat', 'pair'), 0, 0)  13.8 us
    all_to_all x2, starting transfers between devices, deal(): return lax.all_to_all(value, ('lat', 'pair'), 0, 0)  10.8 us
  transfers between devices with their start and end apart: 19, of which 8 were waited for; matrix products, arithmetic and copies ran while one was open for 0% of the time, Pallas kernels for 6%

profile of v3, /device:TPU:0, one launch (start us, length us, event | category | flops | bytes accessed | tf_op | source)
XLA Modules:
  0.0 138.3 jit_solution(10616726015170933840)
XLA Ops:
  0.7 1.0 copy-done.5
  1.7 0.9 copy-done.7
  2.6 0.9 copy-done.28
  3.5 0.8 copy-done.36
  4.7 3.4 %collective-permute-start = (bf16[80,512]{1,0:T(8,128)(2,1)S(1)}, bf16[80,512]{1,0:T(8,128)(2,1)S(1)}, u32[]{:S(2)}, u32[]{:S(2)}) collective-permute-start(bf16[80,512]{1,0:T(8,128)(2,1)S(1)} %get-tuple-element.50), channel_id=1, source_target_pairs={{0,15},{1,0},{2,1},{3,2},{4,3},{5,4},{6,5},{7,6},{8,7},{9,8},{10,9... | collective-permute-start | bytes 245768 | tf_op jit(solution)/shard_map/ppermute | solution.py:524
  8.1 6.4 %collective-permute-start.1 = (bf16[80,512]{1,0:T(8,128)(2,1)S(1)}, bf16[80,512]{1,0:T(8,128)(2,1)S(1)}, u32[]{:S(2)}, u32[]{:S(2)}) collective-permute-start(bf16[80,512]{1,0:T(8,128)(2,1)S(1)} %get-tuple-element.51), channel_id=1, source_target_pairs={{0,112},{1,113},{2,114},{3,115},{4,116},{5,117},{6,118},{7,119},{8... | collective-permute-start | bytes 245768 | tf_op jit(solution)/shard_map/ppermute | solution.py:524
  14.6 4.8 %collective-permute-done.2.corner.ccorner = bf16[48,512]{1,0:T(8,128)(2,1)S(1)} collective-permute-done((bf16[48,512]{1,0:T(8,128)(2,1)S(1)}, bf16[48,512]{1,0:T(8,128)(2,1)S(1)}, u32[]{:S(2)}, u32[]{:S(2)}) %collective-permute-start.2) | collective-permute-done | bytes 49184 | tf_op jit(solution)/shard_map/ppermute | solution.py:524
  19.7 3.9 %shard_map.340 = (bf16[288,512]{1,0:T(8,128)(2,1)S(1)}, bf16[288,512]{1,0:T(8,128)(2,1)S(1)}, f32[288,768]{1,0:T(8,128)S(1)}, f32[8,72,256]{2,1,0:T(8,128)S(1)},...) custom-call(s32[1]{0:T(128)} %bitcast.2.seam, ...), custom_call_target="tpu_custom_call" | custom-call | flops 5000000000 | bytes 4000000 | tf_op jit(solution)/shard_map/pallas_call | solution.py:501
  23.6 0.7 copy-done.51
  24.7 5.2 %collective-permute-start.4 = (bf16[64,512]{1,0:T(8,128)(2,1)S(1)}, bf16[64,512]{1,0:T(8,128)(2,1)S(1)}, u32[]{:S(2)}, u32[]{:S(2)}) collective-permute-start(bf16[64,512]{1,0:T(8,128)(2,1)S(1)} %get-tuple-element.55), channel_id=1, source_target_pairs={{0,112},{1,113},{2,114},{3,115},{4,116},{5,117},{6,118},{7,119},{8... | collective-permute-start | bytes 196616 | tf_op jit(solution)/shard_map/ppermute | solution.py:524
  29.9 4.8 %collective-permute-done.5.corner = bf16[32,512]{1,0:T(8,128)(2,1)S(1)} collective-permute-done((bf16[32,512]{1,0:T(8,128)(2,1)S(1)}, bf16[32,512]{1,0:T(8,128)(2,1)S(1)}, u32[]{:S(2)}, u32[]{:S(2)}) %collective-permute-start.5) | collective-permute-done | bytes 32800 | tf_op jit(solution)/shard_map/ppermute | solution.py:524
  34.8 7.1 %shard_map.341 = (bf16[72,512]{1,0:T(8,128)(2,1)S(1)}, bf16[288,512]{1,0:T(8,128)(2,1)S(1)}, bf16[80,512]{1,0:T(8,128)(2,1)}, bf16[80,512]{1,0:T(8,128)(2,1)}, b...) custom-call(s32[1]{0:T(128)} %bitcast.2.seam, ...), custom_call_target="tpu_custom_call" | custom-call | flops 5000000000 | bytes 4000000 | tf_op jit(solution)/shard_map/pallas_call | solution.py:501
  41.9 0.7 copy-done.47
  42.7 0.6 copy-done.53
  43.3 0.6 copy-done.55
  43.9 0.5 collective-permute-start.9
  44.4 9.8 %collective-permute-done.11.corner = bf16[48,512]{1,0:T(8,128)(2,1)S(1)} collective-permute-done((bf16[48,512]{1,0:T(8,128)(2,1)}, bf16[48,512]{1,0:T(8,128)(2,1)S(1)}, u32[]{:S(2)}, u32[]{:S(2)}) %collective-permute-start.11) | collective-permute-done | bytes 49184 | tf_op jit(solution)/shard_map/ppermute | solution.py:524
  54.2 0.6 copy-done.14
  54.9 0.8 copy-done.15
  55.7 0.7 copy-done.22
  56.4 0.9 copy-done.24
  57.3 0.9 copy-done.30
  58.2 0.9 copy-done.33
  59.1 1.2 copy-done.44
  60.3 1.1 copy-done.46
  61.4 1.0 copy-done.48
  62.3 1.0 copy-done.52
  63.3 0.7 copy-done.56
  64.0 3.8 %shard_map.343 = (bf16[288,512]{1,0:T(8,128)(2,1)S(1)}, bf16[64,512]{1,0:T(8,128)(2,1)S(1)}, bf16[64,512]{1,0:T(8,128)(2,1)S(1)}, bf16[32,512]{1,0:T(8,128)(2,1)...) custom-call(s32[1]{0:T(128)} %bitcast.2.seam, bf16[288,512]{1,0:T(8,128)(2,1)S(1)} %copy-done.48, ...), custom_call_target="tpu_custom_call" | custom-call | flops 5000000000 | bytes 4000000 | tf_op jit(solution)/shard_map/pallas_call | solution.py:501
  68.1 2.1 %shard_map.342 = (bf16[64,16,512]{2,1,0:T(8,128)(2,1)}, bf16[64,16,512]{2,1,0:T(8,128)(2,1)S(1)}) custom-call(s32[1]{0:T(128)} %bitcast.1.place, bf16[80,5632]{1,0:T(8,128)(2,1)S(1)} %get-tuple-element.58.own, bf16[80,5632]{1,0:T(8,128)(2,1)S(1)} %collective-permute-done.6.other), custom_call_target="tpu_custom_call" | custom-call | flops 5000000000 | bytes 4000000 | tf_op jit(solution)/shard_map/pallas_call | solution.py:501
  70.3 1.0 copy-done.41
  71.2 6.0 %all-to-all-start = ((bf16[64,16,512]{2,1,0:T(8,128)(2,1)}), bf16[64,16,512]{2,1,0:T(8,128)(2,1)S(1)}, u32[]{:S(2)}, u32[]{:S(2)}) async-start(bf16[64,16,512]{2,1,0:T(8,128)(2,1)} %get-tuple-element.59), calls=%async_computation | async-start | bytes 2097152 | tf_op jit(solution)/shard_map/all_to_all | solution.py:533
  78.0 1.2 collective-permute-done.8.m_other
  79.2 2.7 %shard_map.344 = bf16[64,24,640]{2,1,0:T(8,128)(2,1)S(1)} custom-call(s32[1]{0:T(128)} %bitcast.1.place, bf16[64,16,512]{2,1,0:T(8,128)(2,1)S(1)} %copy-done.42, bf16[288,512]{1,0:T(8,128)(2,1)S(1)} %get-tuple-element.61.n_own, bf16[288,512]{1,0:T(8,128)(2,1)S(1)} %collective-permute-done.7.n_other, bf16[288,256]{1,0:T(8,128)(2,1)S(1)} %get-tuple-element.62.m_own, ...), custom_call_target="tpu_custom_call" | custom-call | flops 5000000000 | bytes 4000000 | tf_op jit(solution)/shard_map/pallas_call | solution.py:501
  81.9 1.3 copy-done
  83.2 13.1 %all-to-all-done.merge_in = bf16[64,16,512]{2,1,0:T(8,128)(2,1)S(1)} async-done(((bf16[64,16,512]{2,1,0:T(8,128)(2,1)}), bf16[64,16,512]{2,1,0:T(8,128)(2,1)S(1)}, u32[]{:S(2)}, u32[]{:S(2)}) %all-to-all-start) | async-done | bytes 1048608 | tf_op jit(solution)/shard_map/all_to_all | solution.py:533
  96.3 4.8 %all-to-all-start.1 = ((bf16[64,24,640]{2,1,0:T(8,128)(2,1)}), bf16[64,24,640]{2,1,0:T(8,128)(2,1)S(1)}, u32[]{:S(2)}, u32[]{:S(2)}) async-start(bf16[64,24,640]{2,1,0:T(8,128)(2,1)} %copy-done), calls=%async_computation.1 | async-start | bytes 3932160 | tf_op jit(solution)/shard_map/all_to_all | solution.py:533
  101.2 3.1 %collective-permute-start.15 = (bf16[64,512]{1,0:T(8,128)(2,1)S(1)}, bf16[64,512]{1,0:T(8,128)(2,1)S(1)}, u32[]{:S(2)}, u32[]{:S(2)}) collective-permute-start(bf16[64,512]{1,0:T(8,128)(2,1)S(1)} %copy-done.11), channel_id=1, source_target_pairs={{0,16},{1,17},{2,18},{3,19},{4,20},{5,21},{6,22},{7,23},{8,24},{9,... | collective-permute-start | bytes 196616 | tf_op jit(solution)/shard_map/ppermute | solution.py:524
  104.3 2.3 %collective-permute-start.16 = (bf16[32,512]{1,0:T(8,128)(2,1)S(1)}, bf16[32,512]{1,0:T(8,128)(2,1)}, u32[]{:S(2)}, u32[]{:S(2)}) collective-permute-start(bf16[32,512]{1,0:T(8,128)(2,1)S(1)} %copy-done.18), channel_id=1, source_target_pairs={{0,17},{1,18},{2,19},{3,20},{4,21},{5,22},{6,23},{7,24},{8,25},{9,... | collective-permute-start | bytes 98312 | tf_op jit(solution)/shard_map/ppermute | solution.py:524
  106.6 22.4 %collective-permute-done.16.dcorner = bf16[32,512]{1,0:T(8,128)(2,1)} collective-permute-done((bf16[32,512]{1,0:T(8,128)(2,1)S(1)}, bf16[32,512]{1,0:T(8,128)(2,1)}, u32[]{:S(2)}, u32[]{:S(2)}) %collective-permute-start.16) | collective-permute-done | bytes 32800 | tf_op jit(solution)/shard_map/ppermute | solution.py:524
  129.3 0.7 all-to-all-done.1.rest
  130.0 0.9 copy-done.23
  130.9 0.9 copy-done.29
  131.8 0.8 copy-done.37
  132.6 0.7 copy-done.39
  133.3 1.0 copy-done.50
  134.3 0.9 copy-done.54
  135.2 3.1 %shard_map.345 = (bf16[6,12,512]{2,1,0:T(8,128)(2,1)}, bf16[12,24,512]{2,1,0:T(8,128)(2,1)}, f32[1,4]{1,0:T(1,128)}, f32[4,768]{1,0:T(4,128)}, f32[2,512]{1,0:T(...) custom-call(s32[1]{0:T(128)} %bitcast.place, ...), custom_call_target="tpu_custom_call" | custom-call | flops 5000000000 | bytes 4000000 | tf_op jit(solution)/shard_map/pallas_call | solution.py:501
  (111 shorter events, 2.5 us)
Async XLA Ops:
  0.6 18.8 %copy-start.3 = (bf16[512,768]{1,0:T(8,128)(2,1)S(1)}, bf16[512,768]{1,0:T(8,128)(2,1)}, u32[]{:S(2)}) copy-start(bf16[512,768]{1,0:T(8,128)(2,1)} %wqkv.5) | copy-start | bytes 2359300
  4.3 15.2 %copy-start.6 = (bf16[256,512]{1,0:T(8,128)(2,1)S(1)}, bf16[256,512]{1,0:T(8,128)(2,1)}, u32[]{:S(2)}) copy-start(bf16[256,512]{1,0:T(8,128)(2,1)} %wproj.5) | copy-start | bytes 786436
  4.3 15.2 %copy-start.21 = (f32[512]{0:T(512)S(1)}, f32[512]{0:T(512)}, u32[]{:S(2)}) copy-start(f32[512]{0:T(512)} %param.29) | copy-start | bytes 6148
  4.3 15.2 %copy-start.26 = (bf16[288,288]{1,0:T(8,128)(2,1)S(1)}, bf16[288,288]{1,0:T(8,128)(2,1)}, u32[]{:S(2)}) copy-start(bf16[288,288]{1,0:T(8,128)(2,1)} %constant.56.clone.t_main) | copy-start | bytes 497668
  4.3 15.2 %copy-start.32 = (bf16[288,208]{1,0:T(8,128)(2,1)S(1)}, bf16[288,208]{1,0:T(8,128)(2,1)}, u32[]{:S(2)}) copy-start(bf16[288,208]{1,0:T(8,128)(2,1)} %constant.57.clone.t_halo) | copy-start | bytes 359428
  4.3 15.2 %copy-start.34 = (bf16[160,288]{1,0:T(8,128)(2,1)S(1)}, bf16[160,288]{1,0:T(8,128)(2,1)}, u32[]{:S(2)}) copy-start(bf16[160,288]{1,0:T(8,128)(2,1)} %constant.58.clone.y_send) | copy-start | bytes 276484
  4.7 14.8 %collective-permute-start = (bf16[80,512]{1,0:T(8,128)(2,1)S(1)}, bf16[80,512]{1,0:T(8,128)(2,1)S(1)}, u32[]{:S(2)}, u32[]{:S(2)}) collective-permute-start(bf16[80,512]{1,0:T(8,128)(2,1)S(1)} %get-tuple-element.50), channel_id=1, source_target_pairs={{0,15},{1,0},{2,1},{3,2},{4,3},{5,4},{6,5},{7,6},{8,7},{9,8},{10,9... | collective-permute-start | bytes 245768 | tf_op jit(solution)/shard_map/ppermute | solution.py:524
  8.1 11.4 %collective-permute-start.1 = (bf16[80,512]{1,0:T(8,128)(2,1)S(1)}, bf16[80,512]{1,0:T(8,128)(2,1)S(1)}, u32[]{:S(2)}, u32[]{:S(2)}) collective-permute-start(bf16[80,512]{1,0:T(8,128)(2,1)S(1)} %get-tuple-element.51), channel_id=1, source_target_pairs={{0,112},{1,113},{2,114},{3,115},{4,116},{5,117},{6,118},{7,119},{8... | collective-permute-start | bytes 245768 | tf_op jit(solution)/shard_map/ppermute | solution.py:524
  14.4 5.0 %collective-permute-start.2 = (bf16[48,512]{1,0:T(8,128)(2,1)S(1)}, bf16[48,512]{1,0:T(8,128)(2,1)S(1)}, u32[]{:S(2)}, u32[]{:S(2)}) collective-permute-start(bf16[48,512]{1,0:T(8,128)(2,1)S(1)} %get-tuple-element.52), channel_id=1, source_target_pairs={{0,127},{1,112},{2,113},{3,114},{4,115},{5,116},{6,117},{7,118},{8... | collective-permute-start | bytes 147464 | tf_op jit(solution)/shard_map/ppermute | solution.py:524
  19.5 15.2 %copy-start.1 = (bf16[2048,512]{1,0:T(8,128)(2,1)S(1)}, bf16[2048,512]{1,0:T(8,128)(2,1)}, u32[]{:S(2)}) copy-start(bf16[2048,512]{1,0:T(8,128)(2,1)} %mweight.1) | copy-start | bytes 6291460
  19.5 15.2 %copy-start.2 = (bf16[512,1536]{1,0:T(8,128)(2,1)S(1)}, bf16[512,1536]{1,0:T(8,128)(2,1)}, u32[]{:S(2)}) copy-start(bf16[512,1536]{1,0:T(8,128)(2,1)} %wqkv.4) | copy-start | bytes 4718596
  19.5 15.2 %copy-start.4 = (bf16[512,512]{1,0:T(8,128)(2,1)S(1)}, bf16[512,512]{1,0:T(8,128)(2,1)}, u32[]{:S(2)}) copy-start(bf16[512,512]{1,0:T(8,128)(2,1)} %wproj.4) | copy-start | bytes 1572868
  19.6 15.2 %copy-start.19 = (f32[2048]{0:T(1024)S(1)}, f32[2048]{0:T(1024)}, u32[]{:S(2)}) copy-start(f32[2048]{0:T(1024)} %param.32) | copy-start | bytes 24580
  19.6 15.2 %copy-start.20 = (f32[512]{0:T(512)S(1)}, f32[512]{0:T(512)}, u32[]{:S(2)}) copy-start(f32[512]{0:T(512)} %param.34) | copy-start | bytes 6148
  19.6 15.2 %copy-start.25 = (bf16[288,288]{1,0:T(8,128)(2,1)S(1)}, bf16[288,288]{1,0:T(8,128)(2,1)}, u32[]{:S(2)}) copy-start(bf16[288,288]{1,0:T(8,128)(2,1)} %constant.59.clone.y_main) | copy-start | bytes 497668
  19.6 15.2 %copy-start.27 = (bf16[208,288]{1,0:T(8,128)(2,1)S(1)}, bf16[208,288]{1,0:T(8,128)(2,1)}, u32[]{:S(2)}) copy-start(bf16[208,288]{1,0:T(8,128)(2,1)} %constant.63.clone.df_send) | copy-start | bytes 359428
  19.6 15.2 %copy-start.31 = (bf16[288,160]{1,0:T(8,128)(2,1)S(1)}, bf16[288,160]{1,0:T(8,128)(2,1)}, u32[]{:S(2)}) copy-start(bf16[288,160]{1,0:T(8,128)(2,1)} %constant.60.clone.y_halo) | copy-start | bytes 276484
  19.6 15.2 %copy-start.35 = (bf16[208,72]{1,0:T(8,128)(2,1)S(1)}, bf16[208,72]{1,0:T(8,128)(2,1)}, u32[]{:S(2)}) copy-start(bf16[208,72]{1,0:T(8,128)(2,1)} %constant.64.clone.out_send) | copy-start | bytes 89860
  19.6 15.2 %copy-start.38 = (bf16[72,208]{1,0:T(8,128)(2,1)S(1)}, bf16[72,208]{1,0:T(8,128)(2,1)}, u32[]{:S(2)}) copy-start(bf16[72,208]{1,0:T(8,128)(2,1)} %constant.62.clone.c_halo) | copy-start | bytes 89860
  19.6 15.2 %copy-start.40 = (bf16[72,72]{1,0:T(8,128)(2,1)S(1)}, bf16[72,72]{1,0:T(8,128)(2,1)}, u32[]{:S(2)}) copy-start(bf16[72,72]{1,0:T(8,128)(2,1)} %constant.61.clone.c_main) | copy-start | bytes 31108
  24.3 17.6 %copy-start.43 = (f32[288,768]{1,0:T(8,128)}, f32[288,768]{1,0:T(8,128)S(1)}, u32[]{:S(2)}) copy-start(f32[288,768]{1,0:T(8,128)S(1)} %get-tuple-element.68.p_in) | copy-start | bytes 2654212
  24.3 17.6 %copy-start.45 = (f32[8,72,256]{2,1,0:T(8,128)}, f32[8,72,256]{2,1,0:T(8,128)S(1)}, u32[]{:S(2)}) copy-start(f32[8,72,256]{2,1,0:T(8,128)S(1)} %get-tuple-element.69.w_in) | copy-start | bytes 1769476
  24.3 10.4 %collective-permute-start.3 = (bf16[64,512]{1,0:T(8,128)(2,1)S(1)}, bf16[64,512]{1,0:T(8,128)(2,1)S(1)}, u32[]{:S(2)}, u32[]{:S(2)}) collective-permute-start(bf16[64,512]{1,0:T(8,128)(2,1)S(1)} %get-tuple-element.54), channel_id=1, source_target_pairs={{0,15},{1,0},{2,1},{3,2},{4,3},{5,4},{6,5},{7,6},{8,7},{9,8},{10,9... | collective-permute-start | bytes 196616 | tf_op jit(solution)/shard_map/ppermute | solution.py:524
  24.7 10.0 %collective-permute-start.4 = (bf16[64,512]{1,0:T(8,128)(2,1)S(1)}, bf16[64,512]{1,0:T(8,128)(2,1)S(1)}, u32[]{:S(2)}, u32[]{:S(2)}) collective-permute-start(bf16[64,512]{1,0:T(8,128)(2,1)S(1)} %get-tuple-element.55), channel_id=1, source_target_pairs={{0,112},{1,113},{2,114},{3,115},{4,116},{5,117},{6,118},{7,119},{8... | collective-permute-start | bytes 196616 | tf_op jit(solution)/shard_map/ppermute | solution.py:524
  29.9 4.8 %collective-permute-start.5 = (bf16[32,512]{1,0:T(8,128)(2,1)S(1)}, bf16[32,512]{1,0:T(8,128)(2,1)S(1)}, u32[]{:S(2)}, u32[]{:S(2)}) collective-permute-start(bf16[32,512]{1,0:T(8,128)(2,1)S(1)} %get-tuple-element.56), channel_id=1, source_target_pairs={{0,127},{1,112},{2,113},{3,114},{4,115},{5,116},{6,117},{7,118},{8... | collective-permute-start | bytes 98312 | tf_op jit(solution)/shard_map/ppermute | solution.py:524
  43.9 24.2 %collective-permute-start.6 = (bf16[80,5632]{1,0:T(8,128)(2,1)S(1)}, bf16[80,5632]{1,0:T(8,128)(2,1)S(1)}, u32[]{:S(2)}, u32[]{:S(2)}) collective-permute-start(bf16[80,5632]{1,0:T(8,128)(2,1)S(1)} %get-tuple-element.58.own), channel_id=1, source_target_pairs={{0,1},{1,0},{2,3},{3,2},{4,5},{5,4},{6,7},{7,6},{8,9},{9,8},{10,11... | collective-permute-start | bytes 2703368 | tf_op jit(solution)/shard_map/ppermute | solution.py:529
  43.9 11.0 %collective-permute-start.9 = (bf16[80,512]{1,0:T(8,128)(2,1)}, bf16[80,512]{1,0:T(8,128)(2,1)S(1)}, u32[]{:S(2)}, u32[]{:S(2)}) collective-permute-start(bf16[80,512]{1,0:T(8,128)(2,1)} %get-tuple-element.64), channel_id=1, source_target_pairs={{0,1},{1,2},{2,3},{3,4},{4,5},{5,6},{6,7},{7,8},{8,9},{9,10},{10,1... | collective-permute-start | bytes 245768 | tf_op jit(solution)/shard_map/ppermute | solution.py:524
  44.4 10.5 %collective-permute-start.10 = (bf16[80,512]{1,0:T(8,128)(2,1)}, bf16[80,512]{1,0:T(8,128)(2,1)S(1)}, u32[]{:S(2)}, u32[]{:S(2)}) collective-permute-start(bf16[80,512]{1,0:T(8,128)(2,1)} %get-tuple-element.65), channel_id=1, source_target_pairs={{0,16},{1,17},{2,18},{3,19},{4,20},{5,21},{6,22},{7,23},{8,24},{9,... | collective-permute-start | bytes 245768 | tf_op jit(solution)/shard_map/ppermute | solution.py:524
  44.4 9.8 %collective-permute-start.11 = (bf16[48,512]{1,0:T(8,128)(2,1)}, bf16[48,512]{1,0:T(8,128)(2,1)S(1)}, u32[]{:S(2)}, u32[]{:S(2)}) collective-permute-start(bf16[48,512]{1,0:T(8,128)(2,1)} %get-tuple-element.66), channel_id=1, source_target_pairs={{0,17},{1,18},{2,19},{3,20},{4,21},{5,22},{6,23},{7,24},{8,25},{9,... | collective-permute-start | bytes 147464 | tf_op jit(solution)/shard_map/ppermute | solution.py:524
  54.9 12.9 %copy-start.8 = (bf16[80,512]{1,0:T(8,128)(2,1)}, bf16[80,512]{1,0:T(8,128)(2,1)S(1)}, u32[]{:S(2)}) copy-start(bf16[80,512]{1,0:T(8,128)(2,1)S(1)} %collective-permute-done.10.edge) | copy-start | bytes 245764
  67.8 2.4 %copy-start.12 = (bf16[64,512]{1,0:T(8,128)(2,1)}, bf16[64,512]{1,0:T(8,128)(2,1)S(1)}, u32[]{:S(2)}) copy-start(bf16[64,512]{1,0:T(8,128)(2,1)S(1)} %get-tuple-element.75) | copy-start | bytes 196612
  67.8 2.5 %copy-start.17 = (bf16[32,512]{1,0:T(8,128)(2,1)}, bf16[32,512]{1,0:T(8,128)(2,1)S(1)}, u32[]{:S(2)}) copy-start(bf16[32,512]{1,0:T(8,128)(2,1)S(1)} %get-tuple-element.77) | copy-start | bytes 98308
  67.8 2.5 %copy-start.49 = (bf16[288,512]{1,0:T(8,128)(2,1)}, bf16[288,512]{1,0:T(8,128)(2,1)S(1)}, u32[]{:S(2)}) copy-start(bf16[288,512]{1,0:T(8,128)(2,1)S(1)} %get-tuple-element.74.dx) | copy-start | bytes 884740
  67.8 11.4 %collective-permute-start.12 = (bf16[288,1280]{1,0:T(8,128)(2,1)}, bf16[288,1280]{1,0:T(8,128)(2,1)}, u32[]{:S(2)}, u32[]{:S(2)}) collective-permute-start(bf16[288,1280]{1,0:T(8,128)(2,1)} %get-tuple-element.71.own), channel_id=1, source_target_pairs={{0,1},{1,0},{2,3},{3,2},{4,5},{5,4},{6,7},{7,6},{8,9},{9,8},{10,11... | collective-permute-start | bytes 2211848 | tf_op jit(solution)/shard_map/ppermute | solution.py:529
  71.2 8.0 %copy-start.42 = (bf16[64,16,512]{2,1,0:T(8,128)(2,1)S(1)}, bf16[64,16,512]{2,1,0:T(8,128)(2,1)}, u32[]{:S(2)}) copy-start(bf16[64,16,512]{2,1,0:T(8,128)(2,1)} %copy-done.41) | copy-start | bytes 3145732
  71.2 25.0 %all-to-all-start = ((bf16[64,16,512]{2,1,0:T(8,128)(2,1)}), bf16[64,16,512]{2,1,0:T(8,128)(2,1)S(1)}, u32[]{:S(2)}, u32[]{:S(2)}) async-start(bf16[64,16,512]{2,1,0:T(8,128)(2,1)} %get-tuple-element.59), calls=%async_computation | async-start | bytes 2097152 | tf_op jit(solution)/shard_map/all_to_all | solution.py:533
  77.3 1.9 %collective-permute-start.7 = (bf16[288,512]{1,0:T(8,128)(2,1)S(1)}, bf16[288,512]{1,0:T(8,128)(2,1)S(1)}, u32[]{:S(2)}, u32[]{:S(2)}) collective-permute-start(bf16[288,512]{1,0:T(8,128)(2,1)S(1)} %get-tuple-element.61.n_own), channel_id=1, source_target_pairs={{0,1},{1,0},{2,3},{3,2},{4,5},{5,4},{6,7},{7,6},{8,9},{9,8},{10,11... | collective-permute-start | bytes 884744 | tf_op jit(solution)/shard_map/ppermute | solution.py:529
  77.4 1.8 %collective-permute-start.8 = (bf16[288,256]{1,0:T(8,128)(2,1)S(1)}, bf16[288,256]{1,0:T(8,128)(2,1)S(1)}, u32[]{:S(2)}, u32[]{:S(2)}) collective-permute-start(bf16[288,256]{1,0:T(8,128)(2,1)S(1)} %get-tuple-element.62.m_own), channel_id=1, source_target_pairs={{0,1},{1,0},{2,3},{3,2},{4,5},{5,4},{6,7},{7,6},{8,9},{9,8},{10,11... | collective-permute-start | bytes 442376 | tf_op jit(solution)/shard_map/ppermute | solution.py:529
  77.9 1.3 collective-permute-start.13
  83.1 17.9 %copy-start.13 = (bf16[64,512]{1,0:T(8,128)(2,1)S(1)}, bf16[64,512]{1,0:T(8,128)(2,1)}, u32[]{:S(2)}) copy-start(bf16[64,512]{1,0:T(8,128)(2,1)} %copy-done.12) | copy-start | bytes 196612
  83.1 18.0 %copy-start.11 = (bf16[64,512]{1,0:T(8,128)(2,1)S(1)}, bf16[64,512]{1,0:T(8,128)(2,1)}, u32[]{:S(2)}) copy-start(bf16[64,512]{1,0:T(8,128)(2,1)} %copy-done.10) | copy-start | bytes 196612
  83.1 21.2 %copy-start.18 = (bf16[32,512]{1,0:T(8,128)(2,1)S(1)}, bf16[32,512]{1,0:T(8,128)(2,1)}, u32[]{:S(2)}) copy-start(bf16[32,512]{1,0:T(8,128)(2,1)} %copy-done.17) | copy-start | bytes 98308
  83.1 46.8 %copy-start.9 = (bf16[80,512]{1,0:T(8,128)(2,1)S(1)}, bf16[80,512]{1,0:T(8,128)(2,1)}, u32[]{:S(2)}) copy-start(bf16[80,512]{1,0:T(8,128)(2,1)} %copy-done.8) | copy-start | bytes 245764
  83.1 46.8 %copy-start.16 = (bf16[48,512]{1,0:T(8,128)(2,1)S(1)}, bf16[48,512]{1,0:T(8,128)(2,1)}, u32[]{:S(2)}) copy-start(bf16[48,512]{1,0:T(8,128)(2,1)} %copy-done.14) | copy-start | bytes 147460
  96.3 33.7 %all-to-all-start.1 = ((bf16[64,24,640]{2,1,0:T(8,128)(2,1)}), bf16[64,24,640]{2,1,0:T(8,128)(2,1)S(1)}, u32[]{:S(2)}, u32[]{:S(2)}) async-start(bf16[64,24,640]{2,1,0:T(8,128)(2,1)} %copy-done), calls=%async_computation.1 | async-start | bytes 3932160 | tf_op jit(solution)/shard_map/all_to_all | solution.py:533
  101.1 27.9 %collective-permute-start.14 = (bf16[64,512]{1,0:T(8,128)(2,1)S(1)}, bf16[64,512]{1,0:T(8,128)(2,1)S(1)}, u32[]{:S(2)}, u32[]{:S(2)}) collective-permute-start(bf16[64,512]{1,0:T(8,128)(2,1)S(1)} %copy-done.13), channel_id=1, source_target_pairs={{0,1},{1,2},{2,3},{3,4},{4,5},{5,6},{6,7},{7,8},{8,9},{9,10},{10,1... | collective-permute-start | bytes 196616 | tf_op jit(solution)/shard_map/ppermute | solution.py:524
  101.2 28.1 %collective-permute-start.15 = (bf16[64,512]{1,0:T(8,128)(2,1)S(1)}, bf16[64,512]{1,0:T(8,128)(2,1)S(1)}, u32[]{:S(2)}, u32[]{:S(2)}) collective-permute-start(bf16[64,512]{1,0:T(8,128)(2,1)S(1)} %copy-done.11), channel_id=1, source_target_pairs={{0,16},{1,17},{2,18},{3,19},{4,20},{5,21},{6,22},{7,23},{8,24},{9,... | collective-permute-start | bytes 196616 | tf_op jit(solution)/shard_map/ppermute | solution.py:524
  104.3 24.7 %collective-permute-start.16 = (bf16[32,512]{1,0:T(8,128)(2,1)S(1)}, bf16[32,512]{1,0:T(8,128)(2,1)}, u32[]{:S(2)}, u32[]{:S(2)}) collective-permute-start(bf16[32,512]{1,0:T(8,128)(2,1)S(1)} %copy-done.18), channel_id=1, source_target_pairs={{0,17},{1,18},{2,19},{3,20},{4,21},{5,22},{6,23},{7,24},{8,25},{9,... | collective-permute-start | bytes 98312 | tf_op jit(solution)/shard_map/ppermute | solution.py:524
  (28 other events, 26.0 us)

commit v4 on v3

--- a/solution.py
+++ b/solution.py
@@ -18,6 +18,8 @@
 NEGATIVE = -1000000000.0
 LOWEST = -3.0e38
 INTERPRET = False
+VMEM_SPEC = pl.BlockSpec(memory_space=pltpu.VMEM)
+SMEM_SPEC = pl.BlockSpec(memory_space=pltpu.SMEM)
 VMEM_LIMIT = 12 * 1024 * 1024
 FLOPS = 5_000_000_000
 BYTES = 4_000_000
@@ -156,15 +158,21 @@
     return x.astype(BF16).astype(F32)
 
 
-def call(kernel, outs, *args, scratch=()):
+def call(kernel, outs, *args, scratch=(), specs=None, limit=None):
     return pl.pallas_call(
         kernel,
         out_shape=[jax.ShapeDtypeStruct(s, d) for s, d in outs],
+        in_specs=specs or [VMEM_SPEC] * len(args),
+        out_specs=[VMEM_SPEC] * len(outs),
         scratch_shapes=list(scratch),
-        compiler_params=pltpu.CompilerParams(vmem_limit_bytes=VMEM_LIMIT),
+        compiler_params=pltpu.CompilerParams(vmem_limit_bytes=limit or VMEM_LIMIT),
         cost_estimate=pl.CostEstimate(flops=FLOPS, bytes_accessed=BYTES, transcendentals=0),
         interpret=INTERPRET,
     )(*args)
+
+
+def scalar_call(kernel, outs, scalar, *args, scratch=()):
+    return call(kernel, outs, scalar, *args, scratch=scratch, specs=[SMEM_SPEC] + [VMEM_SPEC] * len(args))
 
 
 def cut(stack, *refs):
@@ -242,7 +250,20 @@
     return dq, dk, dv
 
 
-def first_kernel(tok, cot, tok_send, cot_send, tok2d, side, edge, corner, cot2d):
+def first_kernel(
+    tok_in, cot_in, tok_send_in, cot_send_in, tok2d, side, edge, corner, cot2d,
+    tok, cot, tok_send, cot_send, arrived,
+):
+    loads = [
+        pltpu.make_async_copy(source, target, arrived.at[i])
+        for i, (source, target) in enumerate(
+            ((tok_in, tok), (cot_in, cot), (tok_send_in, tok_send), (cot_send_in, cot_send))
+        )
+    ]
+    for load in loads:
+        load.start()
+    for load in loads:
+        load.wait()
     x = tok[...].astype(F32).reshape(ROWS * COLS, D).astype(BF16)
     tok2d[...] = x
     for r in range(6):
@@ -253,7 +274,7 @@
 
 
 def fine_forward_kernel(
-    seam, x_in, side, edge, corner, gain, wqkv, wproj, t_main, t_halo, y_send,
+    place, x_in, side, edge, corner, gain, wqkv, wproj, t_main, t_halo, y_send,
     x_out, n_out, p_out, w_out, m_out, y_out, side_out, edge_out, corner_out, mixed,
 ):
     halo = jnp.concatenate([side[...], edge[...], corner[...]], axis=0)
@@ -264,7 +285,7 @@
     n_out[...] = n
     p_out[...] = rounded(mm(n, wqkv[...]))
     for w in range(WINDOWS):
-        differ = apart((seam[0] == 1) if w >= 2 else False)
+        differ = apart(decode(place)[2] == 1 if w >= 2 else False)
         for p in range(HF // 2):
             rows = pl.ds(CELLS * w, CELLS)
             q, k, v = (p_out[rows, pl.ds(256 * part + 128 * p, 128)] for part in range(3))
@@ -280,7 +301,7 @@
 
 
 def coarse_kernel(
-    seam, y_in, side, edge, corner, cot_in, cside, cedge, ccorner,
+    place, y_in, side, edge, corner, cot_in, cside, cedge, ccorner,
     mgain, mweight, gain, wqkv, wproj, y_main, y_halo, c_main, c_halo, df_send, out_send,
     y2_out, df_out, side_out, edge_out, corner_out, fac_out, gains_out, packed, mixed, dpacked, wsave,
 ):
@@ -293,7 +314,7 @@
     zhat, zinv = normalize(z)
     n = (zhat * gain[...]).astype(BF16)
     packed[...] = rounded(mm(n, wqkv[...]))
-    differ = apart(seam[0] == 1)
+    differ = apart(decode(place)[2] == 1)
     for p in range(HC // 2):
         lanes = pl.ds(128 * p, 128)
         q, k, v = (packed[:, pl.ds(512 * part + 128 * p, 128)] for part in range(3))
@@ -335,14 +356,14 @@
 
 
 def fine_backward_kernel(
-    seam, df_in, side, edge, corner, x_in, p_in, w_in, gain, wqkv, wproj, d_main, d_halo, dx_send, gains_in,
+    place, df_in, side, edge, corner, x_in, p_in, w_in, gain, wqkv, wproj, d_main, d_halo, dx_send, gains_in,
     dx_out, side_out, edge_out, corner_out, fac_out, gains_out, dmixed, dpacked,
 ):
     halo = jnp.concatenate([side[...], edge[...], corner[...]], axis=0)
     dy = mm(d_main[...], df_in[...]) + mm(d_halo[...], halo)
     dmixed[...] = rounded(mm_nt(dy.astype(BF16), wproj[...]))
     for w in range(WINDOWS):
-        differ = apart((seam[0] == 1) if w >= 2 else False)
+        differ = apart(decode(place)[2] == 1 if w >= 2 else False)
         for p in range(HF // 2):
             rows = pl.ds(CELLS * w, CELLS)
             q, k, v = (p_in[rows, pl.ds(256 * part + 128 * p, 128)] for part in range(3))
@@ -363,6 +384,12 @@
     fac_out[:, pl.ds(768, D)] = dy.astype(BF16)
 
 
+def decode(place):
+    code = place[0]
+    shifted = [code] + [lax.shift_right_logical(code, i) for i in (1, 2, 3)]
+    return tuple(lax.bitwise_and(v, 1) for v in shifted[:3]) + (shifted[3],)
+
+
 def one_hot(want, width):
     lane = lax.broadcasted_iota(jnp.int32, (want.shape[0], width), 1)
     return jnp.where(lane == want, 1.0, 0.0).astype(BF16)
@@ -379,42 +406,64 @@
     return one_hot((2 * group + core) * share + i, width)
 
 
-def coarse_weights_kernel(place, own, other, merge_out, out, lines):
-    core = place[0]
-    groups, rows = out.shape[:2]
-    share = D // (2 * groups)
+def coarse_weights_kernel(place, own, other, merge_keep, merge_send, coarse_keep, coarse_send, lines):
+    core, parity, _, _ = decode(place)
+    block, tall = (merge_keep.shape[0] // 2, merge_keep.shape[1])
+    rows = tall // 4
+    groups = 4 * block
+    share = rows // 4
 
     def at(start, size):
         return jnp.concatenate([own[:, pl.ds(start, size)], other[:, pl.ds(start, size)]], axis=0)
 
+    def put(b, h, value, same, differs):
+        place_of = (pl.ds(block * (b // 2), block), pl.ds(rows * h, rows), slice(None))
+
+        @pl.when(parity == b % 2)
+        def _():
+            same[place_of] = value
+
+        @pl.when(parity != b % 2)
+        def _():
+            differs[place_of] = value
+
     dz = at(2048 + 1024, D)
     select = own_rows(rows, D, core, True)
-    g = D // 2 // rows
     for b in range(4):
         left = mm_nt(select, at(D * b, D)).astype(BF16)
-        merge_out[pl.ds(g * b, g), :, :] = mm(left, dz).reshape(g, rows, D).astype(BF16)
+        part = mm(left, dz).reshape(block, rows, D).astype(BF16)
+        for h in range(4):
+            put(b, h, part[:, :, 128 * h : 128 * h + 128], merge_keep, merge_send)
     select = own_rows(share, D, core, False)
     n = mm_nt(select, at(2048, D)).astype(BF16)
     m = mm_nt(select, at(2048 + D, D)).astype(BF16)
     for j in range(4):
         part = mm(n if j < 3 else m, at(2048 + 1536 + D * j, D))
         for i in range(share):
+            line = part[groups * i : groups * (i + 1)]
             for h in range(4):
-                lines[pl.ds(groups * rows * h + share * j + i, groups, rows), :] = part[groups * i : groups * (i + 1), 128 * h : 128 * h + 128]
+                lines[pl.ds(groups * rows * h + share * j + i, groups, rows), :] = line[:, 128 * h : 128 * h + 128]
     for h in range(4):
-        out[:, :, pl.ds(128 * h, 128)] = lines[pl.ds(groups * rows * h, groups * rows), :].reshape(groups, rows, 128).astype(BF16)
+        for b in range(4):
+            chunk = lines[pl.ds(groups * rows * h + block * rows * b, block * rows), :]
+            put(b, h, chunk.reshape(block, rows, 128).astype(BF16), coarse_send, coarse_keep)
 
 
 def fine_weights_kernel(
-    place, coarse, n_own, n_other, m_own, m_other, own, other, gains, gains_other, out, chunks, lines
+    place, merge_keep, merge_came, coarse_keep, coarse_came, n_own, n_other, m_own, m_other, own, other,
+    gains, gains_other, out, chunks, lines,
 ):
-    core = place[0]
+    core, parity, _, _ = decode(place)
     groups = out.shape[0]
+    block, top = (merge_keep.shape[0] // 2, merge_keep.shape[1])
     rows = 8
     share = D // (2 * groups)
-    top = coarse.shape[1]
-    out[:, pl.ds(0, top), pl.ds(0, D)] = coarse[...]
-    out[:, pl.ds(0, top), pl.ds(D, 128)] = jnp.zeros((groups, top, 128), BF16)
+    for k in range(2):
+        part = pl.ds(block * k, block)
+        merge = merge_keep[part].astype(F32) + merge_came[part].astype(F32)
+        coarse = coarse_keep[part].astype(F32) + coarse_came[part].astype(F32)
+        out[pl.ds(block * (2 * k + parity), block), pl.ds(0, top), :] = merge.astype(BF16)
+        out[pl.ds(block * (2 * k + 1 - parity), block), pl.ds(0, top), :] = coarse.astype(BF16)
     select = own_rows(share, D, core, False)
     dp = lambda ref: ref[:, pl.ds(0, 768)]
     dy = lambda ref: ref[:, pl.ds(768, D)]
@@ -435,7 +484,8 @@
         for h in range(4):
             lines[pl.ds(groups * rows * h + share + half + i, groups, rows), :] = line[:, 128 * h : 128 * h + 128]
     for h in range(4):
-        out[:, pl.ds(top, rows), pl.ds(128 * h, 128)] = lines[pl.ds(groups * rows * h, groups * rows), :].reshape(groups, rows, 128).astype(BF16)
+        chunk = lines[pl.ds(groups * rows * h, groups * rows), :]
+        out[:, pl.ds(top + rows * h, rows), :] = chunk.reshape(groups, rows, 128).astype(BF16)
     both_gains = gains[...] + gains_other[...]
     for r in range(6):
         for q in range(4):
@@ -450,40 +500,14 @@
         small,
         jnp.where(r == 1, 4 + lax.shift_right_logical(device * share * 4, 7), jnp.where(r == 2, 20 + small, -1)),
     )
-    out[:, pl.ds(top, rows), pl.ds(512, 128)] = (
+    out[:, pl.ds(top + 4 * rows, rows), :] = (
         mm(one_hot(want, 32), chunks[...].astype(BF16)).reshape(groups, rows, 128).astype(BF16)
     )
 
 
-def total_of(ref):
-    def step(i, acc):
-        return acc + ref[i].astype(F32)
-
-    return lax.fori_loop(1, ref.shape[0], step, ref[0].astype(F32))
-
-
-def last_kernel(
-    place, merge_in, rest, y2, side, edge, corner, dx, dside, dedge, dcorner, out_main, out_halo, dx_main, dx_halo,
-    out, grad, fgain, fqkv, fproj, mgain, merge, cgain, cqkv, cproj,
+def assemble_kernel(
+    y2, side, edge, corner, dx, dside, dedge, dcorner, out_main, out_halo, dx_main, dx_halo, out, grad
 ):
-    rows = merge_in.shape[1]
-    share = rows // 4
-    half = share // 2
-    factor = (ROWS * COLS * D // share // 4) ** (-0.5)
-    merge[...] = total_of(merge_in) * factor
-    total = total_of(rest) * factor
-    for j in range(3):
-        cqkv[:, pl.ds(D * j, D)] = total[share * j : share * (j + 1), :D]
-    cproj[...] = total[3 * share : rows, :D]
-    total = total[rows:]
-    fqkv[:, pl.ds(0, D)] = total[:share, :D]
-    for h in range(2):
-        fqkv[pl.ds(half * h, half), pl.ds(D, 256)] = total[share : share + half, 256 * h : 256 * h + 256]
-    fproj[...] = total[share + half :, :D]
-    for r, (ref, size) in enumerate(((cgain, share), (mgain, rows), (fgain, share))):
-        first = lax.rem(place[0] * size, 128)
-        turned = pltpu.roll(total[:, D:], lax.rem(128 - first, 128), 1)
-        ref[...] = turned[r : r + 1, :size]
     halo = jnp.concatenate([side[...], edge[...], corner[...]], axis=0)
     y = mm(out_main[...], y2[...]) + mm(out_halo[...], halo)
     for r in range(6):
@@ -493,21 +517,41 @@
     grad[...] = d.reshape(ROWS, COLS, D).astype(BF16)
 
 
-SEAM = pl.BlockSpec(memory_space=pltpu.SMEM)
-
-
-def scalar_call(kernel, outs, scalar, *args, scratch=()):
-    vmem = pl.BlockSpec(memory_space=pltpu.VMEM)
-    return pl.pallas_call(
-        kernel,
-        out_shape=[jax.ShapeDtypeStruct(s, d) for s, d in outs],
-        in_specs=[SEAM] + [vmem] * len(args),
-        out_specs=[vmem] * len(outs),
-        scratch_shapes=list(scratch),
-        compiler_params=pltpu.CompilerParams(vmem_limit_bytes=VMEM_LIMIT),
-        cost_estimate=pl.CostEstimate(flops=FLOPS, bytes_accessed=BYTES, transcendentals=0),
-        interpret=INTERPRET,
-    )(scalar, *args)
+def sum_kernel(place, parts, fgain, fqkv, fproj, mgain, merge, cgain, cqkv, cproj):
+    _, parity, _, device = decode(place)
+    groups = parts.shape[0]
+    block = groups // 4
+    rows, share = (merge.shape[0], cqkv.shape[0])
+    half = share // 2
+    top = 4 * rows
+    factor = (ROWS * COLS * 2 * groups // 4) ** (-0.5)
+    sums = []
+    for first in range(2):
+        total = None
+        for k in range(2):
+            for i in range(block):
+                term = parts[block * (2 * k + first) + i].astype(F32)
+                total = term if total is None else total + term
+        sums.append(total * factor)
+    same = (jnp.full((top, 128), parity, jnp.int32) == 0)
+    first, second = (sums[0][:top], sums[1][:top])
+    merged = jnp.where(same, first, second)
+    coarse = jnp.where(same, second, first)
+    total = sums[0][top:] + sums[1][top:]
+    for h in range(4):
+        lanes = pl.ds(128 * h, 128)
+        merge[:, lanes] = merged[rows * h : rows * (h + 1)]
+        for j in range(3):
+            cqkv[:, pl.ds(D * j + 128 * h, 128)] = coarse[rows * h + share * j : rows * h + share * (j + 1)]
+        cproj[:, lanes] = coarse[rows * h + 3 * share : rows * (h + 1)]
+        line = total[8 * h : 8 * h + 8]
+        fqkv[:, lanes] = line[:share]
+        fqkv[pl.ds(half * (h // 2), half), pl.ds(D + 128 * (h % 2), 128)] = line[share : share + half]
+        fproj[:, lanes] = line[share + half : 2 * share]
+    for r, (ref, size) in enumerate(((cgain, share), (mgain, rows), (fgain, share))):
+        first = lax.rem(device * size, 128)
+        turned = pltpu.roll(total[32:40], lax.rem(128 - first, 128), 1)
+        ref[...] = turned[r : r + 1, :size]
 
 
 def exchange(pieces, step):
@@ -529,6 +573,15 @@
     return lax.ppermute(value, "core", [(0, 1), (1, 0)])
 
 
+def fold(value, second):
+    ring = lax.axis_size("lat") // 2
+    pairs = []
+    for z in range(ring):
+        step = 1 if z % 2 == (1 if second else 0) else -1
+        pairs += [(2 * z + y, 2 * ((z + step) % ring) + y) for y in range(2)]
+    return lax.ppermute(value, "lat", pairs)
+
+
 def deal(value):
     return lax.all_to_all(value, ("lat", "pair"), 0, 0)
 
@@ -540,8 +593,11 @@
     groups = lat_count * lax.axis_size("pair")
     share = D // (2 * groups)
     rows = 4 * share
-    seam = (lax.axis_index("lat") == lat_count - 1).astype(jnp.int32).reshape(1)
-    core = lax.axis_index("core").astype(jnp.int32).reshape(1)
+    lat, core = (lax.axis_index("lat"), lax.axis_index("core"))
+    device = (lat * lax.axis_size("pair") + lax.axis_index("pair")) * 2 + core
+    parity = lax.bitwise_and(lax.shift_right_logical(lat, 1), 1)
+    seam = (lat == lat_count - 1).astype(jnp.int32)
+    place = (device * 8 + seam * 4 + parity * 2 + core).astype(jnp.int32).reshape(1)
     fgain, mgain, cgain = (v.reshape(1, -1) for v in (fine_gain, merge_gain, coarse_gain))
     cells = WINDOWS * CELLS
 
@@ -550,7 +606,15 @@
     tok, *sent, cot = call(
         first_kernel,
         [((cells, D), BF16)] + pieces + [((CELLS, D), F32)],
-        tokens, cotangent, table("tok_send"), table("cot_send"),
+        *(
+            pltpu.with_memory_space_constraint(v, pltpu.HBM)
+            for v in (tokens, cotangent, table("tok_send"), table("cot_send"))
+        ),
+        specs=[pl.BlockSpec(memory_space=pltpu.HBM)] * 4,
+        scratch=[
+            pltpu.VMEM((ROWS, COLS, D), BF16), pltpu.VMEM((6, 12, D), BF16), pltpu.VMEM((sum(SLOTS), cells), BF16),
+            pltpu.VMEM((sum(SLOTS), CELLS), BF16), pltpu.SemaphoreType.DMA((4,)),
+        ],
     )
     ahead = exchange(sent, -1)
     x, n, p, w, m, y, *sent = scalar_call(
@@ -560,7 +624,7 @@
             ((cells, 256), BF16), ((cells, D), BF16),
         ]
         + narrow,
-        seam, tok, *ahead, fgain, fine_qkv, fine_proj, table("tok_main"), table("tok_halo"), table("y_send"),
+        place, tok, *ahead, fgain, fine_qkv, fine_proj, table("tok_main"), table("tok_halo"), table("y_send"),
         scratch=[pltpu.VMEM((cells, 256), F32)],
     )
     merged = exchange(sent, -1)
@@ -568,7 +632,7 @@
     y2, df, *sent, fac, gains = scalar_call(
         coarse_kernel,
         [((CELLS, D), BF16), ((cells, D), BF16)] + pieces + [((TALL, 5632), BF16), ((8, D), F32)],
-        seam, y, *merged, cot, *ahead, mgain, merge_weight, cgain, coarse_qkv, coarse_proj,
+        place, y, *merged, cot, *ahead, mgain, merge_weight, cgain, coarse_qkv, coarse_proj,
         table("y_main"), table("y_halo"), table("cot_main"), table("cot_halo"), table("df_send"), table("out_send"),
         scratch=[
             pltpu.VMEM((CELLS, 1536), F32), pltpu.VMEM((CELLS, D), F32), pltpu.VMEM((CELLS, 1536), F32),
@@ -576,38 +640,43 @@
         ],
     )
     back = exchange(sent, 1)
-    merge_part, coarse_part = scalar_call(
+    chunk = ((groups // 2, 4 * rows, 128), BF16)
+    merge_keep, merge_send, coarse_keep, coarse_send = scalar_call(
         coarse_weights_kernel,
-        [((groups, rows, D), BF16)] * 2,
-        core, fac, partner(fac),
+        [chunk] * 4,
+        place, fac, partner(fac),
         scratch=[pltpu.VMEM((4 * groups * rows, 128), F32)],
     )
-    merge_sum = deal(merge_part)
+    merge_came = fold(merge_send, False)
+    coarse_came = fold(coarse_send, True)
     dx, *sent, fac, gains = scalar_call(
         fine_backward_kernel,
         [((cells, D), BF16)] + narrow + [((cells, 1280), BF16), ((8, D), F32)],
-        seam, df, *back, x, p, w, fgain, fine_qkv, fine_proj, table("df_main"), table("df_halo"), table("dx_send"),
+        place, df, *back, x, p, w, fgain, fine_qkv, fine_proj, table("df_main"), table("df_halo"), table("dx_send"),
         gains,
         scratch=[pltpu.VMEM((cells, 256), F32), pltpu.VMEM((cells, 768), F32)],
     )
     ended = exchange(sent, 1)
     (rest,) = scalar_call(
         fine_weights_kernel,
-        [((groups, rows + 8, 640), BF16)],
-        core, coarse_part, n, n_other, m, m_other, fac, partner(fac), gains, partner(gains),
+        [((groups, 4 * rows + 40, 128), BF16)],
+        place, merge_keep, merge_came, coarse_keep, coarse_came, n, n_other, m, m_other,
+        fac, partner(fac), gains, partner(gains),
         scratch=[pltpu.VMEM((32, 128), F32), pltpu.VMEM((4 * groups * 8, 128), F32)],
     )
-    rest_sum = deal(rest)
-    device = (lax.axis_index("lat") * lax.axis_size("pair") + lax.axis_index("pair")) * 2 + lax.axis_index("core")
-    output, grad, fg, fqkv, fproj, mg, merge, cg, cqkv, cproj = scalar_call(
-        last_kernel,
+    parts = deal(rest)
+    output, grad = call(
+        assemble_kernel,
+        [((6, 12, D), BF16), ((ROWS, COLS, D), BF16)],
+        y2, *back, dx, *ended, table("out_main"), table("out_halo"), table("dx_main"), table("dx_halo"),
+    )
+    fg, fqkv, fproj, mg, merge, cg, cqkv, cproj = scalar_call(
+        sum_kernel,
         [
-            ((6, 12, D), BF16), ((ROWS, COLS, D), BF16), ((1, share), F32), ((share, 768), F32),
-            ((share // 2, D), F32), ((1, rows), F32), ((rows, D), F32), ((1, share), F32), ((share, 1536), F32),
-            ((share, D), F32),
+            ((1, share), F32), ((share, 768), F32), ((share // 2, D), F32), ((1, rows), F32), ((rows, D), F32),
+            ((1, share), F32), ((share, 1536), F32), ((share, D), F32),
         ],
-        device.astype(jnp.int32).reshape(1), merge_sum, rest_sum, y2, *back, dx, *ended,
-        table("out_main"), table("out_halo"), table("dx_main"), table("dx_halo"),
+        place, parts,
     )
     fg, mg, cg = (v.reshape(-1) for v in (fg, mg, cg))
     return (output, grad, fg, fqkv, fproj, mg, merge, cg, cqkv, cproj)

time: 140 us -> 109 us (0.78)
  local copies, waits for them, and re-layouts: 23.7 us -> 0.14 us
  waiting for transfers between devices: 57.2 us -> 52.7 us
  starting transfers between devices: 33.3 us -> 30 us
    pallas_call x1 -> x8, Pallas kernels: 0.34 us -> 24.1 us  [call(): pl.pallas_call(kernel, out_shape=[jax.ShapeDtypeStruct(s, d) for s, d in...]
    unnamed x114 -> x48, local copies, waits for them, and re-layouts: 23.7 us -> 0.14 us
    pallas_call x6 -> x0, Pallas kernels: 22.7 us -> none  [scalar_call(): pl.pallas_call(kernel, out_shape=[jax.ShapeDtypeStruct(s, d) for s, d in...]
    all_to_all x2 -> x1, waiting for transfers between devices: 13.8 us -> 0.01 us  [deal(): return lax.all_to_all(value, ('lat', 'pair'), 0, 0)]
    ppermute x0 -> x2, waiting for transfers between devices: none -> 10.9 us  [fold(): return lax.ppermute(value, 'lat', pairs)]
    all_to_all x2 -> x1, starting transfers between devices: 10.8 us -> 5.58 us  [deal(): return lax.all_to_all(value, ('lat', 'pair'), 0, 0)]
    ppermute x12, waiting for transfers between devices: 42.2 us -> 39.5 us  [exchange(): arrived.append(lax.ppermute(piece, ('lat', 'pair', 'core'), pairs))]
    ppermute x0 -> x2, starting transfers between devices: none -> 1.76 us  [fold(): return lax.ppermute(value, 'lat', pairs)]
  transfers between devices with their start and end apart: 19 -> 20, of which waited for: 8 -> 9; matrix products, arithmetic and copies ran while one was open for 0% -> 0% of each run, Pallas kernels for 6% -> 8%
where the time goes in v4:
time: 109 us; the launch traced here: 108 us
  waiting for transfers between devices  52.7 us (48%)
  starting transfers between devices  30 us (28%)
  Pallas kernels  24.1 us (22%)
    ppermute x12, waiting for transfers between devices, exchange(): arrived.append(lax.ppermute(piece, ('lat', 'pair', 'core'), pairs))  39.5 us
    pallas_call x8, Pallas kernels, call(): pl.pallas_call(kernel, out_shape=[jax.ShapeDtypeStruct(s, d) for s, d in...  24.1 us
    ppermute x12, starting transfers between devices, exchange(): arrived.append(lax.ppermute(piece, ('lat', 'pair', 'core'), pairs))  21.6 us
    ppermute x2, waiting for transfers between devices, fold(): return lax.ppermute(value, 'lat', pairs)  10.9 us
    all_to_all x1, starting transfers between devices, deal(): return lax.all_to_all(value, ('lat', 'pair'), 0, 0)  5.58 us
    ppermute x5, waiting for transfers between devices, partner(): return lax.ppermute(value, 'core', [(0, 1), (1, 0)])  2.27 us
  transfers between devices with their start and end apart: 20, of which 9 were waited for; matrix products, arithmetic and copies ran while one was open for 0% of the time, Pallas kernels for 8%

profile of v4, /device:TPU:0, one launch (start us, length us, event | category | flops | bytes accessed | tf_op | source)
XLA Modules:
  0.0 108.0 jit_solution(6375873191374924271)
XLA Ops:
  0.6 0.0 copy-start.11
  0.7 0.0 copy-start.16
  0.7 0.0 copy-start.18
  0.7 1.5 %shard_map.339 = (bf16[288,512]{1,0:T(8,128)(2,1)S(1)}, bf16[80,512]{1,0:T(8,128)(2,1)S(1)}, bf16[80,512]{1,0:T(8,128)(2,1)S(1)}, bf16[48,512]{1,0:T(8,128)(2,1)S(1)}, f32[72,512]{1,0:T(8,128)S(1)}) custom-call(bf16[12,24,512]{2,1,0:T(8,128)(2,1)} %tok_in.1, bf16[6,12,512]{2,1,0:T(8,128)(2,1)} %cot_in.1, bf16[208,288]{1,0:T(8,128)(2,1)} %constant.60.clone.tok_send_in, ...), custom_call_target="tpu_custom_call" | custom-call | flops 5000000000 | bytes 4000000 | tf_op jit(solution)/shard_map/pallas_call | solution.py:162
  2.3 3.4 %collective-permute-start = (bf16[80,512]{1,0:T(8,128)(2,1)S(1)}, bf16[80,512]{1,0:T(8,128)(2,1)S(1)}, u32[]{:S(2)}, u32[]{:S(2)}) collective-permute-start(bf16[80,512]{1,0:T(8,128)(2,1)S(1)} %get-tuple-element.52), channel_id=1, source_target_pairs={{0,15},{1,0},{2,1},{3,2},{4,3},{5,4},{6,5},{7,6},{8,7},{9,8},{10,9... | collective-permute-start | bytes 245768 | tf_op jit(solution)/shard_map/ppermute | solution.py:568
  5.6 6.4 %collective-permute-start.1 = (bf16[80,512]{1,0:T(8,128)(2,1)S(1)}, bf16[80,512]{1,0:T(8,128)(2,1)S(1)}, u32[]{:S(2)}, u32[]{:S(2)}) collective-permute-start(bf16[80,512]{1,0:T(8,128)(2,1)S(1)} %get-tuple-element.53), channel_id=1, source_target_pairs={{0,112},{1,113},{2,114},{3,115},{4,116},{5,117},{6,118},{7,119},{8... | collective-permute-start | bytes 245768 | tf_op jit(solution)/shard_map/ppermute | solution.py:568
  12.0 0.2 collective-permute-start.2
  12.2 4.8 %collective-permute-done.2.corner.ccorner = bf16[48,512]{1,0:T(8,128)(2,1)S(1)} collective-permute-done((bf16[48,512]{1,0:T(8,128)(2,1)S(1)}, bf16[48,512]{1,0:T(8,128)(2,1)S(1)}, u32[]{:S(2)}, u32[]{:S(2)}) %collective-permute-start.2) | collective-permute-done | bytes 49184 | tf_op jit(solution)/shard_map/ppermute | solution.py:568
  17.1 0.0 copy-start
  17.1 0.0 copy-start.5
  17.2 0.0 copy-start.10
  17.2 0.0 copy-start.12
  17.2 0.0 copy-start.15
  17.2 0.0 copy-start.19
  17.2 0.0 copy-start.21
  17.2 0.0 copy-start.23
  17.2 3.9 %shard_map.340 = (bf16[288,512]{1,0:T(8,128)(2,1)S(1)}, bf16[288,512]{1,0:T(8,128)(2,1)S(1)}, f32[288,768]{1,0:T(8,128)S(1)}, f32[8,72,256]{2,1,0:T(8,128)S(1)},...) custom-call(s32[1]{0:T(128)} %bitcast.place, ...), custom_call_target="tpu_custom_call" | custom-call | flops 5000000000 | bytes 4000000 | tf_op jit(solution)/shard_map/pallas_call | solution.py:162
  21.2 0.5 collective-permute-start.3
  21.6 5.2 %collective-permute-start.4 = (bf16[64,512]{1,0:T(8,128)(2,1)S(1)}, bf16[64,512]{1,0:T(8,128)(2,1)S(1)}, u32[]{:S(2)}, u32[]{:S(2)}) collective-permute-start(bf16[64,512]{1,0:T(8,128)(2,1)S(1)} %get-tuple-element.57), channel_id=1, source_target_pairs={{0,112},{1,113},{2,114},{3,115},{4,116},{5,117},{6,118},{7,119},{8... | collective-permute-start | bytes 196616 | tf_op jit(solution)/shard_map/ppermute | solution.py:568
  26.8 4.8 %collective-permute-done.5.corner = bf16[32,512]{1,0:T(8,128)(2,1)S(1)} collective-permute-done((bf16[32,512]{1,0:T(8,128)(2,1)S(1)}, bf16[32,512]{1,0:T(8,128)(2,1)S(1)}, u32[]{:S(2)}, u32[]{:S(2)}) %collective-permute-start.5) | collective-permute-done | bytes 32800 | tf_op jit(solution)/shard_map/ppermute | solution.py:568
  31.8 0.0 copy-start.9
  31.8 0.0 copy-start.14
  31.8 0.0 copy-start.17
  31.8 6.5 %shard_map.341 = (bf16[72,512]{1,0:T(8,128)(2,1)S(1)}, bf16[288,512]{1,0:T(8,128)(2,1)S(1)}, bf16[80,512]{1,0:T(8,128)(2,1)S(1)}, bf16[80,512]{1,0:T(8,128)(2,1)...) custom-call(s32[1]{0:T(128)} %bitcast.place, ...), custom_call_target="tpu_custom_call" | custom-call | flops 5000000000 | bytes 4000000 | tf_op jit(solution)/shard_map/pallas_call | solution.py:162
  38.3 0.1 collective-permute-start.12
  38.4 0.5 collective-permute-start.6
  38.9 9.7 %collective-permute-done.8.corner = bf16[48,512]{1,0:T(8,128)(2,1)S(1)} collective-permute-done((bf16[48,512]{1,0:T(8,128)(2,1)S(1)}, bf16[48,512]{1,0:T(8,128)(2,1)S(1)}, u32[]{:S(2)}, u32[]{:S(2)}) %collective-permute-start.8) | collective-permute-done | bytes 49184 | tf_op jit(solution)/shard_map/ppermute | solution.py:568
  48.6 3.6 %shard_map.342 = (bf16[288,512]{1,0:T(8,128)(2,1)S(1)}, bf16[64,512]{1,0:T(8,128)(2,1)S(1)}, bf16[64,512]{1,0:T(8,128)(2,1)S(1)}, bf16[32,512]{1,0:T(8,128)(2,1)...) custom-call(s32[1]{0:T(128)} %bitcast.place, bf16[288,512]{1,0:T(8,128)(2,1)S(1)} %get-tuple-element.64.df_in, ...), custom_call_target="tpu_custom_call" | custom-call | flops 5000000000 | bytes 4000000 | tf_op jit(solution)/shard_map/pallas_call | solution.py:162
  52.1 0.3 collective-permute-start.17
  52.4 3.7 %shard_map.344 = (bf16[32,64,128]{2,1,0:T(8,128)(2,1)S(1)}, bf16[32,64,128]{2,1,0:T(8,128)(2,1)S(1)}, bf16[32,64,128]{2,1,0:T(8,128)(2,1)S(1)}, bf16[32,64,128]{2,1,0:T(8,128)(2,1)S(1)}) custom-call(s32[1]{0:T(128)} %bitcast.place, bf16[80,5632]{1,0:T(8,128)(2,1)S(1)} %get-tuple-element.75.own, bf16[80,5632]{1,0:T(8,128)(2,1)S(1)} %collective-permute-done.12.other), custom_call_target="tpu_custom_call" | custom-call | flops 5000000000 | bytes 4000000 | tf_op jit(solution)/shard_map/pallas_call | solution.py:162
  56.1 0.1 collective-permute-start.13
  56.2 1.7 %collective-permute-start.14 = (bf16[32,64,128]{2,1,0:T(8,128)(2,1)S(1)}, bf16[32,64,128]{2,1,0:T(8,128)(2,1)S(1)}, u32[]{:S(2)}, u32[]{:S(2)}) collective-permute-start(bf16[32,64,128]{2,1,0:T(8,128)(2,1)S(1)} %get-tuple-element.79), channel_id=1, source_target_pairs={{0,96},{16,112},{32,64},{48,80},{64,32},{80,48},{96,0},{112,16},{1... | collective-permute-start | bytes 1572872 | tf_op jit(solution)/shard_map/ppermute | solution.py:582
  57.9 0.2 collective-permute-start.15
  58.1 0.3 collective-permute-start.16
  58.4 1.3 %collective-permute-done.16.m_other = bf16[288,256]{1,0:T(8,128)(2,1)S(1)} collective-permute-done((bf16[288,256]{1,0:T(8,128)(2,1)S(1)}, bf16[288,256]{1,0:T(8,128)(2,1)S(1)}, u32[]{:S(2)}, u32[]{:S(2)}) %collective-permute-start.16) | collective-permute-done | bytes 147488 | tf_op jit(solution)/shard_map/ppermute | solution.py:573
  59.7 0.2 collective-permute-start.18
  59.9 1.0 collective-permute-done.18.gains_other
  60.9 9.6 %collective-permute-done.13.merge_came = bf16[32,64,128]{2,1,0:T(8,128)(2,1)S(1)} collective-permute-done((bf16[32,64,128]{2,1,0:T(8,128)(2,1)S(1)}, bf16[32,64,128]{2,1,0:T(8,128)(2,1)S(1)}, u32[]{:S(2)}, u32[]{:S(2)}) %collective-permute-start.13) | collective-permute-done | bytes 524320 | tf_op jit(solution)/shard_map/ppermute | solution.py:582
  70.5 1.3 %collective-permute-done.14.coarse_came = bf16[32,64,128]{2,1,0:T(8,128)(2,1)S(1)} collective-permute-done((bf16[32,64,128]{2,1,0:T(8,128)(2,1)S(1)}, bf16[32,64,128]{2,1,0:T(8,128)(2,1)S(1)}, u32[]{:S(2)}, u32[]{:S(2)}) %collective-permute-start.14) | collective-permute-done | bytes 524320 | tf_op jit(solution)/shard_map/ppermute | solution.py:582
  71.8 2.9 %shard_map.345 = bf16[64,104,128]{2,1,0:T(8,128)(2,1)} custom-call(s32[1]{0:T(128)} %bitcast.place, bf16[32,64,128]{2,1,0:T(8,128)(2,1)S(1)} %get-tuple-element.76.merge_keep, bf16[32,64,128]{2,1,0:T(8,128)(2,1)S(1)} %collective-permute-done.13.merge_came, bf16[32,64,128]{2,1,0:T(8,128)(2,1)S(1)} %get-tuple-element.78.coarse_keep, ...), custom_call_target="tpu_custom_call" | custom-call | flops 5000000000 | bytes 4000000 | tf_op jit(solution)/shard_map/pallas_call | solution.py:162
  74.7 5.6 %all-to-all-start = ((bf16[64,104,128]{2,1,0:T(8,128)(2,1)}), bf16[64,104,128]{2,1,0:T(8,128)(2,1)S(1)}, u32[]{:S(2)}, u32[]{:S(2)}) async-start(bf16[64,104,128]{2,1,0:T(8,128)(2,1)} %shard_map.345), calls=%async_computation | async-start | bytes 3407872 | tf_op jit(solution)/shard_map/all_to_all | solution.py:586
  80.3 0.1 collective-permute-start.9
  80.4 3.1 %collective-permute-start.10 = (bf16[64,512]{1,0:T(8,128)(2,1)S(1)}, bf16[64,512]{1,0:T(8,128)(2,1)S(1)}, u32[]{:S(2)}, u32[]{:S(2)}) collective-permute-start(bf16[64,512]{1,0:T(8,128)(2,1)S(1)} %get-tuple-element.71), channel_id=1, source_target_pairs={{0,16},{1,17},{2,18},{3,19},{4,20},{5,21},{6,22},{7,23},{8,24},{9,... | collective-permute-start | bytes 196616 | tf_op jit(solution)/shard_map/ppermute | solution.py:568
  83.5 2.3 %collective-permute-start.11 = (bf16[32,512]{1,0:T(8,128)(2,1)S(1)}, bf16[32,512]{1,0:T(8,128)(2,1)S(1)}, u32[]{:S(2)}, u32[]{:S(2)}) collective-permute-start(bf16[32,512]{1,0:T(8,128)(2,1)S(1)} %get-tuple-element.72), channel_id=1, source_target_pairs={{0,17},{1,18},{2,19},{3,20},{4,21},{5,22},{6,23},{7,24},{8,25},{9,... | collective-permute-start | bytes 98312 | tf_op jit(solution)/shard_map/ppermute | solution.py:568
  85.8 19.8 %collective-permute-done.11.dcorner = bf16[32,512]{1,0:T(8,128)(2,1)S(1)} collective-permute-done((bf16[32,512]{1,0:T(8,128)(2,1)S(1)}, bf16[32,512]{1,0:T(8,128)(2,1)S(1)}, u32[]{:S(2)}, u32[]{:S(2)}) %collective-permute-start.11) | collective-permute-done | bytes 32800 | tf_op jit(solution)/shard_map/ppermute | solution.py:568
  105.6 0.3 collective-permute-done.10.dedge
  105.9 1.2 %shard_map.343 = (bf16[6,12,512]{2,1,0:T(8,128)(2,1)}, bf16[12,24,512]{2,1,0:T(8,128)(2,1)}) custom-call(bf16[72,512]{1,0:T(8,128)(2,1)S(1)} %get-tuple-element.60.y2, bf16[80,512]{1,0:T(8,128)(2,1)S(1)} %collective-permute-done.6.side, bf16[80,512]{1,0:T(8,128)(2,1)S(1)} %collective-permute-done.7.edge, bf16[48,512]{1,0:T(8,128)(2,1)S(1)} %collective-permute-done.8.corner, ...), custom_call_target="tpu_custom_call" | custom-call | flops 5000000000 | bytes 4000000 | tf_op jit(solution)/shard_map/pallas_call | solution.py:162
  107.1 0.9 shard_map.346
  (48 shorter events, 0.1 us)
Async XLA Ops:
  0.6 16.4 %copy-start.11 = (bf16[288,288]{1,0:T(8,128)(2,1)S(1)}, bf16[288,288]{1,0:T(8,128)(2,1)}, u32[]{:S(2)}) copy-start(bf16[288,288]{1,0:T(8,128)(2,1)} %constant.62.clone.t_main) | copy-start | bytes 497668
  0.7 16.4 %copy-start.16 = (bf16[288,208]{1,0:T(8,128)(2,1)S(1)}, bf16[288,208]{1,0:T(8,128)(2,1)}, u32[]{:S(2)}) copy-start(bf16[288,208]{1,0:T(8,128)(2,1)} %constant.63.clone.t_halo) | copy-start | bytes 359428
  0.7 16.4 %copy-start.18 = (bf16[160,288]{1,0:T(8,128)(2,1)S(1)}, bf16[160,288]{1,0:T(8,128)(2,1)}, u32[]{:S(2)}) copy-start(bf16[160,288]{1,0:T(8,128)(2,1)} %constant.64.clone.y_send) | copy-start | bytes 276484
  0.7 16.4 %copy-start.7 = (f32[512]{0:T(512)S(1)}, f32[512]{0:T(512)}, u32[]{:S(2)}) copy-start(f32[512]{0:T(512)} %param.29) | copy-start | bytes 6148
  0.7 16.4 %copy-start.2 = (bf16[512,768]{1,0:T(8,128)(2,1)S(1)}, bf16[512,768]{1,0:T(8,128)(2,1)}, u32[]{:S(2)}) copy-start(bf16[512,768]{1,0:T(8,128)(2,1)} %wqkv.5) | copy-start | bytes 2359300
  0.7 16.4 %copy-start.4 = (bf16[256,512]{1,0:T(8,128)(2,1)S(1)}, bf16[256,512]{1,0:T(8,128)(2,1)}, u32[]{:S(2)}) copy-start(bf16[256,512]{1,0:T(8,128)(2,1)} %wproj.5) | copy-start | bytes 786436
  2.3 14.8 %collective-permute-start = (bf16[80,512]{1,0:T(8,128)(2,1)S(1)}, bf16[80,512]{1,0:T(8,128)(2,1)S(1)}, u32[]{:S(2)}, u32[]{:S(2)}) collective-permute-start(bf16[80,512]{1,0:T(8,128)(2,1)S(1)} %get-tuple-element.52), channel_id=1, source_target_pairs={{0,15},{1,0},{2,1},{3,2},{4,3},{5,4},{6,5},{7,6},{8,7},{9,8},{10,9... | collective-permute-start | bytes 245768 | tf_op jit(solution)/shard_map/ppermute | solution.py:568
  5.6 11.4 %collective-permute-start.1 = (bf16[80,512]{1,0:T(8,128)(2,1)S(1)}, bf16[80,512]{1,0:T(8,128)(2,1)S(1)}, u32[]{:S(2)}, u32[]{:S(2)}) collective-permute-start(bf16[80,512]{1,0:T(8,128)(2,1)S(1)} %get-tuple-element.53), channel_id=1, source_target_pairs={{0,112},{1,113},{2,114},{3,115},{4,116},{5,117},{6,118},{7,119},{8... | collective-permute-start | bytes 245768 | tf_op jit(solution)/shard_map/ppermute | solution.py:568
  12.0 5.0 %collective-permute-start.2 = (bf16[48,512]{1,0:T(8,128)(2,1)S(1)}, bf16[48,512]{1,0:T(8,128)(2,1)S(1)}, u32[]{:S(2)}, u32[]{:S(2)}) collective-permute-start(bf16[48,512]{1,0:T(8,128)(2,1)S(1)} %get-tuple-element.54), channel_id=1, source_target_pairs={{0,127},{1,112},{2,113},{3,114},{4,115},{5,116},{6,117},{7,118},{8... | collective-permute-start | bytes 147464 | tf_op jit(solution)/shard_map/ppermute | solution.py:568
  17.1 14.5 %copy-start = (bf16[2048,512]{1,0:T(8,128)(2,1)S(1)}, bf16[2048,512]{1,0:T(8,128)(2,1)}, u32[]{:S(2)}) copy-start(bf16[2048,512]{1,0:T(8,128)(2,1)} %mweight.1) | copy-start | bytes 6291460
  17.1 14.5 %copy-start.1 = (bf16[512,1536]{1,0:T(8,128)(2,1)S(1)}, bf16[512,1536]{1,0:T(8,128)(2,1)}, u32[]{:S(2)}) copy-start(bf16[512,1536]{1,0:T(8,128)(2,1)} %wqkv.4) | copy-start | bytes 4718596
  17.1 14.5 %copy-start.3 = (bf16[512,512]{1,0:T(8,128)(2,1)S(1)}, bf16[512,512]{1,0:T(8,128)(2,1)}, u32[]{:S(2)}) copy-start(bf16[512,512]{1,0:T(8,128)(2,1)} %wproj.4) | copy-start | bytes 1572868
  17.1 14.5 %copy-start.5 = (f32[2048]{0:T(1024)S(1)}, f32[2048]{0:T(1024)}, u32[]{:S(2)}) copy-start(f32[2048]{0:T(1024)} %param.32) | copy-start | bytes 24580
  17.2 14.5 %copy-start.6 = (f32[512]{0:T(512)S(1)}, f32[512]{0:T(512)}, u32[]{:S(2)}) copy-start(f32[512]{0:T(512)} %param.34) | copy-start | bytes 6148
  17.2 14.5 %copy-start.10 = (bf16[288,288]{1,0:T(8,128)(2,1)S(1)}, bf16[288,288]{1,0:T(8,128)(2,1)}, u32[]{:S(2)}) copy-start(bf16[288,288]{1,0:T(8,128)(2,1)} %constant.65.clone.y_main) | copy-start | bytes 497668
  17.2 14.5 %copy-start.12 = (bf16[208,288]{1,0:T(8,128)(2,1)S(1)}, bf16[208,288]{1,0:T(8,128)(2,1)}, u32[]{:S(2)}) copy-start(bf16[208,288]{1,0:T(8,128)(2,1)} %constant.69.clone.df_send) | copy-start | bytes 359428
  17.2 14.5 %copy-start.15 = (bf16[288,160]{1,0:T(8,128)(2,1)S(1)}, bf16[288,160]{1,0:T(8,128)(2,1)}, u32[]{:S(2)}) copy-start(bf16[288,160]{1,0:T(8,128)(2,1)} %constant.66.clone.y_halo) | copy-start | bytes 276484
  17.2 14.5 %copy-start.19 = (bf16[208,72]{1,0:T(8,128)(2,1)S(1)}, bf16[208,72]{1,0:T(8,128)(2,1)}, u32[]{:S(2)}) copy-start(bf16[208,72]{1,0:T(8,128)(2,1)} %constant.70.clone.out_send) | copy-start | bytes 89860
  17.2 14.5 %copy-start.21 = (bf16[72,208]{1,0:T(8,128)(2,1)S(1)}, bf16[72,208]{1,0:T(8,128)(2,1)}, u32[]{:S(2)}) copy-start(bf16[72,208]{1,0:T(8,128)(2,1)} %constant.68.clone.c_halo) | copy-start | bytes 89860
  17.2 14.5 %copy-start.23 = (bf16[72,72]{1,0:T(8,128)(2,1)S(1)}, bf16[72,72]{1,0:T(8,128)(2,1)}, u32[]{:S(2)}) copy-start(bf16[72,72]{1,0:T(8,128)(2,1)} %constant.67.clone.c_main) | copy-start | bytes 31108
  21.2 10.5 %collective-permute-start.3 = (bf16[64,512]{1,0:T(8,128)(2,1)S(1)}, bf16[64,512]{1,0:T(8,128)(2,1)S(1)}, u32[]{:S(2)}, u32[]{:S(2)}) collective-permute-start(bf16[64,512]{1,0:T(8,128)(2,1)S(1)} %get-tuple-element.56), channel_id=1, source_target_pairs={{0,15},{1,0},{2,1},{3,2},{4,3},{5,4},{6,5},{7,6},{8,7},{9,8},{10,9... | collective-permute-start | bytes 196616 | tf_op jit(solution)/shard_map/ppermute | solution.py:568
  21.6 10.0 %collective-permute-start.4 = (bf16[64,512]{1,0:T(8,128)(2,1)S(1)}, bf16[64,512]{1,0:T(8,128)(2,1)S(1)}, u32[]{:S(2)}, u32[]{:S(2)}) collective-permute-start(bf16[64,512]{1,0:T(8,128)(2,1)S(1)} %get-tuple-element.57), channel_id=1, source_target_pairs={{0,112},{1,113},{2,114},{3,115},{4,116},{5,117},{6,118},{7,119},{8... | collective-permute-start | bytes 196616 | tf_op jit(solution)/shard_map/ppermute | solution.py:568
  26.8 4.8 %collective-permute-start.5 = (bf16[32,512]{1,0:T(8,128)(2,1)S(1)}, bf16[32,512]{1,0:T(8,128)(2,1)S(1)}, u32[]{:S(2)}, u32[]{:S(2)}) collective-permute-start(bf16[32,512]{1,0:T(8,128)(2,1)S(1)} %get-tuple-element.58), channel_id=1, source_target_pairs={{0,127},{1,112},{2,113},{3,114},{4,115},{5,116},{6,117},{7,118},{8... | collective-permute-start | bytes 98312 | tf_op jit(solution)/shard_map/ppermute | solution.py:568
  31.8 16.8 %copy-start.9 = (bf16[288,288]{1,0:T(8,128)(2,1)S(1)}, bf16[288,288]{1,0:T(8,128)(2,1)}, u32[]{:S(2)}) copy-start(bf16[288,288]{1,0:T(8,128)(2,1)} %constant.71.clone.d_main) | copy-start | bytes 497668
  31.8 16.8 %copy-start.14 = (bf16[288,208]{1,0:T(8,128)(2,1)S(1)}, bf16[288,208]{1,0:T(8,128)(2,1)}, u32[]{:S(2)}) copy-start(bf16[288,208]{1,0:T(8,128)(2,1)} %constant.72.clone.d_halo) | copy-start | bytes 359428
  31.8 16.8 %copy-start.17 = (bf16[160,288]{1,0:T(8,128)(2,1)S(1)}, bf16[160,288]{1,0:T(8,128)(2,1)}, u32[]{:S(2)}) copy-start(bf16[160,288]{1,0:T(8,128)(2,1)} %constant.73.clone.dx_send) | copy-start | bytes 276484
  38.3 14.2 %collective-permute-start.12 = (bf16[80,5632]{1,0:T(8,128)(2,1)S(1)}, bf16[80,5632]{1,0:T(8,128)(2,1)S(1)}, u32[]{:S(2)}, u32[]{:S(2)}) collective-permute-start(bf16[80,5632]{1,0:T(8,128)(2,1)S(1)} %get-tuple-element.75.own), channel_id=1, source_target_pairs={{0,1},{1,0},{2,3},{3,2},{4,5},{5,4},{6,7},{7,6},{8,9},{9,8},{10,11... | collective-permute-start | bytes 2703368 | tf_op jit(solution)/shard_map/ppermute | solution.py:573
  38.4 10.2 %collective-permute-start.6 = (bf16[80,512]{1,0:T(8,128)(2,1)S(1)}, bf16[80,512]{1,0:T(8,128)(2,1)S(1)}, u32[]{:S(2)}, u32[]{:S(2)}) collective-permute-start(bf16[80,512]{1,0:T(8,128)(2,1)S(1)} %get-tuple-element.61), channel_id=1, source_target_pairs={{0,1},{1,2},{2,3},{3,4},{4,5},{5,6},{6,7},{7,8},{8,9},{9,10},{10,1... | collective-permute-start | bytes 245768 | tf_op jit(solution)/shard_map/ppermute | solution.py:568
  38.9 9.7 %collective-permute-start.7 = (bf16[80,512]{1,0:T(8,128)(2,1)S(1)}, bf16[80,512]{1,0:T(8,128)(2,1)S(1)}, u32[]{:S(2)}, u32[]{:S(2)}) collective-permute-start(bf16[80,512]{1,0:T(8,128)(2,1)S(1)} %get-tuple-element.62), channel_id=1, source_target_pairs={{0,16},{1,17},{2,18},{3,19},{4,20},{5,21},{6,22},{7,23},{8,24},{9,... | collective-permute-start | bytes 245768 | tf_op jit(solution)/shard_map/ppermute | solution.py:568
  38.9 9.7 %collective-permute-start.8 = (bf16[48,512]{1,0:T(8,128)(2,1)S(1)}, bf16[48,512]{1,0:T(8,128)(2,1)S(1)}, u32[]{:S(2)}, u32[]{:S(2)}) collective-permute-start(bf16[48,512]{1,0:T(8,128)(2,1)S(1)} %get-tuple-element.63), channel_id=1, source_target_pairs={{0,17},{1,18},{2,19},{3,20},{4,21},{5,22},{6,23},{7,24},{8,25},{9,... | collective-permute-start | bytes 147464 | tf_op jit(solution)/shard_map/ppermute | solution.py:568
  52.1 8.7 %collective-permute-start.17 = (bf16[288,1280]{1,0:T(8,128)(2,1)S(1)}, bf16[288,1280]{1,0:T(8,128)(2,1)S(1)}, u32[]{:S(2)}, u32[]{:S(2)}) collective-permute-start(bf16[288,1280]{1,0:T(8,128)(2,1)S(1)} %get-tuple-element.82.own), channel_id=1, source_target_pairs={{0,1},{1,0},{2,3},{3,2},{4,5},{5,4},{6,7},{7,6},{8,9},{9,8},{10,11... | collective-permute-start | bytes 2211848 | tf_op jit(solution)/shard_map/ppermute | solution.py:573
  56.1 14.4 %collective-permute-start.13 = (bf16[32,64,128]{2,1,0:T(8,128)(2,1)S(1)}, bf16[32,64,128]{2,1,0:T(8,128)(2,1)S(1)}, u32[]{:S(2)}, u32[]{:S(2)}) collective-permute-start(bf16[32,64,128]{2,1,0:T(8,128)(2,1)S(1)} %get-tuple-element.77), channel_id=1, source_target_pairs={{0,32},{16,48},{32,0},{48,16},{64,96},{80,112},{96,64},{112,80},{1... | collective-permute-start | bytes 1572872 | tf_op jit(solution)/shard_map/ppermute | solution.py:582
  56.2 15.6 %collective-permute-start.14 = (bf16[32,64,128]{2,1,0:T(8,128)(2,1)S(1)}, bf16[32,64,128]{2,1,0:T(8,128)(2,1)S(1)}, u32[]{:S(2)}, u32[]{:S(2)}) collective-permute-start(bf16[32,64,128]{2,1,0:T(8,128)(2,1)S(1)} %get-tuple-element.79), channel_id=1, source_target_pairs={{0,96},{16,112},{32,64},{48,80},{64,32},{80,48},{96,0},{112,16},{1... | collective-permute-start | bytes 1572872 | tf_op jit(solution)/shard_map/ppermute | solution.py:582
  57.9 3.0 %collective-permute-start.15 = (bf16[288,512]{1,0:T(8,128)(2,1)S(1)}, bf16[288,512]{1,0:T(8,128)(2,1)S(1)}, u32[]{:S(2)}, u32[]{:S(2)}) collective-permute-start(bf16[288,512]{1,0:T(8,128)(2,1)S(1)} %get-tuple-element.80.n_own), channel_id=1, source_target_pairs={{0,1},{1,0},{2,3},{3,2},{4,5},{5,4},{6,7},{7,6},{8,9},{9,8},{10,11... | collective-permute-start | bytes 884744 | tf_op jit(solution)/shard_map/ppermute | solution.py:573
  58.1 1.6 %collective-permute-start.16 = (bf16[288,256]{1,0:T(8,128)(2,1)S(1)}, bf16[288,256]{1,0:T(8,128)(2,1)S(1)}, u32[]{:S(2)}, u32[]{:S(2)}) collective-permute-start(bf16[288,256]{1,0:T(8,128)(2,1)S(1)} %get-tuple-element.81.m_own), channel_id=1, source_target_pairs={{0,1},{1,0},{2,3},{3,2},{4,5},{5,4},{6,7},{7,6},{8,9},{9,8},{10,11... | collective-permute-start | bytes 442376 | tf_op jit(solution)/shard_map/ppermute | solution.py:573
  59.7 1.2 %collective-permute-start.18 = (f32[8,512]{1,0:T(8,128)S(1)}, f32[8,512]{1,0:T(8,128)S(1)}, u32[]{:S(2)}, u32[]{:S(2)}) collective-permute-start(f32[8,512]{1,0:T(8,128)S(1)} %get-tuple-element.83.gains), channel_id=1, source_target_pairs={{0,1},{1,0},{2,3},{3,2},{4,5},{5,4},{6,7},{7,6},{8,9},{9,8},{10,11... | collective-permute-start | bytes 49160 | tf_op jit(solution)/shard_map/ppermute | solution.py:573
  74.7 31.2 %copy-start.8 = (bf16[288,288]{1,0:T(8,128)(2,1)S(1)}, bf16[288,288]{1,0:T(8,128)(2,1)}, u32[]{:S(2)}) copy-start(bf16[288,288]{1,0:T(8,128)(2,1)} %constant.76.clone.dx_main) | copy-start | bytes 497668
  74.7 31.2 %copy-start.13 = (bf16[288,160]{1,0:T(8,128)(2,1)S(1)}, bf16[288,160]{1,0:T(8,128)(2,1)}, u32[]{:S(2)}) copy-start(bf16[288,160]{1,0:T(8,128)(2,1)} %constant.77.clone.dx_halo) | copy-start | bytes 276484
  74.7 31.2 %copy-start.20 = (bf16[96,208]{1,0:T(8,128)(2,1)S(1)}, bf16[96,208]{1,0:T(8,128)(2,1)}, u32[]{:S(2)}) copy-start(bf16[96,208]{1,0:T(8,128)(2,1)} %constant.75.clone.out_halo) | copy-start | bytes 119812
  74.7 31.2 %copy-start.22 = (bf16[96,72]{1,0:T(8,128)(2,1)S(1)}, bf16[96,72]{1,0:T(8,128)(2,1)}, u32[]{:S(2)}) copy-start(bf16[96,72]{1,0:T(8,128)(2,1)} %constant.74.clone.out_main) | copy-start | bytes 41476
  74.7 32.4 %all-to-all-start = ((bf16[64,104,128]{2,1,0:T(8,128)(2,1)}), bf16[64,104,128]{2,1,0:T(8,128)(2,1)S(1)}, u32[]{:S(2)}, u32[]{:S(2)}) async-start(bf16[64,104,128]{2,1,0:T(8,128)(2,1)} %shard_map.345), calls=%async_computation | async-start | bytes 3407872 | tf_op jit(solution)/shard_map/all_to_all | solution.py:586
  80.3 25.3 %collective-permute-start.9 = (bf16[64,512]{1,0:T(8,128)(2,1)S(1)}, bf16[64,512]{1,0:T(8,128)(2,1)S(1)}, u32[]{:S(2)}, u32[]{:S(2)}) collective-permute-start(bf16[64,512]{1,0:T(8,128)(2,1)S(1)} %get-tuple-element.70), channel_id=1, source_target_pairs={{0,1},{1,2},{2,3},{3,4},{4,5},{5,6},{6,7},{7,8},{8,9},{9,10},{10,1... | collective-permute-start | bytes 196616 | tf_op jit(solution)/shard_map/ppermute | solution.py:568
  80.4 25.5 %collective-permute-start.10 = (bf16[64,512]{1,0:T(8,128)(2,1)S(1)}, bf16[64,512]{1,0:T(8,128)(2,1)S(1)}, u32[]{:S(2)}, u32[]{:S(2)}) collective-permute-start(bf16[64,512]{1,0:T(8,128)(2,1)S(1)} %get-tuple-element.71), channel_id=1, source_target_pairs={{0,16},{1,17},{2,18},{3,19},{4,20},{5,21},{6,22},{7,23},{8,24},{9,... | collective-permute-start | bytes 196616 | tf_op jit(solution)/shard_map/ppermute | solution.py:568
  83.5 22.0 %collective-permute-start.11 = (bf16[32,512]{1,0:T(8,128)(2,1)S(1)}, bf16[32,512]{1,0:T(8,128)(2,1)S(1)}, u32[]{:S(2)}, u32[]{:S(2)}) collective-permute-start(bf16[32,512]{1,0:T(8,128)(2,1)S(1)} %get-tuple-element.72), channel_id=1, source_target_pairs={{0,17},{1,18},{2,19},{3,20},{4,21},{5,22},{6,23},{7,24},{8,25},{9,... | collective-permute-start | bytes 98312 | tf_op jit(solution)/shard_map/ppermute | solution.py:568

commit v5 on v4

--- a/solution.py
+++ b/solution.py
@@ -285,7 +285,7 @@
     n_out[...] = n
     p_out[...] = rounded(mm(n, wqkv[...]))
     for w in range(WINDOWS):
-        differ = apart(decode(place)[2] == 1 if w >= 2 else False)
+        differ = apart(decode(place)[3] == 1 if w >= 2 else False)
         for p in range(HF // 2):
             rows = pl.ds(CELLS * w, CELLS)
             q, k, v = (p_out[rows, pl.ds(256 * part + 128 * p, 128)] for part in range(3))
@@ -303,7 +303,7 @@
 def coarse_kernel(
     place, y_in, side, edge, corner, cot_in, cside, cedge, ccorner,
     mgain, mweight, gain, wqkv, wproj, y_main, y_halo, c_main, c_halo, df_send, out_send,
-    y2_out, df_out, side_out, edge_out, corner_out, fac_out, gains_out, packed, mixed, dpacked, wsave,
+    y2_out, df_out, side_out, edge_out, corner_out, fac_out, packed, mixed, dpacked, wsave,
 ):
     halo = jnp.concatenate([side[...], edge[...], corner[...]], axis=0)
     patches = mm(y_main[...], y_in[...]) + mm(y_halo[...], halo)
@@ -314,7 +314,7 @@
     zhat, zinv = normalize(z)
     n = (zhat * gain[...]).astype(BF16)
     packed[...] = rounded(mm(n, wqkv[...]))
-    differ = apart(decode(place)[2] == 1)
+    differ = apart(decode(place)[3] == 1)
     for p in range(HC // 2):
         lanes = pl.ds(128 * p, 128)
         q, k, v = (packed[:, pl.ds(512 * part + 128 * p, 128)] for part in range(3))
@@ -335,10 +335,8 @@
             dpacked[:, pl.ds(512 * part + 128 * p, 128)] = grads[part]
     dp = dpacked[...].astype(BF16)
     dn = rounded(mm_nt(dp, wqkv[...]))
-    gain_sum = jnp.sum(dn * zhat, axis=0, keepdims=True)
     dz = (dy + normalize_back(dn * gain[...], zhat, zinv)).astype(BF16)
     dmn = rounded(mm_nt(dz, mweight[...]))
-    mgain_sum = jnp.sum(dmn * ghat, axis=0, keepdims=True)
     dg = normalize_back(dmn * mgain[...], ghat, ginv)
     df = jnp.concatenate([dg[:, D * i : D * (i + 1)] for i in range(4)], axis=0).astype(BF16)
     df_out[...] = df
@@ -349,21 +347,17 @@
         fac_out[pl.ds(0, CELLS), pl.ds(at, piece.shape[1])] = piece
         at += piece.shape[1]
     fac_out[pl.ds(CELLS, TALL - CELLS), :] = jnp.zeros((TALL - CELLS, at), BF16)
-    for i in range(4):
-        gains_out[pl.ds(1 + i, 1), :] = mgain_sum[:, D * i : D * (i + 1)]
-    gains_out[pl.ds(0, 1), :] = gain_sum
-    gains_out[pl.ds(5, 3), :] = jnp.zeros((3, D), F32)
 
 
 def fine_backward_kernel(
-    place, df_in, side, edge, corner, x_in, p_in, w_in, gain, wqkv, wproj, d_main, d_halo, dx_send, gains_in,
-    dx_out, side_out, edge_out, corner_out, fac_out, gains_out, dmixed, dpacked,
+    place, df_in, side, edge, corner, x_in, p_in, w_in, gain, wqkv, wproj, d_main, d_halo, dx_send,
+    dx_out, side_out, edge_out, corner_out, fac_out, dmixed, dpacked,
 ):
     halo = jnp.concatenate([side[...], edge[...], corner[...]], axis=0)
     dy = mm(d_main[...], df_in[...]) + mm(d_halo[...], halo)
     dmixed[...] = rounded(mm_nt(dy.astype(BF16), wproj[...]))
     for w in range(WINDOWS):
-        differ = apart(decode(place)[2] == 1 if w >= 2 else False)
+        differ = apart(decode(place)[3] == 1 if w >= 2 else False)
         for p in range(HF // 2):
             rows = pl.ds(CELLS * w, CELLS)
             q, k, v = (p_in[rows, pl.ds(256 * part + 128 * p, 128)] for part in range(3))
@@ -374,8 +368,6 @@
     dp = dpacked[...].astype(BF16)
     dn = rounded(mm_nt(dp, wqkv[...]))
     xhat, inverse = normalize(x_in[...].astype(F32))
-    gains_out[...] = gains_in[...]
-    gains_out[pl.ds(5, 1), :] = jnp.sum(dn * xhat, axis=0, keepdims=True)
     dx = (dy + normalize_back(dn * gain[...], xhat, inverse)).astype(BF16)
     dx_out[...] = dx
     stack = mm(dx_send[...], dx).astype(BF16)
@@ -386,8 +378,8 @@
 
 def decode(place):
     code = place[0]
-    shifted = [code] + [lax.shift_right_logical(code, i) for i in (1, 2, 3)]
-    return tuple(lax.bitwise_and(v, 1) for v in shifted[:3]) + (shifted[3],)
+    bits = tuple(lax.bitwise_and(lax.shift_right_logical(code, i), 1) for i in range(4))
+    return bits + (lax.shift_right_logical(code, 4),)
 
 
 def one_hot(want, width):
@@ -395,119 +387,122 @@
     return jnp.where(lane == want, 1.0, 0.0).astype(BF16)
 
 
-def own_rows(share, width, core, by_group):
-    count = width // 2
-    groups = count // share
-    row = lax.broadcasted_iota(jnp.int32, (count, 1), 0)
-    low = share if by_group else groups
-    high_part = lax.shift_right_logical(row, low.bit_length() - 1)
-    low_part = lax.bitwise_and(row, low - 1)
-    group, i = (high_part, low_part) if by_group else (low_part, high_part)
-    return one_hot((2 * group + core) * share + i, width)
-
-
-def coarse_weights_kernel(place, own, other, merge_keep, merge_send, coarse_keep, coarse_send, lines):
-    core, parity, _, _ = decode(place)
-    block, tall = (merge_keep.shape[0] // 2, merge_keep.shape[1])
-    rows = tall // 4
-    groups = 4 * block
-    share = rows // 4
+def row_index(count):
+    return lax.broadcasted_iota(jnp.int32, (count, 1), 0)
+
+
+def field(x, low, bits):
+    return lax.bitwise_and(lax.shift_right_logical(x, low), (1 << bits) - 1)
+
+
+def coarse_weights_kernel(
+    place, own, other, m0k, m0s, m1k, m1s, c0k, c0s, c1k, c1s, lines
+):
+    core, zp, yp, _, _ = decode(place)
 
     def at(start, size):
         return jnp.concatenate([own[:, pl.ds(start, size)], other[:, pl.ds(start, size)]], axis=0)
 
-    def put(b, h, value, same, differs):
-        place_of = (pl.ds(block * (b // 2), block), pl.ds(rows * h, rows), slice(None))
-
-        @pl.when(parity == b % 2)
-        def _():
-            same[place_of] = value
-
-        @pl.when(parity != b % 2)
-        def _():
-            differs[place_of] = value
-
     dz = at(2048 + 1024, D)
-    select = own_rows(rows, D, core, True)
-    for b in range(4):
-        left = mm_nt(select, at(D * b, D)).astype(BF16)
-        part = mm(left, dz).reshape(block, rows, D).astype(BF16)
-        for h in range(4):
-            put(b, h, part[:, :, 128 * h : 128 * h + 128], merge_keep, merge_send)
-    select = own_rows(share, D, core, False)
+    row = row_index(256)
+    group = field(row, 4, 3) * 2 + lax.bitwise_xor(field(row, 7, 1), yp)
+    select = one_hot((2 * group + core) * 16 + field(row, 0, 4), D)
+    for zh in range(2):
+        pair = [at(D * (2 * zh + k), D) for k in range(2)]
+        plain = jnp.full(pair[0].shape, zp, jnp.int32) == 0
+        ordered = (
+            jnp.where(plain, pair[0].astype(F32), pair[1].astype(F32)).astype(BF16),
+            jnp.where(plain, pair[1].astype(F32), pair[0].astype(F32)).astype(BF16),
+        )
+        for zd in range(2):
+            left = mm_nt(select, ordered[zd]).astype(BF16)
+            part = mm(left, dz).reshape(16, 16, D)
+            for yd in range(2):
+                for h in range(4):
+                    piece = part[8 * yd : 8 * yd + 8, :, 128 * h : 128 * h + 128]
+                    (m0s if zd else m0k)[pl.ds(16 * yd + 8 * zh, 8), pl.ds(8 * h, 8), :] = piece[:, :8].astype(BF16)
+                    (m1s if yd else m1k)[pl.ds(16 * zd + 8 * zh, 8), pl.ds(8 * h, 8), :] = piece[:, 8:].astype(BF16)
+    row = row_index(256)
+    z = field(row, 3, 1) * 2 + lax.bitwise_xor(field(row, 5, 1), zp)
+    group = z * 16 + field(row, 0, 3) * 2 + lax.bitwise_xor(field(row, 4, 1), yp)
+    select = one_hot((2 * group + core) * 4 + field(row, 6, 2), D)
     n = mm_nt(select, at(2048, D)).astype(BF16)
     m = mm_nt(select, at(2048 + D, D)).astype(BF16)
     for j in range(4):
         part = mm(n if j < 3 else m, at(2048 + 1536 + D * j, D))
-        for i in range(share):
-            line = part[groups * i : groups * (i + 1)]
+        for i in range(4):
+            line = part[64 * i : 64 * (i + 1)]
             for h in range(4):
-                lines[pl.ds(groups * rows * h + share * j + i, groups, rows), :] = line[:, 128 * h : 128 * h + 128]
+                lines[pl.ds(512 * (4 * (j // 2) + h) + 4 * (j % 2) + i, 64, 8), :] = line[:, 128 * h : 128 * h + 128]
     for h in range(4):
-        for b in range(4):
-            chunk = lines[pl.ds(groups * rows * h + block * rows * b, block * rows), :]
-            put(b, h, chunk.reshape(block, rows, 128).astype(BF16), coarse_send, coarse_keep)
-
-
-def fine_weights_kernel(
-    place, merge_keep, merge_came, coarse_keep, coarse_came, n_own, n_other, m_own, m_other, own, other,
-    gains, gains_other, out, chunks, lines,
-):
-    core, parity, _, _ = decode(place)
-    groups = out.shape[0]
-    block, top = (merge_keep.shape[0] // 2, merge_keep.shape[1])
-    rows = 8
-    share = D // (2 * groups)
-    for k in range(2):
-        part = pl.ds(block * k, block)
-        merge = merge_keep[part].astype(F32) + merge_came[part].astype(F32)
-        coarse = coarse_keep[part].astype(F32) + coarse_came[part].astype(F32)
-        out[pl.ds(block * (2 * k + parity), block), pl.ds(0, top), :] = merge.astype(BF16)
-        out[pl.ds(block * (2 * k + 1 - parity), block), pl.ds(0, top), :] = coarse.astype(BF16)
-    select = own_rows(share, D, core, False)
+        first = lines[pl.ds(512 * h, 512), :].reshape(64, 8, 128).astype(BF16)
+        c0s[:, pl.ds(8 * h, 8), :] = first[:32]
+        c0k[:, pl.ds(8 * h, 8), :] = first[32:]
+        second = lines[pl.ds(512 * (4 + h), 512), :].reshape(64, 8, 128).astype(BF16)
+        for zd in range(2):
+            c1s[pl.ds(16 * zd, 16), pl.ds(8 * h, 8), :] = second[32 * zd : 32 * zd + 16]
+            c1k[pl.ds(16 * zd, 16), pl.ds(8 * h, 8), :] = second[32 * zd + 16 : 32 * zd + 32]
+
+
+def middle_kernel(m0k, m0c, m1k, m1c, c0k, c0c, c1k, c1c, m0, m0s, m1, m1s, c0, c0s, c1, c1s):
+    for keep, came, first, second in (
+        (m0k, m0c, m0, m0s), (m1k, m1c, m1s, m1), (c0k, c0c, c0s, c0), (c1k, c1c, c1, c1s)
+    ):
+        total = (keep[...].astype(F32) + came[...].astype(F32)).astype(BF16)
+        first[...] = total[:16]
+        second[...] = total[16:]
+
+
+def fine_weights_kernel(place, n_own, n_other, m_own, m_other, own, other, out, lines):
+    core = decode(place)[0]
+    row = row_index(256)
+    select = one_hot((2 * field(row, 0, 6) + core) * 4 + field(row, 6, 2), D)
     dp = lambda ref: ref[:, pl.ds(0, 768)]
     dy = lambda ref: ref[:, pl.ds(768, D)]
     n = [mm_nt(select, ref[...]).astype(BF16) for ref in (n_own, n_other)]
     part = mm(n[0], dp(own)) + mm(n[1], dp(other))
-    half = share // 2
-    for i in range(share):
-        line = part[groups * i : groups * (i + 1)]
+    for i in range(4):
+        line = part[64 * i : 64 * (i + 1)]
         for h in range(4):
-            lines[pl.ds(groups * rows * h + i, groups, rows), :] = line[:, 128 * h : 128 * h + 128]
+            lines[pl.ds(512 * h + i, 64, 8), :] = line[:, 128 * h : 128 * h + 128]
         for h in range(2):
-            lines[pl.ds(groups * rows * (2 * (i // half) + h) + share + i % half, groups, rows), :] = line[:, 512 + 128 * h : 640 + 128 * h]
-    select = own_rows(half, 256, core, False)
+            lines[pl.ds(512 * (2 * (i // 2) + h) + 4 + i % 2, 64, 8), :] = line[:, 512 + 128 * h : 640 + 128 * h]
+    row = row_index(128)
+    select = one_hot((2 * field(row, 0, 6) + core) * 2 + field(row, 6, 1), 256)
     m = [mm_nt(select, ref[...]).astype(BF16) for ref in (m_own, m_other)]
     part = mm(m[0], dy(own)) + mm(m[1], dy(other))
-    for i in range(half):
-        line = part[groups * i : groups * (i + 1)]
+    for i in range(2):
+        line = part[64 * i : 64 * (i + 1)]
         for h in range(4):
-            lines[pl.ds(groups * rows * h + share + half + i, groups, rows), :] = line[:, 128 * h : 128 * h + 128]
+            lines[pl.ds(512 * h + 6 + i, 64, 8), :] = line[:, 128 * h : 128 * h + 128]
     for h in range(4):
-        chunk = lines[pl.ds(groups * rows * h, groups * rows), :]
-        out[:, pl.ds(top + rows * h, rows), :] = chunk.reshape(groups, rows, 128).astype(BF16)
-    both_gains = gains[...] + gains_other[...]
-    for r in range(6):
-        for q in range(4):
-            chunks[pl.ds(4 * r + q, 1), :] = both_gains[r : r + 1, 128 * q : 128 * (q + 1)]
-    chunks[pl.ds(24, 8), :] = jnp.zeros((8, 128), F32)
-    row = lax.broadcasted_iota(jnp.int32, (groups * rows, 1), 0)
-    device = 2 * lax.shift_right_logical(row, 3) + core
-    r = lax.bitwise_and(row, 7)
-    small = lax.shift_right_logical(device * share, 7)
-    want = jnp.where(
-        r == 0,
-        small,
-        jnp.where(r == 1, 4 + lax.shift_right_logical(device * share * 4, 7), jnp.where(r == 2, 20 + small, -1)),
-    )
-    out[:, pl.ds(top + 4 * rows, rows), :] = (
-        mm(one_hot(want, 32), chunks[...].astype(BF16)).reshape(groups, rows, 128).astype(BF16)
-    )
+        out[:, pl.ds(8 * h, 8), :] = lines[pl.ds(512 * h, 512), :].reshape(64, 8, 128).astype(BF16)
+
+
+def join_kernel(place, m0, m0c, m1, m1c, c0, c0c, c1, c1c, fine, out):
+    _, zp, yp, _, _ = decode(place)
+    for keep, came, zd, yd in ((m0, m0c, 0, 0), (m1, m1c, 1, 0), (c0, c0c, 1, 1), (c1, c1c, 0, 1)):
+        total = (keep[...].astype(F32) + came[...].astype(F32)).astype(BF16)
+        for zh in range(2):
+            out[zh, lax.bitwise_xor(zp, zd), :, lax.bitwise_xor(yp, yd), pl.ds(0, 32), :] = total[8 * zh : 8 * zh + 8]
+    out[:, :, :, :, pl.ds(32, 32), :] = fine[...].reshape(2, 2, 8, 2, 32, 128)
+
+
+def gain_rows(weight, gain, device, share):
+    count = max(8, share)
+    pick_rows = one_hot(device * share + row_index(count), gain.shape[1])
+    over = jnp.sum(pick_rows.astype(F32) * gain, axis=1, keepdims=True)
+    return mm(pick_rows, weight)[:share] / over[:share]
 
 
 def assemble_kernel(
-    y2, side, edge, corner, dx, dside, dedge, dcorner, out_main, out_halo, dx_main, dx_halo, out, grad
+    place, y2, side, edge, corner, dx, dside, dedge, dcorner, out_main, out_halo, dx_main, dx_halo,
+    fgain, fqkv, mgain, mweight, cgain, cqkv, out, grad, fcoef, mcoef, ccoef,
 ):
+    device = decode(place)[4]
+    fcoef[...] = gain_rows(fqkv[...], fgain[...], device, 4)
+    mcoef[...] = gain_rows(mweight[...], mgain[...], device, 16)
+    ccoef[...] = gain_rows(cqkv[...], cgain[...], device, 4)
     halo = jnp.concatenate([side[...], edge[...], corner[...]], axis=0)
     y = mm(out_main[...], y2[...]) + mm(out_halo[...], halo)
     for r in range(6):
@@ -517,41 +512,49 @@
     grad[...] = d.reshape(ROWS, COLS, D).astype(BF16)
 
 
-def sum_kernel(place, parts, fgain, fqkv, fproj, mgain, merge, cgain, cqkv, cproj):
-    _, parity, _, device = decode(place)
-    groups = parts.shape[0]
-    block = groups // 4
-    rows, share = (merge.shape[0], cqkv.shape[0])
-    half = share // 2
-    top = 4 * rows
-    factor = (ROWS * COLS * 2 * groups // 4) ** (-0.5)
+def as_row(column):
+    size = column.shape[0]
+    row = lax.broadcasted_iota(jnp.int32, (size, size), 0)
+    lane = lax.broadcasted_iota(jnp.int32, (size, size), 1)
+    return jnp.sum(jnp.where(row == lane, column, 0.0), axis=0, keepdims=True)
+
+
+def sum_kernel(place, parts, fcoef, mcoef, ccoef, fgain, fqkv, fproj, mgain, merge, cgain, cqkv, cproj):
+    _, zp, yp, _, _ = decode(place)
+    factor = (ROWS * COLS * 128 // 4) ** (-0.5)
     sums = []
-    for first in range(2):
-        total = None
-        for k in range(2):
-            for i in range(block):
-                term = parts[block * (2 * k + first) + i].astype(F32)
-                total = term if total is None else total + term
-        sums.append(total * factor)
-    same = (jnp.full((top, 128), parity, jnp.int32) == 0)
-    first, second = (sums[0][:top], sums[1][:top])
-    merged = jnp.where(same, first, second)
-    coarse = jnp.where(same, second, first)
-    total = sums[0][top:] + sums[1][top:]
+    for z in range(2):
+        for y in range(2):
+            total = None
+            for zh in range(2):
+                for k in range(8):
+                    term = parts[zh, z, k, y].astype(F32)
+                    total = term if total is None else total + term
+            sums.append(total * factor)
+    fine = (sums[0] + sums[1] + sums[2] + sums[3])[32:]
+    tops = [v[:32] for v in sums]
+    z_same = jnp.full((32, 128), zp, jnp.int32) == 0
+    y_same = jnp.full((32, 128), yp, jnp.int32) == 0
+
+    def related(zd, yd):
+        low = [jnp.where(z_same, tops[2 * zd + y], tops[2 * (1 - zd) + y]) for y in range(2)]
+        return jnp.where(y_same, low[yd], low[1 - yd])
+
+    m0, m1, c0, c1 = (related(0, 0), related(1, 0), related(1, 1), related(0, 1))
     for h in range(4):
         lanes = pl.ds(128 * h, 128)
-        merge[:, lanes] = merged[rows * h : rows * (h + 1)]
-        for j in range(3):
-            cqkv[:, pl.ds(D * j + 128 * h, 128)] = coarse[rows * h + share * j : rows * h + share * (j + 1)]
-        cproj[:, lanes] = coarse[rows * h + 3 * share : rows * (h + 1)]
-        line = total[8 * h : 8 * h + 8]
-        fqkv[:, lanes] = line[:share]
-        fqkv[pl.ds(half * (h // 2), half), pl.ds(D + 128 * (h % 2), 128)] = line[share : share + half]
-        fproj[:, lanes] = line[share + half : 2 * share]
-    for r, (ref, size) in enumerate(((cgain, share), (mgain, rows), (fgain, share))):
-        first = lax.rem(device * size, 128)
-        turned = pltpu.roll(total[32:40], lax.rem(128 - first, 128), 1)
-        ref[...] = turned[r : r + 1, :size]
+        rows = slice(8 * h, 8 * h + 8)
+        merge[pl.ds(0, 8), lanes] = m0[rows]
+        merge[pl.ds(8, 8), lanes] = m1[rows]
+        cqkv[:, lanes] = c0[8 * h : 8 * h + 4]
+        cqkv[:, pl.ds(D + 128 * h, 128)] = c0[8 * h + 4 : 8 * h + 8]
+        cqkv[:, pl.ds(2 * D + 128 * h, 128)] = c1[8 * h : 8 * h + 4]
+        cproj[:, lanes] = c1[8 * h + 4 : 8 * h + 8]
+        fqkv[:, lanes] = fine[8 * h : 8 * h + 4]
+        fqkv[pl.ds(2 * (h // 2), 2), pl.ds(D + 128 * (h % 2), 128)] = fine[8 * h + 4 : 8 * h + 6]
+        fproj[:, lanes] = fine[8 * h + 6 : 8 * h + 8]
+    for ref, coef, grad in ((fgain, fcoef, fqkv), (mgain, mcoef, merge), (cgain, ccoef, cqkv)):
+        ref[...] = as_row(jnp.sum(coef[...] * grad[...], axis=1, keepdims=True))
 
 
 def exchange(pieces, step):
@@ -573,13 +576,17 @@
     return lax.ppermute(value, "core", [(0, 1), (1, 0)])
 
 
-def fold(value, second):
-    ring = lax.axis_size("lat") // 2
+def fold(value, axis, second):
+    lat, pair = (lax.axis_size("lat"), lax.axis_size("pair"))
     pairs = []
-    for z in range(ring):
-        step = 1 if z % 2 == (1 if second else 0) else -1
-        pairs += [(2 * z + y, 2 * ((z + step) % ring) + y) for y in range(2)]
-    return lax.ppermute(value, "lat", pairs)
+    for r in range(lat):
+        for p in range(pair):
+            z, y = (r // 2, (r % 2) * 2 + p % 2)
+            at = z if axis == "z" else y
+            at = (at + (1 if at % 2 == (1 if second else 0) else -1)) % 4
+            z, y = (at, y) if axis == "z" else (z, at)
+            pairs.append((r * pair + p, (2 * z + y // 2) * pair + (p // 2) * 2 + y % 2))
+    return lax.ppermute(value, ("lat", "pair"), pairs)
 
 
 def deal(value):
@@ -590,14 +597,12 @@
     tokens, fine_gain, fine_qkv, fine_proj, merge_gain, merge_weight, coarse_gain, coarse_qkv, coarse_proj, cotangent
 ):
     lat_count = lax.axis_size("lat")
-    groups = lat_count * lax.axis_size("pair")
-    share = D // (2 * groups)
-    rows = 4 * share
     lat, core = (lax.axis_index("lat"), lax.axis_index("core"))
     device = (lat * lax.axis_size("pair") + lax.axis_index("pair")) * 2 + core
     parity = lax.bitwise_and(lax.shift_right_logical(lat, 1), 1)
     seam = (lat == lat_count - 1).astype(jnp.int32)
-    place = (device * 8 + seam * 4 + parity * 2 + core).astype(jnp.int32).reshape(1)
+    flip = lax.bitwise_and(lax.axis_index("pair"), 1)
+    place = (device * 16 + seam * 8 + flip * 4 + parity * 2 + core).astype(jnp.int32).reshape(1)
     fgain, mgain, cgain = (v.reshape(1, -1) for v in (fine_gain, merge_gain, coarse_gain))
     cells = WINDOWS * CELLS
 
@@ -629,9 +634,9 @@
     )
     merged = exchange(sent, -1)
     n_other, m_other = (partner(n), partner(m))
-    y2, df, *sent, fac, gains = scalar_call(
+    y2, df, *sent, fac = scalar_call(
         coarse_kernel,
-        [((CELLS, D), BF16), ((cells, D), BF16)] + pieces + [((TALL, 5632), BF16), ((8, D), F32)],
+        [((CELLS, D), BF16), ((cells, D), BF16)] + pieces + [((TALL, 5632), BF16)],
         place, y, *merged, cot, *ahead, mgain, merge_weight, cgain, coarse_qkv, coarse_proj,
         table("y_main"), table("y_halo"), table("cot_main"), table("cot_halo"), table("df_send"), table("out_send"),
         scratch=[
@@ -640,43 +645,57 @@
         ],
     )
     back = exchange(sent, 1)
-    chunk = ((groups // 2, 4 * rows, 128), BF16)
-    merge_keep, merge_send, coarse_keep, coarse_send = scalar_call(
+    m0k, m0s, m1k, m1s, c0k, c0s, c1k, c1s = scalar_call(
         coarse_weights_kernel,
-        [chunk] * 4,
+        [((32, 32, 128), BF16)] * 8,
         place, fac, partner(fac),
-        scratch=[pltpu.VMEM((4 * groups * rows, 128), F32)],
-    )
-    merge_came = fold(merge_send, False)
-    coarse_came = fold(coarse_send, True)
-    dx, *sent, fac, gains = scalar_call(
+        scratch=[pltpu.VMEM((4096, 128), F32)],
+    )
+    first = [
+        fold(v, axis, second)
+        for v, axis, second in ((m0s, "z", False), (m1s, "y", False), (c0s, "z", True), (c1s, "y", True))
+    ]
+    dx, *sent, fac = scalar_call(
         fine_backward_kernel,
-        [((cells, D), BF16)] + narrow + [((cells, 1280), BF16), ((8, D), F32)],
+        [((cells, D), BF16)] + narrow + [((cells, 1280), BF16)],
         place, df, *back, x, p, w, fgain, fine_qkv, fine_proj, table("df_main"), table("df_halo"), table("dx_send"),
-        gains,
         scratch=[pltpu.VMEM((cells, 256), F32), pltpu.VMEM((cells, 768), F32)],
     )
     ended = exchange(sent, 1)
-    (rest,) = scalar_call(
+    m0, m0s, m1, m1s, c0, c0s, c1, c1s = call(
+        middle_kernel,
+        [((16, 32, 128), BF16)] * 8,
+        m0k, first[0], m1k, first[1], c0k, first[2], c1k, first[3],
+    )
+    again = [
+        fold(v, axis, second)
+        for v, axis, second in ((m0s, "y", False), (m1s, "z", False), (c0s, "y", True), (c1s, "z", True))
+    ]
+    (fine_part,) = scalar_call(
         fine_weights_kernel,
-        [((groups, 4 * rows + 40, 128), BF16)],
-        place, merge_keep, merge_came, coarse_keep, coarse_came, n, n_other, m, m_other,
-        fac, partner(fac), gains, partner(gains),
-        scratch=[pltpu.VMEM((32, 128), F32), pltpu.VMEM((4 * groups * 8, 128), F32)],
-    )
-    parts = deal(rest)
-    output, grad = call(
+        [((64, 32, 128), BF16)],
+        place, n, n_other, m, m_other, fac, partner(fac),
+        scratch=[pltpu.VMEM((2048, 128), F32)],
+    )
+    (joined,) = scalar_call(
+        join_kernel,
+        [((2, 2, 8, 2, 64, 128), BF16)],
+        place, m0, again[0], m1, again[1], c0, again[2], c1, again[3], fine_part,
+    )
+    parts = deal(joined.reshape(64, 64, 128)).reshape(2, 2, 8, 2, 64, 128)
+    output, grad, fcoef, mcoef, ccoef = scalar_call(
         assemble_kernel,
-        [((6, 12, D), BF16), ((ROWS, COLS, D), BF16)],
-        y2, *back, dx, *ended, table("out_main"), table("out_halo"), table("dx_main"), table("dx_halo"),
+        [((6, 12, D), BF16), ((ROWS, COLS, D), BF16), ((4, 768), F32), ((16, D), F32), ((4, 1536), F32)],
+        place, y2, *back, dx, *ended, table("out_main"), table("out_halo"), table("dx_main"), table("dx_halo"),
+        fgain, fine_qkv, mgain, merge_weight, cgain, coarse_qkv,
     )
     fg, fqkv, fproj, mg, merge, cg, cqkv, cproj = scalar_call(
         sum_kernel,
         [
-            ((1, share), F32), ((share, 768), F32), ((share // 2, D), F32), ((1, rows), F32), ((rows, D), F32),
-            ((1, share), F32), ((share, 1536), F32), ((share, D), F32),
+            ((1, 4), F32), ((4, 768), F32), ((2, D), F32), ((1, 16), F32), ((16, D), F32), ((1, 4), F32),
+            ((4, 1536), F32), ((4, D), F32),
         ],
-        place, parts,
+        place, parts, fcoef, mcoef, ccoef,
     )
     fg, mg, cg = (v.reshape(-1) for v in (fg, mg, cg))
     return (output, grad, fg, fqkv, fproj, mg, merge, cg, cqkv, cproj)

time: 109 us -> 116 us (1.064)
  local copies, waits for them, and re-layouts: 0.14 us -> 13.4 us
  waiting for transfers between devices: 52.7 us -> 40.6 us
  starting transfers between devices: 30 us -> 36.5 us
  Pallas kernels: 24.1 us -> 22.4 us
    unnamed x48 -> x68, local copies, waits for them, and re-layouts: 0.14 us -> 13.4 us
    ppermute x12, waiting for transfers between devices: 39.5 us -> 29 us  [exchange(): arrived.append(lax.ppermute(piece, ('lat', 'pair', 'core'), pairs))]
    ppermute x2 -> x8, starting transfers between devices: 1.76 us -> 6.94 us  [fold(): return lax.ppermute(value, ('lat', 'pair'), pairs)]
    ppermute x5 -> x4, waiting for transfers between devices: 2.27 us -> 0.01 us  [partner(): return lax.ppermute(value, 'core', [(0, 1), (1, 0)])]
    pallas_call x8 -> x10, Pallas kernels: 24.1 us -> 22.4 us  [call(): pl.pallas_call(kernel, out_shape=[jax.ShapeDtypeStruct(s, d) for s, d in...]
    ppermute x2 -> x8, waiting for transfers between devices: 10.9 us -> 11.6 us  [fold(): return lax.ppermute(value, ('lat', 'pair'), pairs)]
  transfers between devices with their start and end apart: 20 -> 25, of which waited for: 9 -> 12; matrix products, arithmetic and copies ran while one was open for 0% -> 0% of each run, Pallas kernels for 8% -> 7%
where the time goes in v5:
time: 116 us; the launch traced here: 114 us
  waiting for transfers between devices  40.6 us (35%)
  starting transfers between devices  36.5 us (31%)
  Pallas kernels  22.4 us (19%)
  local copies, waits for them, and re-layouts  13.4 us (12%)
    ppermute x12, waiting for transfers between devices, exchange(): arrived.append(lax.ppermute(piece, ('lat', 'pair', 'core'), pairs))  29 us
    pallas_call x10, Pallas kernels, call(): pl.pallas_call(kernel, out_shape=[jax.ShapeDtypeStruct(s, d) for s, d in...  22.4 us
    ppermute x12, starting transfers between devices, exchange(): arrived.append(lax.ppermute(piece, ('lat', 'pair', 'core'), pairs))  22.4 us
    unnamed x68, local copies, waits for them, and re-layouts  13.4 us
    ppermute x8, waiting for transfers between devices, fold(): return lax.ppermute(value, ('lat', 'pair'), pairs)  11.6 us
    ppermute x8, starting transfers between devices, fold(): return lax.ppermute(value, ('lat', 'pair'), pairs)  6.94 us
    all_to_all x1, starting transfers between devices, deal(): return lax.all_to_all(value, ('lat', 'pair'), 0, 0)  6.7 us
  transfers between devices with their start and end apart: 25, of which 12 were waited for; matrix products, arithmetic and copies ran while one was open for 0% of the time, Pallas kernels for 7%

profile of v5, /device:TPU:0, one launch (start us, length us, event | category | flops | bytes accessed | tf_op | source)
XLA Modules:
  0.0 113.9 jit_solution(4381629179176535579)
XLA Ops:
  0.7 1.5 %shard_map.339 = (bf16[288,512]{1,0:T(8,128)(2,1)S(1)}, bf16[80,512]{1,0:T(8,128)(2,1)S(1)}, bf16[80,512]{1,0:T(8,128)(2,1)S(1)}, bf16[48,512]{1,0:T(8,128)(2,1)S(1)}, f32[72,512]{1,0:T(8,128)S(1)}) custom-call(bf16[12,24,512]{2,1,0:T(8,128)(2,1)} %tok_in.1, bf16[6,12,512]{2,1,0:T(8,128)(2,1)} %cot_in.1, bf16[208,288]{1,0:T(8,128)(2,1)} %constant.62.clone.tok_send_in, ...), custom_call_target="tpu_custom_call" | custom-call | flops 5000000000 | bytes 4000000 | tf_op jit(solution)/shard_map/pallas_call | solution.py:162
  2.2 0.7 copy-done.28
  2.9 0.7 copy-done.30
  3.6 3.3 %collective-permute-start = (bf16[80,512]{1,0:T(8,128)(2,1)S(1)}, bf16[80,512]{1,0:T(8,128)(2,1)S(1)}, u32[]{:S(2)}, u32[]{:S(2)}) collective-permute-start(bf16[80,512]{1,0:T(8,128)(2,1)S(1)} %get-tuple-element.65), channel_id=1, source_target_pairs={{0,15},{1,0},{2,1},{3,2},{4,3},{5,4},{6,5},{7,6},{8,7},{9,8},{10,9... | collective-permute-start | bytes 245768 | tf_op jit(solution)/shard_map/ppermute | solution.py:571
  6.9 6.4 %collective-permute-start.1 = (bf16[80,512]{1,0:T(8,128)(2,1)S(1)}, bf16[80,512]{1,0:T(8,128)(2,1)S(1)}, u32[]{:S(2)}, u32[]{:S(2)}) collective-permute-start(bf16[80,512]{1,0:T(8,128)(2,1)S(1)} %get-tuple-element.66), channel_id=1, source_target_pairs={{0,112},{1,113},{2,114},{3,115},{4,116},{5,117},{6,118},{7,119},{8... | collective-permute-start | bytes 245768 | tf_op jit(solution)/shard_map/ppermute | solution.py:571
  13.5 4.9 %collective-permute-done.2.corner.ccorner = bf16[48,512]{1,0:T(8,128)(2,1)S(1)} collective-permute-done((bf16[48,512]{1,0:T(8,128)(2,1)S(1)}, bf16[48,512]{1,0:T(8,128)(2,1)S(1)}, u32[]{:S(2)}, u32[]{:S(2)}) %collective-permute-start.2) | collective-permute-done | bytes 49184 | tf_op jit(solution)/shard_map/ppermute | solution.py:571
  18.4 0.9 copy-done.13
  19.3 0.9 copy-done.20
  20.2 1.0 copy-done.29
  21.3 3.9 %shard_map.340 = (bf16[288,512]{1,0:T(8,128)(2,1)S(1)}, bf16[288,512]{1,0:T(8,128)(2,1)S(1)}, f32[288,768]{1,0:T(8,128)S(1)}, f32[8,72,256]{2,1,0:T(8,128)S(1)},...) custom-call(s32[1]{0:T(128)} %bitcast.place, ...), custom_call_target="tpu_custom_call" | custom-call | flops 5000000000 | bytes 4000000 | tf_op jit(solution)/shard_map/pallas_call | solution.py:162
  25.2 0.5 collective-permute-start.3
  25.7 5.2 %collective-permute-start.4 = (bf16[64,512]{1,0:T(8,128)(2,1)S(1)}, bf16[64,512]{1,0:T(8,128)(2,1)S(1)}, u32[]{:S(2)}, u32[]{:S(2)}) collective-permute-start(bf16[64,512]{1,0:T(8,128)(2,1)S(1)} %get-tuple-element.70), channel_id=1, source_target_pairs={{0,112},{1,113},{2,114},{3,115},{4,116},{5,117},{6,118},{7,119},{8... | collective-permute-start | bytes 196616 | tf_op jit(solution)/shard_map/ppermute | solution.py:571
  30.8 4.8 %collective-permute-done.5.corner = bf16[32,512]{1,0:T(8,128)(2,1)S(1)} collective-permute-done((bf16[32,512]{1,0:T(8,128)(2,1)S(1)}, bf16[32,512]{1,0:T(8,128)(2,1)S(1)}, u32[]{:S(2)}, u32[]{:S(2)}) %collective-permute-start.5) | collective-permute-done | bytes 32800 | tf_op jit(solution)/shard_map/ppermute | solution.py:571
  35.8 6.5 %shard_map.341 = (bf16[72,512]{1,0:T(8,128)(2,1)S(1)}, bf16[288,512]{1,0:T(8,128)(2,1)S(1)}, bf16[80,512]{1,0:T(8,128)(2,1)S(1)}, bf16[80,512]{1,0:T(8,128)(2,1)...) custom-call(s32[1]{0:T(128)} %bitcast.place, bf16[288,512]{1,0:T(8,128)(2,1)S(1)} %get-tuple-element.68.y_in, ...), custom_call_target="tpu_custom_call" | custom-call | flops 5000000000 | bytes 4000000 | tf_op jit(solution)/shard_map/pallas_call | solution.py:162
  42.3 0.6 copy-done.32
  42.9 0.5 collective-permute-start.6
  43.4 9.6 %collective-permute-done.8.corner = bf16[48,512]{1,0:T(8,128)(2,1)S(1)} collective-permute-done((bf16[48,512]{1,0:T(8,128)(2,1)S(1)}, bf16[48,512]{1,0:T(8,128)(2,1)S(1)}, u32[]{:S(2)}, u32[]{:S(2)}) %collective-permute-start.8) | collective-permute-done | bytes 49184 | tf_op jit(solution)/shard_map/ppermute | solution.py:571
  53.1 3.5 %shard_map.342 = (bf16[288,512]{1,0:T(8,128)(2,1)S(1)}, bf16[64,512]{1,0:T(8,128)(2,1)S(1)}, bf16[64,512]{1,0:T(8,128)(2,1)S(1)}, bf16[32,512]{1,0:T(8,128)(2,1)S(1)}, bf16[288,1280]{1,0:T(8,128)(2,1)S(1)}) custom-call(s32[1]{0:T(128)} %bitcast.place, bf16[288,512]{1,0:T(8,128)(2,1)S(1)} %get-tuple-element.77.df_in, ...), custom_call_target="tpu_custom_call" | custom-call | flops 5000000000 | bytes 4000000 | tf_op jit(solution)/shard_map/pallas_call | solution.py:162
  56.6 0.7 copy-done.26
  57.3 1.8 %shard_map.344 = (bf16[32,32,128]{2,1,0:T(8,128)(2,1)S(1)}, bf16[32,32,128]{2,1,0:T(8,128)(2,1)S(1)}, bf16[32,32,128]{2,1,0:T(8,128)(2,1)S(1)}, bf16[32,32,128]{...) custom-call(s32[1]{0:T(128)} %bitcast.place, ...), custom_call_target="tpu_custom_call" | custom-call | flops 5000000000 | bytes 4000000 | tf_op jit(solution)/shard_map/pallas_call | solution.py:162
  59.3 1.8 %collective-permute-start.15 = (bf16[32,32,128]{2,1,0:T(8,128)(2,1)S(1)}, bf16[32,32,128]{2,1,0:T(8,128)(2,1)S(1)}, u32[]{:S(2)}, u32[]{:S(2)}) collective-permute-start(bf16[32,32,128]{2,1,0:T(8,128)(2,1)S(1)} %get-tuple-element.93), channel_id=1, source_target_pairs={{0,96},{2,98},{4,100},{6,102},{8,104},{10,106},{12,108},{14,110},{... | collective-permute-start | bytes 786440 | tf_op jit(solution)/shard_map/ppermute | solution.py:589
  61.1 1.0 collective-permute-start.16
  62.1 5.8 %collective-permute-done.13.m0c = bf16[32,32,128]{2,1,0:T(8,128)(2,1)S(1)} collective-permute-done((bf16[32,32,128]{2,1,0:T(8,128)(2,1)S(1)}, bf16[32,32,128]{2,1,0:T(8,128)(2,1)S(1)}, u32[]{:S(2)}, u32[]{:S(2)}) %collective-permute-start.13) | collective-permute-done | bytes 262176 | tf_op jit(solution)/shard_map/ppermute | solution.py:589
  68.5 0.9 collective-permute-done.15.c0c
  69.3 1.4 %collective-permute-done.16.c1c = bf16[32,32,128]{2,1,0:T(8,128)(2,1)S(1)} collective-permute-done((bf16[32,32,128]{2,1,0:T(8,128)(2,1)S(1)}, bf16[32,32,128]{2,1,0:T(8,128)(2,1)S(1)}, u32[]{:S(2)}, u32[]{:S(2)}) %collective-permute-start.16) | collective-permute-done | bytes 262176 | tf_op jit(solution)/shard_map/ppermute | solution.py:589
  71.0 0.5 collective-permute-start.17
  71.5 1.0 collective-permute-start.18
  72.6 0.9 collective-permute-start.19
  73.5 1.6 %collective-permute-start.20 = (bf16[16,32,128]{2,1,0:T(8,128)(2,1)S(1)}, bf16[16,32,128]{2,1,0:T(8,128)(2,1)S(1)}, u32[]{:S(2)}, u32[]{:S(2)}) collective-permute-start(bf16[16,32,128]{2,1,0:T(8,128)(2,1)S(1)} %get-tuple-element.103), channel_id=1, source_target_pairs={{0,96},{2,98},{4,100},{6,102},{8,104},{10,106},{12,108},{14,110},{... | collective-permute-start | bytes 393224 | tf_op jit(solution)/shard_map/ppermute | solution.py:589
  75.0 1.2 %shard_map.346.fine = bf16[64,32,128]{2,1,0:T(8,128)(2,1)S(1)} custom-call(s32[1]{0:T(128)} %bitcast.place, bf16[288,512]{1,0:T(8,128)(2,1)S(1)} %get-tuple-element.104.n_own, bf16[288,512]{1,0:T(8,128)(2,1)S(1)} %collective-permute-done.21.n_other, bf16[288,256]{1,0:T(8,128)(2,1)S(1)} %get-tuple-element.105.m_own, ...), custom_call_target="tpu_custom_call" | custom-call | flops 5000000000 | bytes 4000000 | tf_op jit(solution)/shard_map/pallas_call | solution.py:162
  76.5 2.3 %collective-permute-done.19.c0c = bf16[16,32,128]{2,1,0:T(8,128)(2,1)S(1)} collective-permute-done((bf16[16,32,128]{2,1,0:T(8,128)(2,1)S(1)}, bf16[16,32,128]{2,1,0:T(8,128)(2,1)S(1)}, u32[]{:S(2)}, u32[]{:S(2)}) %collective-permute-start.19) | collective-permute-done | bytes 131104 | tf_op jit(solution)/shard_map/ppermute | solution.py:589
  78.8 0.9 collective-permute-done.20.c1c
  79.6 1.2 %shard_map.347 = bf16[2,2,8,2,64,128]{5,4,3,2,1,0:T(8,128)(2,1)} custom-call(s32[1]{0:T(128)} %bitcast.place, bf16[16,32,128]{2,1,0:T(8,128)(2,1)S(1)} %get-tuple-element.96.m0, bf16[16,32,128]{2,1,0:T(8,128)(2,1)S(1)} %collective-permute-done.17.m0c, bf16[16,32,128]{2,1,0:T(8,128)(2,1)S(1)} %get-tuple-element.98.m1, ...), custom_call_target="tpu_custom_call" | custom-call | flops 5000000000 | bytes 4000000 | tf_op jit(solution)/shard_map/pallas_call | solution.py:162
  80.8 6.7 %all-to-all-start = ((bf16[64,64,128]{2,1,0:T(8,128)(2,1)}), bf16[64,64,128]{2,1,0:T(8,128)(2,1)S(1)}, u32[]{:S(2)}, u32[]{:S(2)}) async-start(bf16[64,64,128]{2,1,0:T(8,128)(2,1)} %bitcast.4), calls=%async_computation | async-start | bytes 2097152 | tf_op jit(solution)/shard_map/all_to_all | solution.py:593
  87.6 3.1 %collective-permute-start.10 = (bf16[64,512]{1,0:T(8,128)(2,1)S(1)}, bf16[64,512]{1,0:T(8,128)(2,1)S(1)}, u32[]{:S(2)}, u32[]{:S(2)}) collective-permute-start(bf16[64,512]{1,0:T(8,128)(2,1)S(1)} %get-tuple-element.83), channel_id=1, source_target_pairs={{0,16},{1,17},{2,18},{3,19},{4,20},{5,21},{6,22},{7,23},{8,24},{9,... | collective-permute-start | bytes 196616 | tf_op jit(solution)/shard_map/ppermute | solution.py:571
  90.7 3.3 %collective-permute-start.11 = (bf16[32,512]{1,0:T(8,128)(2,1)S(1)}, bf16[32,512]{1,0:T(8,128)(2,1)S(1)}, u32[]{:S(2)}, u32[]{:S(2)}) collective-permute-start(bf16[32,512]{1,0:T(8,128)(2,1)S(1)} %get-tuple-element.84), channel_id=1, source_target_pairs={{0,17},{1,18},{2,19},{3,20},{4,21},{5,22},{6,23},{7,24},{8,25},{9,... | collective-permute-start | bytes 98312 | tf_op jit(solution)/shard_map/ppermute | solution.py:571
  94.0 6.6 %collective-permute-done.11.dcorner = bf16[32,512]{1,0:T(8,128)(2,1)S(1)} collective-permute-done((bf16[32,512]{1,0:T(8,128)(2,1)S(1)}, bf16[32,512]{1,0:T(8,128)(2,1)S(1)}, u32[]{:S(2)}, u32[]{:S(2)}) %collective-permute-start.11) | collective-permute-done | bytes 32800 | tf_op jit(solution)/shard_map/ppermute | solution.py:571
  100.5 3.1 %collective-permute-done.10.dedge = bf16[64,512]{1,0:T(8,128)(2,1)S(1)} collective-permute-done((bf16[64,512]{1,0:T(8,128)(2,1)S(1)}, bf16[64,512]{1,0:T(8,128)(2,1)S(1)}, u32[]{:S(2)}, u32[]{:S(2)}) %collective-permute-start.10) | collective-permute-done | bytes 65568 | tf_op jit(solution)/shard_map/ppermute | solution.py:571
  103.7 1.4 %copy-done.2 = bf16[512,1536]{1,0:T(8,128)(2,1)S(1)} copy-done((bf16[512,1536]{1,0:T(8,128)(2,1)S(1)}, bf16[512,1536]{1,0:T(8,128)(2,1)}, u32[]{:S(2)}) %copy-start.2) | copy-done | bytes 1572888
  105.1 1.1 copy-done.4
  106.2 0.9 copy-done.10
  107.1 0.9 copy-done.15
  108.0 0.8 copy-done.22
  108.8 0.7 copy-done.24
  109.6 1.0 copy-done.27
  110.5 0.9 copy-done.33
  111.4 1.7 %shard_map.343 = (bf16[6,12,512]{2,1,0:T(8,128)(2,1)}, bf16[12,24,512]{2,1,0:T(8,128)(2,1)}, f32[4,768]{1,0:T(4,128)S(1)}, f32[16,512]{1,0:T(8,128)S(1)}, f32[4,1536]{1,0:T(4,128)S(1)}) custom-call(s32[1]{0:T(128)} %bitcast.place, bf16[72,512]{1,0:T(8,128)(2,1)S(1)} %copy-done.33, bf16[80,512]{1,0:T(8,128)(2,1)S(1)} %collective-permute-done.6.side, ...), custom_call_target="tpu_custom_call" | custom-call | flops 5000000000 | bytes 4000000 | tf_op jit(solution)/shard_map/pallas_call | solution.py:162
  113.2 0.8 shard_map.348
  (80 shorter events, 1.5 us)
Async XLA Ops:
  0.6 17.7 %copy-start.18 = (bf16[288,208]{1,0:T(8,128)(2,1)S(1)}, bf16[288,208]{1,0:T(8,128)(2,1)}, u32[]{:S(2)}) copy-start(bf16[288,208]{1,0:T(8,128)(2,1)} %constant.65.clone.t_halo) | copy-start | bytes 359428
  0.7 17.7 %copy-start.8 = (f32[512]{0:T(512)S(1)}, f32[512]{0:T(512)}, u32[]{:S(2)}) copy-start(f32[512]{0:T(512)} %param.29) | copy-start | bytes 6148
  0.7 17.7 %copy-start.3 = (bf16[512,768]{1,0:T(8,128)(2,1)S(1)}, bf16[512,768]{1,0:T(8,128)(2,1)}, u32[]{:S(2)}) copy-start(bf16[512,768]{1,0:T(8,128)(2,1)} %fqkv.1) | copy-start | bytes 2359300
  0.7 17.7 %copy-start.6 = (bf16[256,512]{1,0:T(8,128)(2,1)S(1)}, bf16[256,512]{1,0:T(8,128)(2,1)}, u32[]{:S(2)}) copy-start(bf16[256,512]{1,0:T(8,128)(2,1)} %wproj.5) | copy-start | bytes 786436
  3.6 14.7 %collective-permute-start = (bf16[80,512]{1,0:T(8,128)(2,1)S(1)}, bf16[80,512]{1,0:T(8,128)(2,1)S(1)}, u32[]{:S(2)}, u32[]{:S(2)}) collective-permute-start(bf16[80,512]{1,0:T(8,128)(2,1)S(1)} %get-tuple-element.65), channel_id=1, source_target_pairs={{0,15},{1,0},{2,1},{3,2},{4,3},{5,4},{6,5},{7,6},{8,7},{9,8},{10,9... | collective-permute-start | bytes 245768 | tf_op jit(solution)/shard_map/ppermute | solution.py:571
  6.9 11.4 %collective-permute-start.1 = (bf16[80,512]{1,0:T(8,128)(2,1)S(1)}, bf16[80,512]{1,0:T(8,128)(2,1)S(1)}, u32[]{:S(2)}, u32[]{:S(2)}) collective-permute-start(bf16[80,512]{1,0:T(8,128)(2,1)S(1)} %get-tuple-element.66), channel_id=1, source_target_pairs={{0,112},{1,113},{2,114},{3,115},{4,116},{5,117},{6,118},{7,119},{8... | collective-permute-start | bytes 245768 | tf_op jit(solution)/shard_map/ppermute | solution.py:571
  13.3 5.0 %collective-permute-start.2 = (bf16[48,512]{1,0:T(8,128)(2,1)S(1)}, bf16[48,512]{1,0:T(8,128)(2,1)S(1)}, u32[]{:S(2)}, u32[]{:S(2)}) collective-permute-start(bf16[48,512]{1,0:T(8,128)(2,1)S(1)} %get-tuple-element.67), channel_id=1, source_target_pairs={{0,127},{1,112},{2,113},{3,114},{4,115},{5,116},{6,117},{7,118},{8... | collective-permute-start | bytes 147464 | tf_op jit(solution)/shard_map/ppermute | solution.py:571
  20.2 1.0 copy-start.29
  21.2 14.5 %copy-start = (bf16[2048,512]{1,0:T(8,128)(2,1)S(1)}, bf16[2048,512]{1,0:T(8,128)(2,1)}, u32[]{:S(2)}) copy-start(bf16[2048,512]{1,0:T(8,128)(2,1)} %mweight.3) | copy-start | bytes 6291460
  21.2 14.5 %copy-start.1 = (bf16[512,1536]{1,0:T(8,128)(2,1)S(1)}, bf16[512,1536]{1,0:T(8,128)(2,1)}, u32[]{:S(2)}) copy-start(bf16[512,1536]{1,0:T(8,128)(2,1)} %cqkv.1) | copy-start | bytes 4718596
  21.2 14.5 %copy-start.5 = (bf16[512,512]{1,0:T(8,128)(2,1)S(1)}, bf16[512,512]{1,0:T(8,128)(2,1)}, u32[]{:S(2)}) copy-start(bf16[512,512]{1,0:T(8,128)(2,1)} %wproj.4) | copy-start | bytes 1572868
  21.2 14.5 %copy-start.7 = (f32[2048]{0:T(1024)S(1)}, f32[2048]{0:T(1024)}, u32[]{:S(2)}) copy-start(f32[2048]{0:T(1024)} %param.32) | copy-start | bytes 24580
  21.2 14.5 %copy-start.9 = (f32[512]{0:T(512)S(1)}, f32[512]{0:T(512)}, u32[]{:S(2)}) copy-start(f32[512]{0:T(512)} %param.34) | copy-start | bytes 6148
  21.2 14.5 %copy-start.12 = (bf16[288,288]{1,0:T(8,128)(2,1)S(1)}, bf16[288,288]{1,0:T(8,128)(2,1)}, u32[]{:S(2)}) copy-start(bf16[288,288]{1,0:T(8,128)(2,1)} %constant.67.clone.y_main) | copy-start | bytes 497668
  21.2 14.5 %copy-start.14 = (bf16[208,288]{1,0:T(8,128)(2,1)S(1)}, bf16[208,288]{1,0:T(8,128)(2,1)}, u32[]{:S(2)}) copy-start(bf16[208,288]{1,0:T(8,128)(2,1)} %constant.71.clone.df_send) | copy-start | bytes 359428
  21.2 14.5 %copy-start.17 = (bf16[288,160]{1,0:T(8,128)(2,1)S(1)}, bf16[288,160]{1,0:T(8,128)(2,1)}, u32[]{:S(2)}) copy-start(bf16[288,160]{1,0:T(8,128)(2,1)} %constant.68.clone.y_halo) | copy-start | bytes 276484
  21.2 14.5 %copy-start.21 = (bf16[208,72]{1,0:T(8,128)(2,1)S(1)}, bf16[208,72]{1,0:T(8,128)(2,1)}, u32[]{:S(2)}) copy-start(bf16[208,72]{1,0:T(8,128)(2,1)} %constant.72.clone.out_send) | copy-start | bytes 89860
  21.2 14.5 %copy-start.23 = (bf16[72,208]{1,0:T(8,128)(2,1)S(1)}, bf16[72,208]{1,0:T(8,128)(2,1)}, u32[]{:S(2)}) copy-start(bf16[72,208]{1,0:T(8,128)(2,1)} %constant.70.clone.c_halo) | copy-start | bytes 89860
  21.2 14.5 %copy-start.25 = (bf16[72,72]{1,0:T(8,128)(2,1)S(1)}, bf16[72,72]{1,0:T(8,128)(2,1)}, u32[]{:S(2)}) copy-start(bf16[72,72]{1,0:T(8,128)(2,1)} %constant.69.clone.c_main) | copy-start | bytes 31108
  21.3 14.5 %copy-start.31 = (f32[72,512]{1,0:T(8,128)S(1)}, f32[72,512]{1,0:T(8,128)}, u32[]{:S(2)}) copy-start(f32[72,512]{1,0:T(8,128)} %copy-done.30) | copy-start | bytes 442372
  25.2 10.5 %collective-permute-start.3 = (bf16[64,512]{1,0:T(8,128)(2,1)S(1)}, bf16[64,512]{1,0:T(8,128)(2,1)S(1)}, u32[]{:S(2)}, u32[]{:S(2)}) collective-permute-start(bf16[64,512]{1,0:T(8,128)(2,1)S(1)} %get-tuple-element.69), channel_id=1, source_target_pairs={{0,15},{1,0},{2,1},{3,2},{4,3},{5,4},{6,5},{7,6},{8,7},{9,8},{10,9... | collective-permute-start | bytes 196616 | tf_op jit(solution)/shard_map/ppermute | solution.py:571
  25.7 10.0 %collective-permute-start.4 = (bf16[64,512]{1,0:T(8,128)(2,1)S(1)}, bf16[64,512]{1,0:T(8,128)(2,1)S(1)}, u32[]{:S(2)}, u32[]{:S(2)}) collective-permute-start(bf16[64,512]{1,0:T(8,128)(2,1)S(1)} %get-tuple-element.70), channel_id=1, source_target_pairs={{0,112},{1,113},{2,114},{3,115},{4,116},{5,117},{6,118},{7,119},{8... | collective-permute-start | bytes 196616 | tf_op jit(solution)/shard_map/ppermute | solution.py:571
  30.8 4.8 %collective-permute-start.5 = (bf16[32,512]{1,0:T(8,128)(2,1)S(1)}, bf16[32,512]{1,0:T(8,128)(2,1)S(1)}, u32[]{:S(2)}, u32[]{:S(2)}) collective-permute-start(bf16[32,512]{1,0:T(8,128)(2,1)S(1)} %get-tuple-element.71), channel_id=1, source_target_pairs={{0,127},{1,112},{2,113},{3,114},{4,115},{5,116},{6,117},{7,118},{8... | collective-permute-start | bytes 98312 | tf_op jit(solution)/shard_map/ppermute | solution.py:571
  35.8 17.3 %copy-start.11 = (bf16[288,288]{1,0:T(8,128)(2,1)S(1)}, bf16[288,288]{1,0:T(8,128)(2,1)}, u32[]{:S(2)}) copy-start(bf16[288,288]{1,0:T(8,128)(2,1)} %constant.73.clone.d_main) | copy-start | bytes 497668
  35.8 17.3 %copy-start.16 = (bf16[288,208]{1,0:T(8,128)(2,1)S(1)}, bf16[288,208]{1,0:T(8,128)(2,1)}, u32[]{:S(2)}) copy-start(bf16[288,208]{1,0:T(8,128)(2,1)} %constant.74.clone.d_halo) | copy-start | bytes 359428
  35.8 17.3 %copy-start.19 = (bf16[160,288]{1,0:T(8,128)(2,1)S(1)}, bf16[160,288]{1,0:T(8,128)(2,1)}, u32[]{:S(2)}) copy-start(bf16[160,288]{1,0:T(8,128)(2,1)} %constant.75.clone.dx_send) | copy-start | bytes 276484
  42.9 14.4 %collective-permute-start.12 = (bf16[80,5632]{1,0:T(8,128)(2,1)S(1)}, bf16[80,5632]{1,0:T(8,128)(2,1)S(1)}, u32[]{:S(2)}, u32[]{:S(2)}) collective-permute-start(bf16[80,5632]{1,0:T(8,128)(2,1)S(1)} %get-tuple-element.87.own), channel_id=1, source_target_pairs={{0,1},{1,0},{2,3},{3,2},{4,5},{5,4},{6,7},{7,6},{8,9},{9,8},{10,11... | collective-permute-start | bytes 2703368 | tf_op jit(solution)/shard_map/ppermute | solution.py:576
  42.9 10.1 %collective-permute-start.6 = (bf16[80,512]{1,0:T(8,128)(2,1)S(1)}, bf16[80,512]{1,0:T(8,128)(2,1)S(1)}, u32[]{:S(2)}, u32[]{:S(2)}) collective-permute-start(bf16[80,512]{1,0:T(8,128)(2,1)S(1)} %get-tuple-element.74), channel_id=1, source_target_pairs={{0,1},{1,2},{2,3},{3,4},{4,5},{5,6},{6,7},{7,8},{8,9},{9,10},{10,1... | collective-permute-start | bytes 245768 | tf_op jit(solution)/shard_map/ppermute | solution.py:571
  43.4 9.6 %collective-permute-start.7 = (bf16[80,512]{1,0:T(8,128)(2,1)S(1)}, bf16[80,512]{1,0:T(8,128)(2,1)S(1)}, u32[]{:S(2)}, u32[]{:S(2)}) collective-permute-start(bf16[80,512]{1,0:T(8,128)(2,1)S(1)} %get-tuple-element.75), channel_id=1, source_target_pairs={{0,16},{1,17},{2,18},{3,19},{4,20},{5,21},{6,22},{7,23},{8,24},{9,... | collective-permute-start | bytes 245768 | tf_op jit(solution)/shard_map/ppermute | solution.py:571
  43.4 9.6 %collective-permute-start.8 = (bf16[48,512]{1,0:T(8,128)(2,1)S(1)}, bf16[48,512]{1,0:T(8,128)(2,1)S(1)}, u32[]{:S(2)}, u32[]{:S(2)}) collective-permute-start(bf16[48,512]{1,0:T(8,128)(2,1)S(1)} %get-tuple-element.76), channel_id=1, source_target_pairs={{0,17},{1,18},{2,19},{3,20},{4,21},{5,22},{6,23},{7,24},{8,25},{9,... | collective-permute-start | bytes 147464 | tf_op jit(solution)/shard_map/ppermute | solution.py:571
  57.3 17.7 %collective-permute-start.23 = (bf16[288,1280]{1,0:T(8,128)(2,1)S(1)}, bf16[288,1280]{1,0:T(8,128)(2,1)S(1)}, u32[]{:S(2)}, u32[]{:S(2)}) collective-permute-start(bf16[288,1280]{1,0:T(8,128)(2,1)S(1)} %get-tuple-element.106.own), channel_id=1, source_target_pairs={{0,1},{1,0},{2,3},{3,2},{4,5},{5,4},{6,7},{7,6},{8,9},{9,8},{10,11... | collective-permute-start | bytes 2211848 | tf_op jit(solution)/shard_map/ppermute | solution.py:576
  59.2 8.8 %collective-permute-start.13 = (bf16[32,32,128]{2,1,0:T(8,128)(2,1)S(1)}, bf16[32,32,128]{2,1,0:T(8,128)(2,1)S(1)}, u32[]{:S(2)}, u32[]{:S(2)}) collective-permute-start(bf16[32,32,128]{2,1,0:T(8,128)(2,1)S(1)} %get-tuple-element.89), channel_id=1, source_target_pairs={{0,32},{2,34},{4,36},{6,38},{8,40},{10,42},{12,44},{14,46},{16,48}... | collective-permute-start | bytes 786440 | tf_op jit(solution)/shard_map/ppermute | solution.py:589
  59.2 8.8 %collective-permute-start.14 = (bf16[32,32,128]{2,1,0:T(8,128)(2,1)S(1)}, bf16[32,32,128]{2,1,0:T(8,128)(2,1)S(1)}, u32[]{:S(2)}, u32[]{:S(2)}) collective-permute-start(bf16[32,32,128]{2,1,0:T(8,128)(2,1)S(1)} %get-tuple-element.91), channel_id=1, source_target_pairs={{0,2},{2,0},{4,6},{6,4},{8,10},{10,8},{12,14},{14,12},{16,18},{18,... | collective-permute-start | bytes 786440 | tf_op jit(solution)/shard_map/ppermute | solution.py:589
  59.3 10.0 %collective-permute-start.15 = (bf16[32,32,128]{2,1,0:T(8,128)(2,1)S(1)}, bf16[32,32,128]{2,1,0:T(8,128)(2,1)S(1)}, u32[]{:S(2)}, u32[]{:S(2)}) collective-permute-start(bf16[32,32,128]{2,1,0:T(8,128)(2,1)S(1)} %get-tuple-element.93), channel_id=1, source_target_pairs={{0,96},{2,98},{4,100},{6,102},{8,104},{10,106},{12,108},{14,110},{... | collective-permute-start | bytes 786440 | tf_op jit(solution)/shard_map/ppermute | solution.py:589
  61.1 9.6 %collective-permute-start.16 = (bf16[32,32,128]{2,1,0:T(8,128)(2,1)S(1)}, bf16[32,32,128]{2,1,0:T(8,128)(2,1)S(1)}, u32[]{:S(2)}, u32[]{:S(2)}) collective-permute-start(bf16[32,32,128]{2,1,0:T(8,128)(2,1)S(1)} %get-tuple-element.95), channel_id=1, source_target_pairs={{0,18},{2,16},{4,22},{6,20},{8,26},{10,24},{12,30},{14,28},{16,2},... | collective-permute-start | bytes 786440 | tf_op jit(solution)/shard_map/ppermute | solution.py:589
  68.0 5.5 %collective-permute-start.21 = (bf16[288,512]{1,0:T(8,128)(2,1)S(1)}, bf16[288,512]{1,0:T(8,128)(2,1)S(1)}, u32[]{:S(2)}, u32[]{:S(2)}) collective-permute-start(bf16[288,512]{1,0:T(8,128)(2,1)S(1)} %get-tuple-element.104.n_own), channel_id=1, source_target_pairs={{0,1},{1,0},{2,3},{3,2},{4,5},{5,4},{6,7},{7,6},{8,9},{9,8},{10,11... | collective-permute-start | bytes 884744 | tf_op jit(solution)/shard_map/ppermute | solution.py:576
  68.0 4.5 %collective-permute-start.22 = (bf16[288,256]{1,0:T(8,128)(2,1)S(1)}, bf16[288,256]{1,0:T(8,128)(2,1)S(1)}, u32[]{:S(2)}, u32[]{:S(2)}) collective-permute-start(bf16[288,256]{1,0:T(8,128)(2,1)S(1)} %get-tuple-element.105.m_own), channel_id=1, source_target_pairs={{0,1},{1,0},{2,3},{3,2},{4,5},{5,4},{6,7},{7,6},{8,9},{9,8},{10,11... | collective-permute-start | bytes 442376 | tf_op jit(solution)/shard_map/ppermute | solution.py:576
  71.0 5.3 %collective-permute-start.17 = (bf16[16,32,128]{2,1,0:T(8,128)(2,1)S(1)}, bf16[16,32,128]{2,1,0:T(8,128)(2,1)S(1)}, u32[]{:S(2)}, u32[]{:S(2)}) collective-permute-start(bf16[16,32,128]{2,1,0:T(8,128)(2,1)S(1)} %get-tuple-element.97), channel_id=1, source_target_pairs={{0,2},{2,0},{4,6},{6,4},{8,10},{10,8},{12,14},{14,12},{16,18},{18,... | collective-permute-start | bytes 393224 | tf_op jit(solution)/shard_map/ppermute | solution.py:589
  71.5 5.0 %collective-permute-start.18 = (bf16[16,32,128]{2,1,0:T(8,128)(2,1)S(1)}, bf16[16,32,128]{2,1,0:T(8,128)(2,1)S(1)}, u32[]{:S(2)}, u32[]{:S(2)}) collective-permute-start(bf16[16,32,128]{2,1,0:T(8,128)(2,1)S(1)} %get-tuple-element.99), channel_id=1, source_target_pairs={{0,32},{2,34},{4,36},{6,38},{8,40},{10,42},{12,44},{14,46},{16,48}... | collective-permute-start | bytes 393224 | tf_op jit(solution)/shard_map/ppermute | solution.py:589
  72.6 6.2 %collective-permute-start.19 = (bf16[16,32,128]{2,1,0:T(8,128)(2,1)S(1)}, bf16[16,32,128]{2,1,0:T(8,128)(2,1)S(1)}, u32[]{:S(2)}, u32[]{:S(2)}) collective-permute-start(bf16[16,32,128]{2,1,0:T(8,128)(2,1)S(1)} %get-tuple-element.101), channel_id=1, source_target_pairs={{0,18},{2,16},{4,22},{6,20},{8,26},{10,24},{12,30},{14,28},{16,2},... | collective-permute-start | bytes 393224 | tf_op jit(solution)/shard_map/ppermute | solution.py:589
  73.5 6.2 %collective-permute-start.20 = (bf16[16,32,128]{2,1,0:T(8,128)(2,1)S(1)}, bf16[16,32,128]{2,1,0:T(8,128)(2,1)S(1)}, u32[]{:S(2)}, u32[]{:S(2)}) collective-permute-start(bf16[16,32,128]{2,1,0:T(8,128)(2,1)S(1)} %get-tuple-element.103), channel_id=1, source_target_pairs={{0,96},{2,98},{4,100},{6,102},{8,104},{10,106},{12,108},{14,110},{... | collective-permute-start | bytes 393224 | tf_op jit(solution)/shard_map/ppermute | solution.py:589
  80.8 32.3 %all-to-all-start = ((bf16[64,64,128]{2,1,0:T(8,128)(2,1)}), bf16[64,64,128]{2,1,0:T(8,128)(2,1)S(1)}, u32[]{:S(2)}, u32[]{:S(2)}) async-start(bf16[64,64,128]{2,1,0:T(8,128)(2,1)} %bitcast.4), calls=%async_computation | async-start | bytes 2097152 | tf_op jit(solution)/shard_map/all_to_all | solution.py:593
  87.6 16.1 %collective-permute-start.10 = (bf16[64,512]{1,0:T(8,128)(2,1)S(1)}, bf16[64,512]{1,0:T(8,128)(2,1)S(1)}, u32[]{:S(2)}, u32[]{:S(2)}) collective-permute-start(bf16[64,512]{1,0:T(8,128)(2,1)S(1)} %get-tuple-element.83), channel_id=1, source_target_pairs={{0,16},{1,17},{2,18},{3,19},{4,20},{5,21},{6,22},{7,23},{8,24},{9,... | collective-permute-start | bytes 196616 | tf_op jit(solution)/shard_map/ppermute | solution.py:571
  90.7 13.0 %collective-permute-start.9 = (bf16[64,512]{1,0:T(8,128)(2,1)S(1)}, bf16[64,512]{1,0:T(8,128)(2,1)S(1)}, u32[]{:S(2)}, u32[]{:S(2)}) collective-permute-start(bf16[64,512]{1,0:T(8,128)(2,1)S(1)} %get-tuple-element.82), channel_id=1, source_target_pairs={{0,1},{1,2},{2,3},{3,4},{4,5},{5,6},{6,7},{7,8},{8,9},{9,10},{10,1... | collective-permute-start | bytes 196616 | tf_op jit(solution)/shard_map/ppermute | solution.py:571
  90.7 9.8 %collective-permute-start.11 = (bf16[32,512]{1,0:T(8,128)(2,1)S(1)}, bf16[32,512]{1,0:T(8,128)(2,1)S(1)}, u32[]{:S(2)}, u32[]{:S(2)}) collective-permute-start(bf16[32,512]{1,0:T(8,128)(2,1)S(1)} %get-tuple-element.84), channel_id=1, source_target_pairs={{0,17},{1,18},{2,19},{3,20},{4,21},{5,22},{6,23},{7,24},{8,25},{9,... | collective-permute-start | bytes 98312 | tf_op jit(solution)/shard_map/ppermute | solution.py:571
  103.7 1.4 %copy-start.2 = (bf16[512,1536]{1,0:T(8,128)(2,1)S(1)}, bf16[512,1536]{1,0:T(8,128)(2,1)}, u32[]{:S(2)}) copy-start(bf16[512,1536]{1,0:T(8,128)(2,1)} %cqkv.1) | copy-start | bytes 4718596
  105.1 1.1 copy-start.4
  109.6 1.0 copy-start.27
  (11 other events, 8.8 us)

commit v6 on v5

--- a/solution.py
+++ b/solution.py
@@ -251,7 +251,7 @@
 
 
 def first_kernel(
-    tok_in, cot_in, tok_send_in, cot_send_in, tok2d, side, edge, corner, cot2d,
+    place, tok_in, cot_in, tok_send_in, cot_send_in, tok2d, side, edge, corner, cot2d,
     tok, cot, tok_send, cot_send, arrived,
 ):
     loads = [
@@ -275,14 +275,14 @@
 
 def fine_forward_kernel(
     place, x_in, side, edge, corner, gain, wqkv, wproj, t_main, t_halo, y_send,
-    x_out, n_out, p_out, w_out, m_out, y_out, side_out, edge_out, corner_out, mixed,
+    x_out, nm_out, p_out, w_out, y_out, side_out, edge_out, corner_out, mixed,
 ):
     halo = jnp.concatenate([side[...], edge[...], corner[...]], axis=0)
     x = mm(t_main[...], x_in[...]) + mm(t_halo[...], halo)
     x_out[...] = x.astype(BF16)
     xhat, _ = normalize(x)
     n = (xhat * gain[...]).astype(BF16)
-    n_out[...] = n
+    nm_out[:, pl.ds(0, D)] = n
     p_out[...] = rounded(mm(n, wqkv[...]))
     for w in range(WINDOWS):
         differ = apart(decode(place)[3] == 1 if w >= 2 else False)
@@ -293,7 +293,7 @@
             w_out[2 * w + p] = weights
             mixed[rows, pl.ds(128 * p, 128)] = out
     m = mixed[...].astype(BF16)
-    m_out[...] = m
+    nm_out[:, pl.ds(D, 256)] = m
     y = (x + mm(m, wproj[...])).astype(BF16)
     y_out[...] = y
     stack = mm(y_send[...], y).astype(BF16)
@@ -395,9 +395,7 @@
     return lax.bitwise_and(lax.shift_right_logical(x, low), (1 << bits) - 1)
 
 
-def coarse_weights_kernel(
-    place, own, other, m0k, m0s, m1k, m1s, c0k, c0s, c1k, c1s, lines
-):
+def coarse_weights_kernel(place, own, other, mk, ms, ck, cs, lines):
     core, zp, yp, _, _ = decode(place)
 
     def at(start, size):
@@ -416,12 +414,11 @@
         )
         for zd in range(2):
             left = mm_nt(select, ordered[zd]).astype(BF16)
-            part = mm(left, dz).reshape(16, 16, D)
+            part = mm(left, dz).reshape(16, 16, D).astype(BF16)
             for yd in range(2):
                 for h in range(4):
                     piece = part[8 * yd : 8 * yd + 8, :, 128 * h : 128 * h + 128]
-                    (m0s if zd else m0k)[pl.ds(16 * yd + 8 * zh, 8), pl.ds(8 * h, 8), :] = piece[:, :8].astype(BF16)
-                    (m1s if yd else m1k)[pl.ds(16 * zd + 8 * zh, 8), pl.ds(8 * h, 8), :] = piece[:, 8:].astype(BF16)
+                    (ms if zd else mk)[pl.ds(16 * yd + 8 * zh, 8), pl.ds(16 * h, 16), :] = piece
     row = row_index(256)
     z = field(row, 3, 1) * 2 + lax.bitwise_xor(field(row, 5, 1), zp)
     group = z * 16 + field(row, 0, 3) * 2 + lax.bitwise_xor(field(row, 4, 1), yp)
@@ -433,33 +430,32 @@
         for i in range(4):
             line = part[64 * i : 64 * (i + 1)]
             for h in range(4):
-                lines[pl.ds(512 * (4 * (j // 2) + h) + 4 * (j % 2) + i, 64, 8), :] = line[:, 128 * h : 128 * h + 128]
+                lines[pl.ds(1024 * h + 4 * j + i, 64, 16), :] = line[:, 128 * h : 128 * h + 128]
     for h in range(4):
-        first = lines[pl.ds(512 * h, 512), :].reshape(64, 8, 128).astype(BF16)
-        c0s[:, pl.ds(8 * h, 8), :] = first[:32]
-        c0k[:, pl.ds(8 * h, 8), :] = first[32:]
-        second = lines[pl.ds(512 * (4 + h), 512), :].reshape(64, 8, 128).astype(BF16)
-        for zd in range(2):
-            c1s[pl.ds(16 * zd, 16), pl.ds(8 * h, 8), :] = second[32 * zd : 32 * zd + 16]
-            c1k[pl.ds(16 * zd, 16), pl.ds(8 * h, 8), :] = second[32 * zd + 16 : 32 * zd + 32]
-
-
-def middle_kernel(m0k, m0c, m1k, m1c, c0k, c0c, c1k, c1c, m0, m0s, m1, m1s, c0, c0s, c1, c1s):
-    for keep, came, first, second in (
-        (m0k, m0c, m0, m0s), (m1k, m1c, m1s, m1), (c0k, c0c, c0s, c0), (c1k, c1c, c1, c1s)
-    ):
-        total = (keep[...].astype(F32) + came[...].astype(F32)).astype(BF16)
-        first[...] = total[:16]
-        second[...] = total[16:]
-
-
-def fine_weights_kernel(place, n_own, n_other, m_own, m_other, own, other, out, lines):
+        chunk = lines[pl.ds(1024 * h, 1024), :].reshape(64, 16, 128).astype(BF16)
+        cs[:, pl.ds(16 * h, 16), :] = chunk[:32]
+        ck[:, pl.ds(16 * h, 16), :] = chunk[32:]
+
+
+def middle_kernel(mk, mc, ck, cc, m_keep, m_send, c_keep, c_send):
+    for keep, came, stay, send, first in ((mk, mc, m_keep, m_send, 0), (ck, cc, c_keep, c_send, 1)):
+        total = keep[...].astype(F32) + came[...].astype(F32)
+        for part in range(2):
+            same = total[16 * (part ^ first) : 16 * (part ^ first) + 16]
+            other = total[16 * (1 - (part ^ first)) : 16 * (1 - (part ^ first)) + 16]
+            for h in range(4):
+                rows = slice(16 * h + 8 * part, 16 * h + 8 * part + 8)
+                stay[pl.ds(16 * part, 16), pl.ds(8 * h, 8), :] = same[:, rows].astype(BF16)
+                send[pl.ds(16 * part, 16), pl.ds(8 * h, 8), :] = other[:, rows].astype(BF16)
+
+
+def fine_weights_kernel(place, nm_own, nm_other, own, other, out, lines):
     core = decode(place)[0]
     row = row_index(256)
     select = one_hot((2 * field(row, 0, 6) + core) * 4 + field(row, 6, 2), D)
     dp = lambda ref: ref[:, pl.ds(0, 768)]
     dy = lambda ref: ref[:, pl.ds(768, D)]
-    n = [mm_nt(select, ref[...]).astype(BF16) for ref in (n_own, n_other)]
+    n = [mm_nt(select, ref[:, pl.ds(0, D)]).astype(BF16) for ref in (nm_own, nm_other)]
     part = mm(n[0], dp(own)) + mm(n[1], dp(other))
     for i in range(4):
         line = part[64 * i : 64 * (i + 1)]
@@ -469,7 +465,7 @@
             lines[pl.ds(512 * (2 * (i // 2) + h) + 4 + i % 2, 64, 8), :] = line[:, 512 + 128 * h : 640 + 128 * h]
     row = row_index(128)
     select = one_hot((2 * field(row, 0, 6) + core) * 2 + field(row, 6, 1), 256)
-    m = [mm_nt(select, ref[...]).astype(BF16) for ref in (m_own, m_other)]
+    m = [mm_nt(select, ref[:, pl.ds(D, 256)]).astype(BF16) for ref in (nm_own, nm_other)]
     part = mm(m[0], dy(own)) + mm(m[1], dy(other))
     for i in range(2):
         line = part[64 * i : 64 * (i + 1)]
@@ -479,12 +475,15 @@
         out[:, pl.ds(8 * h, 8), :] = lines[pl.ds(512 * h, 512), :].reshape(64, 8, 128).astype(BF16)
 
 
-def join_kernel(place, m0, m0c, m1, m1c, c0, c0c, c1, c1c, fine, out):
+def join_kernel(place, m, mc, c, cc, fine, out):
     _, zp, yp, _, _ = decode(place)
-    for keep, came, zd, yd in ((m0, m0c, 0, 0), (m1, m1c, 1, 0), (c0, c0c, 1, 1), (c1, c1c, 0, 1)):
+    for keep, came, zd in ((m, mc, 0), (c, cc, 1)):
         total = (keep[...].astype(F32) + came[...].astype(F32)).astype(BF16)
-        for zh in range(2):
-            out[zh, lax.bitwise_xor(zp, zd), :, lax.bitwise_xor(yp, yd), pl.ds(0, 32), :] = total[8 * zh : 8 * zh + 8]
+        for part in range(2):
+            yd = part ^ zd
+            for zh in range(2):
+                at = 16 * part + 8 * zh
+                out[zh, lax.bitwise_xor(zp, zd), :, lax.bitwise_xor(yp, yd), pl.ds(0, 32), :] = total[at : at + 8]
     out[:, :, :, :, pl.ds(32, 32), :] = fine[...].reshape(2, 2, 8, 2, 32, 128)
 
 
@@ -495,19 +494,22 @@
     return mm(pick_rows, weight)[:share] / over[:share]
 
 
-def assemble_kernel(
-    place, y2, side, edge, corner, dx, dside, dedge, dcorner, out_main, out_halo, dx_main, dx_halo,
-    fgain, fqkv, mgain, mweight, cgain, cqkv, out, grad, fcoef, mcoef, ccoef,
-):
+def coefficients_kernel(place, fgain, fqkv, mgain, mweight, cgain, cqkv, fcoef, mcoef, ccoef):
     device = decode(place)[4]
     fcoef[...] = gain_rows(fqkv[...], fgain[...], device, 4)
     mcoef[...] = gain_rows(mweight[...], mgain[...], device, 16)
     ccoef[...] = gain_rows(cqkv[...], cgain[...], device, 4)
+
+
+def output_kernel(y2, side, edge, corner, out_main, out_halo, out):
     halo = jnp.concatenate([side[...], edge[...], corner[...]], axis=0)
     y = mm(out_main[...], y2[...]) + mm(out_halo[...], halo)
     for r in range(6):
         out[r] = y[16 * r : 16 * r + 12].astype(BF16)
-    halo = jnp.concatenate([dside[...], dedge[...], dcorner[...]], axis=0)
+
+
+def tokens_kernel(dx, side, edge, corner, dx_main, dx_halo, grad):
+    halo = jnp.concatenate([side[...], edge[...], corner[...]], axis=0)
     d = mm(dx_main[...], dx[...]) + mm(dx_halo[...], halo)
     grad[...] = d.reshape(ROWS, COLS, D).astype(BF16)
 
@@ -540,7 +542,7 @@
         low = [jnp.where(z_same, tops[2 * zd + y], tops[2 * (1 - zd) + y]) for y in range(2)]
         return jnp.where(y_same, low[yd], low[1 - yd])
 
-    m0, m1, c0, c1 = (related(0, 0), related(1, 0), related(1, 1), related(0, 1))
+    m0, m1, c0, c1 = (related(0, 0), related(0, 1), related(1, 1), related(1, 0))
     for h in range(4):
         lanes = pl.ds(128 * h, 128)
         rows = slice(8 * h, 8 * h + 8)
@@ -611,29 +613,30 @@
     tok, *sent, cot = call(
         first_kernel,
         [((cells, D), BF16)] + pieces + [((CELLS, D), F32)],
+        place,
         *(
             pltpu.with_memory_space_constraint(v, pltpu.HBM)
             for v in (tokens, cotangent, table("tok_send"), table("cot_send"))
         ),
-        specs=[pl.BlockSpec(memory_space=pltpu.HBM)] * 4,
+        specs=[SMEM_SPEC] + [pl.BlockSpec(memory_space=pltpu.HBM)] * 4,
         scratch=[
             pltpu.VMEM((ROWS, COLS, D), BF16), pltpu.VMEM((6, 12, D), BF16), pltpu.VMEM((sum(SLOTS), cells), BF16),
             pltpu.VMEM((sum(SLOTS), CELLS), BF16), pltpu.SemaphoreType.DMA((4,)),
         ],
     )
     ahead = exchange(sent, -1)
-    x, n, p, w, m, y, *sent = scalar_call(
+    x, nm, p, w, y, *sent = scalar_call(
         fine_forward_kernel,
         [
-            ((cells, D), BF16), ((cells, D), BF16), ((cells, 768), F32), ((8, CELLS, 256), F32),
-            ((cells, 256), BF16), ((cells, D), BF16),
+            ((cells, D), BF16), ((cells, 768), BF16), ((cells, 768), F32), ((8, CELLS, 256), F32),
+            ((cells, D), BF16),
         ]
         + narrow,
         place, tok, *ahead, fgain, fine_qkv, fine_proj, table("tok_main"), table("tok_halo"), table("y_send"),
         scratch=[pltpu.VMEM((cells, 256), F32)],
     )
     merged = exchange(sent, -1)
-    n_other, m_other = (partner(n), partner(m))
+    nm_other = partner(nm)
     y2, df, *sent, fac = scalar_call(
         coarse_kernel,
         [((CELLS, D), BF16), ((cells, D), BF16)] + pieces + [((TALL, 5632), BF16)],
@@ -645,16 +648,13 @@
         ],
     )
     back = exchange(sent, 1)
-    m0k, m0s, m1k, m1s, c0k, c0s, c1k, c1s = scalar_call(
+    mk, ms, ck, cs = scalar_call(
         coarse_weights_kernel,
-        [((32, 32, 128), BF16)] * 8,
+        [((32, 64, 128), BF16)] * 4,
         place, fac, partner(fac),
         scratch=[pltpu.VMEM((4096, 128), F32)],
     )
-    first = [
-        fold(v, axis, second)
-        for v, axis, second in ((m0s, "z", False), (m1s, "y", False), (c0s, "z", True), (c1s, "y", True))
-    ]
+    mc, cc = (fold(ms, "z", False), fold(cs, "z", True))
     dx, *sent, fac = scalar_call(
         fine_backward_kernel,
         [((cells, D), BF16)] + narrow + [((cells, 1280), BF16)],
@@ -662,32 +662,26 @@
         scratch=[pltpu.VMEM((cells, 256), F32), pltpu.VMEM((cells, 768), F32)],
     )
     ended = exchange(sent, 1)
-    m0, m0s, m1, m1s, c0, c0s, c1, c1s = call(
-        middle_kernel,
-        [((16, 32, 128), BF16)] * 8,
-        m0k, first[0], m1k, first[1], c0k, first[2], c1k, first[3],
-    )
-    again = [
-        fold(v, axis, second)
-        for v, axis, second in ((m0s, "y", False), (m1s, "z", False), (c0s, "y", True), (c1s, "z", True))
-    ]
+    m, ms, c, cs = call(middle_kernel, [((32, 32, 128), BF16)] * 4, mk, mc, ck, cc)
+    mc, cc = (fold(ms, "y", False), fold(cs, "y", True))
     (fine_part,) = scalar_call(
         fine_weights_kernel,
         [((64, 32, 128), BF16)],
-        place, n, n_other, m, m_other, fac, partner(fac),
+        place, nm, nm_other, fac, partner(fac),
         scratch=[pltpu.VMEM((2048, 128), F32)],
     )
     (joined,) = scalar_call(
         join_kernel,
         [((2, 2, 8, 2, 64, 128), BF16)],
-        place, m0, again[0], m1, again[1], c0, again[2], c1, again[3], fine_part,
+        place, m, mc, c, cc, fine_part,
     )
     parts = deal(joined.reshape(64, 64, 128)).reshape(2, 2, 8, 2, 64, 128)
-    output, grad, fcoef, mcoef, ccoef = scalar_call(
-        assemble_kernel,
-        [((6, 12, D), BF16), ((ROWS, COLS, D), BF16), ((4, 768), F32), ((16, D), F32), ((4, 1536), F32)],
-        place, y2, *back, dx, *ended, table("out_main"), table("out_halo"), table("dx_main"), table("dx_halo"),
-        fgain, fine_qkv, mgain, merge_weight, cgain, coarse_qkv,
+    (output,) = call(output_kernel, [((6, 12, D), BF16)], y2, *back, table("out_main"), table("out_halo"))
+    (grad,) = call(tokens_kernel, [((ROWS, COLS, D), BF16)], dx, *ended, table("dx_main"), table("dx_halo"))
+    fcoef, mcoef, ccoef = scalar_call(
+        coefficients_kernel,
+        [((4, 768), F32), ((16, D), F32), ((4, 1536), F32)],
+        place, fgain, fine_qkv, mgain, merge_weight, cgain, coarse_qkv,
     )
     fg, fqkv, fproj, mg, merge, cg, cqkv, cproj = scalar_call(
         sum_kernel,

time: 116 us -> 100 us (0.86)
  local copies, waits for them, and re-layouts: 13.4 us -> 3.34 us
  waiting for transfers between devices: 40.6 us -> 34.2 us
  Pallas kernels: 22.4 us -> 23.8 us
    ppermute x12, waiting for transfers between devices: 29 us -> 18.7 us  [exchange(): arrived.append(lax.ppermute(piece, ('lat', 'pair', 'core'), pairs))]
    unnamed x68, local copies, waits for them, and re-layouts: 13.4 us -> 3.34 us
    ppermute x8 -> x4, starting transfers between devices: 6.94 us -> 4.77 us  [fold(): return lax.ppermute(value, ('lat', 'pair'), pairs)]
    ppermute x8 -> x4, waiting for transfers between devices: 11.6 us -> 13.7 us  [fold(): return lax.ppermute(value, ('lat', 'pair'), pairs)]
    ppermute x4 -> x3, waiting for transfers between devices: 0.01 us -> 1.85 us  [partner(): return lax.ppermute(value, 'core', [(0, 1), (1, 0)])]
    all_to_all x1, starting transfers between devices: 6.7 us -> 8.46 us  [deal(): return lax.all_to_all(value, ('lat', 'pair'), 0, 0)]
    pallas_call x10 -> x12, Pallas kernels: 22.4 us -> 23.8 us  [call(): pl.pallas_call(kernel, out_shape=[jax.ShapeDtypeStruct(s, d) for s, d in...]
  transfers between devices with their start and end apart: 25 -> 20, of which waited for: 12 -> 10; matrix products, arithmetic and copies ran while one was open for 0% -> 0% of each run, Pallas kernels for 7% -> 10%
where the time goes in v6:
time: 100 us; the launch traced here: 98.9 us
  starting transfers between devices  36.4 us (36%)
  waiting for transfers between devices  34.2 us (34%)
  Pallas kernels  23.8 us (24%)
  local copies, waits for them, and re-layouts  3.34 us (3%)
  between operations  1.15 us (1%)
    pallas_call x12, Pallas kernels, call(): pl.pallas_call(kernel, out_shape=[jax.ShapeDtypeStruct(s, d) for s, d in...  23.8 us
    ppermute x12, starting transfers between devices, exchange(): arrived.append(lax.ppermute(piece, ('lat', 'pair', 'core'), pairs))  22.5 us
    ppermute x12, waiting for transfers between devices, exchange(): arrived.append(lax.ppermute(piece, ('lat', 'pair', 'core'), pairs))  18.7 us
    ppermute x4, waiting for transfers between devices, fold(): return lax.ppermute(value, ('lat', 'pair'), pairs)  13.7 us
    all_to_all x1, starting transfers between devices, deal(): return lax.all_to_all(value, ('lat', 'pair'), 0, 0)  8.46 us
    ppermute x4, starting transfers between devices, fold(): return lax.ppermute(value, ('lat', 'pair'), pairs)  4.77 us
    unnamed x68, local copies, waits for them, and re-layouts  3.34 us
  transfers between devices with their start and end apart: 20, of which 10 were waited for; matrix products, arithmetic and copies ran while one was open for 0% of the time, Pallas kernels for 10%

profile of v6, /device:TPU:0, one launch (start us, length us, event | category | flops | bytes accessed | tf_op | source)
XLA Modules:
  0.0 98.9 jit_solution(2220322729621632669)
XLA Ops:
  0.7 0.0 copy-start.13
  0.7 0.0 copy-start.20
  0.7 1.5 %shard_map.339 = (bf16[288,512]{1,0:T(8,128)(2,1)S(1)}, bf16[80,512]{1,0:T(8,128)(2,1)S(1)}, bf16[80,512]{1,0:T(8,128)(2,1)S(1)}, bf16[48,512]{1,0:T(8,128)(2,1)S(1)}, f32[72,512]{1,0:T(8,128)S(1)}) custom-call(s32[1]{0:T(128)} %bitcast.place, bf16[12,24,512]{2,1,0:T(8,128)(2,1)} %tok_in.1, bf16[6,12,512]{2,1,0:T(8,128)(2,1)} %cot_in.1, ...), custom_call_target="tpu_custom_call" | custom-call | flops 5000000000 | bytes 4000000 | tf_op jit(solution)/shard_map/pallas_call | solution.py:162
  2.3 3.4 %collective-permute-start = (bf16[80,512]{1,0:T(8,128)(2,1)S(1)}, bf16[80,512]{1,0:T(8,128)(2,1)S(1)}, u32[]{:S(2)}, u32[]{:S(2)}) collective-permute-start(bf16[80,512]{1,0:T(8,128)(2,1)S(1)} %get-tuple-element.54), channel_id=1, source_target_pairs={{0,15},{1,0},{2,1},{3,2},{4,3},{5,4},{6,5},{7,6},{8,7},{9,8},{10,9... | collective-permute-start | bytes 245768 | tf_op jit(solution)/shard_map/ppermute | solution.py:573
  5.7 6.4 %collective-permute-start.1 = (bf16[80,512]{1,0:T(8,128)(2,1)S(1)}, bf16[80,512]{1,0:T(8,128)(2,1)S(1)}, u32[]{:S(2)}, u32[]{:S(2)}) collective-permute-start(bf16[80,512]{1,0:T(8,128)(2,1)S(1)} %get-tuple-element.55), channel_id=1, source_target_pairs={{0,112},{1,113},{2,114},{3,115},{4,116},{5,117},{6,118},{7,119},{8... | collective-permute-start | bytes 245768 | tf_op jit(solution)/shard_map/ppermute | solution.py:573
  12.0 0.2 collective-permute-start.2
  12.2 4.8 %collective-permute-done.2.corner.ccorner = bf16[48,512]{1,0:T(8,128)(2,1)S(1)} collective-permute-done((bf16[48,512]{1,0:T(8,128)(2,1)S(1)}, bf16[48,512]{1,0:T(8,128)(2,1)S(1)}, u32[]{:S(2)}, u32[]{:S(2)}) %collective-permute-start.2) | collective-permute-done | bytes 49184 | tf_op jit(solution)/shard_map/ppermute | solution.py:573
  17.2 0.0 copy-start.12
  17.2 0.0 copy-start.14
  17.2 0.0 copy-start.21
  17.2 0.0 copy-start.23
  17.2 0.0 copy-start.25
  17.2 3.9 %shard_map.340 = (bf16[288,512]{1,0:T(8,128)(2,1)S(1)}, bf16[288,768]{1,0:T(8,128)(2,1)S(1)}, f32[288,768]{1,0:T(8,128)S(1)}, f32[8,72,256]{2,1,0:T(8,128)S(1)},...) custom-call(s32[1]{0:T(128)} %bitcast.place, ...), custom_call_target="tpu_custom_call" | custom-call | flops 5000000000 | bytes 4000000 | tf_op jit(solution)/shard_map/pallas_call | solution.py:162
  21.2 0.5 collective-permute-start.3
  21.7 5.2 %collective-permute-start.4 = (bf16[64,512]{1,0:T(8,128)(2,1)S(1)}, bf16[64,512]{1,0:T(8,128)(2,1)S(1)}, u32[]{:S(2)}, u32[]{:S(2)}) collective-permute-start(bf16[64,512]{1,0:T(8,128)(2,1)S(1)} %get-tuple-element.59), channel_id=1, source_target_pairs={{0,112},{1,113},{2,114},{3,115},{4,116},{5,117},{6,118},{7,119},{8... | collective-permute-start | bytes 196616 | tf_op jit(solution)/shard_map/ppermute | solution.py:573
  26.8 4.8 %collective-permute-done.5.corner = bf16[32,512]{1,0:T(8,128)(2,1)S(1)} collective-permute-done((bf16[32,512]{1,0:T(8,128)(2,1)S(1)}, bf16[32,512]{1,0:T(8,128)(2,1)S(1)}, u32[]{:S(2)}, u32[]{:S(2)}) %collective-permute-start.5) | collective-permute-done | bytes 32800 | tf_op jit(solution)/shard_map/ppermute | solution.py:573
  31.8 6.5 %shard_map.341 = (bf16[72,512]{1,0:T(8,128)(2,1)S(1)}, bf16[288,512]{1,0:T(8,128)(2,1)S(1)}, bf16[80,512]{1,0:T(8,128)(2,1)S(1)}, bf16[80,512]{1,0:T(8,128)(2,1)...) custom-call(s32[1]{0:T(128)} %bitcast.place, bf16[288,512]{1,0:T(8,128)(2,1)S(1)} %get-tuple-element.57.y_in, ...), custom_call_target="tpu_custom_call" | custom-call | flops 5000000000 | bytes 4000000 | tf_op jit(solution)/shard_map/pallas_call | solution.py:162
  38.3 0.6 copy-done.28
  38.9 0.5 collective-permute-start.6
  39.4 0.1 collective-permute-start.8
  39.5 1.8 %collective-permute-done.12.other = bf16[80,5632]{1,0:T(8,128)(2,1)S(1)} collective-permute-done((bf16[80,5632]{1,0:T(8,128)(2,1)S(1)}, bf16[80,5632]{1,0:T(8,128)(2,1)S(1)}, u32[]{:S(2)}, u32[]{:S(2)}) %collective-permute-start.12) | collective-permute-done | bytes 901152 | tf_op jit(solution)/shard_map/ppermute | solution.py:578
  41.3 2.1 %shard_map.345 = (bf16[32,64,128]{2,1,0:T(8,128)(2,1)S(1)}, bf16[32,64,128]{2,1,0:T(8,128)(2,1)S(1)}, bf16[32,64,128]{2,1,0:T(8,128)(2,1)S(1)}, bf16[32,64,128]{2,1,0:T(8,128)(2,1)S(1)}) custom-call(s32[1]{0:T(128)} %bitcast.place, bf16[80,5632]{1,0:T(8,128)(2,1)S(1)} %get-tuple-element.74.own, bf16[80,5632]{1,0:T(8,128)(2,1)S(1)} %collective-permute-done.12.other), custom_call_target="tpu_custom_call" | custom-call | flops 5000000000 | bytes 4000000 | tf_op jit(solution)/shard_map/pallas_call | solution.py:162
  43.5 0.1 collective-permute-start.13
  43.6 3.9 %collective-permute-start.14 = (bf16[32,64,128]{2,1,0:T(8,128)(2,1)S(1)}, bf16[32,64,128]{2,1,0:T(8,128)(2,1)S(1)}, u32[]{:S(2)}, u32[]{:S(2)}) collective-permute-start(bf16[32,64,128]{2,1,0:T(8,128)(2,1)S(1)} %get-tuple-element.78), channel_id=1, source_target_pairs={{0,96},{2,98},{4,100},{6,102},{8,104},{10,106},{12,108},{14,110},{... | collective-permute-start | bytes 1572872 | tf_op jit(solution)/shard_map/ppermute | solution.py:591
  47.4 1.6 %collective-permute-done.8.corner = bf16[48,512]{1,0:T(8,128)(2,1)S(1)} collective-permute-done((bf16[48,512]{1,0:T(8,128)(2,1)S(1)}, bf16[48,512]{1,0:T(8,128)(2,1)S(1)}, u32[]{:S(2)}, u32[]{:S(2)}) %collective-permute-start.8) | collective-permute-done | bytes 49184 | tf_op jit(solution)/shard_map/ppermute | solution.py:573
  49.1 3.5 %shard_map.343 = (bf16[288,512]{1,0:T(8,128)(2,1)S(1)}, bf16[64,512]{1,0:T(8,128)(2,1)S(1)}, bf16[64,512]{1,0:T(8,128)(2,1)S(1)}, bf16[32,512]{1,0:T(8,128)(2,1)S(1)}, bf16[288,1280]{1,0:T(8,128)(2,1)S(1)}) custom-call(s32[1]{0:T(128)} %bitcast.place, bf16[288,512]{1,0:T(8,128)(2,1)S(1)} %get-tuple-element.66.df_in, ...), custom_call_target="tpu_custom_call" | custom-call | flops 5000000000 | bytes 4000000 | tf_op jit(solution)/shard_map/pallas_call | solution.py:162
  52.6 0.1 collective-permute-start.18
  52.7 0.5 collective-permute-start.17
  53.2 4.3 %collective-permute-done.13.mc = bf16[32,64,128]{2,1,0:T(8,128)(2,1)S(1)} collective-permute-done((bf16[32,64,128]{2,1,0:T(8,128)(2,1)S(1)}, bf16[32,64,128]{2,1,0:T(8,128)(2,1)S(1)}, u32[]{:S(2)}, u32[]{:S(2)}) %collective-permute-start.13) | collective-permute-done | bytes 524320 | tf_op jit(solution)/shard_map/ppermute | solution.py:591
  57.5 2.2 %collective-permute-done.14.cc = bf16[32,64,128]{2,1,0:T(8,128)(2,1)S(1)} collective-permute-done((bf16[32,64,128]{2,1,0:T(8,128)(2,1)S(1)}, bf16[32,64,128]{2,1,0:T(8,128)(2,1)S(1)}, u32[]{:S(2)}, u32[]{:S(2)}) %collective-permute-start.14) | collective-permute-done | bytes 524320 | tf_op jit(solution)/shard_map/ppermute | solution.py:591
  59.7 0.4 shard_map.346
  60.1 0.1 collective-permute-start.15
  60.2 0.7 collective-permute-start.16
  61.0 1.2 %shard_map.347.fine = bf16[64,32,128]{2,1,0:T(8,128)(2,1)S(1)} custom-call(s32[1]{0:T(128)} %bitcast.place, bf16[288,768]{1,0:T(8,128)(2,1)S(1)} %get-tuple-element.83.nm_own, bf16[288,768]{1,0:T(8,128)(2,1)S(1)} %collective-permute-done.17.nm_other, bf16[288,1280]{1,0:T(8,128)(2,1)S(1)} %get-tuple-element.84.own, ...), custom_call_target="tpu_custom_call" | custom-call | flops 5000000000 | bytes 4000000 | tf_op jit(solution)/shard_map/pallas_call | solution.py:162
  62.2 5.8 %collective-permute-done.15.mc = bf16[32,32,128]{2,1,0:T(8,128)(2,1)S(1)} collective-permute-done((bf16[32,32,128]{2,1,0:T(8,128)(2,1)S(1)}, bf16[32,32,128]{2,1,0:T(8,128)(2,1)S(1)}, u32[]{:S(2)}, u32[]{:S(2)}) %collective-permute-start.15) | collective-permute-done | bytes 262176 | tf_op jit(solution)/shard_map/ppermute | solution.py:591
  68.0 1.3 %collective-permute-done.16.cc = bf16[32,32,128]{2,1,0:T(8,128)(2,1)S(1)} collective-permute-done((bf16[32,32,128]{2,1,0:T(8,128)(2,1)S(1)}, bf16[32,32,128]{2,1,0:T(8,128)(2,1)S(1)}, u32[]{:S(2)}, u32[]{:S(2)}) %collective-permute-start.16) | collective-permute-done | bytes 262176 | tf_op jit(solution)/shard_map/ppermute | solution.py:591
  69.3 1.2 %shard_map.348 = bf16[2,2,8,2,64,128]{5,4,3,2,1,0:T(8,128)(2,1)} custom-call(s32[1]{0:T(128)} %bitcast.place, bf16[32,32,128]{2,1,0:T(8,128)(2,1)S(1)} %get-tuple-element.79.m, bf16[32,32,128]{2,1,0:T(8,128)(2,1)S(1)} %collective-permute-done.15.mc, bf16[32,32,128]{2,1,0:T(8,128)(2,1)S(1)} %get-tuple-element.81.c, ...), custom_call_target="tpu_custom_call" | custom-call | flops 5000000000 | bytes 4000000 | tf_op jit(solution)/shard_map/pallas_call | solution.py:162
  70.5 8.5 %all-to-all-start = ((bf16[64,64,128]{2,1,0:T(8,128)(2,1)}), bf16[64,64,128]{2,1,0:T(8,128)(2,1)S(1)}, u32[]{:S(2)}, u32[]{:S(2)}) async-start(bf16[64,64,128]{2,1,0:T(8,128)(2,1)} %bitcast.4), calls=%async_computation | async-start | bytes 2097152 | tf_op jit(solution)/shard_map/all_to_all | solution.py:595
  79.0 1.4 %copy-done.2 = bf16[512,1536]{1,0:T(8,128)(2,1)S(1)} copy-done((bf16[512,1536]{1,0:T(8,128)(2,1)S(1)}, bf16[512,1536]{1,0:T(8,128)(2,1)}, u32[]{:S(2)}) %copy-start.2) | copy-done | bytes 1572888
  80.4 1.1 %copy-done.4 = bf16[512,768]{1,0:T(8,128)(2,1)S(1)} copy-done((bf16[512,768]{1,0:T(8,128)(2,1)S(1)}, bf16[512,768]{1,0:T(8,128)(2,1)}, u32[]{:S(2)}) %copy-start.4) | copy-done | bytes 786456
  81.6 0.7 shard_map.349
  82.2 3.1 %collective-permute-start.10 = (bf16[64,512]{1,0:T(8,128)(2,1)S(1)}, bf16[64,512]{1,0:T(8,128)(2,1)S(1)}, u32[]{:S(2)}, u32[]{:S(2)}) collective-permute-start(bf16[64,512]{1,0:T(8,128)(2,1)S(1)} %get-tuple-element.72), channel_id=1, source_target_pairs={{0,16},{1,17},{2,18},{3,19},{4,20},{5,21},{6,22},{7,23},{8,24},{9,... | collective-permute-start | bytes 196616 | tf_op jit(solution)/shard_map/ppermute | solution.py:573
  85.4 3.3 %collective-permute-start.11 = (bf16[32,512]{1,0:T(8,128)(2,1)S(1)}, bf16[32,512]{1,0:T(8,128)(2,1)S(1)}, u32[]{:S(2)}, u32[]{:S(2)}) collective-permute-start(bf16[32,512]{1,0:T(8,128)(2,1)S(1)} %get-tuple-element.73), channel_id=1, source_target_pairs={{0,17},{1,18},{2,19},{3,20},{4,21},{5,22},{6,23},{7,24},{8,25},{9,... | collective-permute-start | bytes 98312 | tf_op jit(solution)/shard_map/ppermute | solution.py:573
  88.7 0.8 shard_map.342
  89.5 5.9 %collective-permute-done.11.corner = bf16[32,512]{1,0:T(8,128)(2,1)S(1)} collective-permute-done((bf16[32,512]{1,0:T(8,128)(2,1)S(1)}, bf16[32,512]{1,0:T(8,128)(2,1)S(1)}, u32[]{:S(2)}, u32[]{:S(2)}) %collective-permute-start.11) | collective-permute-done | bytes 32800 | tf_op jit(solution)/shard_map/ppermute | solution.py:573
  95.4 1.5 %collective-permute-done.10.edge = bf16[64,512]{1,0:T(8,128)(2,1)S(1)} collective-permute-done((bf16[64,512]{1,0:T(8,128)(2,1)S(1)}, bf16[64,512]{1,0:T(8,128)(2,1)S(1)}, u32[]{:S(2)}, u32[]{:S(2)}) %collective-permute-start.10) | collective-permute-done | bytes 65568 | tf_op jit(solution)/shard_map/ppermute | solution.py:573
  97.0 1.1 %shard_map.344 = bf16[12,24,512]{2,1,0:T(8,128)(2,1)} custom-call(bf16[288,512]{1,0:T(8,128)(2,1)S(1)} %copy-done.27, bf16[64,512]{1,0:T(8,128)(2,1)S(1)} %collective-permute-done.9.side, bf16[64,512]{1,0:T(8,128)(2,1)S(1)} %collective-permute-done.10.edge, bf16[32,512]{1,0:T(8,128)(2,1)S(1)} %collective-permute-done.11.corner, ...), custom_call_target="tpu_custom_call" | custom-call | flops 5000000000 | bytes 4000000 | tf_op jit(solution)/shard_map/pallas_call | solution.py:162
  98.1 0.8 shard_map.350
  (72 shorter events, 0.2 us)
Async XLA Ops:
  0.7 16.4 %copy-start.3 = (bf16[512,768]{1,0:T(8,128)(2,1)S(1)}, bf16[512,768]{1,0:T(8,128)(2,1)}, u32[]{:S(2)}) copy-start(bf16[512,768]{1,0:T(8,128)(2,1)} %fqkv.1) | copy-start | bytes 2359300
  0.7 16.4 %copy-start.6 = (bf16[256,512]{1,0:T(8,128)(2,1)S(1)}, bf16[256,512]{1,0:T(8,128)(2,1)}, u32[]{:S(2)}) copy-start(bf16[256,512]{1,0:T(8,128)(2,1)} %wproj.5) | copy-start | bytes 786436
  0.7 16.4 %copy-start.8 = (f32[512]{0:T(512)S(1)}, f32[512]{0:T(512)}, u32[]{:S(2)}) copy-start(f32[512]{0:T(512)} %param.29) | copy-start | bytes 6148
  0.7 16.4 %copy-start.13 = (bf16[288,288]{1,0:T(8,128)(2,1)S(1)}, bf16[288,288]{1,0:T(8,128)(2,1)}, u32[]{:S(2)}) copy-start(bf16[288,288]{1,0:T(8,128)(2,1)} %constant.64.clone.t_main) | copy-start | bytes 497668
  0.7 16.4 %copy-start.18 = (bf16[288,208]{1,0:T(8,128)(2,1)S(1)}, bf16[288,208]{1,0:T(8,128)(2,1)}, u32[]{:S(2)}) copy-start(bf16[288,208]{1,0:T(8,128)(2,1)} %constant.65.clone.t_halo) | copy-start | bytes 359428
  0.7 16.4 %copy-start.20 = (bf16[160,288]{1,0:T(8,128)(2,1)S(1)}, bf16[160,288]{1,0:T(8,128)(2,1)}, u32[]{:S(2)}) copy-start(bf16[160,288]{1,0:T(8,128)(2,1)} %constant.66.clone.y_send) | copy-start | bytes 276484
  2.3 14.8 %collective-permute-start = (bf16[80,512]{1,0:T(8,128)(2,1)S(1)}, bf16[80,512]{1,0:T(8,128)(2,1)S(1)}, u32[]{:S(2)}, u32[]{:S(2)}) collective-permute-start(bf16[80,512]{1,0:T(8,128)(2,1)S(1)} %get-tuple-element.54), channel_id=1, source_target_pairs={{0,15},{1,0},{2,1},{3,2},{4,3},{5,4},{6,5},{7,6},{8,7},{9,8},{10,9... | collective-permute-start | bytes 245768 | tf_op jit(solution)/shard_map/ppermute | solution.py:573
  5.7 11.4 %collective-permute-start.1 = (bf16[80,512]{1,0:T(8,128)(2,1)S(1)}, bf16[80,512]{1,0:T(8,128)(2,1)S(1)}, u32[]{:S(2)}, u32[]{:S(2)}) collective-permute-start(bf16[80,512]{1,0:T(8,128)(2,1)S(1)} %get-tuple-element.55), channel_id=1, source_target_pairs={{0,112},{1,113},{2,114},{3,115},{4,116},{5,117},{6,118},{7,119},{8... | collective-permute-start | bytes 245768 | tf_op jit(solution)/shard_map/ppermute | solution.py:573
  12.0 5.0 %collective-permute-start.2 = (bf16[48,512]{1,0:T(8,128)(2,1)S(1)}, bf16[48,512]{1,0:T(8,128)(2,1)S(1)}, u32[]{:S(2)}, u32[]{:S(2)}) collective-permute-start(bf16[48,512]{1,0:T(8,128)(2,1)S(1)} %get-tuple-element.56), channel_id=1, source_target_pairs={{0,127},{1,112},{2,113},{3,114},{4,115},{5,116},{6,117},{7,118},{8... | collective-permute-start | bytes 147464 | tf_op jit(solution)/shard_map/ppermute | solution.py:573
  17.1 14.6 %copy-start = (bf16[2048,512]{1,0:T(8,128)(2,1)S(1)}, bf16[2048,512]{1,0:T(8,128)(2,1)}, u32[]{:S(2)}) copy-start(bf16[2048,512]{1,0:T(8,128)(2,1)} %mweight.3) | copy-start | bytes 6291460
  17.1 14.6 %copy-start.1 = (bf16[512,1536]{1,0:T(8,128)(2,1)S(1)}, bf16[512,1536]{1,0:T(8,128)(2,1)}, u32[]{:S(2)}) copy-start(bf16[512,1536]{1,0:T(8,128)(2,1)} %cqkv.1) | copy-start | bytes 4718596
  17.1 14.6 %copy-start.5 = (bf16[512,512]{1,0:T(8,128)(2,1)S(1)}, bf16[512,512]{1,0:T(8,128)(2,1)}, u32[]{:S(2)}) copy-start(bf16[512,512]{1,0:T(8,128)(2,1)} %wproj.4) | copy-start | bytes 1572868
  17.1 14.6 %copy-start.7 = (f32[2048]{0:T(1024)S(1)}, f32[2048]{0:T(1024)}, u32[]{:S(2)}) copy-start(f32[2048]{0:T(1024)} %param.32) | copy-start | bytes 24580
  17.2 14.6 %copy-start.9 = (f32[512]{0:T(512)S(1)}, f32[512]{0:T(512)}, u32[]{:S(2)}) copy-start(f32[512]{0:T(512)} %param.34) | copy-start | bytes 6148
  17.2 14.6 %copy-start.12 = (bf16[288,288]{1,0:T(8,128)(2,1)S(1)}, bf16[288,288]{1,0:T(8,128)(2,1)}, u32[]{:S(2)}) copy-start(bf16[288,288]{1,0:T(8,128)(2,1)} %constant.67.clone.y_main) | copy-start | bytes 497668
  17.2 14.5 %copy-start.14 = (bf16[208,288]{1,0:T(8,128)(2,1)S(1)}, bf16[208,288]{1,0:T(8,128)(2,1)}, u32[]{:S(2)}) copy-start(bf16[208,288]{1,0:T(8,128)(2,1)} %constant.71.clone.df_send) | copy-start | bytes 359428
  17.2 14.5 %copy-start.17 = (bf16[288,160]{1,0:T(8,128)(2,1)S(1)}, bf16[288,160]{1,0:T(8,128)(2,1)}, u32[]{:S(2)}) copy-start(bf16[288,160]{1,0:T(8,128)(2,1)} %constant.68.clone.y_halo) | copy-start | bytes 276484
  17.2 14.5 %copy-start.21 = (bf16[208,72]{1,0:T(8,128)(2,1)S(1)}, bf16[208,72]{1,0:T(8,128)(2,1)}, u32[]{:S(2)}) copy-start(bf16[208,72]{1,0:T(8,128)(2,1)} %constant.72.clone.out_send) | copy-start | bytes 89860
  17.2 14.5 %copy-start.23 = (bf16[72,208]{1,0:T(8,128)(2,1)S(1)}, bf16[72,208]{1,0:T(8,128)(2,1)}, u32[]{:S(2)}) copy-start(bf16[72,208]{1,0:T(8,128)(2,1)} %constant.70.clone.c_halo) | copy-start | bytes 89860
  17.2 14.5 %copy-start.25 = (bf16[72,72]{1,0:T(8,128)(2,1)S(1)}, bf16[72,72]{1,0:T(8,128)(2,1)}, u32[]{:S(2)}) copy-start(bf16[72,72]{1,0:T(8,128)(2,1)} %constant.69.clone.c_main) | copy-start | bytes 31108
  21.2 10.5 %collective-permute-start.3 = (bf16[64,512]{1,0:T(8,128)(2,1)S(1)}, bf16[64,512]{1,0:T(8,128)(2,1)S(1)}, u32[]{:S(2)}, u32[]{:S(2)}) collective-permute-start(bf16[64,512]{1,0:T(8,128)(2,1)S(1)} %get-tuple-element.58), channel_id=1, source_target_pairs={{0,15},{1,0},{2,1},{3,2},{4,3},{5,4},{6,5},{7,6},{8,7},{9,8},{10,9... | collective-permute-start | bytes 196616 | tf_op jit(solution)/shard_map/ppermute | solution.py:573
  21.7 10.0 %collective-permute-start.4 = (bf16[64,512]{1,0:T(8,128)(2,1)S(1)}, bf16[64,512]{1,0:T(8,128)(2,1)S(1)}, u32[]{:S(2)}, u32[]{:S(2)}) collective-permute-start(bf16[64,512]{1,0:T(8,128)(2,1)S(1)} %get-tuple-element.59), channel_id=1, source_target_pairs={{0,112},{1,113},{2,114},{3,115},{4,116},{5,117},{6,118},{7,119},{8... | collective-permute-start | bytes 196616 | tf_op jit(solution)/shard_map/ppermute | solution.py:573
  26.8 4.8 %collective-permute-start.5 = (bf16[32,512]{1,0:T(8,128)(2,1)S(1)}, bf16[32,512]{1,0:T(8,128)(2,1)S(1)}, u32[]{:S(2)}, u32[]{:S(2)}) collective-permute-start(bf16[32,512]{1,0:T(8,128)(2,1)S(1)} %get-tuple-element.60), channel_id=1, source_target_pairs={{0,127},{1,112},{2,113},{3,114},{4,115},{5,116},{6,117},{7,118},{8... | collective-permute-start | bytes 98312 | tf_op jit(solution)/shard_map/ppermute | solution.py:573
  38.9 2.4 %collective-permute-start.12 = (bf16[80,5632]{1,0:T(8,128)(2,1)S(1)}, bf16[80,5632]{1,0:T(8,128)(2,1)S(1)}, u32[]{:S(2)}, u32[]{:S(2)}) collective-permute-start(bf16[80,5632]{1,0:T(8,128)(2,1)S(1)} %get-tuple-element.74.own), channel_id=1, source_target_pairs={{0,1},{1,0},{2,3},{3,2},{4,5},{5,4},{6,7},{7,6},{8,9},{9,8},{10,11... | collective-permute-start | bytes 2703368 | tf_op jit(solution)/shard_map/ppermute | solution.py:578
  38.9 10.1 %collective-permute-start.6 = (bf16[80,512]{1,0:T(8,128)(2,1)S(1)}, bf16[80,512]{1,0:T(8,128)(2,1)S(1)}, u32[]{:S(2)}, u32[]{:S(2)}) collective-permute-start(bf16[80,512]{1,0:T(8,128)(2,1)S(1)} %get-tuple-element.63), channel_id=1, source_target_pairs={{0,1},{1,2},{2,3},{3,4},{4,5},{5,6},{6,7},{7,8},{8,9},{9,10},{10,1... | collective-permute-start | bytes 245768 | tf_op jit(solution)/shard_map/ppermute | solution.py:573
  39.4 9.6 %collective-permute-start.7 = (bf16[80,512]{1,0:T(8,128)(2,1)S(1)}, bf16[80,512]{1,0:T(8,128)(2,1)S(1)}, u32[]{:S(2)}, u32[]{:S(2)}) collective-permute-start(bf16[80,512]{1,0:T(8,128)(2,1)S(1)} %get-tuple-element.64), channel_id=1, source_target_pairs={{0,16},{1,17},{2,18},{3,19},{4,20},{5,21},{6,22},{7,23},{8,24},{9,... | collective-permute-start | bytes 245768 | tf_op jit(solution)/shard_map/ppermute | solution.py:573
  39.4 9.6 %copy-start.11 = (bf16[288,288]{1,0:T(8,128)(2,1)S(1)}, bf16[288,288]{1,0:T(8,128)(2,1)}, u32[]{:S(2)}) copy-start(bf16[288,288]{1,0:T(8,128)(2,1)} %constant.73.clone.d_main) | copy-start | bytes 497668
  39.4 9.6 %copy-start.16 = (bf16[288,208]{1,0:T(8,128)(2,1)S(1)}, bf16[288,208]{1,0:T(8,128)(2,1)}, u32[]{:S(2)}) copy-start(bf16[288,208]{1,0:T(8,128)(2,1)} %constant.74.clone.d_halo) | copy-start | bytes 359428
  39.4 9.6 %copy-start.19 = (bf16[160,288]{1,0:T(8,128)(2,1)S(1)}, bf16[160,288]{1,0:T(8,128)(2,1)}, u32[]{:S(2)}) copy-start(bf16[160,288]{1,0:T(8,128)(2,1)} %constant.75.clone.dx_send) | copy-start | bytes 276484
  39.4 9.6 %collective-permute-start.8 = (bf16[48,512]{1,0:T(8,128)(2,1)S(1)}, bf16[48,512]{1,0:T(8,128)(2,1)S(1)}, u32[]{:S(2)}, u32[]{:S(2)}) collective-permute-start(bf16[48,512]{1,0:T(8,128)(2,1)S(1)} %get-tuple-element.65), channel_id=1, source_target_pairs={{0,17},{1,18},{2,19},{3,20},{4,21},{5,22},{6,23},{7,24},{8,25},{9,... | collective-permute-start | bytes 147464 | tf_op jit(solution)/shard_map/ppermute | solution.py:573
  43.5 14.0 %collective-permute-start.13 = (bf16[32,64,128]{2,1,0:T(8,128)(2,1)S(1)}, bf16[32,64,128]{2,1,0:T(8,128)(2,1)S(1)}, u32[]{:S(2)}, u32[]{:S(2)}) collective-permute-start(bf16[32,64,128]{2,1,0:T(8,128)(2,1)S(1)} %get-tuple-element.76), channel_id=1, source_target_pairs={{0,32},{2,34},{4,36},{6,38},{8,40},{10,42},{12,44},{14,46},{16,48}... | collective-permute-start | bytes 1572872 | tf_op jit(solution)/shard_map/ppermute | solution.py:591
  43.6 16.2 %collective-permute-start.14 = (bf16[32,64,128]{2,1,0:T(8,128)(2,1)S(1)}, bf16[32,64,128]{2,1,0:T(8,128)(2,1)S(1)}, u32[]{:S(2)}, u32[]{:S(2)}) collective-permute-start(bf16[32,64,128]{2,1,0:T(8,128)(2,1)S(1)} %get-tuple-element.78), channel_id=1, source_target_pairs={{0,96},{2,98},{4,100},{6,102},{8,104},{10,106},{12,108},{14,110},{... | collective-permute-start | bytes 1572872 | tf_op jit(solution)/shard_map/ppermute | solution.py:591
  52.6 7.5 %copy-start.26 = (bf16[288,512]{1,0:T(8,128)(2,1)}, bf16[288,512]{1,0:T(8,128)(2,1)S(1)}, u32[]{:S(2)}) copy-start(bf16[288,512]{1,0:T(8,128)(2,1)S(1)} %get-tuple-element.70.dx) | copy-start | bytes 884740
  52.6 8.4 %collective-permute-start.18 = (bf16[288,1280]{1,0:T(8,128)(2,1)S(1)}, bf16[288,1280]{1,0:T(8,128)(2,1)S(1)}, u32[]{:S(2)}, u32[]{:S(2)}) collective-permute-start(bf16[288,1280]{1,0:T(8,128)(2,1)S(1)} %get-tuple-element.84.own), channel_id=1, source_target_pairs={{0,1},{1,0},{2,3},{3,2},{4,5},{5,4},{6,7},{7,6},{8,9},{9,8},{10,11... | collective-permute-start | bytes 2211848 | tf_op jit(solution)/shard_map/ppermute | solution.py:578
  52.7 8.3 %collective-permute-start.17 = (bf16[288,768]{1,0:T(8,128)(2,1)S(1)}, bf16[288,768]{1,0:T(8,128)(2,1)S(1)}, u32[]{:S(2)}, u32[]{:S(2)}) collective-permute-start(bf16[288,768]{1,0:T(8,128)(2,1)S(1)} %get-tuple-element.83.nm_own), channel_id=1, source_target_pairs={{0,1},{1,0},{2,3},{3,2},{4,5},{5,4},{6,7},{7,6},{8,9},{9,8},{10,11... | collective-permute-start | bytes 1327112 | tf_op jit(solution)/shard_map/ppermute | solution.py:578
  60.1 7.9 %collective-permute-start.15 = (bf16[32,32,128]{2,1,0:T(8,128)(2,1)S(1)}, bf16[32,32,128]{2,1,0:T(8,128)(2,1)S(1)}, u32[]{:S(2)}, u32[]{:S(2)}) collective-permute-start(bf16[32,32,128]{2,1,0:T(8,128)(2,1)S(1)} %get-tuple-element.80), channel_id=1, source_target_pairs={{0,2},{2,0},{4,6},{6,4},{8,10},{10,8},{12,14},{14,12},{16,18},{18,... | collective-permute-start | bytes 786440 | tf_op jit(solution)/shard_map/ppermute | solution.py:591
  60.2 9.1 %collective-permute-start.16 = (bf16[32,32,128]{2,1,0:T(8,128)(2,1)S(1)}, bf16[32,32,128]{2,1,0:T(8,128)(2,1)S(1)}, u32[]{:S(2)}, u32[]{:S(2)}) collective-permute-start(bf16[32,32,128]{2,1,0:T(8,128)(2,1)S(1)} %get-tuple-element.82), channel_id=1, source_target_pairs={{0,18},{2,16},{4,22},{6,20},{8,26},{10,24},{12,30},{14,28},{16,2},... | collective-permute-start | bytes 786440 | tf_op jit(solution)/shard_map/ppermute | solution.py:591
  70.5 27.5 %all-to-all-start = ((bf16[64,64,128]{2,1,0:T(8,128)(2,1)}), bf16[64,64,128]{2,1,0:T(8,128)(2,1)S(1)}, u32[]{:S(2)}, u32[]{:S(2)}) async-start(bf16[64,64,128]{2,1,0:T(8,128)(2,1)} %bitcast.4), calls=%async_computation | async-start | bytes 2097152 | tf_op jit(solution)/shard_map/all_to_all | solution.py:595
  81.5 7.1 %copy-start.24 = (bf16[96,72]{1,0:T(8,128)(2,1)S(1)}, bf16[96,72]{1,0:T(8,128)(2,1)}, u32[]{:S(2)}) copy-start(bf16[96,72]{1,0:T(8,128)(2,1)} %constant.76.clone.out_main) | copy-start | bytes 41476
  81.5 7.1 %copy-start.29 = (bf16[72,512]{1,0:T(8,128)(2,1)S(1)}, bf16[72,512]{1,0:T(8,128)(2,1)}, u32[]{:S(2)}) copy-start(bf16[72,512]{1,0:T(8,128)(2,1)} %copy-done.28) | copy-start | bytes 221188
  82.2 7.3 %copy-start.30 = (f32[16,512]{1,0:T(8,128)}, f32[16,512]{1,0:T(8,128)S(1)}, u32[]{:S(2)}) copy-start(f32[16,512]{1,0:T(8,128)S(1)} %get-tuple-element.86.mcoef) | copy-start | bytes 98308
  82.2 7.3 %copy-start.32 = (f32[4,1536]{1,0:T(4,128)}, f32[4,1536]{1,0:T(4,128)S(1)}, u32[]{:S(2)}) copy-start(f32[4,1536]{1,0:T(4,128)S(1)} %get-tuple-element.87.ccoef) | copy-start | bytes 73732
  82.2 14.7 %collective-permute-start.10 = (bf16[64,512]{1,0:T(8,128)(2,1)S(1)}, bf16[64,512]{1,0:T(8,128)(2,1)S(1)}, u32[]{:S(2)}, u32[]{:S(2)}) collective-permute-start(bf16[64,512]{1,0:T(8,128)(2,1)S(1)} %get-tuple-element.72), channel_id=1, source_target_pairs={{0,16},{1,17},{2,18},{3,19},{4,20},{5,21},{6,22},{7,23},{8,24},{9,... | collective-permute-start | bytes 196616 | tf_op jit(solution)/shard_map/ppermute | solution.py:573
  85.4 11.6 %collective-permute-start.9 = (bf16[64,512]{1,0:T(8,128)(2,1)S(1)}, bf16[64,512]{1,0:T(8,128)(2,1)S(1)}, u32[]{:S(2)}, u32[]{:S(2)}) collective-permute-start(bf16[64,512]{1,0:T(8,128)(2,1)S(1)} %get-tuple-element.71), channel_id=1, source_target_pairs={{0,1},{1,2},{2,3},{3,4},{4,5},{5,6},{6,7},{7,8},{8,9},{9,10},{10,1... | collective-permute-start | bytes 196616 | tf_op jit(solution)/shard_map/ppermute | solution.py:573
  85.4 10.1 %collective-permute-start.11 = (bf16[32,512]{1,0:T(8,128)(2,1)S(1)}, bf16[32,512]{1,0:T(8,128)(2,1)S(1)}, u32[]{:S(2)}, u32[]{:S(2)}) collective-permute-start(bf16[32,512]{1,0:T(8,128)(2,1)S(1)} %get-tuple-element.73), channel_id=1, source_target_pairs={{0,17},{1,18},{2,19},{3,20},{4,21},{5,22},{6,23},{7,24},{8,25},{9,... | collective-permute-start | bytes 98312 | tf_op jit(solution)/shard_map/ppermute | solution.py:573
  88.6 8.3 %copy-start.10 = (bf16[288,288]{1,0:T(8,128)(2,1)S(1)}, bf16[288,288]{1,0:T(8,128)(2,1)}, u32[]{:S(2)}) copy-start(bf16[288,288]{1,0:T(8,128)(2,1)} %constant.78.clone.dx_main) | copy-start | bytes 497668
  88.6 8.3 %copy-start.15 = (bf16[288,160]{1,0:T(8,128)(2,1)S(1)}, bf16[288,160]{1,0:T(8,128)(2,1)}, u32[]{:S(2)}) copy-start(bf16[288,160]{1,0:T(8,128)(2,1)} %constant.79.clone.dx_halo) | copy-start | bytes 276484
  88.7 8.3 %copy-start.27 = (bf16[288,512]{1,0:T(8,128)(2,1)S(1)}, bf16[288,512]{1,0:T(8,128)(2,1)}, u32[]{:S(2)}) copy-start(bf16[288,512]{1,0:T(8,128)(2,1)} %copy-done.26) | copy-start | bytes 884740
  (6 other events, 12.5 us)

commit v7 on v6

--- a/solution.py
+++ b/solution.py
@@ -395,7 +395,9 @@
     return lax.bitwise_and(lax.shift_right_logical(x, low), (1 << bits) - 1)
 
 
-def coarse_weights_kernel(place, own, other, mk, ms, ck, cs, lines):
+def coarse_weights_kernel(
+    place, own, other, m0k, m0s, m1k, m1s, c0k, c0s, c1k, c1s, lines
+):
     core, zp, yp, _, _ = decode(place)
 
     def at(start, size):
@@ -414,11 +416,12 @@
         )
         for zd in range(2):
             left = mm_nt(select, ordered[zd]).astype(BF16)
-            part = mm(left, dz).reshape(16, 16, D).astype(BF16)
+            part = mm(left, dz).reshape(16, 16, D)
             for yd in range(2):
                 for h in range(4):
                     piece = part[8 * yd : 8 * yd + 8, :, 128 * h : 128 * h + 128]
-                    (ms if zd else mk)[pl.ds(16 * yd + 8 * zh, 8), pl.ds(16 * h, 16), :] = piece
+                    (m0s if zd else m0k)[pl.ds(16 * yd + 8 * zh, 8), pl.ds(8 * h, 8), :] = piece[:, :8].astype(BF16)
+                    (m1s if yd else m1k)[pl.ds(16 * zd + 8 * zh, 8), pl.ds(8 * h, 8), :] = piece[:, 8:].astype(BF16)
     row = row_index(256)
     z = field(row, 3, 1) * 2 + lax.bitwise_xor(field(row, 5, 1), zp)
     group = z * 16 + field(row, 0, 3) * 2 + lax.bitwise_xor(field(row, 4, 1), yp)
@@ -430,23 +433,25 @@
         for i in range(4):
             line = part[64 * i : 64 * (i + 1)]
             for h in range(4):
-                lines[pl.ds(1024 * h + 4 * j + i, 64, 16), :] = line[:, 128 * h : 128 * h + 128]
+                lines[pl.ds(512 * (4 * (j // 2) + h) + 4 * (j % 2) + i, 64, 8), :] = line[:, 128 * h : 128 * h + 128]
     for h in range(4):
-        chunk = lines[pl.ds(1024 * h, 1024), :].reshape(64, 16, 128).astype(BF16)
-        cs[:, pl.ds(16 * h, 16), :] = chunk[:32]
-        ck[:, pl.ds(16 * h, 16), :] = chunk[32:]
-
-
-def middle_kernel(mk, mc, ck, cc, m_keep, m_send, c_keep, c_send):
-    for keep, came, stay, send, first in ((mk, mc, m_keep, m_send, 0), (ck, cc, c_keep, c_send, 1)):
-        total = keep[...].astype(F32) + came[...].astype(F32)
-        for part in range(2):
-            same = total[16 * (part ^ first) : 16 * (part ^ first) + 16]
-            other = total[16 * (1 - (part ^ first)) : 16 * (1 - (part ^ first)) + 16]
-            for h in range(4):
-                rows = slice(16 * h + 8 * part, 16 * h + 8 * part + 8)
-                stay[pl.ds(16 * part, 16), pl.ds(8 * h, 8), :] = same[:, rows].astype(BF16)
-                send[pl.ds(16 * part, 16), pl.ds(8 * h, 8), :] = other[:, rows].astype(BF16)
+        first = lines[pl.ds(512 * h, 512), :].reshape(64, 8, 128).astype(BF16)
+        c0s[:, pl.ds(8 * h, 8), :] = first[:32]
+        c0k[:, pl.ds(8 * h, 8), :] = first[32:]
+        second = lines[pl.ds(512 * (4 + h), 512), :].reshape(64, 8, 128).astype(BF16)
+        for zd in range(2):
+            c1s[pl.ds(16 * zd, 16), pl.ds(8 * h, 8), :] = second[32 * zd : 32 * zd + 16]
+            c1k[pl.ds(16 * zd, 16), pl.ds(8 * h, 8), :] = second[32 * zd + 16 : 32 * zd + 32]
+
+
+def middle_kernel(m0k, m0c, m1k, m1c, c0k, c0c, c1k, c1c, y_keep, y_send, z_keep, z_send):
+    for keep, came, at, first, second in (
+        (m0k, m0c, 0, y_keep, y_send), (c0k, c0c, 16, y_send, y_keep),
+        (m1k, m1c, 0, z_send, z_keep), (c1k, c1c, 16, z_keep, z_send),
+    ):
+        total = (keep[...].astype(F32) + came[...].astype(F32)).astype(BF16)
+        first[pl.ds(at, 16)] = total[:16]
+        second[pl.ds(at, 16)] = total[16:]
 
 
 def fine_weights_kernel(place, nm_own, nm_other, own, other, out, lines):
@@ -475,12 +480,11 @@
         out[:, pl.ds(8 * h, 8), :] = lines[pl.ds(512 * h, 512), :].reshape(64, 8, 128).astype(BF16)
 
 
-def join_kernel(place, m, mc, c, cc, fine, out):
+def join_kernel(place, yk, yc, zk, zc, fine, out):
     _, zp, yp, _, _ = decode(place)
-    for keep, came, zd in ((m, mc, 0), (c, cc, 1)):
+    for keep, came, relations in ((yk, yc, ((0, 0), (1, 1))), (zk, zc, ((1, 0), (0, 1)))):
         total = (keep[...].astype(F32) + came[...].astype(F32)).astype(BF16)
-        for part in range(2):
-            yd = part ^ zd
+        for part, (zd, yd) in enumerate(relations):
             for zh in range(2):
                 at = 16 * part + 8 * zh
                 out[zh, lax.bitwise_xor(zp, zd), :, lax.bitwise_xor(yp, yd), pl.ds(0, 32), :] = total[at : at + 8]
@@ -542,7 +546,7 @@
         low = [jnp.where(z_same, tops[2 * zd + y], tops[2 * (1 - zd) + y]) for y in range(2)]
         return jnp.where(y_same, low[yd], low[1 - yd])
 
-    m0, m1, c0, c1 = (related(0, 0), related(0, 1), related(1, 1), related(1, 0))
+    m0, m1, c0, c1 = (related(0, 0), related(1, 0), related(1, 1), related(0, 1))
     for h in range(4):
         lanes = pl.ds(128 * h, 128)
         rows = slice(8 * h, 8 * h + 8)
@@ -648,13 +652,16 @@
         ],
     )
     back = exchange(sent, 1)
-    mk, ms, ck, cs = scalar_call(
+    m0k, m0s, m1k, m1s, c0k, c0s, c1k, c1s = scalar_call(
         coarse_weights_kernel,
-        [((32, 64, 128), BF16)] * 4,
+        [((32, 32, 128), BF16)] * 8,
         place, fac, partner(fac),
         scratch=[pltpu.VMEM((4096, 128), F32)],
     )
-    mc, cc = (fold(ms, "z", False), fold(cs, "z", True))
+    first = [
+        fold(v, axis, second)
+        for v, axis, second in ((m0s, "z", False), (m1s, "y", False), (c0s, "z", True), (c1s, "y", True))
+    ]
     dx, *sent, fac = scalar_call(
         fine_backward_kernel,
         [((cells, D), BF16)] + narrow + [((cells, 1280), BF16)],
@@ -662,8 +669,12 @@
         scratch=[pltpu.VMEM((cells, 256), F32), pltpu.VMEM((cells, 768), F32)],
     )
     ended = exchange(sent, 1)
-    m, ms, c, cs = call(middle_kernel, [((32, 32, 128), BF16)] * 4, mk, mc, ck, cc)
-    mc, cc = (fold(ms, "y", False), fold(cs, "y", True))
+    y_keep, y_send, z_keep, z_send = call(
+        middle_kernel,
+        [((32, 32, 128), BF16)] * 4,
+        m0k, first[0], m1k, first[1], c0k, first[2], c1k, first[3],
+    )
+    y_came, z_came = (fold(y_send, "y", False), fold(z_send, "z", False))
     (fine_part,) = scalar_call(
         fine_weights_kernel,
         [((64, 32, 128), BF16)],
@@ -673,7 +684,7 @@
     (joined,) = scalar_call(
         join_kernel,
         [((2, 2, 8, 2, 64, 128), BF16)],
-        place, m, mc, c, cc, fine_part,
+        place, y_keep, y_came, z_keep, z_came, fine_part,
     )
     parts = deal(joined.reshape(64, 64, 128)).reshape(2, 2, 8, 2, 64, 128)
     (output,) = call(output_kernel, [((6, 12, D), BF16)], y2, *back, table("out_main"), table("out_halo"))

time: 100 us -> 103 us (1.030)
  waiting for transfers between devices: 34.2 us -> 40.2 us
  starting transfers between devices: 36.4 us -> 32.6 us
    ppermute x12, waiting for transfers between devices: 18.7 us -> 26.6 us  [exchange(): arrived.append(lax.ppermute(piece, ('lat', 'pair', 'core'), pairs))]
    all_to_all x1, starting transfers between devices: 8.46 us -> 5.6 us  [deal(): return lax.all_to_all(value, ('lat', 'pair'), 0, 0)]
    ppermute x3, waiting for transfers between devices: 1.85 us -> 0.01 us  [partner(): return lax.ppermute(value, 'core', [(0, 1), (1, 0)])]
    ppermute x4 -> x6, starting transfers between devices: 4.77 us -> 4.5 us  [fold(): return lax.ppermute(value, ('lat', 'pair'), pairs)]
    ppermute x4 -> x6, waiting for transfers between devices: 13.7 us -> 13.6 us  [fold(): return lax.ppermute(value, ('lat', 'pair'), pairs)]
  transfers between devices with their start and end apart: 20 -> 22, of which waited for: 10 -> 11; matrix products, arithmetic and copies ran while one was open for 0% -> 0% of each run, Pallas kernels for 10% -> 9%
where the time goes in v7:
time: 103 us; the launch traced here: 101 us
  waiting for transfers between devices  40.2 us (39%)
  starting transfers between devices  32.6 us (32%)
  Pallas kernels  23.3 us (23%)
  local copies, waits for them, and re-layouts  4.05 us (4%)
  between operations  1.14 us (1%)
    ppermute x12, waiting for transfers between devices, exchange(): arrived.append(lax.ppermute(piece, ('lat', 'pair', 'core'), pairs))  26.6 us
    pallas_call x12, Pallas kernels, call(): pl.pallas_call(kernel, out_shape=[jax.ShapeDtypeStruct(s, d) for s, d in...  23.3 us
    ppermute x12, starting transfers between devices, exchange(): arrived.append(lax.ppermute(piece, ('lat', 'pair', 'core'), pairs))  22.5 us
    ppermute x6, waiting for transfers between devices, fold(): return lax.ppermute(value, ('lat', 'pair'), pairs)  13.6 us
    all_to_all x1, starting transfers between devices, deal(): return lax.all_to_all(value, ('lat', 'pair'), 0, 0)  5.6 us
    ppermute x6, starting transfers between devices, fold(): return lax.ppermute(value, ('lat', 'pair'), pairs)  4.5 us
    unnamed x68, local copies, waits for them, and re-layouts  4.05 us
  transfers between devices with their start and end apart: 22, of which 11 were waited for; matrix products, arithmetic and copies ran while one was open for 0% of the time, Pallas kernels for 9%

profile of v7, /device:TPU:0, one launch (start us, length us, event | category | flops | bytes accessed | tf_op | source)
XLA Modules:
  0.0 101.4 jit_solution(15994292439967122282)
XLA Ops:
  0.7 0.0 copy-start.13
  0.7 0.0 copy-start.20
  0.7 1.5 %shard_map.339 = (bf16[288,512]{1,0:T(8,128)(2,1)S(1)}, bf16[80,512]{1,0:T(8,128)(2,1)S(1)}, bf16[80,512]{1,0:T(8,128)(2,1)S(1)}, bf16[48,512]{1,0:T(8,128)(2,1)S(1)}, f32[72,512]{1,0:T(8,128)S(1)}) custom-call(s32[1]{0:T(128)} %bitcast.place, bf16[12,24,512]{2,1,0:T(8,128)(2,1)} %tok_in.1, bf16[6,12,512]{2,1,0:T(8,128)(2,1)} %cot_in.1, ...), custom_call_target="tpu_custom_call" | custom-call | flops 5000000000 | bytes 4000000 | tf_op jit(solution)/shard_map/pallas_call | solution.py:162
  2.3 3.4 %collective-permute-start = (bf16[80,512]{1,0:T(8,128)(2,1)S(1)}, bf16[80,512]{1,0:T(8,128)(2,1)S(1)}, u32[]{:S(2)}, u32[]{:S(2)}) collective-permute-start(bf16[80,512]{1,0:T(8,128)(2,1)S(1)} %get-tuple-element.58), channel_id=1, source_target_pairs={{0,15},{1,0},{2,1},{3,2},{4,3},{5,4},{6,5},{7,6},{8,7},{9,8},{10,9... | collective-permute-start | bytes 245768 | tf_op jit(solution)/shard_map/ppermute | solution.py:577
  5.7 6.4 %collective-permute-start.1 = (bf16[80,512]{1,0:T(8,128)(2,1)S(1)}, bf16[80,512]{1,0:T(8,128)(2,1)S(1)}, u32[]{:S(2)}, u32[]{:S(2)}) collective-permute-start(bf16[80,512]{1,0:T(8,128)(2,1)S(1)} %get-tuple-element.59), channel_id=1, source_target_pairs={{0,112},{1,113},{2,114},{3,115},{4,116},{5,117},{6,118},{7,119},{8... | collective-permute-start | bytes 245768 | tf_op jit(solution)/shard_map/ppermute | solution.py:577
  12.0 0.2 collective-permute-start.2
  12.2 4.9 %collective-permute-done.2.corner.ccorner = bf16[48,512]{1,0:T(8,128)(2,1)S(1)} collective-permute-done((bf16[48,512]{1,0:T(8,128)(2,1)S(1)}, bf16[48,512]{1,0:T(8,128)(2,1)S(1)}, u32[]{:S(2)}, u32[]{:S(2)}) %collective-permute-start.2) | collective-permute-done | bytes 49184 | tf_op jit(solution)/shard_map/ppermute | solution.py:577
  17.2 0.0 copy-start.12
  17.2 0.0 copy-start.14
  17.2 0.0 copy-start.17
  17.2 0.0 copy-start.23
  17.3 3.9 %shard_map.340 = (bf16[288,512]{1,0:T(8,128)(2,1)S(1)}, bf16[288,768]{1,0:T(8,128)(2,1)S(1)}, f32[288,768]{1,0:T(8,128)S(1)}, f32[8,72,256]{2,1,0:T(8,128)S(1)},...) custom-call(s32[1]{0:T(128)} %bitcast.place, ...), custom_call_target="tpu_custom_call" | custom-call | flops 5000000000 | bytes 4000000 | tf_op jit(solution)/shard_map/pallas_call | solution.py:162
  21.2 0.5 collective-permute-start.3
  21.6 5.2 %collective-permute-start.4 = (bf16[64,512]{1,0:T(8,128)(2,1)S(1)}, bf16[64,512]{1,0:T(8,128)(2,1)S(1)}, u32[]{:S(2)}, u32[]{:S(2)}) collective-permute-start(bf16[64,512]{1,0:T(8,128)(2,1)S(1)} %get-tuple-element.63), channel_id=1, source_target_pairs={{0,112},{1,113},{2,114},{3,115},{4,116},{5,117},{6,118},{7,119},{8... | collective-permute-start | bytes 196616 | tf_op jit(solution)/shard_map/ppermute | solution.py:577
  26.8 4.8 %collective-permute-done.5.corner = bf16[32,512]{1,0:T(8,128)(2,1)S(1)} collective-permute-done((bf16[32,512]{1,0:T(8,128)(2,1)S(1)}, bf16[32,512]{1,0:T(8,128)(2,1)S(1)}, u32[]{:S(2)}, u32[]{:S(2)}) %collective-permute-start.5) | collective-permute-done | bytes 32800 | tf_op jit(solution)/shard_map/ppermute | solution.py:577
  31.8 6.5 %shard_map.341 = (bf16[72,512]{1,0:T(8,128)(2,1)S(1)}, bf16[288,512]{1,0:T(8,128)(2,1)S(1)}, bf16[80,512]{1,0:T(8,128)(2,1)S(1)}, bf16[80,512]{1,0:T(8,128)(2,1)...) custom-call(s32[1]{0:T(128)} %bitcast.place, bf16[288,512]{1,0:T(8,128)(2,1)S(1)} %get-tuple-element.61.y_in, ...), custom_call_target="tpu_custom_call" | custom-call | flops 5000000000 | bytes 4000000 | tf_op jit(solution)/shard_map/pallas_call | solution.py:162
  38.3 0.6 copy-done.28
  38.9 0.5 collective-permute-start.6
  39.4 9.6 %collective-permute-done.8.corner = bf16[48,512]{1,0:T(8,128)(2,1)S(1)} collective-permute-done((bf16[48,512]{1,0:T(8,128)(2,1)S(1)}, bf16[48,512]{1,0:T(8,128)(2,1)S(1)}, u32[]{:S(2)}, u32[]{:S(2)}) %collective-permute-start.8) | collective-permute-done | bytes 49184 | tf_op jit(solution)/shard_map/ppermute | solution.py:577
  49.1 3.5 %shard_map.343 = (bf16[288,512]{1,0:T(8,128)(2,1)S(1)}, bf16[64,512]{1,0:T(8,128)(2,1)S(1)}, bf16[64,512]{1,0:T(8,128)(2,1)S(1)}, bf16[32,512]{1,0:T(8,128)(2,1)S(1)}, bf16[288,1280]{1,0:T(8,128)(2,1)S(1)}) custom-call(s32[1]{0:T(128)} %bitcast.place, bf16[288,512]{1,0:T(8,128)(2,1)S(1)} %get-tuple-element.70.df_in, ...), custom_call_target="tpu_custom_call" | custom-call | flops 5000000000 | bytes 4000000 | tf_op jit(solution)/shard_map/pallas_call | solution.py:162
  52.6 0.7 copy-done.26
  53.3 1.8 %shard_map.345 = (bf16[32,32,128]{2,1,0:T(8,128)(2,1)S(1)}, bf16[32,32,128]{2,1,0:T(8,128)(2,1)S(1)}, bf16[32,32,128]{2,1,0:T(8,128)(2,1)S(1)}, bf16[32,32,128]{...) custom-call(s32[1]{0:T(128)} %bitcast.place, ...), custom_call_target="tpu_custom_call" | custom-call | flops 5000000000 | bytes 4000000 | tf_op jit(solution)/shard_map/pallas_call | solution.py:162
  55.1 0.1 collective-permute-start.13
  55.2 0.1 collective-permute-start.14
  55.3 1.8 %collective-permute-start.15 = (bf16[32,32,128]{2,1,0:T(8,128)(2,1)S(1)}, bf16[32,32,128]{2,1,0:T(8,128)(2,1)S(1)}, u32[]{:S(2)}, u32[]{:S(2)}) collective-permute-start(bf16[32,32,128]{2,1,0:T(8,128)(2,1)S(1)} %get-tuple-element.84), channel_id=1, source_target_pairs={{0,96},{2,98},{4,100},{6,102},{8,104},{10,106},{12,108},{14,110},{... | collective-permute-start | bytes 786440 | tf_op jit(solution)/shard_map/ppermute | solution.py:595
  57.1 1.0 collective-permute-start.16
  58.1 5.8 %collective-permute-done.13.m0c = bf16[32,32,128]{2,1,0:T(8,128)(2,1)S(1)} collective-permute-done((bf16[32,32,128]{2,1,0:T(8,128)(2,1)S(1)}, bf16[32,32,128]{2,1,0:T(8,128)(2,1)S(1)}, u32[]{:S(2)}, u32[]{:S(2)}) %collective-permute-start.13) | collective-permute-done | bytes 262176 | tf_op jit(solution)/shard_map/ppermute | solution.py:595
  63.9 0.1 collective-permute-done.14.m1c
  64.0 1.3 %collective-permute-done.15.c0c = bf16[32,32,128]{2,1,0:T(8,128)(2,1)S(1)} collective-permute-done((bf16[32,32,128]{2,1,0:T(8,128)(2,1)S(1)}, bf16[32,32,128]{2,1,0:T(8,128)(2,1)S(1)}, u32[]{:S(2)}, u32[]{:S(2)}) %collective-permute-start.15) | collective-permute-done | bytes 262176 | tf_op jit(solution)/shard_map/ppermute | solution.py:595
  65.3 1.4 %collective-permute-done.16.c1c = bf16[32,32,128]{2,1,0:T(8,128)(2,1)S(1)} collective-permute-done((bf16[32,32,128]{2,1,0:T(8,128)(2,1)S(1)}, bf16[32,32,128]{2,1,0:T(8,128)(2,1)S(1)}, u32[]{:S(2)}, u32[]{:S(2)}) %collective-permute-start.16) | collective-permute-done | bytes 262176 | tf_op jit(solution)/shard_map/ppermute | solution.py:595
  66.8 0.2 shard_map.346
  67.0 0.5 collective-permute-start.17
  67.5 1.0 %collective-permute-start.18 = (bf16[32,32,128]{2,1,0:T(8,128)(2,1)S(1)}, bf16[32,32,128]{2,1,0:T(8,128)(2,1)S(1)}, u32[]{:S(2)}, u32[]{:S(2)}) collective-permute-start(bf16[32,32,128]{2,1,0:T(8,128)(2,1)S(1)} %get-tuple-element.90), channel_id=1, source_target_pairs={{0,32},{2,34},{4,36},{6,38},{8,40},{10,42},{12,44},{14,46},{16,48}... | collective-permute-start | bytes 786440 | tf_op jit(solution)/shard_map/ppermute | solution.py:595
  68.6 1.2 %shard_map.347.fine = bf16[64,32,128]{2,1,0:T(8,128)(2,1)S(1)} custom-call(s32[1]{0:T(128)} %bitcast.place, bf16[288,768]{1,0:T(8,128)(2,1)S(1)} %get-tuple-element.91.nm_own, bf16[288,768]{1,0:T(8,128)(2,1)S(1)} %collective-permute-done.19.nm_other, bf16[288,1280]{1,0:T(8,128)(2,1)S(1)} %get-tuple-element.92.own, ...), custom_call_target="tpu_custom_call" | custom-call | flops 5000000000 | bytes 4000000 | tf_op jit(solution)/shard_map/pallas_call | solution.py:162
  69.8 4.8 %collective-permute-done.17.yc = bf16[32,32,128]{2,1,0:T(8,128)(2,1)S(1)} collective-permute-done((bf16[32,32,128]{2,1,0:T(8,128)(2,1)S(1)}, bf16[32,32,128]{2,1,0:T(8,128)(2,1)S(1)}, u32[]{:S(2)}, u32[]{:S(2)}) %collective-permute-start.17) | collective-permute-done | bytes 262176 | tf_op jit(solution)/shard_map/ppermute | solution.py:595
  74.7 0.1 collective-permute-done.18.zc
  74.7 1.2 %shard_map.348 = bf16[2,2,8,2,64,128]{5,4,3,2,1,0:T(8,128)(2,1)} custom-call(s32[1]{0:T(128)} %bitcast.place, bf16[32,32,128]{2,1,0:T(8,128)(2,1)S(1)} %get-tuple-element.87.yk, bf16[32,32,128]{2,1,0:T(8,128)(2,1)S(1)} %collective-permute-done.17.yc, bf16[32,32,128]{2,1,0:T(8,128)(2,1)S(1)} %get-tuple-element.89.zk, ...), custom_call_target="tpu_custom_call" | custom-call | flops 5000000000 | bytes 4000000 | tf_op jit(solution)/shard_map/pallas_call | solution.py:162
  76.0 5.6 %all-to-all-start = ((bf16[64,64,128]{2,1,0:T(8,128)(2,1)}), bf16[64,64,128]{2,1,0:T(8,128)(2,1)S(1)}, u32[]{:S(2)}, u32[]{:S(2)}) async-start(bf16[64,64,128]{2,1,0:T(8,128)(2,1)} %bitcast.4), calls=%async_computation | async-start | bytes 2097152 | tf_op jit(solution)/shard_map/all_to_all | solution.py:599
  81.6 1.4 %copy-done.2 = bf16[512,1536]{1,0:T(8,128)(2,1)S(1)} copy-done((bf16[512,1536]{1,0:T(8,128)(2,1)S(1)}, bf16[512,1536]{1,0:T(8,128)(2,1)}, u32[]{:S(2)}) %copy-start.2) | copy-done | bytes 1572888
  83.0 1.1 %copy-done.4 = bf16[512,768]{1,0:T(8,128)(2,1)S(1)} copy-done((bf16[512,768]{1,0:T(8,128)(2,1)S(1)}, bf16[512,768]{1,0:T(8,128)(2,1)}, u32[]{:S(2)}) %copy-start.4) | copy-done | bytes 786456
  84.1 0.7 shard_map.349
  84.8 3.1 %collective-permute-start.10 = (bf16[64,512]{1,0:T(8,128)(2,1)S(1)}, bf16[64,512]{1,0:T(8,128)(2,1)S(1)}, u32[]{:S(2)}, u32[]{:S(2)}) collective-permute-start(bf16[64,512]{1,0:T(8,128)(2,1)S(1)} %get-tuple-element.76), channel_id=1, source_target_pairs={{0,16},{1,17},{2,18},{3,19},{4,20},{5,21},{6,22},{7,23},{8,24},{9,... | collective-permute-start | bytes 196616 | tf_op jit(solution)/shard_map/ppermute | solution.py:577
  87.9 3.3 %collective-permute-start.11 = (bf16[32,512]{1,0:T(8,128)(2,1)S(1)}, bf16[32,512]{1,0:T(8,128)(2,1)S(1)}, u32[]{:S(2)}, u32[]{:S(2)}) collective-permute-start(bf16[32,512]{1,0:T(8,128)(2,1)S(1)} %get-tuple-element.77), channel_id=1, source_target_pairs={{0,17},{1,18},{2,19},{3,20},{4,21},{5,22},{6,23},{7,24},{8,25},{9,... | collective-permute-start | bytes 98312 | tf_op jit(solution)/shard_map/ppermute | solution.py:577
  91.2 0.8 shard_map.342
  92.1 5.8 %collective-permute-done.11.corner = bf16[32,512]{1,0:T(8,128)(2,1)S(1)} collective-permute-done((bf16[32,512]{1,0:T(8,128)(2,1)S(1)}, bf16[32,512]{1,0:T(8,128)(2,1)S(1)}, u32[]{:S(2)}, u32[]{:S(2)}) %collective-permute-start.11) | collective-permute-done | bytes 32800 | tf_op jit(solution)/shard_map/ppermute | solution.py:577
  97.9 1.5 %collective-permute-done.10.edge = bf16[64,512]{1,0:T(8,128)(2,1)S(1)} collective-permute-done((bf16[64,512]{1,0:T(8,128)(2,1)S(1)}, bf16[64,512]{1,0:T(8,128)(2,1)S(1)}, u32[]{:S(2)}, u32[]{:S(2)}) %collective-permute-start.10) | collective-permute-done | bytes 65568 | tf_op jit(solution)/shard_map/ppermute | solution.py:577
  99.4 1.1 %shard_map.344 = bf16[12,24,512]{2,1,0:T(8,128)(2,1)} custom-call(bf16[288,512]{1,0:T(8,128)(2,1)S(1)} %copy-done.27, bf16[64,512]{1,0:T(8,128)(2,1)S(1)} %collective-permute-done.9.side, bf16[64,512]{1,0:T(8,128)(2,1)S(1)} %collective-permute-done.10.edge, bf16[32,512]{1,0:T(8,128)(2,1)S(1)} %collective-permute-done.11.corner, ...), custom_call_target="tpu_custom_call" | custom-call | flops 5000000000 | bytes 4000000 | tf_op jit(solution)/shard_map/pallas_call | solution.py:162
  100.6 0.8 shard_map.350
  (76 shorter events, 0.2 us)
Async XLA Ops:
  0.7 16.4 %copy-start.3 = (bf16[512,768]{1,0:T(8,128)(2,1)S(1)}, bf16[512,768]{1,0:T(8,128)(2,1)}, u32[]{:S(2)}) copy-start(bf16[512,768]{1,0:T(8,128)(2,1)} %fqkv.1) | copy-start | bytes 2359300
  0.7 16.4 %copy-start.6 = (bf16[256,512]{1,0:T(8,128)(2,1)S(1)}, bf16[256,512]{1,0:T(8,128)(2,1)}, u32[]{:S(2)}) copy-start(bf16[256,512]{1,0:T(8,128)(2,1)} %wproj.5) | copy-start | bytes 786436
  0.7 16.4 %copy-start.8 = (f32[512]{0:T(512)S(1)}, f32[512]{0:T(512)}, u32[]{:S(2)}) copy-start(f32[512]{0:T(512)} %param.29) | copy-start | bytes 6148
  0.7 16.4 %copy-start.13 = (bf16[288,288]{1,0:T(8,128)(2,1)S(1)}, bf16[288,288]{1,0:T(8,128)(2,1)}, u32[]{:S(2)}) copy-start(bf16[288,288]{1,0:T(8,128)(2,1)} %constant.64.clone.t_main) | copy-start | bytes 497668
  0.7 16.4 %copy-start.18 = (bf16[288,208]{1,0:T(8,128)(2,1)S(1)}, bf16[288,208]{1,0:T(8,128)(2,1)}, u32[]{:S(2)}) copy-start(bf16[288,208]{1,0:T(8,128)(2,1)} %constant.65.clone.t_halo) | copy-start | bytes 359428
  0.7 16.4 %copy-start.20 = (bf16[160,288]{1,0:T(8,128)(2,1)S(1)}, bf16[160,288]{1,0:T(8,128)(2,1)}, u32[]{:S(2)}) copy-start(bf16[160,288]{1,0:T(8,128)(2,1)} %constant.66.clone.y_send) | copy-start | bytes 276484
  2.3 14.8 %collective-permute-start = (bf16[80,512]{1,0:T(8,128)(2,1)S(1)}, bf16[80,512]{1,0:T(8,128)(2,1)S(1)}, u32[]{:S(2)}, u32[]{:S(2)}) collective-permute-start(bf16[80,512]{1,0:T(8,128)(2,1)S(1)} %get-tuple-element.58), channel_id=1, source_target_pairs={{0,15},{1,0},{2,1},{3,2},{4,3},{5,4},{6,5},{7,6},{8,7},{9,8},{10,9... | collective-permute-start | bytes 245768 | tf_op jit(solution)/shard_map/ppermute | solution.py:577
  5.7 11.4 %collective-permute-start.1 = (bf16[80,512]{1,0:T(8,128)(2,1)S(1)}, bf16[80,512]{1,0:T(8,128)(2,1)S(1)}, u32[]{:S(2)}, u32[]{:S(2)}) collective-permute-start(bf16[80,512]{1,0:T(8,128)(2,1)S(1)} %get-tuple-element.59), channel_id=1, source_target_pairs={{0,112},{1,113},{2,114},{3,115},{4,116},{5,117},{6,118},{7,119},{8... | collective-permute-start | bytes 245768 | tf_op jit(solution)/shard_map/ppermute | solution.py:577
  12.0 5.0 %collective-permute-start.2 = (bf16[48,512]{1,0:T(8,128)(2,1)S(1)}, bf16[48,512]{1,0:T(8,128)(2,1)S(1)}, u32[]{:S(2)}, u32[]{:S(2)}) collective-permute-start(bf16[48,512]{1,0:T(8,128)(2,1)S(1)} %get-tuple-element.60), channel_id=1, source_target_pairs={{0,127},{1,112},{2,113},{3,114},{4,115},{5,116},{6,117},{7,118},{8... | collective-permute-start | bytes 147464 | tf_op jit(solution)/shard_map/ppermute | solution.py:577
  17.1 14.6 %copy-start = (bf16[2048,512]{1,0:T(8,128)(2,1)S(1)}, bf16[2048,512]{1,0:T(8,128)(2,1)}, u32[]{:S(2)}) copy-start(bf16[2048,512]{1,0:T(8,128)(2,1)} %mweight.3) | copy-start | bytes 6291460
  17.1 14.5 %copy-start.1 = (bf16[512,1536]{1,0:T(8,128)(2,1)S(1)}, bf16[512,1536]{1,0:T(8,128)(2,1)}, u32[]{:S(2)}) copy-start(bf16[512,1536]{1,0:T(8,128)(2,1)} %cqkv.1) | copy-start | bytes 4718596
  17.1 14.5 %copy-start.5 = (bf16[512,512]{1,0:T(8,128)(2,1)S(1)}, bf16[512,512]{1,0:T(8,128)(2,1)}, u32[]{:S(2)}) copy-start(bf16[512,512]{1,0:T(8,128)(2,1)} %wproj.4) | copy-start | bytes 1572868
  17.2 14.5 %copy-start.7 = (f32[2048]{0:T(1024)S(1)}, f32[2048]{0:T(1024)}, u32[]{:S(2)}) copy-start(f32[2048]{0:T(1024)} %param.32) | copy-start | bytes 24580
  17.2 14.5 %copy-start.9 = (f32[512]{0:T(512)S(1)}, f32[512]{0:T(512)}, u32[]{:S(2)}) copy-start(f32[512]{0:T(512)} %param.34) | copy-start | bytes 6148
  17.2 14.5 %copy-start.12 = (bf16[288,288]{1,0:T(8,128)(2,1)S(1)}, bf16[288,288]{1,0:T(8,128)(2,1)}, u32[]{:S(2)}) copy-start(bf16[288,288]{1,0:T(8,128)(2,1)} %constant.67.clone.y_main) | copy-start | bytes 497668
  17.2 14.5 %copy-start.14 = (bf16[208,288]{1,0:T(8,128)(2,1)S(1)}, bf16[208,288]{1,0:T(8,128)(2,1)}, u32[]{:S(2)}) copy-start(bf16[208,288]{1,0:T(8,128)(2,1)} %constant.71.clone.df_send) | copy-start | bytes 359428
  17.2 14.5 %copy-start.17 = (bf16[288,160]{1,0:T(8,128)(2,1)S(1)}, bf16[288,160]{1,0:T(8,128)(2,1)}, u32[]{:S(2)}) copy-start(bf16[288,160]{1,0:T(8,128)(2,1)} %constant.68.clone.y_halo) | copy-start | bytes 276484
  17.2 14.5 %copy-start.21 = (bf16[208,72]{1,0:T(8,128)(2,1)S(1)}, bf16[208,72]{1,0:T(8,128)(2,1)}, u32[]{:S(2)}) copy-start(bf16[208,72]{1,0:T(8,128)(2,1)} %constant.72.clone.out_send) | copy-start | bytes 89860
  17.2 14.5 %copy-start.23 = (bf16[72,208]{1,0:T(8,128)(2,1)S(1)}, bf16[72,208]{1,0:T(8,128)(2,1)}, u32[]{:S(2)}) copy-start(bf16[72,208]{1,0:T(8,128)(2,1)} %constant.70.clone.c_halo) | copy-start | bytes 89860
  17.2 14.5 %copy-start.25 = (bf16[72,72]{1,0:T(8,128)(2,1)S(1)}, bf16[72,72]{1,0:T(8,128)(2,1)}, u32[]{:S(2)}) copy-start(bf16[72,72]{1,0:T(8,128)(2,1)} %constant.69.clone.c_main) | copy-start | bytes 31108
  21.2 10.5 %collective-permute-start.3 = (bf16[64,512]{1,0:T(8,128)(2,1)S(1)}, bf16[64,512]{1,0:T(8,128)(2,1)S(1)}, u32[]{:S(2)}, u32[]{:S(2)}) collective-permute-start(bf16[64,512]{1,0:T(8,128)(2,1)S(1)} %get-tuple-element.62), channel_id=1, source_target_pairs={{0,15},{1,0},{2,1},{3,2},{4,3},{5,4},{6,5},{7,6},{8,7},{9,8},{10,9... | collective-permute-start | bytes 196616 | tf_op jit(solution)/shard_map/ppermute | solution.py:577
  21.6 10.0 %collective-permute-start.4 = (bf16[64,512]{1,0:T(8,128)(2,1)S(1)}, bf16[64,512]{1,0:T(8,128)(2,1)S(1)}, u32[]{:S(2)}, u32[]{:S(2)}) collective-permute-start(bf16[64,512]{1,0:T(8,128)(2,1)S(1)} %get-tuple-element.63), channel_id=1, source_target_pairs={{0,112},{1,113},{2,114},{3,115},{4,116},{5,117},{6,118},{7,119},{8... | collective-permute-start | bytes 196616 | tf_op jit(solution)/shard_map/ppermute | solution.py:577
  26.8 4.8 %collective-permute-start.5 = (bf16[32,512]{1,0:T(8,128)(2,1)S(1)}, bf16[32,512]{1,0:T(8,128)(2,1)S(1)}, u32[]{:S(2)}, u32[]{:S(2)}) collective-permute-start(bf16[32,512]{1,0:T(8,128)(2,1)S(1)} %get-tuple-element.64), channel_id=1, source_target_pairs={{0,127},{1,112},{2,113},{3,114},{4,115},{5,116},{6,117},{7,118},{8... | collective-permute-start | bytes 98312 | tf_op jit(solution)/shard_map/ppermute | solution.py:577
  31.8 17.3 %copy-start.11 = (bf16[288,288]{1,0:T(8,128)(2,1)S(1)}, bf16[288,288]{1,0:T(8,128)(2,1)}, u32[]{:S(2)}) copy-start(bf16[288,288]{1,0:T(8,128)(2,1)} %constant.73.clone.d_main) | copy-start | bytes 497668
  31.8 17.3 %copy-start.16 = (bf16[288,208]{1,0:T(8,128)(2,1)S(1)}, bf16[288,208]{1,0:T(8,128)(2,1)}, u32[]{:S(2)}) copy-start(bf16[288,208]{1,0:T(8,128)(2,1)} %constant.74.clone.d_halo) | copy-start | bytes 359428
  31.8 17.3 %copy-start.19 = (bf16[160,288]{1,0:T(8,128)(2,1)S(1)}, bf16[160,288]{1,0:T(8,128)(2,1)}, u32[]{:S(2)}) copy-start(bf16[160,288]{1,0:T(8,128)(2,1)} %constant.75.clone.dx_send) | copy-start | bytes 276484
  38.9 14.4 %collective-permute-start.12 = (bf16[80,5632]{1,0:T(8,128)(2,1)S(1)}, bf16[80,5632]{1,0:T(8,128)(2,1)S(1)}, u32[]{:S(2)}, u32[]{:S(2)}) collective-permute-start(bf16[80,5632]{1,0:T(8,128)(2,1)S(1)} %get-tuple-element.78.own), channel_id=1, source_target_pairs={{0,1},{1,0},{2,3},{3,2},{4,5},{5,4},{6,7},{7,6},{8,9},{9,8},{10,11... | collective-permute-start | bytes 2703368 | tf_op jit(solution)/shard_map/ppermute | solution.py:582
  38.9 10.1 %collective-permute-start.6 = (bf16[80,512]{1,0:T(8,128)(2,1)S(1)}, bf16[80,512]{1,0:T(8,128)(2,1)S(1)}, u32[]{:S(2)}, u32[]{:S(2)}) collective-permute-start(bf16[80,512]{1,0:T(8,128)(2,1)S(1)} %get-tuple-element.67), channel_id=1, source_target_pairs={{0,1},{1,2},{2,3},{3,4},{4,5},{5,6},{6,7},{7,8},{8,9},{9,10},{10,1... | collective-permute-start | bytes 245768 | tf_op jit(solution)/shard_map/ppermute | solution.py:577
  39.4 9.6 %collective-permute-start.7 = (bf16[80,512]{1,0:T(8,128)(2,1)S(1)}, bf16[80,512]{1,0:T(8,128)(2,1)S(1)}, u32[]{:S(2)}, u32[]{:S(2)}) collective-permute-start(bf16[80,512]{1,0:T(8,128)(2,1)S(1)} %get-tuple-element.68), channel_id=1, source_target_pairs={{0,16},{1,17},{2,18},{3,19},{4,20},{5,21},{6,22},{7,23},{8,24},{9,... | collective-permute-start | bytes 245768 | tf_op jit(solution)/shard_map/ppermute | solution.py:577
  39.4 9.6 %collective-permute-start.8 = (bf16[48,512]{1,0:T(8,128)(2,1)S(1)}, bf16[48,512]{1,0:T(8,128)(2,1)S(1)}, u32[]{:S(2)}, u32[]{:S(2)}) collective-permute-start(bf16[48,512]{1,0:T(8,128)(2,1)S(1)} %get-tuple-element.69), channel_id=1, source_target_pairs={{0,17},{1,18},{2,19},{3,20},{4,21},{5,22},{6,23},{7,24},{8,25},{9,... | collective-permute-start | bytes 147464 | tf_op jit(solution)/shard_map/ppermute | solution.py:577
  53.3 15.2 %collective-permute-start.20 = (bf16[288,1280]{1,0:T(8,128)(2,1)S(1)}, bf16[288,1280]{1,0:T(8,128)(2,1)S(1)}, u32[]{:S(2)}, u32[]{:S(2)}) collective-permute-start(bf16[288,1280]{1,0:T(8,128)(2,1)S(1)} %get-tuple-element.92.own), channel_id=1, source_target_pairs={{0,1},{1,0},{2,3},{3,2},{4,5},{5,4},{6,7},{7,6},{8,9},{9,8},{10,11... | collective-permute-start | bytes 2211848 | tf_op jit(solution)/shard_map/ppermute | solution.py:582
  55.1 8.8 %collective-permute-start.13 = (bf16[32,32,128]{2,1,0:T(8,128)(2,1)S(1)}, bf16[32,32,128]{2,1,0:T(8,128)(2,1)S(1)}, u32[]{:S(2)}, u32[]{:S(2)}) collective-permute-start(bf16[32,32,128]{2,1,0:T(8,128)(2,1)S(1)} %get-tuple-element.80), channel_id=1, source_target_pairs={{0,32},{2,34},{4,36},{6,38},{8,40},{10,42},{12,44},{14,46},{16,48}... | collective-permute-start | bytes 786440 | tf_op jit(solution)/shard_map/ppermute | solution.py:595
  55.2 8.8 %collective-permute-start.14 = (bf16[32,32,128]{2,1,0:T(8,128)(2,1)S(1)}, bf16[32,32,128]{2,1,0:T(8,128)(2,1)S(1)}, u32[]{:S(2)}, u32[]{:S(2)}) collective-permute-start(bf16[32,32,128]{2,1,0:T(8,128)(2,1)S(1)} %get-tuple-element.82), channel_id=1, source_target_pairs={{0,2},{2,0},{4,6},{6,4},{8,10},{10,8},{12,14},{14,12},{16,18},{18,... | collective-permute-start | bytes 786440 | tf_op jit(solution)/shard_map/ppermute | solution.py:595
  55.3 10.0 %collective-permute-start.15 = (bf16[32,32,128]{2,1,0:T(8,128)(2,1)S(1)}, bf16[32,32,128]{2,1,0:T(8,128)(2,1)S(1)}, u32[]{:S(2)}, u32[]{:S(2)}) collective-permute-start(bf16[32,32,128]{2,1,0:T(8,128)(2,1)S(1)} %get-tuple-element.84), channel_id=1, source_target_pairs={{0,96},{2,98},{4,100},{6,102},{8,104},{10,106},{12,108},{14,110},{... | collective-permute-start | bytes 786440 | tf_op jit(solution)/shard_map/ppermute | solution.py:595
  57.1 9.6 %collective-permute-start.16 = (bf16[32,32,128]{2,1,0:T(8,128)(2,1)S(1)}, bf16[32,32,128]{2,1,0:T(8,128)(2,1)S(1)}, u32[]{:S(2)}, u32[]{:S(2)}) collective-permute-start(bf16[32,32,128]{2,1,0:T(8,128)(2,1)S(1)} %get-tuple-element.86), channel_id=1, source_target_pairs={{0,18},{2,16},{4,22},{6,20},{8,26},{10,24},{12,30},{14,28},{16,2},... | collective-permute-start | bytes 786440 | tf_op jit(solution)/shard_map/ppermute | solution.py:595
  63.9 4.6 %collective-permute-start.19 = (bf16[288,768]{1,0:T(8,128)(2,1)S(1)}, bf16[288,768]{1,0:T(8,128)(2,1)S(1)}, u32[]{:S(2)}, u32[]{:S(2)}) collective-permute-start(bf16[288,768]{1,0:T(8,128)(2,1)S(1)} %get-tuple-element.91.nm_own), channel_id=1, source_target_pairs={{0,1},{1,0},{2,3},{3,2},{4,5},{5,4},{6,7},{7,6},{8,9},{9,8},{10,11... | collective-permute-start | bytes 1327112 | tf_op jit(solution)/shard_map/ppermute | solution.py:582
  67.0 7.7 %collective-permute-start.17 = (bf16[32,32,128]{2,1,0:T(8,128)(2,1)S(1)}, bf16[32,32,128]{2,1,0:T(8,128)(2,1)S(1)}, u32[]{:S(2)}, u32[]{:S(2)}) collective-permute-start(bf16[32,32,128]{2,1,0:T(8,128)(2,1)S(1)} %get-tuple-element.88), channel_id=1, source_target_pairs={{0,2},{2,0},{4,6},{6,4},{8,10},{10,8},{12,14},{14,12},{16,18},{18,... | collective-permute-start | bytes 786440 | tf_op jit(solution)/shard_map/ppermute | solution.py:595
  67.5 7.2 %collective-permute-start.18 = (bf16[32,32,128]{2,1,0:T(8,128)(2,1)S(1)}, bf16[32,32,128]{2,1,0:T(8,128)(2,1)S(1)}, u32[]{:S(2)}, u32[]{:S(2)}) collective-permute-start(bf16[32,32,128]{2,1,0:T(8,128)(2,1)S(1)} %get-tuple-element.90), channel_id=1, source_target_pairs={{0,32},{2,34},{4,36},{6,38},{8,40},{10,42},{12,44},{14,46},{16,48}... | collective-permute-start | bytes 786440 | tf_op jit(solution)/shard_map/ppermute | solution.py:595
  76.0 24.6 %all-to-all-start = ((bf16[64,64,128]{2,1,0:T(8,128)(2,1)}), bf16[64,64,128]{2,1,0:T(8,128)(2,1)S(1)}, u32[]{:S(2)}, u32[]{:S(2)}) async-start(bf16[64,64,128]{2,1,0:T(8,128)(2,1)} %bitcast.4), calls=%async_computation | async-start | bytes 2097152 | tf_op jit(solution)/shard_map/all_to_all | solution.py:599
  84.1 7.1 %copy-start.29 = (bf16[72,512]{1,0:T(8,128)(2,1)S(1)}, bf16[72,512]{1,0:T(8,128)(2,1)}, u32[]{:S(2)}) copy-start(bf16[72,512]{1,0:T(8,128)(2,1)} %copy-done.28) | copy-start | bytes 221188
  84.8 7.3 %copy-start.30 = (f32[16,512]{1,0:T(8,128)}, f32[16,512]{1,0:T(8,128)S(1)}, u32[]{:S(2)}) copy-start(f32[16,512]{1,0:T(8,128)S(1)} %get-tuple-element.94.mcoef) | copy-start | bytes 98308
  84.8 7.3 %copy-start.32 = (f32[4,1536]{1,0:T(4,128)}, f32[4,1536]{1,0:T(4,128)S(1)}, u32[]{:S(2)}) copy-start(f32[4,1536]{1,0:T(4,128)S(1)} %get-tuple-element.95.ccoef) | copy-start | bytes 73732
  84.8 14.6 %collective-permute-start.10 = (bf16[64,512]{1,0:T(8,128)(2,1)S(1)}, bf16[64,512]{1,0:T(8,128)(2,1)S(1)}, u32[]{:S(2)}, u32[]{:S(2)}) collective-permute-start(bf16[64,512]{1,0:T(8,128)(2,1)S(1)} %get-tuple-element.76), channel_id=1, source_target_pairs={{0,16},{1,17},{2,18},{3,19},{4,20},{5,21},{6,22},{7,23},{8,24},{9,... | collective-permute-start | bytes 196616 | tf_op jit(solution)/shard_map/ppermute | solution.py:577
  87.9 11.5 %collective-permute-start.9 = (bf16[64,512]{1,0:T(8,128)(2,1)S(1)}, bf16[64,512]{1,0:T(8,128)(2,1)S(1)}, u32[]{:S(2)}, u32[]{:S(2)}) collective-permute-start(bf16[64,512]{1,0:T(8,128)(2,1)S(1)} %get-tuple-element.75), channel_id=1, source_target_pairs={{0,1},{1,2},{2,3},{3,4},{4,5},{5,6},{6,7},{7,8},{8,9},{9,10},{10,1... | collective-permute-start | bytes 196616 | tf_op jit(solution)/shard_map/ppermute | solution.py:577
  87.9 10.0 %collective-permute-start.11 = (bf16[32,512]{1,0:T(8,128)(2,1)S(1)}, bf16[32,512]{1,0:T(8,128)(2,1)S(1)}, u32[]{:S(2)}, u32[]{:S(2)}) collective-permute-start(bf16[32,512]{1,0:T(8,128)(2,1)S(1)} %get-tuple-element.77), channel_id=1, source_target_pairs={{0,17},{1,18},{2,19},{3,20},{4,21},{5,22},{6,23},{7,24},{8,25},{9,... | collective-permute-start | bytes 98312 | tf_op jit(solution)/shard_map/ppermute | solution.py:577
  91.2 8.2 %copy-start.10 = (bf16[288,288]{1,0:T(8,128)(2,1)S(1)}, bf16[288,288]{1,0:T(8,128)(2,1)}, u32[]{:S(2)}) copy-start(bf16[288,288]{1,0:T(8,128)(2,1)} %constant.78.clone.dx_main) | copy-start | bytes 497668
  91.2 8.2 %copy-start.15 = (bf16[288,160]{1,0:T(8,128)(2,1)S(1)}, bf16[288,160]{1,0:T(8,128)(2,1)}, u32[]{:S(2)}) copy-start(bf16[288,160]{1,0:T(8,128)(2,1)} %constant.79.clone.dx_halo) | copy-start | bytes 276484
  91.2 8.2 %copy-start.27 = (bf16[288,512]{1,0:T(8,128)(2,1)S(1)}, bf16[288,512]{1,0:T(8,128)(2,1)}, u32[]{:S(2)}) copy-start(bf16[288,512]{1,0:T(8,128)(2,1)} %copy-done.26) | copy-start | bytes 884740
  (8 other events, 20.3 us)

commit v8 on v7

--- a/solution.py
+++ b/solution.py
@@ -274,11 +274,11 @@
 
 
 def fine_forward_kernel(
-    place, x_in, side, edge, corner, gain, wqkv, wproj, t_main, t_halo, y_send,
+    place, x_in, side, edge, corner, gain, wqkv, wproj, t_halo, y_send,
     x_out, nm_out, p_out, w_out, y_out, side_out, edge_out, corner_out, mixed,
 ):
     halo = jnp.concatenate([side[...], edge[...], corner[...]], axis=0)
-    x = mm(t_main[...], x_in[...]) + mm(t_halo[...], halo)
+    x = x_in[...].astype(F32) + mm(t_halo[...], halo)
     x_out[...] = x.astype(BF16)
     xhat, _ = normalize(x)
     n = (xhat * gain[...]).astype(BF16)
@@ -301,12 +301,12 @@
 
 
 def coarse_kernel(
-    place, y_in, side, edge, corner, cot_in, cside, cedge, ccorner,
-    mgain, mweight, gain, wqkv, wproj, y_main, y_halo, c_main, c_halo, df_send, out_send,
+    place, y_in, side, edge, corner, dy_in, dmixed,
+    mgain, mweight, gain, wqkv, wproj, y_halo, df_send, out_send,
     y2_out, df_out, side_out, edge_out, corner_out, fac_out, packed, mixed, dpacked, wsave,
 ):
     halo = jnp.concatenate([side[...], edge[...], corner[...]], axis=0)
-    patches = mm(y_main[...], y_in[...]) + mm(y_halo[...], halo)
+    patches = y_in[...].astype(F32) + mm(y_halo[...], halo)
     g = jnp.concatenate([patches[CELLS * i : CELLS * (i + 1)] for i in range(4)], axis=1)
     ghat, ginv = normalize(g)
     mn = (ghat * mgain[...]).astype(BF16)
@@ -325,12 +325,10 @@
     y2 = (z + mm(m, wproj[...])).astype(BF16)
     y2_out[...] = y2
 
-    chalo = jnp.concatenate([cside[...], cedge[...], ccorner[...]], axis=0)
-    dy = mm(c_main[...], cot_in[...].astype(BF16)) + mm(c_halo[...], chalo)
-    mixed[...] = rounded(mm_nt(dy.astype(BF16), wproj[...]))
+    dy = dy_in[...].astype(F32)
     for p in range(HC // 2):
         q, k, v = (packed[:, pl.ds(512 * part + 128 * p, 128)] for part in range(3))
-        grads = attend_back(q, stacked(k), stacked(v), wsave[p], differ, mixed[:, pl.ds(128 * p, 128)])
+        grads = attend_back(q, stacked(k), stacked(v), wsave[p], differ, dmixed[:, pl.ds(128 * p, 128)])
         for part in range(3):
             dpacked[:, pl.ds(512 * part + 128 * p, 128)] = grads[part]
     dp = dpacked[...].astype(BF16)
@@ -347,6 +345,18 @@
         fac_out[pl.ds(0, CELLS), pl.ds(at, piece.shape[1])] = piece
         at += piece.shape[1]
     fac_out[pl.ds(CELLS, TALL - CELLS), :] = jnp.zeros((TALL - CELLS, at), BF16)
+
+
+def own_rows_kernel(rows, main, out):
+    out[...] = mm(main[...], rows[...]).astype(BF16)
+
+
+def before_coarse_kernel(y_in, y_main, cot_in, side, edge, corner, c_main, c_halo, wproj, y_out, dy_out, dmixed):
+    y_out[...] = mm(y_main[...], y_in[...]).astype(BF16)
+    halo = jnp.concatenate([side[...], edge[...], corner[...]], axis=0)
+    dy = (mm(c_main[...], cot_in[...].astype(BF16)) + mm(c_halo[...], halo)).astype(BF16)
+    dy_out[...] = dy
+    dmixed[...] = rounded(mm_nt(dy, wproj[...]))
 
 
 def fine_backward_kernel(
@@ -512,9 +522,9 @@
         out[r] = y[16 * r : 16 * r + 12].astype(BF16)
 
 
-def tokens_kernel(dx, side, edge, corner, dx_main, dx_halo, grad):
+def tokens_kernel(dx, side, edge, corner, dx_halo, grad):
     halo = jnp.concatenate([side[...], edge[...], corner[...]], axis=0)
-    d = mm(dx_main[...], dx[...]) + mm(dx_halo[...], halo)
+    d = dx[...].astype(F32) + mm(dx_halo[...], halo)
     grad[...] = d.reshape(ROWS, COLS, D).astype(BF16)
 
 
@@ -629,6 +639,7 @@
         ],
     )
     ahead = exchange(sent, -1)
+    (tok,) = call(own_rows_kernel, [((cells, D), BF16)], tok, table("tok_main"))
     x, nm, p, w, y, *sent = scalar_call(
         fine_forward_kernel,
         [
@@ -636,16 +647,21 @@
             ((cells, D), BF16),
         ]
         + narrow,
-        place, tok, *ahead, fgain, fine_qkv, fine_proj, table("tok_main"), table("tok_halo"), table("y_send"),
+        place, tok, *ahead, fgain, fine_qkv, fine_proj, table("tok_halo"), table("y_send"),
         scratch=[pltpu.VMEM((cells, 256), F32)],
     )
     merged = exchange(sent, -1)
+    y, dy, dmixed = call(
+        before_coarse_kernel,
+        [((cells, D), BF16), ((CELLS, D), BF16), ((CELLS, D), F32)],
+        y, table("y_main"), cot, *ahead, table("cot_main"), table("cot_halo"), coarse_proj,
+    )
     nm_other = partner(nm)
     y2, df, *sent, fac = scalar_call(
         coarse_kernel,
         [((CELLS, D), BF16), ((cells, D), BF16)] + pieces + [((TALL, 5632), BF16)],
-        place, y, *merged, cot, *ahead, mgain, merge_weight, cgain, coarse_qkv, coarse_proj,
-        table("y_main"), table("y_halo"), table("cot_main"), table("cot_halo"), table("df_send"), table("out_send"),
+        place, y, *merged, dy, dmixed, mgain, merge_weight, cgain, coarse_qkv, coarse_proj,
+        table("y_halo"), table("df_send"), table("out_send"),
         scratch=[
             pltpu.VMEM((CELLS, 1536), F32), pltpu.VMEM((CELLS, D), F32), pltpu.VMEM((CELLS, 1536), F32),
             pltpu.VMEM((4, CELLS, 256), F32),
@@ -656,7 +672,7 @@
         coarse_weights_kernel,
         [((32, 32, 128), BF16)] * 8,
         place, fac, partner(fac),
-        scratch=[pltpu.VMEM((4096, 128), F32)],
+        scratch=[pltpu.VMEM((4104, 128), F32)],
     )
     first = [
         fold(v, axis, second)
@@ -679,7 +695,7 @@
         fine_weights_kernel,
         [((64, 32, 128), BF16)],
         place, nm, nm_other, fac, partner(fac),
-        scratch=[pltpu.VMEM((2048, 128), F32)],
+        scratch=[pltpu.VMEM((2056, 128), F32)],
     )
     (joined,) = scalar_call(
         join_kernel,
@@ -688,7 +704,8 @@
     )
     parts = deal(joined.reshape(64, 64, 128)).reshape(2, 2, 8, 2, 64, 128)
     (output,) = call(output_kernel, [((6, 12, D), BF16)], y2, *back, table("out_main"), table("out_halo"))
-    (grad,) = call(tokens_kernel, [((ROWS, COLS, D), BF16)], dx, *ended, table("dx_main"), table("dx_halo"))
+    (dx,) = call(own_rows_kernel, [((cells, D), BF16)], dx, table("dx_main"))
+    (grad,) = call(tokens_kernel, [((ROWS, COLS, D), BF16)], dx, *ended, table("dx_halo"))
     fcoef, mcoef, ccoef = scalar_call(
         coefficients_kernel,
         [((4, 768), F32), ((16, D), F32), ((4, 1536), F32)],

time: 103 us -> 105 us (1.019); the launches traced: 101 us -> 105 us
  waiting for transfers between devices: 40.2 us -> 46.3 us
  local copies, waits for them, and re-layouts: 4.05 us -> 0.66 us
    all_to_all x1, waiting for transfers between devices: 0.01 us -> 15.4 us  [deal(): return lax.all_to_all(value, ('lat', 'pair'), 0, 0)]
    ppermute x12, waiting for transfers between devices: 26.6 us -> 18 us  [exchange(): arrived.append(lax.ppermute(piece, ('lat', 'pair', 'core'), pairs))]
    all_to_all x1, starting transfers between devices: 5.6 us -> 9.46 us  [deal(): return lax.all_to_all(value, ('lat', 'pair'), 0, 0)]
    ppermute x12, starting transfers between devices: 22.5 us -> 19.1 us  [exchange(): arrived.append(lax.ppermute(piece, ('lat', 'pair', 'core'), pairs))]
    unnamed x68 -> x48, local copies, waits for them, and re-layouts: 4.05 us -> 0.66 us
    pallas_call x12 -> x15, Pallas kernels: 23.3 us -> 23.7 us  [call(): pl.pallas_call(kernel, out_shape=[jax.ShapeDtypeStruct(s, d) for s, d in...]
  transfers between devices with their start and end apart: 22 -> 22, of which waited for: 11 -> 10; matrix products, arithmetic and copies ran while one was open for 0% -> 0% of each run, Pallas kernels for 9% -> 11%
where the time goes in v8:
time: 105 us
  waiting for transfers between devices  46.3 us (44%)
  starting transfers between devices  32.9 us (31%)
  Pallas kernels  23.7 us (23%)
  between operations  1.11 us (1%)
    pallas_call x15, Pallas kernels, call(): pl.pallas_call(kernel, out_shape=[jax.ShapeDtypeStruct(s, d) for s, d in...  23.7 us
    ppermute x12, starting transfers between devices, exchange(): arrived.append(lax.ppermute(piece, ('lat', 'pair', 'core'), pairs))  19.1 us
    ppermute x12, waiting for transfers between devices, exchange(): arrived.append(lax.ppermute(piece, ('lat', 'pair', 'core'), pairs))  18 us
    all_to_all x1, waiting for transfers between devices, deal(): return lax.all_to_all(value, ('lat', 'pair'), 0, 0)  15.4 us
    ppermute x6, waiting for transfers between devices, fold(): return lax.ppermute(value, ('lat', 'pair'), pairs)  12.9 us
    all_to_all x1, starting transfers between devices, deal(): return lax.all_to_all(value, ('lat', 'pair'), 0, 0)  9.46 us
    ppermute x6, starting transfers between devices, fold(): return lax.ppermute(value, ('lat', 'pair'), pairs)  4.02 us
  transfers between devices with their start and end apart: 22, of which 10 were waited for; matrix products, arithmetic and copies ran while one was open for 0% of the time, Pallas kernels for 11%

profile of v8, /device:TPU:0, one launch (start us, length us, event | category | flops | bytes accessed | tf_op | source)
XLA Modules:
  0.0 104.7 jit_solution(12063916529606183885)
XLA Ops:
  0.7 0.0 copy-start.11
  0.7 1.5 %shard_map.339 = (bf16[288,512]{1,0:T(8,128)(2,1)S(1)}, bf16[80,512]{1,0:T(8,128)(2,1)S(1)}, bf16[80,512]{1,0:T(8,128)(2,1)S(1)}, bf16[48,512]{1,0:T(8,128)(2,1)S(1)}, f32[72,512]{1,0:T(8,128)S(1)}) custom-call(s32[1]{0:T(128)} %bitcast.place, bf16[12,24,512]{2,1,0:T(8,128)(2,1)} %tok_in.1, bf16[6,12,512]{2,1,0:T(8,128)(2,1)} %cot_in.1, ...), custom_call_target="tpu_custom_call" | custom-call | flops 5000000000 | bytes 4000000 | tf_op jit(solution)/shard_map/pallas_call | solution.py:162
  2.1 3.4 %collective-permute-start = (bf16[80,512]{1,0:T(8,128)(2,1)S(1)}, bf16[80,512]{1,0:T(8,128)(2,1)S(1)}, u32[]{:S(2)}, u32[]{:S(2)}) collective-permute-start(bf16[80,512]{1,0:T(8,128)(2,1)S(1)} %get-tuple-element.61), channel_id=1, source_target_pairs={{0,15},{1,0},{2,1},{3,2},{4,3},{5,4},{6,5},{7,6},{8,7},{9,8},{10,9... | collective-permute-start | bytes 245768 | tf_op jit(solution)/shard_map/ppermute | solution.py:587
  5.5 6.4 %collective-permute-start.1 = (bf16[80,512]{1,0:T(8,128)(2,1)S(1)}, bf16[80,512]{1,0:T(8,128)(2,1)S(1)}, u32[]{:S(2)}, u32[]{:S(2)}) collective-permute-start(bf16[80,512]{1,0:T(8,128)(2,1)S(1)} %get-tuple-element.62), channel_id=1, source_target_pairs={{0,112},{1,113},{2,114},{3,115},{4,116},{5,117},{6,118},{7,119},{8... | collective-permute-start | bytes 245768 | tf_op jit(solution)/shard_map/ppermute | solution.py:587
  11.9 0.2 collective-permute-start.2
  12.1 0.0 copy-start.16
  12.1 0.3 shard_map.340.x_in
  12.4 4.5 %collective-permute-done.2.corner = bf16[48,512]{1,0:T(8,128)(2,1)S(1)} collective-permute-done((bf16[48,512]{1,0:T(8,128)(2,1)S(1)}, bf16[48,512]{1,0:T(8,128)(2,1)S(1)}, u32[]{:S(2)}, u32[]{:S(2)}) %collective-permute-start.2) | collective-permute-done | bytes 49184 | tf_op jit(solution)/shard_map/ppermute | solution.py:587
  17.0 0.0 copy-start.10
  17.0 0.0 copy-start.21
  17.0 3.8 %shard_map.341 = (bf16[288,512]{1,0:T(8,128)(2,1)S(1)}, bf16[288,768]{1,0:T(8,128)(2,1)S(1)}, f32[288,768]{1,0:T(8,128)S(1)}, f32[8,72,256]{2,1,0:T(8,128)S(1)},...) custom-call(s32[1]{0:T(128)} %bitcast.place, ...), custom_call_target="tpu_custom_call" | custom-call | flops 5000000000 | bytes 4000000 | tf_op jit(solution)/shard_map/pallas_call | solution.py:162
  20.8 0.5 collective-permute-start.3
  21.3 5.1 %collective-permute-start.4 = (bf16[64,512]{1,0:T(8,128)(2,1)S(1)}, bf16[64,512]{1,0:T(8,128)(2,1)S(1)}, u32[]{:S(2)}, u32[]{:S(2)}) collective-permute-start(bf16[64,512]{1,0:T(8,128)(2,1)S(1)} %get-tuple-element.68), channel_id=1, source_target_pairs={{0,112},{1,113},{2,114},{3,115},{4,116},{5,117},{6,118},{7,119},{8... | collective-permute-start | bytes 196616 | tf_op jit(solution)/shard_map/ppermute | solution.py:587
  26.5 0.6 shard_map.342
  27.1 4.2 %collective-permute-done.5.corner = bf16[32,512]{1,0:T(8,128)(2,1)S(1)} collective-permute-done((bf16[32,512]{1,0:T(8,128)(2,1)S(1)}, bf16[32,512]{1,0:T(8,128)(2,1)S(1)}, u32[]{:S(2)}, u32[]{:S(2)}) %collective-permute-start.5) | collective-permute-done | bytes 32800 | tf_op jit(solution)/shard_map/ppermute | solution.py:587
  31.4 6.0 %shard_map.343 = (bf16[72,512]{1,0:T(8,128)(2,1)S(1)}, bf16[288,512]{1,0:T(8,128)(2,1)S(1)}, bf16[80,512]{1,0:T(8,128)(2,1)S(1)}, bf16[80,512]{1,0:T(8,128)(2,1)...) custom-call(s32[1]{0:T(128)} %bitcast.place, bf16[288,512]{1,0:T(8,128)(2,1)S(1)} %get-tuple-element.66.y_in, ...), custom_call_target="tpu_custom_call" | custom-call | flops 5000000000 | bytes 4000000 | tf_op jit(solution)/shard_map/pallas_call | solution.py:162
  37.4 0.1 collective-permute-start.12
  37.5 0.5 collective-permute-start.6
  38.0 0.4 collective-permute-start.7
  38.4 9.3 %collective-permute-done.8.corner = bf16[48,512]{1,0:T(8,128)(2,1)S(1)} collective-permute-done((bf16[48,512]{1,0:T(8,128)(2,1)S(1)}, bf16[48,512]{1,0:T(8,128)(2,1)S(1)}, u32[]{:S(2)}, u32[]{:S(2)}) %collective-permute-start.8) | collective-permute-done | bytes 49184 | tf_op jit(solution)/shard_map/ppermute | solution.py:587
  47.7 3.5 %shard_map.345 = (bf16[288,512]{1,0:T(8,128)(2,1)S(1)}, bf16[64,512]{1,0:T(8,128)(2,1)S(1)}, bf16[64,512]{1,0:T(8,128)(2,1)S(1)}, bf16[32,512]{1,0:T(8,128)(2,1)S(1)}, bf16[288,1280]{1,0:T(8,128)(2,1)S(1)}) custom-call(s32[1]{0:T(128)} %bitcast.place, bf16[288,512]{1,0:T(8,128)(2,1)S(1)} %get-tuple-element.76.df_in, ...), custom_call_target="tpu_custom_call" | custom-call | flops 5000000000 | bytes 4000000 | tf_op jit(solution)/shard_map/pallas_call | solution.py:162
  51.3 0.3 collective-permute-start.20
  51.5 1.8 %shard_map.348 = (bf16[32,32,128]{2,1,0:T(8,128)(2,1)S(1)}, bf16[32,32,128]{2,1,0:T(8,128)(2,1)S(1)}, bf16[32,32,128]{2,1,0:T(8,128)(2,1)S(1)}, bf16[32,32,128]{...) custom-call(s32[1]{0:T(128)} %bitcast.place, ...), custom_call_target="tpu_custom_call" | custom-call | flops 5000000000 | bytes 4000000 | tf_op jit(solution)/shard_map/pallas_call | solution.py:162
  53.4 0.1 collective-permute-start.13
  53.4 0.1 collective-permute-start.14
  53.5 1.7 %collective-permute-start.15 = (bf16[32,32,128]{2,1,0:T(8,128)(2,1)S(1)}, bf16[32,32,128]{2,1,0:T(8,128)(2,1)S(1)}, u32[]{:S(2)}, u32[]{:S(2)}) collective-permute-start(bf16[32,32,128]{2,1,0:T(8,128)(2,1)S(1)} %get-tuple-element.90), channel_id=1, source_target_pairs={{0,96},{2,98},{4,100},{6,102},{8,104},{10,106},{12,108},{14,110},{... | collective-permute-start | bytes 786440 | tf_op jit(solution)/shard_map/ppermute | solution.py:605
  55.2 1.0 collective-permute-start.16
  56.2 0.7 shard_map.352
  56.9 5.2 %collective-permute-done.13.m0c = bf16[32,32,128]{2,1,0:T(8,128)(2,1)S(1)} collective-permute-done((bf16[32,32,128]{2,1,0:T(8,128)(2,1)S(1)}, bf16[32,32,128]{2,1,0:T(8,128)(2,1)S(1)}, u32[]{:S(2)}, u32[]{:S(2)}) %collective-permute-start.13) | collective-permute-done | bytes 262176 | tf_op jit(solution)/shard_map/ppermute | solution.py:605
  62.1 0.1 collective-permute-done.14.m1c
  62.2 1.3 %collective-permute-done.15.c0c = bf16[32,32,128]{2,1,0:T(8,128)(2,1)S(1)} collective-permute-done((bf16[32,32,128]{2,1,0:T(8,128)(2,1)S(1)}, bf16[32,32,128]{2,1,0:T(8,128)(2,1)S(1)}, u32[]{:S(2)}, u32[]{:S(2)}) %collective-permute-start.15) | collective-permute-done | bytes 262176 | tf_op jit(solution)/shard_map/ppermute | solution.py:605
  63.5 1.3 %collective-permute-done.16.c1c = bf16[32,32,128]{2,1,0:T(8,128)(2,1)S(1)} collective-permute-done((bf16[32,32,128]{2,1,0:T(8,128)(2,1)S(1)}, bf16[32,32,128]{2,1,0:T(8,128)(2,1)S(1)}, u32[]{:S(2)}, u32[]{:S(2)}) %collective-permute-start.16) | collective-permute-done | bytes 262176 | tf_op jit(solution)/shard_map/ppermute | solution.py:605
  64.9 2.6 %collective-permute-start.11 = (bf16[32,512]{1,0:T(8,128)(2,1)S(1)}, bf16[32,512]{1,0:T(8,128)(2,1)S(1)}, u32[]{:S(2)}, u32[]{:S(2)}) collective-permute-start(bf16[32,512]{1,0:T(8,128)(2,1)S(1)} %get-tuple-element.83), channel_id=1, source_target_pairs={{0,17},{1,18},{2,19},{3,20},{4,21},{5,22},{6,23},{7,24},{8,25},{9,... | collective-permute-start | bytes 98312 | tf_op jit(solution)/shard_map/ppermute | solution.py:587
  67.5 0.2 shard_map.349
  67.7 0.1 collective-permute-start.17
  67.8 1.1 %collective-permute-start.18 = (bf16[32,32,128]{2,1,0:T(8,128)(2,1)S(1)}, bf16[32,32,128]{2,1,0:T(8,128)(2,1)S(1)}, u32[]{:S(2)}, u32[]{:S(2)}) collective-permute-start(bf16[32,32,128]{2,1,0:T(8,128)(2,1)S(1)} %get-tuple-element.96), channel_id=1, source_target_pairs={{0,32},{2,34},{4,36},{6,38},{8,40},{10,42},{12,44},{14,46},{16,48}... | collective-permute-start | bytes 786440 | tf_op jit(solution)/shard_map/ppermute | solution.py:605
  68.9 1.2 %shard_map.350.fine = bf16[64,32,128]{2,1,0:T(8,128)(2,1)S(1)} custom-call(s32[1]{0:T(128)} %bitcast.place, bf16[288,768]{1,0:T(8,128)(2,1)S(1)} %get-tuple-element.97.nm_own, bf16[288,768]{1,0:T(8,128)(2,1)S(1)} %collective-permute-done.19.nm_other, bf16[288,1280]{1,0:T(8,128)(2,1)S(1)} %get-tuple-element.98.own, ...), custom_call_target="tpu_custom_call" | custom-call | flops 5000000000 | bytes 4000000 | tf_op jit(solution)/shard_map/pallas_call | solution.py:162
  70.1 4.9 %collective-permute-done.17.yc = bf16[32,32,128]{2,1,0:T(8,128)(2,1)S(1)} collective-permute-done((bf16[32,32,128]{2,1,0:T(8,128)(2,1)S(1)}, bf16[32,32,128]{2,1,0:T(8,128)(2,1)S(1)}, u32[]{:S(2)}, u32[]{:S(2)}) %collective-permute-start.17) | collective-permute-done | bytes 262176 | tf_op jit(solution)/shard_map/ppermute | solution.py:605
  75.0 0.1 collective-permute-done.18.zc
  75.1 1.2 %shard_map.351 = bf16[2,2,8,2,64,128]{5,4,3,2,1,0:T(8,128)(2,1)} custom-call(s32[1]{0:T(128)} %bitcast.place, bf16[32,32,128]{2,1,0:T(8,128)(2,1)S(1)} %get-tuple-element.93.yk, bf16[32,32,128]{2,1,0:T(8,128)(2,1)S(1)} %collective-permute-done.17.yc, bf16[32,32,128]{2,1,0:T(8,128)(2,1)S(1)} %get-tuple-element.95.zk, ...), custom_call_target="tpu_custom_call" | custom-call | flops 5000000000 | bytes 4000000 | tf_op jit(solution)/shard_map/pallas_call | solution.py:162
  76.3 9.5 %all-to-all-start = ((bf16[64,64,128]{2,1,0:T(8,128)(2,1)}), bf16[64,64,128]{2,1,0:T(8,128)(2,1)S(1)}, u32[]{:S(2)}, u32[]{:S(2)}) async-start(bf16[64,64,128]{2,1,0:T(8,128)(2,1)} %bitcast.4), calls=%async_computation | async-start | bytes 2097152 | tf_op jit(solution)/shard_map/all_to_all | solution.py:609
  85.8 0.3 shard_map.346.dx
  86.1 0.5 copy-done.20
  86.6 0.8 shard_map.344
  87.4 0.1 copy-done.13
  87.5 0.9 shard_map.347
  88.4 15.4 %all-to-all-done = bf16[64,64,128]{2,1,0:T(8,128)(2,1)S(1)} async-done(((bf16[64,64,128]{2,1,0:T(8,128)(2,1)}), bf16[64,64,128]{2,1,0:T(8,128)(2,1)S(1)}, u32[]{:S(2)}, u32[]{:S(2)}) %all-to-all-start) | async-done | bytes 1048608 | tf_op jit(solution)/shard_map/all_to_all | solution.py:609
  103.9 0.8 shard_map.353
  (59 shorter events, 0.2 us)
Async XLA Ops:
  0.7 11.4 %copy-start.11 = (bf16[288,288]{1,0:T(8,128)(2,1)S(1)}, bf16[288,288]{1,0:T(8,128)(2,1)}, u32[]{:S(2)}) copy-start(bf16[288,288]{1,0:T(8,128)(2,1)} %constant.64.clone.main) | copy-start | bytes 497668
  2.1 14.8 %collective-permute-start = (bf16[80,512]{1,0:T(8,128)(2,1)S(1)}, bf16[80,512]{1,0:T(8,128)(2,1)S(1)}, u32[]{:S(2)}, u32[]{:S(2)}) collective-permute-start(bf16[80,512]{1,0:T(8,128)(2,1)S(1)} %get-tuple-element.61), channel_id=1, source_target_pairs={{0,15},{1,0},{2,1},{3,2},{4,3},{5,4},{6,5},{7,6},{8,7},{9,8},{10,9... | collective-permute-start | bytes 245768 | tf_op jit(solution)/shard_map/ppermute | solution.py:587
  5.5 11.4 %collective-permute-start.1 = (bf16[80,512]{1,0:T(8,128)(2,1)S(1)}, bf16[80,512]{1,0:T(8,128)(2,1)S(1)}, u32[]{:S(2)}, u32[]{:S(2)}) collective-permute-start(bf16[80,512]{1,0:T(8,128)(2,1)S(1)} %get-tuple-element.62), channel_id=1, source_target_pairs={{0,112},{1,113},{2,114},{3,115},{4,116},{5,117},{6,118},{7,119},{8... | collective-permute-start | bytes 245768 | tf_op jit(solution)/shard_map/ppermute | solution.py:587
  11.9 5.0 %collective-permute-start.2 = (bf16[48,512]{1,0:T(8,128)(2,1)S(1)}, bf16[48,512]{1,0:T(8,128)(2,1)S(1)}, u32[]{:S(2)}, u32[]{:S(2)}) collective-permute-start(bf16[48,512]{1,0:T(8,128)(2,1)S(1)} %get-tuple-element.63), channel_id=1, source_target_pairs={{0,127},{1,112},{2,113},{3,114},{4,115},{5,116},{6,117},{7,118},{8... | collective-permute-start | bytes 147464 | tf_op jit(solution)/shard_map/ppermute | solution.py:587
  12.1 4.9 %copy-start.2 = (bf16[512,768]{1,0:T(8,128)(2,1)S(1)}, bf16[512,768]{1,0:T(8,128)(2,1)}, u32[]{:S(2)}) copy-start(bf16[512,768]{1,0:T(8,128)(2,1)} %fqkv.1) | copy-start | bytes 2359300
  12.1 4.9 %copy-start.4 = (bf16[256,512]{1,0:T(8,128)(2,1)S(1)}, bf16[256,512]{1,0:T(8,128)(2,1)}, u32[]{:S(2)}) copy-start(bf16[256,512]{1,0:T(8,128)(2,1)} %wproj.7) | copy-start | bytes 786436
  12.1 4.9 %copy-start.6 = (f32[512]{0:T(512)S(1)}, f32[512]{0:T(512)}, u32[]{:S(2)}) copy-start(f32[512]{0:T(512)} %param.29) | copy-start | bytes 6148
  12.1 4.9 %copy-start.16 = (bf16[288,208]{1,0:T(8,128)(2,1)S(1)}, bf16[288,208]{1,0:T(8,128)(2,1)}, u32[]{:S(2)}) copy-start(bf16[288,208]{1,0:T(8,128)(2,1)} %constant.65.clone.t_halo) | copy-start | bytes 359428
  12.1 4.9 %copy-start.18 = (bf16[160,288]{1,0:T(8,128)(2,1)S(1)}, bf16[160,288]{1,0:T(8,128)(2,1)}, u32[]{:S(2)}) copy-start(bf16[160,288]{1,0:T(8,128)(2,1)} %constant.66.clone.y_send) | copy-start | bytes 276484
  17.0 9.4 %copy-start.3 = (bf16[512,512]{1,0:T(8,128)(2,1)S(1)}, bf16[512,512]{1,0:T(8,128)(2,1)}, u32[]{:S(2)}) copy-start(bf16[512,512]{1,0:T(8,128)(2,1)} %wproj.6) | copy-start | bytes 1572868
  17.0 9.4 %copy-start.10 = (bf16[288,288]{1,0:T(8,128)(2,1)S(1)}, bf16[288,288]{1,0:T(8,128)(2,1)}, u32[]{:S(2)}) copy-start(bf16[288,288]{1,0:T(8,128)(2,1)} %constant.67.clone.y_main) | copy-start | bytes 497668
  17.0 9.4 %copy-start.21 = (bf16[72,208]{1,0:T(8,128)(2,1)S(1)}, bf16[72,208]{1,0:T(8,128)(2,1)}, u32[]{:S(2)}) copy-start(bf16[72,208]{1,0:T(8,128)(2,1)} %constant.69.clone.c_halo) | copy-start | bytes 89860
  17.0 9.4 %copy-start.23 = (bf16[72,72]{1,0:T(8,128)(2,1)S(1)}, bf16[72,72]{1,0:T(8,128)(2,1)}, u32[]{:S(2)}) copy-start(bf16[72,72]{1,0:T(8,128)(2,1)} %constant.68.clone.c_main) | copy-start | bytes 31108
  20.8 10.5 %collective-permute-start.3 = (bf16[64,512]{1,0:T(8,128)(2,1)S(1)}, bf16[64,512]{1,0:T(8,128)(2,1)S(1)}, u32[]{:S(2)}, u32[]{:S(2)}) collective-permute-start(bf16[64,512]{1,0:T(8,128)(2,1)S(1)} %get-tuple-element.67), channel_id=1, source_target_pairs={{0,15},{1,0},{2,1},{3,2},{4,3},{5,4},{6,5},{7,6},{8,7},{9,8},{10,9... | collective-permute-start | bytes 196616 | tf_op jit(solution)/shard_map/ppermute | solution.py:587
  21.3 10.0 %collective-permute-start.4 = (bf16[64,512]{1,0:T(8,128)(2,1)S(1)}, bf16[64,512]{1,0:T(8,128)(2,1)S(1)}, u32[]{:S(2)}, u32[]{:S(2)}) collective-permute-start(bf16[64,512]{1,0:T(8,128)(2,1)S(1)} %get-tuple-element.68), channel_id=1, source_target_pairs={{0,112},{1,113},{2,114},{3,115},{4,116},{5,117},{6,118},{7,119},{8... | collective-permute-start | bytes 196616 | tf_op jit(solution)/shard_map/ppermute | solution.py:587
  26.4 4.8 %collective-permute-start.5 = (bf16[32,512]{1,0:T(8,128)(2,1)S(1)}, bf16[32,512]{1,0:T(8,128)(2,1)S(1)}, u32[]{:S(2)}, u32[]{:S(2)}) collective-permute-start(bf16[32,512]{1,0:T(8,128)(2,1)S(1)} %get-tuple-element.69), channel_id=1, source_target_pairs={{0,127},{1,112},{2,113},{3,114},{4,115},{5,116},{6,117},{7,118},{8... | collective-permute-start | bytes 98312 | tf_op jit(solution)/shard_map/ppermute | solution.py:587
  26.5 4.8 %copy-start = (bf16[2048,512]{1,0:T(8,128)(2,1)S(1)}, bf16[2048,512]{1,0:T(8,128)(2,1)}, u32[]{:S(2)}) copy-start(bf16[2048,512]{1,0:T(8,128)(2,1)} %mweight.3) | copy-start | bytes 6291460
  26.5 4.8 %copy-start.1 = (bf16[512,1536]{1,0:T(8,128)(2,1)S(1)}, bf16[512,1536]{1,0:T(8,128)(2,1)}, u32[]{:S(2)}) copy-start(bf16[512,1536]{1,0:T(8,128)(2,1)} %cqkv.1) | copy-start | bytes 4718596
  26.5 4.8 %copy-start.5 = (f32[2048]{0:T(1024)S(1)}, f32[2048]{0:T(1024)}, u32[]{:S(2)}) copy-start(f32[2048]{0:T(1024)} %param.32) | copy-start | bytes 24580
  26.5 4.8 %copy-start.7 = (f32[512]{0:T(512)S(1)}, f32[512]{0:T(512)}, u32[]{:S(2)}) copy-start(f32[512]{0:T(512)} %param.34) | copy-start | bytes 6148
  26.5 4.8 %copy-start.12 = (bf16[208,288]{1,0:T(8,128)(2,1)S(1)}, bf16[208,288]{1,0:T(8,128)(2,1)}, u32[]{:S(2)}) copy-start(bf16[208,288]{1,0:T(8,128)(2,1)} %constant.71.clone.df_send) | copy-start | bytes 359428
  26.5 4.8 %copy-start.15 = (bf16[288,160]{1,0:T(8,128)(2,1)S(1)}, bf16[288,160]{1,0:T(8,128)(2,1)}, u32[]{:S(2)}) copy-start(bf16[288,160]{1,0:T(8,128)(2,1)} %constant.70.clone.y_halo) | copy-start | bytes 276484
  26.5 4.8 %copy-start.19 = (bf16[208,72]{1,0:T(8,128)(2,1)S(1)}, bf16[208,72]{1,0:T(8,128)(2,1)}, u32[]{:S(2)}) copy-start(bf16[208,72]{1,0:T(8,128)(2,1)} %constant.72.clone.out_send) | copy-start | bytes 89860
  31.3 16.4 %copy-start.9 = (bf16[288,288]{1,0:T(8,128)(2,1)S(1)}, bf16[288,288]{1,0:T(8,128)(2,1)}, u32[]{:S(2)}) copy-start(bf16[288,288]{1,0:T(8,128)(2,1)} %constant.73.clone.d_main) | copy-start | bytes 497668
  31.4 16.4 %copy-start.14 = (bf16[288,208]{1,0:T(8,128)(2,1)S(1)}, bf16[288,208]{1,0:T(8,128)(2,1)}, u32[]{:S(2)}) copy-start(bf16[288,208]{1,0:T(8,128)(2,1)} %constant.74.clone.d_halo) | copy-start | bytes 359428
  31.4 16.4 %copy-start.17 = (bf16[160,288]{1,0:T(8,128)(2,1)S(1)}, bf16[160,288]{1,0:T(8,128)(2,1)}, u32[]{:S(2)}) copy-start(bf16[160,288]{1,0:T(8,128)(2,1)} %constant.75.clone.dx_send) | copy-start | bytes 276484
  37.4 14.1 %collective-permute-start.12 = (bf16[80,5632]{1,0:T(8,128)(2,1)S(1)}, bf16[80,5632]{1,0:T(8,128)(2,1)S(1)}, u32[]{:S(2)}, u32[]{:S(2)}) collective-permute-start(bf16[80,5632]{1,0:T(8,128)(2,1)S(1)} %get-tuple-element.84.own), channel_id=1, source_target_pairs={{0,1},{1,0},{2,3},{3,2},{4,5},{5,4},{6,7},{7,6},{8,9},{9,8},{10,11... | collective-permute-start | bytes 2703368 | tf_op jit(solution)/shard_map/ppermute | solution.py:592
  37.5 10.2 %collective-permute-start.6 = (bf16[80,512]{1,0:T(8,128)(2,1)S(1)}, bf16[80,512]{1,0:T(8,128)(2,1)S(1)}, u32[]{:S(2)}, u32[]{:S(2)}) collective-permute-start(bf16[80,512]{1,0:T(8,128)(2,1)S(1)} %get-tuple-element.73), channel_id=1, source_target_pairs={{0,1},{1,2},{2,3},{3,4},{4,5},{5,6},{6,7},{7,8},{8,9},{9,10},{10,1... | collective-permute-start | bytes 245768 | tf_op jit(solution)/shard_map/ppermute | solution.py:587
  38.0 9.7 %collective-permute-start.7 = (bf16[80,512]{1,0:T(8,128)(2,1)S(1)}, bf16[80,512]{1,0:T(8,128)(2,1)S(1)}, u32[]{:S(2)}, u32[]{:S(2)}) collective-permute-start(bf16[80,512]{1,0:T(8,128)(2,1)S(1)} %get-tuple-element.74), channel_id=1, source_target_pairs={{0,16},{1,17},{2,18},{3,19},{4,20},{5,21},{6,22},{7,23},{8,24},{9,... | collective-permute-start | bytes 245768 | tf_op jit(solution)/shard_map/ppermute | solution.py:587
  38.4 9.3 %collective-permute-start.8 = (bf16[48,512]{1,0:T(8,128)(2,1)S(1)}, bf16[48,512]{1,0:T(8,128)(2,1)S(1)}, u32[]{:S(2)}, u32[]{:S(2)}) collective-permute-start(bf16[48,512]{1,0:T(8,128)(2,1)S(1)} %get-tuple-element.75), channel_id=1, source_target_pairs={{0,17},{1,18},{2,19},{3,20},{4,21},{5,22},{6,23},{7,24},{8,25},{9,... | collective-permute-start | bytes 147464 | tf_op jit(solution)/shard_map/ppermute | solution.py:587
  51.3 16.6 %collective-permute-start.20 = (bf16[288,1280]{1,0:T(8,128)(2,1)S(1)}, bf16[288,1280]{1,0:T(8,128)(2,1)S(1)}, u32[]{:S(2)}, u32[]{:S(2)}) collective-permute-start(bf16[288,1280]{1,0:T(8,128)(2,1)S(1)} %get-tuple-element.98.own), channel_id=1, source_target_pairs={{0,1},{1,0},{2,3},{3,2},{4,5},{5,4},{6,7},{7,6},{8,9},{9,8},{10,11... | collective-permute-start | bytes 2211848 | tf_op jit(solution)/shard_map/ppermute | solution.py:592
  53.4 8.8 %collective-permute-start.13 = (bf16[32,32,128]{2,1,0:T(8,128)(2,1)S(1)}, bf16[32,32,128]{2,1,0:T(8,128)(2,1)S(1)}, u32[]{:S(2)}, u32[]{:S(2)}) collective-permute-start(bf16[32,32,128]{2,1,0:T(8,128)(2,1)S(1)} %get-tuple-element.86), channel_id=1, source_target_pairs={{0,32},{2,34},{4,36},{6,38},{8,40},{10,42},{12,44},{14,46},{16,48}... | collective-permute-start | bytes 786440 | tf_op jit(solution)/shard_map/ppermute | solution.py:605
  53.4 8.8 %collective-permute-start.14 = (bf16[32,32,128]{2,1,0:T(8,128)(2,1)S(1)}, bf16[32,32,128]{2,1,0:T(8,128)(2,1)S(1)}, u32[]{:S(2)}, u32[]{:S(2)}) collective-permute-start(bf16[32,32,128]{2,1,0:T(8,128)(2,1)S(1)} %get-tuple-element.88), channel_id=1, source_target_pairs={{0,2},{2,0},{4,6},{6,4},{8,10},{10,8},{12,14},{14,12},{16,18},{18,... | collective-permute-start | bytes 786440 | tf_op jit(solution)/shard_map/ppermute | solution.py:605
  53.5 10.0 %collective-permute-start.15 = (bf16[32,32,128]{2,1,0:T(8,128)(2,1)S(1)}, bf16[32,32,128]{2,1,0:T(8,128)(2,1)S(1)}, u32[]{:S(2)}, u32[]{:S(2)}) collective-permute-start(bf16[32,32,128]{2,1,0:T(8,128)(2,1)S(1)} %get-tuple-element.90), channel_id=1, source_target_pairs={{0,96},{2,98},{4,100},{6,102},{8,104},{10,106},{12,108},{14,110},{... | collective-permute-start | bytes 786440 | tf_op jit(solution)/shard_map/ppermute | solution.py:605
  55.2 9.6 %collective-permute-start.16 = (bf16[32,32,128]{2,1,0:T(8,128)(2,1)S(1)}, bf16[32,32,128]{2,1,0:T(8,128)(2,1)S(1)}, u32[]{:S(2)}, u32[]{:S(2)}) collective-permute-start(bf16[32,32,128]{2,1,0:T(8,128)(2,1)S(1)} %get-tuple-element.92), channel_id=1, source_target_pairs={{0,18},{2,16},{4,22},{6,20},{8,26},{10,24},{12,30},{14,28},{16,2},... | collective-permute-start | bytes 786440 | tf_op jit(solution)/shard_map/ppermute | solution.py:605
  62.1 5.6 %collective-permute-start.19 = (bf16[288,768]{1,0:T(8,128)(2,1)S(1)}, bf16[288,768]{1,0:T(8,128)(2,1)S(1)}, u32[]{:S(2)}, u32[]{:S(2)}) collective-permute-start(bf16[288,768]{1,0:T(8,128)(2,1)S(1)} %get-tuple-element.97.nm_own), channel_id=1, source_target_pairs={{0,1},{1,0},{2,3},{3,2},{4,5},{5,4},{6,7},{7,6},{8,9},{9,8},{10,11... | collective-permute-start | bytes 1327112 | tf_op jit(solution)/shard_map/ppermute | solution.py:592
  62.2 25.2 %collective-permute-start.10 = (bf16[64,512]{1,0:T(8,128)(2,1)S(1)}, bf16[64,512]{1,0:T(8,128)(2,1)S(1)}, u32[]{:S(2)}, u32[]{:S(2)}) collective-permute-start(bf16[64,512]{1,0:T(8,128)(2,1)S(1)} %get-tuple-element.82), channel_id=1, source_target_pairs={{0,16},{1,17},{2,18},{3,19},{4,20},{5,21},{6,22},{7,23},{8,24},{9,... | collective-permute-start | bytes 196616 | tf_op jit(solution)/shard_map/ppermute | solution.py:587
  63.5 23.9 %collective-permute-start.9 = (bf16[64,512]{1,0:T(8,128)(2,1)S(1)}, bf16[64,512]{1,0:T(8,128)(2,1)S(1)}, u32[]{:S(2)}, u32[]{:S(2)}) collective-permute-start(bf16[64,512]{1,0:T(8,128)(2,1)S(1)} %get-tuple-element.81), channel_id=1, source_target_pairs={{0,1},{1,2},{2,3},{3,4},{4,5},{5,6},{6,7},{7,8},{8,9},{9,10},{10,1... | collective-permute-start | bytes 196616 | tf_op jit(solution)/shard_map/ppermute | solution.py:587
  64.9 22.6 %collective-permute-start.11 = (bf16[32,512]{1,0:T(8,128)(2,1)S(1)}, bf16[32,512]{1,0:T(8,128)(2,1)S(1)}, u32[]{:S(2)}, u32[]{:S(2)}) collective-permute-start(bf16[32,512]{1,0:T(8,128)(2,1)S(1)} %get-tuple-element.83), channel_id=1, source_target_pairs={{0,17},{1,18},{2,19},{3,20},{4,21},{5,22},{6,23},{7,24},{8,25},{9,... | collective-permute-start | bytes 98312 | tf_op jit(solution)/shard_map/ppermute | solution.py:587
  67.7 7.3 %collective-permute-start.17 = (bf16[32,32,128]{2,1,0:T(8,128)(2,1)S(1)}, bf16[32,32,128]{2,1,0:T(8,128)(2,1)S(1)}, u32[]{:S(2)}, u32[]{:S(2)}) collective-permute-start(bf16[32,32,128]{2,1,0:T(8,128)(2,1)S(1)} %get-tuple-element.94), channel_id=1, source_target_pairs={{0,2},{2,0},{4,6},{6,4},{8,10},{10,8},{12,14},{14,12},{16,18},{18,... | collective-permute-start | bytes 786440 | tf_op jit(solution)/shard_map/ppermute | solution.py:605
  67.8 7.3 %collective-permute-start.18 = (bf16[32,32,128]{2,1,0:T(8,128)(2,1)S(1)}, bf16[32,32,128]{2,1,0:T(8,128)(2,1)S(1)}, u32[]{:S(2)}, u32[]{:S(2)}) collective-permute-start(bf16[32,32,128]{2,1,0:T(8,128)(2,1)S(1)} %get-tuple-element.96), channel_id=1, source_target_pairs={{0,32},{2,34},{4,36},{6,38},{8,40},{10,42},{12,44},{14,46},{16,48}... | collective-permute-start | bytes 786440 | tf_op jit(solution)/shard_map/ppermute | solution.py:605
  76.3 9.5 %copy-start.8 = (bf16[288,288]{1,0:T(8,128)(2,1)S(1)}, bf16[288,288]{1,0:T(8,128)(2,1)}, u32[]{:S(2)}) copy-start(bf16[288,288]{1,0:T(8,128)(2,1)} %constant.78.clone.main) | copy-start | bytes 497668
  76.3 27.6 %all-to-all-start = ((bf16[64,64,128]{2,1,0:T(8,128)(2,1)}), bf16[64,64,128]{2,1,0:T(8,128)(2,1)S(1)}, u32[]{:S(2)}, u32[]{:S(2)}) async-start(bf16[64,64,128]{2,1,0:T(8,128)(2,1)} %bitcast.4), calls=%async_computation | async-start | bytes 2097152 | tf_op jit(solution)/shard_map/all_to_all | solution.py:609
  85.8 0.8 copy-start.20
  85.8 0.8 copy-start.22
  86.6 0.9 copy-start.13
